TPU v7x, 32 devices: a whole 2x2x4 slice. The times are simulated.
32 devices in a mesh: section: 2 (over x), dp: 4 (over z), tensor: 4 (over y, core).
Axes of the slice: x: 2, y: 2, z: 4, core: 2. Of those that a mesh axis runs over, the one named last changes fastest.
Arguments:
- boundary: bfloat16 [2, 8, 1024, 1024], P('section', 'dp', 'tensor'), may hold values from -6 to 6
- norm_gain: float32 [2, 2, 1024], P('section'), may hold values from 0.5 to 1.5
- mix_in: bfloat16 [2, 1024, 2048], P('section', 'dp', 'tensor'), may hold values from -0.1875 to 0.1875
- mix_out: bfloat16 [2, 1024, 1024], P('section', 'tensor', 'dp'), may hold values from -0.375 to 0.375
- w_gate: bfloat16 [2, 1024, 4608], P('section', 'dp', 'tensor'), may hold values from -0.1875 to 0.1875
- w_up: bfloat16 [2, 1024, 4608], P('section', 'dp', 'tensor'), may hold values from -0.1875 to 0.1875
- w_down: bfloat16 [2, 4608, 1024], P('section', 'tensor', 'dp'), may hold values from -0.09375 to 0.09375
- conv_x: bfloat16 [1024, 1024], P(('section', 'dp'), 'tensor'), may hold values from -0.1875 to 0.1875
- conv_kernel: float32 [3, 1024], P(None, 'tensor'), may hold values from -3 to 3
- qk_gain: float32 [2, 64], replicated, may hold values from 0.7 to 1.6, as said below
Outputs:
- result: bfloat16 [2, 8, 1024, 1024], P('section', 'dp', 'tensor')
- grad_norm_gain: float32 [2, 2, 1024], P('section')
- grad_mix_in: float32 [2, 1024, 2048], P('section', 'dp', 'tensor')
- grad_mix_out: float32 [2, 1024, 1024], P('section', 'tensor', 'dp')
- grad_w_gate: float32 [2, 1024, 4608], P('section', 'dp', 'tensor')
- grad_w_up: float32 [2, 1024, 4608], P('section', 'dp', 'tensor')
- grad_w_down: float32 [2, 4608, 1024], P('section', 'tensor', 'dp')
- grad_conv_x: float32 [1024, 1024], P(('section', 'dp'), 'tensor')
- grad_conv_kernel: float32 [3, 1024], P(None, 'tensor')
- grad_qk_gain: float32 [2, 64], replicated
Inputs may be any that keep to these rules, and one draw needn't show every extreme that they name: `qk_gain`: positive per-entry gains.
All inputs are finite; a program needn't handle non-finite values.
Results may differ from a plain program's by a relative error of at most 0.018.
The roundings to bfloat16 on the way count: a program that leaves them out, or rounds other values in their place, can miss the bound.
Values may be sent and summed in bfloat16 or wider, within the bound.
A program may use at most 192 MiB of HBM per device.

v0:
```python
import jax
import jax.numpy as jnp
from jax import lax
from jax.sharding import PartitionSpec as P

HEADS = 16
KV_HEADS = 8


EPS = 1e-05
ROPE_BASE = 1000000.0
MASKED = -1e30


def shifted(shard, axis, by):
    peers = lax.axis_size(axis)
    pairs = [(i, i + by) for i in range(peers) if 0 <= i + by < peers]
    return lax.ppermute(shard, axis, pairs)


def matmul(left_op, right_op):
    return jnp.dot(left_op, right_op, preferred_element_type=jnp.float32)


def contract_rows(left_op, right_op):
    return lax.dot_general(
        left_op, right_op, (((0,), (0,)), ((), ())), preferred_element_type=jnp.float32
    )


def contract_cols(left_op, right_op):
    return lax.dot_general(
        left_op, right_op, (((1,), (1,)), ((), ())), preferred_element_type=jnp.float32
    )


def norm_rows(values, gain):
    return values * lax.rsqrt(jnp.mean(values * values, axis=-1, keepdims=True) + EPS) * gain


def norm_back(values, gain, grad_in):
    row_scale = lax.rsqrt(jnp.mean(values * values, axis=-1, keepdims=True) + EPS)
    normed = values * row_scale
    feature_count = values.shape[-1]
    gain_grad = jnp.sum((grad_in * normed).reshape(-1, feature_count), axis=0)
    scaled = grad_in * gain
    value_grad = row_scale * (scaled - normed * jnp.mean(scaled * normed, axis=-1, keepdims=True))
    return (value_grad, gain_grad)


def rotation(length, head_size):
    half_size = head_size // 2
    frequency = ROPE_BASE ** (-(jnp.arange(half_size, dtype=jnp.float32) * 2.0 / head_size))
    angles = jnp.arange(length, dtype=jnp.float32)[:, None] * frequency[None, :]
    cosine_table = jnp.concatenate([jnp.cos(angles), jnp.cos(angles)], axis=1)
    sine_table = jnp.concatenate([jnp.sin(angles), jnp.sin(angles)], axis=1)
    return (cosine_table, sine_table)


def rotate(values, cosine_table, sine_table):
    half_size = values.shape[-1] // 2
    turned = jnp.concatenate([-values[..., half_size:], values[..., :half_size]], axis=-1)
    return values * cosine_table + turned * sine_table


def rotate_back(grad_in, cosine_table, sine_table):
    half_size = grad_in.shape[-1] // 2
    shifted_grad = grad_in * sine_table
    return grad_in * cosine_table + jnp.concatenate(
        [shifted_grad[..., half_size:], -shifted_grad[..., :half_size]], axis=-1
    )


def delayed(values, delay_by):
    if delay_by == 0:
        return values
    return jnp.concatenate(
        [jnp.zeros((delay_by, values.shape[1]), values.dtype), values[:-delay_by]], axis=0
    )


def advanced(values, delay_by):
    if delay_by == 0:
        return values
    return jnp.concatenate(
        [values[delay_by:], jnp.zeros((delay_by, values.shape[1]), values.dtype)], axis=0
    )


def spread(row_part):
    return lax.all_gather(row_part, "tensor", axis=0, tiled=True)


def collect(partial_value):
    return lax.psum_scatter(partial_value, "tensor", scatter_dimension=0, tiled=True)


def total_shape(length, w_cols, head_gain):
    group_size = HEADS // KV_HEADS
    kv_local = w_cols.shape[1] // head_gain.shape[1] // group_size
    return (kv_local, group_size, length)


def conv_parts(normed_in, w_in, w_cols, kernel):
    channels = w_cols.shape[1]
    projected = matmul(normed_in, w_in)
    b_gate = projected[:, :channels]
    c_gate = projected[:, channels:]
    x_value = matmul(normed_in, w_cols)
    product = b_gate * x_value
    tap_count = kernel.shape[0]
    causal = jnp.zeros_like(product)
    for offset in range(tap_count):
        causal = causal + kernel[offset] * delayed(product, tap_count - 1 - offset)
    return (b_gate, c_gate, x_value, product, causal)


def conv_forward(operands):
    normed_in, w_in, w_cols, kernel, head_gain = operands
    b_gate, c_gate, x_value, product, causal = conv_parts(normed_in, w_in, w_cols, kernel)
    empty_total = jnp.zeros(total_shape(normed_in.shape[0], w_cols, head_gain), jnp.float32)
    return ((c_gate * causal).astype(jnp.bfloat16), empty_total)


def conv_backward(operands):
    normed_in, grad_y, log_total, w_in, w_cols, kernel, head_gain = operands
    b_gate, c_gate, x_value, product, causal = conv_parts(normed_in, w_in, w_cols, kernel)
    grad_c = grad_y * causal
    grad_causal = grad_y * c_gate
    tap_count = kernel.shape[0]
    kernel_rows = []
    grad_product = jnp.zeros_like(product)
    for offset in range(tap_count):
        delay_by = tap_count - 1 - offset
        kernel_rows.append(jnp.sum(grad_causal * delayed(product, delay_by), axis=0))
        grad_product = grad_product + kernel[offset] * advanced(grad_causal, delay_by)
    kernel_grad = jnp.stack(kernel_rows)
    grad_proj = jnp.concatenate([grad_product * x_value, grad_c], axis=1).astype(jnp.bfloat16)
    grad_value = (grad_product * b_gate).astype(jnp.bfloat16)
    in_grad = contract_rows(normed_in, grad_proj)
    cols_grad = contract_rows(normed_in, grad_value)
    input_grad = contract_cols(grad_proj, w_in) + contract_cols(grad_value, w_cols)
    return (input_grad, in_grad, cols_grad, kernel_grad, jnp.zeros_like(head_gain))


def attention_inputs(normed_in, w_in, head_gain):
    length = normed_in.shape[0]
    group_width = w_in.shape[1] // 2
    head_size = head_gain.shape[1]
    group_size = HEADS // KV_HEADS
    kv_local = group_width // head_size // group_size
    projected = matmul(normed_in, w_in)
    queries = projected[:, :group_width].reshape(length, kv_local, group_size, head_size)
    key_part = projected[:, group_width : group_width + group_width // 2].reshape(
        length, kv_local, head_size
    )
    values = projected[:, group_width + group_width // 2 :].reshape(length, kv_local, head_size)
    cosine_table, sine_table = rotation(length, head_size)
    q_rot = rotate(
        norm_rows(queries, head_gain[0]),
        cosine_table[:, None, None, :],
        sine_table[:, None, None, :],
    ).astype(jnp.bfloat16)
    k_rot = rotate(
        norm_rows(key_part, head_gain[1]), cosine_table[:, None, :], sine_table[:, None, :]
    ).astype(jnp.bfloat16)
    return (queries, key_part, q_rot, k_rot, values.astype(jnp.bfloat16), cosine_table, sine_table)


def masked_scores(q_piece, k_rot, first_row, length):
    row_block = q_piece.shape[0]
    score_scale = q_piece.shape[-1] ** (-0.5)
    scores = (
        jnp.einsum("ahgd,bhd->hgab", q_piece, k_rot, preferred_element_type=jnp.float32)
        * score_scale
    )
    query_pos = first_row + jnp.arange(row_block, dtype=jnp.int32)
    key_pos = jnp.arange(length, dtype=jnp.int32)
    allowed = key_pos[None, :] <= query_pos[:, None]
    return jnp.where(allowed, scores, MASKED)


def attention_forward(operands):
    normed_in, w_in, w_cols, kernel, head_gain = operands
    parts = attention_inputs(normed_in, w_in, head_gain)
    q_rot, k_rot, v_low = (parts[2], parts[3], parts[4])
    length = normed_in.shape[0]
    row_block = min(512, length)
    out_blocks = []
    total_blocks = []
    for first_row in range(0, length, row_block):
        scores = masked_scores(q_rot[first_row : first_row + row_block], k_rot, first_row, length)
        row_max = jnp.max(scores, axis=-1, keepdims=True)
        exp_scores = jnp.exp(scores - row_max)
        row_sum = jnp.sum(exp_scores, axis=-1, keepdims=True)
        weights = (exp_scores / row_sum).astype(jnp.bfloat16)
        attended = jnp.einsum("hgab,bhd->ahgd", weights, v_low, preferred_element_type=jnp.float32)
        out_blocks.append(attended.reshape(row_block, -1))
        total_blocks.append((row_max + jnp.log(row_sum))[..., 0])
    return (
        jnp.concatenate(out_blocks, axis=0).astype(jnp.bfloat16),
        jnp.concatenate(total_blocks, axis=-1),
    )


def attention_backward(operands):
    normed_in, grad_y, log_total, w_in, w_cols, kernel, head_gain = operands
    queries, key_part, q_rot, k_rot, v_low, cosine_table, sine_table = attention_inputs(
        normed_in, w_in, head_gain
    )
    length, kv_local, group_size, head_size = queries.shape
    score_scale = head_size ** (-0.5)
    row_block = min(512, length)
    grad_low = grad_y.astype(jnp.bfloat16).reshape(length, kv_local, group_size, head_size)
    q_grads = []
    key_grad = jnp.zeros((length, kv_local, head_size), jnp.float32)
    value_grad = jnp.zeros((length, kv_local, head_size), jnp.float32)
    for first_row in range(0, length, row_block):
        q_piece = q_rot[first_row : first_row + row_block]
        scores = masked_scores(q_piece, k_rot, first_row, length)
        probability = jnp.exp(scores - log_total[:, :, first_row : first_row + row_block, None])
        weights = probability.astype(jnp.bfloat16)
        grad_piece = grad_low[first_row : first_row + row_block]
        grad_weights = jnp.einsum(
            "ahgd,bhd->hgab", grad_piece, v_low, preferred_element_type=jnp.float32
        )
        value_grad = value_grad + jnp.einsum(
            "hgab,ahgd->bhd", weights, grad_piece, preferred_element_type=jnp.float32
        )
        grad_scores = probability * (
            grad_weights - jnp.sum(probability * grad_weights, axis=-1, keepdims=True)
        )
        grad_scores = grad_scores.astype(jnp.bfloat16)
        q_grads.append(
            jnp.einsum("hgab,bhd->ahgd", grad_scores, k_rot, preferred_element_type=jnp.float32)
            * score_scale
        )
        key_grad = (
            key_grad
            + jnp.einsum("hgab,ahgd->bhd", grad_scores, q_piece, preferred_element_type=jnp.float32)
            * score_scale
        )
    query_grad = jnp.concatenate(q_grads, axis=0)
    query_grad = rotate_back(
        query_grad, cosine_table[:, None, None, :], sine_table[:, None, None, :]
    )
    key_grad = rotate_back(key_grad, cosine_table[:, None, :], sine_table[:, None, :])
    query_raw, q_gain_grad = norm_back(queries, head_gain[0], query_grad)
    key_raw, k_gain_grad = norm_back(key_part, head_gain[1], key_grad)
    grad_proj = jnp.concatenate(
        [
            query_raw.reshape(length, -1),
            key_raw.reshape(length, -1),
            value_grad.reshape(length, -1),
        ],
        axis=1,
    ).astype(jnp.bfloat16)
    in_grad = contract_rows(normed_in, grad_proj)
    input_grad = contract_cols(grad_proj, w_in)
    return (
        input_grad,
        in_grad,
        jnp.zeros(w_cols.shape, jnp.float32),
        jnp.zeros_like(kernel),
        jnp.stack([q_gain_grad, k_gain_grad]),
    )


def block_forward(row_part, norm_gains, matrices, extras, conv_section):
    w_in, w_out, gate_w, up_w, down_w = matrices
    w_cols, kernel, head_gain = extras
    normed_in = spread(norm_rows(row_part, norm_gains[0]).astype(jnp.bfloat16))
    mixer_out, log_total = lax.cond(
        conv_section, conv_forward, attention_forward, (normed_in, w_in, w_cols, kernel, head_gain)
    )
    middle = row_part + collect(matmul(mixer_out, w_out))
    normed_mid = spread(norm_rows(middle, norm_gains[1]).astype(jnp.bfloat16))
    gate_pre = matmul(normed_mid, gate_w)
    up_pre = matmul(normed_mid, up_w)
    hidden = (gate_pre * jax.nn.sigmoid(gate_pre) * up_pre).astype(jnp.bfloat16)
    block_out = middle + collect(matmul(hidden, down_w))
    return (block_out, (row_part, normed_in, mixer_out, log_total, middle, normed_mid))


def block_backward(grad_out, saved_now, norm_gains, matrices, extras, conv_section):
    row_part, normed_in, mixer_out, log_total, middle, normed_mid = saved_now
    w_in, w_out, gate_w, up_w, down_w = matrices
    w_cols, kernel, head_gain = extras
    grad_full = spread(grad_out.astype(jnp.bfloat16))
    gate_pre = matmul(normed_mid, gate_w)
    up_pre = matmul(normed_mid, up_w)
    gate_sig = jax.nn.sigmoid(gate_pre)
    gate_silu = gate_pre * gate_sig
    hidden = (gate_silu * up_pre).astype(jnp.bfloat16)
    down_grad = contract_rows(hidden, grad_full)
    grad_hidden = contract_cols(grad_full, down_w)
    grad_gate = (grad_hidden * up_pre * gate_sig * (1.0 + gate_pre * (1.0 - gate_sig))).astype(
        jnp.bfloat16
    )
    grad_up = (grad_hidden * gate_silu).astype(jnp.bfloat16)
    gate_grad = contract_rows(normed_mid, grad_gate)
    up_grad = contract_rows(normed_mid, grad_up)
    grad_norm_mid = collect(contract_cols(grad_gate, gate_w) + contract_cols(grad_up, up_w))
    grad_middle, mid_gain_grad = norm_back(middle, norm_gains[1], grad_norm_mid)
    grad_middle = grad_middle + grad_out
    grad_branch = spread(grad_middle.astype(jnp.bfloat16))
    out_grad = contract_rows(mixer_out, grad_branch)
    grad_mixer = contract_cols(grad_branch, w_out)
    input_grad, in_grad, cols_grad, kernel_grad, head_grad = lax.cond(
        conv_section,
        conv_backward,
        attention_backward,
        (normed_in, grad_mixer, log_total, w_in, w_cols, kernel, head_gain),
    )
    grad_rows, in_gain_grad = norm_back(row_part, norm_gains[0], collect(input_grad))
    grad_rows = grad_rows + grad_middle
    new_terms = (
        in_grad,
        out_grad,
        gate_grad,
        up_grad,
        down_grad,
        cols_grad,
        kernel_grad,
        head_grad,
        jnp.stack([in_gain_grad, mid_gain_grad]),
    )
    return (grad_rows, new_terms)


def store(buffer, new_item, slot_index, is_live):
    old_item = lax.dynamic_index_in_dim(buffer, slot_index, 0, keepdims=False)
    return lax.dynamic_update_index_in_dim(
        buffer, jnp.where(is_live, new_item, old_item), slot_index, 0
    )


def body(boundary, norm_gain, mix_in, mix_out, w_gate, w_up, w_down, conv_x, conv_kernel, qk_gain):
    section_index = lax.axis_index("section")
    conv_section = section_index == 0
    micro_count = boundary.shape[1]
    row_count = boundary.shape[2]
    model_width = boundary.shape[3]
    seq_rows = row_count * lax.axis_size("tensor")
    channels = mix_out.shape[1]
    norm_gains = norm_gain[0]
    w_cols = lax.all_gather(conv_x, ("section", "dp"), axis=0, tiled=True)
    extras = (w_cols, conv_kernel, qk_gain)

    def fetch_weights():
        return (
            lax.all_gather(mix_in[0], "dp", axis=0, tiled=True),
            lax.all_gather(mix_out[0], "dp", axis=1, tiled=True),
            lax.all_gather(w_gate[0], "dp", axis=0, tiled=True),
            lax.all_gather(w_up[0], "dp", axis=0, tiled=True),
            lax.all_gather(w_down[0], "dp", axis=1, tiled=True),
        )

    log_shape = total_shape(seq_rows, w_cols, qk_gain)
    saved_start = (
        jnp.zeros((micro_count, row_count, model_width), jnp.float32),
        jnp.zeros((micro_count, seq_rows, model_width), jnp.bfloat16),
        jnp.zeros((micro_count, seq_rows, channels), jnp.bfloat16),
        jnp.zeros((micro_count,) + log_shape, jnp.float32),
        jnp.zeros((micro_count, row_count, model_width), jnp.float32),
        jnp.zeros((micro_count, seq_rows, model_width), jnp.bfloat16),
    )
    produced_start = jnp.zeros((micro_count, row_count, model_width), jnp.bfloat16)
    incoming_start = jnp.zeros((row_count, model_width), jnp.bfloat16)

    def forward_step(step_index, loop_state):
        incoming, saved, produced = loop_state
        mb_index = step_index - section_index
        is_live = (mb_index >= 0) & (mb_index < micro_count)
        slot_index = jnp.clip(mb_index, 0, micro_count - 1)
        own_rows = lax.dynamic_index_in_dim(boundary[0], slot_index, 0, keepdims=False)
        row_part = jnp.where(conv_section, own_rows, incoming).astype(jnp.float32)
        block_out, fresh = block_forward(
            row_part, norm_gains, fetch_weights(), extras, conv_section
        )
        saved = tuple(
            (store(buffer, new_item, slot_index, is_live) for buffer, new_item in zip(saved, fresh))
        )
        out_low = block_out.astype(jnp.bfloat16)
        produced = store(produced, out_low, slot_index, is_live & jnp.logical_not(conv_section))
        incoming = shifted(out_low, "section", 1)
        return (incoming, saved, produced)

    unused_rows, saved, produced = lax.fori_loop(
        0, micro_count + 1, forward_step, (incoming_start, saved_start, produced_start)
    )
    in_width = mix_in.shape[2]
    hidden_local = w_gate.shape[2]
    grad_start = (
        jnp.zeros((model_width, in_width), jnp.float32),
        jnp.zeros((channels, model_width), jnp.float32),
        jnp.zeros((model_width, hidden_local), jnp.float32),
        jnp.zeros((model_width, hidden_local), jnp.float32),
        jnp.zeros((hidden_local, model_width), jnp.float32),
        jnp.zeros((model_width, channels), jnp.float32),
        jnp.zeros(conv_kernel.shape, jnp.float32),
        jnp.zeros(qk_gain.shape, jnp.float32),
        jnp.zeros((2, model_width), jnp.float32),
    )

    def backward_step(step_index, loop_state):
        incoming, produced, grad_sums = loop_state
        mb_index = step_index - 1 + section_index
        is_live = (mb_index >= 0) & (mb_index < micro_count)
        slot_index = jnp.clip(mb_index, 0, micro_count - 1)
        own_rows = lax.dynamic_index_in_dim(boundary[0], slot_index, 0, keepdims=False)
        grad_out = jnp.where(conv_section, incoming, own_rows).astype(jnp.float32)
        saved_now = tuple(
            (lax.dynamic_index_in_dim(buffer, slot_index, 0, keepdims=False) for buffer in saved)
        )
        grad_rows, new_terms = block_backward(
            grad_out, saved_now, norm_gains, fetch_weights(), extras, conv_section
        )
        grad_sums = tuple(
            (
                running + jnp.where(is_live, new_term, 0.0)
                for running, new_term in zip(grad_sums, new_terms)
            )
        )
        sent_rows = grad_rows.astype(jnp.bfloat16)
        produced = store(produced, sent_rows, slot_index, is_live & conv_section)
        incoming = shifted(sent_rows, "section", -1)
        return (incoming, produced, grad_sums)

    unused_grad, produced, grad_sums = lax.fori_loop(
        0, micro_count + 1, backward_step, (incoming_start, produced, grad_start)
    )
    in_sum, out_sum, gate_sum, up_sum, down_sum, cols_sum, kernel_sum, head_sum, norm_sum = (
        grad_sums
    )
    weight_parts = (
        lax.psum_scatter(in_sum, "dp", scatter_dimension=0, tiled=True),
        lax.psum_scatter(out_sum, "dp", scatter_dimension=1, tiled=True),
        lax.psum_scatter(gate_sum, "dp", scatter_dimension=0, tiled=True),
        lax.psum_scatter(up_sum, "dp", scatter_dimension=0, tiled=True),
        lax.psum_scatter(down_sum, "dp", scatter_dimension=1, tiled=True),
    )
    cols_part = lax.psum_scatter(cols_sum, ("section", "dp"), scatter_dimension=0, tiled=True)
    tensor_index = lax.axis_index("tensor")
    kernel_full = lax.dynamic_update_slice_in_dim(
        jnp.zeros((conv_kernel.shape[0], model_width), jnp.float32),
        kernel_sum,
        tensor_index * channels,
        1,
    )
    empty_gain = jnp.zeros_like(norm_sum)
    gains_full = jnp.where(
        conv_section, jnp.stack([norm_sum, empty_gain]), jnp.stack([empty_gain, norm_sum])
    )
    gains_total, kernel_total, head_total = lax.psum(
        (gains_full, kernel_full, head_sum), ("section", "dp", "tensor")
    )
    gain_out = lax.dynamic_slice_in_dim(gains_total, section_index, 1, 0)
    kernel_out = lax.dynamic_slice_in_dim(kernel_total, tensor_index * channels, channels, 1)
    return (
        produced[None],
        gain_out,
        weight_parts[0][None],
        weight_parts[1][None],
        weight_parts[2][None],
        weight_parts[3][None],
        weight_parts[4][None],
        cols_part,
        kernel_out,
        head_total,
    )


def solution(mesh):
    in_specs = (
        P("section", "dp", "tensor", None),
        P("section", None, None),
        P("section", "dp", "tensor"),
        P("section", "tensor", "dp"),
        P("section", "dp", "tensor"),
        P("section", "dp", "tensor"),
        P("section", "tensor", "dp"),
        P(("section", "dp"), "tensor"),
        P(None, "tensor"),
        P(),
    )
    out_specs = (
        P("section", "dp", "tensor", None),
        P("section", None, None),
        P("section", "dp", "tensor"),
        P("section", "tensor", "dp"),
        P("section", "dp", "tensor"),
        P("section", "dp", "tensor"),
        P("section", "tensor", "dp"),
        P(("section", "dp"), "tensor"),
        P(None, "tensor"),
        P(),
    )
    return jax.shard_map(body, mesh=mesh, in_specs=in_specs, out_specs=out_specs, check_vma=False)
```

profile of v0, /device:TPU:0, one launch (start us, length us, event | category | flops | bytes accessed | tf_op | source)
XLA Modules:
  0.0 2869.2 jit_solution(2567316851110948855)
XLA Ops:
  8.1 36.4 %all_gather.129 = bf16[1024,256]{1,0:T(8,128)(2,1)} all-gather(bf16[128,256]{1,0:T(8,128)(2,1)} %param.25), channel_id=1, replica_groups=mesh['section'=2,'dp'=4,'tensor'=4] {'section','dp'}, dimensions={0}, use_global_device_ids=true | all-gather | bytes 589824 | tf_op jit(solution)/shard_map/all_gather | solution.py:347
  55.9 1125.6 %while.64 = (s32[]{:T(128)}, bf16[256,1024]{1,0:T(8,128)(2,1)}, f32[2,256,1024]{2,1,0:T(8,128)}, bf16[2,1024,1024]{2,1,0:T(8,128)(2,1)}, bf16[2,1024,256]{1,2,0:...) while((s32[]{:T(128)}, bf16[256,1024]{1,0:T(8,128)(2,1)}, ...), condition=%wide.region_13.14_spmd, body=%wide.region_0.13_spmd.sunk | while | flops 10006014976 | bytes 326188832 | solution.py:389
  90.0 24.9 all-gather.50.cloned.1.call-done
  124.0 57.3 %reduce-scatter.23.cloned.1.call-done = f32[256,1024]{1,0:T(8,128)} async-done(((f32[1024,1024]{1,0:T(8,128)}), f32[256,1024]{1,0:T(8,128)}) %reduce-scatter.23.cloned.1.call-update) | async-done | bytes 1048592 | tf_op jit(solution)/shard_map/while/body/eval_jaxpr/reduce_scatter | solution.py:95
  186.4 46.4 %all-gather.56.cloned.1.call-done = bf16[1,1024,1152]{2,1,0:T(8,128)(2,1)} async-done(((bf16[1,256,1152]{2,1,0:T(8,128)(2,1)}), bf16[1,1024,1152]{2,1,0:T(8,128)(2,1)}) %all-gather.56.cloned.1.call-update) | async-done | bytes 2359312 | tf_op jit(solution)/shard_map/while/body/eval_jaxpr/all_gather | solution.py:354
  232.8 23.3 all-gather.54.cloned.1.call-done
  263.6 44.5 %all-gather.48.cloned.1.call-done = bf16[1,1152,1024]{2,1,0:T(8,128)(2,1)} async-done(((bf16[1,1152,256]{2,1,0:T(8,128)(2,1)}), bf16[1,1152,1024]{2,1,0:T(8,128)(2,1)}) %all-gather.48.cloned.1.call-update) | async-done | bytes 2359312 | tf_op jit(solution)/shard_map/while/body/eval_jaxpr/all_gather | solution.py:356
  308.1 49.8 %all-gather.58.cloned.1.call-done = bf16[1,1024,1152]{2,1,0:T(8,128)(2,1)} async-done(((bf16[1,256,1152]{2,1,0:T(8,128)(2,1)}), bf16[1,1024,1152]{2,1,0:T(8,128)(2,1)}) %all-gather.58.cloned.1.call-update) | async-done | bytes 2359312 | tf_op jit(solution)/shard_map/while/body/eval_jaxpr/all_gather | solution.py:355
  380.9 32.0 %reduce-scatter.25.cloned.1.call-done = f32[256,1024]{1,0:T(8,128)} async-done(((f32[1024,1024]{1,0:T(8,128)}), f32[256,1024]{1,0:T(8,128)}) %reduce-scatter.25.cloned.1.call-update) | async-done | bytes 1048592 | tf_op jit(solution)/shard_map/while/body/eval_jaxpr/reduce_scatter | solution.py:95
  466.3 24.4 all-gather.50.cloned.1.call-done
  499.8 57.3 %reduce-scatter.23.cloned.1.call-done = f32[256,1024]{1,0:T(8,128)} async-done(((f32[1024,1024]{1,0:T(8,128)}), f32[256,1024]{1,0:T(8,128)}) %reduce-scatter.23.cloned.1.call-update) | async-done | bytes 1048592 | tf_op jit(solution)/shard_map/while/body/eval_jaxpr/reduce_scatter | solution.py:95
  562.0 46.5 %all-gather.56.cloned.1.call-done = bf16[1,1024,1152]{2,1,0:T(8,128)(2,1)} async-done(((bf16[1,256,1152]{2,1,0:T(8,128)(2,1)}), bf16[1,1024,1152]{2,1,0:T(8,128)(2,1)}) %all-gather.56.cloned.1.call-update) | async-done | bytes 2359312 | tf_op jit(solution)/shard_map/while/body/eval_jaxpr/all_gather | solution.py:354
  608.5 23.5 all-gather.54.cloned.1.call-done
  639.5 44.5 %all-gather.48.cloned.1.call-done = bf16[1,1152,1024]{2,1,0:T(8,128)(2,1)} async-done(((bf16[1,1152,256]{2,1,0:T(8,128)(2,1)}), bf16[1,1152,1024]{2,1,0:T(8,128)(2,1)}) %all-gather.48.cloned.1.call-update) | async-done | bytes 2359312 | tf_op jit(solution)/shard_map/while/body/eval_jaxpr/all_gather | solution.py:356
  684.0 49.6 %all-gather.58.cloned.1.call-done = bf16[1,1024,1152]{2,1,0:T(8,128)(2,1)} async-done(((bf16[1,256,1152]{2,1,0:T(8,128)(2,1)}), bf16[1,1024,1152]{2,1,0:T(8,128)(2,1)}) %all-gather.58.cloned.1.call-update) | async-done | bytes 2359312 | tf_op jit(solution)/shard_map/while/body/eval_jaxpr/all_gather | solution.py:355
  756.6 31.9 %reduce-scatter.25.cloned.1.call-done = f32[256,1024]{1,0:T(8,128)} async-done(((f32[1024,1024]{1,0:T(8,128)}), f32[256,1024]{1,0:T(8,128)}) %reduce-scatter.25.cloned.1.call-update) | async-done | bytes 1048592 | tf_op jit(solution)/shard_map/while/body/eval_jaxpr/reduce_scatter | solution.py:95
  841.4 24.9 all-gather.50.cloned.1.call-done
  875.4 57.3 %reduce-scatter.23.cloned.1.call-done = f32[256,1024]{1,0:T(8,128)} async-done(((f32[1024,1024]{1,0:T(8,128)}), f32[256,1024]{1,0:T(8,128)}) %reduce-scatter.23.cloned.1.call-update) | async-done | bytes 1048592 | tf_op jit(solution)/shard_map/while/body/eval_jaxpr/reduce_scatter | solution.py:95
  937.9 46.2 %all-gather.56.cloned.1.call-done = bf16[1,1024,1152]{2,1,0:T(8,128)(2,1)} async-done(((bf16[1,256,1152]{2,1,0:T(8,128)(2,1)}), bf16[1,1024,1152]{2,1,0:T(8,128)(2,1)}) %all-gather.56.cloned.1.call-update) | async-done | bytes 2359312 | tf_op jit(solution)/shard_map/while/body/eval_jaxpr/all_gather | solution.py:354
  984.1 23.5 all-gather.54.cloned.1.call-done
  1015.1 44.6 %all-gather.48.cloned.1.call-done = bf16[1,1152,1024]{2,1,0:T(8,128)(2,1)} async-done(((bf16[1,1152,256]{2,1,0:T(8,128)(2,1)}), bf16[1,1152,1024]{2,1,0:T(8,128)(2,1)}) %all-gather.48.cloned.1.call-update) | async-done | bytes 2359312 | tf_op jit(solution)/shard_map/while/body/eval_jaxpr/all_gather | solution.py:356
  1059.7 49.8 %all-gather.58.cloned.1.call-done = bf16[1,1024,1152]{2,1,0:T(8,128)(2,1)} async-done(((bf16[1,256,1152]{2,1,0:T(8,128)(2,1)}), bf16[1,1024,1152]{2,1,0:T(8,128)(2,1)}) %all-gather.58.cloned.1.call-update) | async-done | bytes 2359312 | tf_op jit(solution)/shard_map/while/body/eval_jaxpr/all_gather | solution.py:355
  1132.6 31.9 %reduce-scatter.25.cloned.1.call-done = f32[256,1024]{1,0:T(8,128)} async-done(((f32[1024,1024]{1,0:T(8,128)}), f32[256,1024]{1,0:T(8,128)}) %reduce-scatter.25.cloned.1.call-update) | async-done | bytes 1048592 | tf_op jit(solution)/shard_map/while/body/eval_jaxpr/reduce_scatter | solution.py:95
  1181.7 1273.4 %while.65 = (s32[]{:T(128)}, bf16[256,1024]{1,0:T(8,128)(2,1)S(1)}, bf16[2,256,1024]{2,1,0:T(8,128)(2,1)}, f32[1024,512]{0,1:T(8,128)}, f32[256,1024]{1,0:T(8,12...) while((s32[]{:T(128)}, bf16[256,1024]{1,0:T(8,128)(2,1)S(1)}, ...), condition=%wide.region_37.38_spmd.clone, body=%wide.region_14.37_spmd.clone.sunk | while | flops 26438049792 | bytes 682932224 | solution.py:430
  1194.7 49.4 %all-gather.62.cloned.1.call-done = bf16[1,1024,1152]{2,1,0:T(8,128)(2,1)} async-done(((bf16[1,256,1152]{2,1,0:T(8,128)(2,1)}), bf16[1,1024,1152]{2,1,0:T(8,128)(2,1)}) %all-gather.62.cloned.1.call-update) | async-done | bytes 2359312 | tf_op jit(solution)/shard_map/while/body/eval_jaxpr/all_gather | solution.py:355
  1251.4 42.9 %all-gather.60.cloned.1.call-done = bf16[1,1024,1152]{2,1,0:T(8,128)(2,1)} async-done(((bf16[1,256,1152]{2,1,0:T(8,128)(2,1)}), bf16[1,1024,1152]{2,1,0:T(8,128)(2,1)}) %all-gather.60.cloned.1.call-update) | async-done | bytes 2359312 | tf_op jit(solution)/shard_map/while/body/eval_jaxpr/all_gather | solution.py:354
  1317.0 52.1 %all-gather.66.cloned.1.call-done = bf16[1,1152,1024]{2,1,0:T(8,128)(2,1)} async-done(((bf16[1,1152,256]{2,1,0:T(8,128)(2,1)}), bf16[1,1152,1024]{2,1,0:T(8,128)(2,1)}) %all-gather.66.cloned.1.call-update) | async-done | bytes 2359312 | tf_op jit(solution)/shard_map/while/body/eval_jaxpr/all_gather | solution.py:356
  1387.8 41.2 %reduce-scatter.27.cloned.1.call-done = f32[256,1024]{1,0:T(8,128)} async-done(((f32[1024,1024]{1,0:T(8,128)}), f32[256,1024]{1,0:T(8,128)}) %reduce-scatter.27.cloned.1.call-update) | async-done | bytes 1048592 | tf_op jit(solution)/shard_map/while/body/eval_jaxpr/reduce_scatter | solution.py:95
  1458.1 27.2 all-gather.68.cloned.1.call-done
  1527.4 64.1 %reduce-scatter.29.cloned.1.call-done = f32[256,1024]{1,0:T(8,128)} async-done(((f32[1024,1024]{1,0:T(8,128)}), f32[256,1024]{1,0:T(8,128)}) %reduce-scatter.29.cloned.1.call-update) | async-done | bytes 1048592 | tf_op jit(solution)/shard_map/while/body/eval_jaxpr/reduce_scatter | solution.py:95
  1616.8 47.2 %all-gather.62.cloned.1.call-done = bf16[1,1024,1152]{2,1,0:T(8,128)(2,1)} async-done(((bf16[1,256,1152]{2,1,0:T(8,128)(2,1)}), bf16[1,1024,1152]{2,1,0:T(8,128)(2,1)}) %all-gather.62.cloned.1.call-update) | async-done | bytes 2359312 | tf_op jit(solution)/shard_map/while/body/eval_jaxpr/all_gather | solution.py:355
  1671.3 43.1 %all-gather.60.cloned.1.call-done = bf16[1,1024,1152]{2,1,0:T(8,128)(2,1)} async-done(((bf16[1,256,1152]{2,1,0:T(8,128)(2,1)}), bf16[1,1024,1152]{2,1,0:T(8,128)(2,1)}) %all-gather.60.cloned.1.call-update) | async-done | bytes 2359312 | tf_op jit(solution)/shard_map/while/body/eval_jaxpr/all_gather | solution.py:354
  1737.3 52.0 %all-gather.66.cloned.1.call-done = bf16[1,1152,1024]{2,1,0:T(8,128)(2,1)} async-done(((bf16[1,1152,256]{2,1,0:T(8,128)(2,1)}), bf16[1,1152,1024]{2,1,0:T(8,128)(2,1)}) %all-gather.66.cloned.1.call-update) | async-done | bytes 2359312 | tf_op jit(solution)/shard_map/while/body/eval_jaxpr/all_gather | solution.py:356
  1807.9 41.2 %reduce-scatter.27.cloned.1.call-done = f32[256,1024]{1,0:T(8,128)} async-done(((f32[1024,1024]{1,0:T(8,128)}), f32[256,1024]{1,0:T(8,128)}) %reduce-scatter.27.cloned.1.call-update) | async-done | bytes 1048592 | tf_op jit(solution)/shard_map/while/body/eval_jaxpr/reduce_scatter | solution.py:95
  1878.2 27.0 all-gather.68.cloned.1.call-done
  1951.2 60.3 %reduce-scatter.29.cloned.1.call-done = f32[256,1024]{1,0:T(8,128)} async-done(((f32[1024,1024]{1,0:T(8,128)}), f32[256,1024]{1,0:T(8,128)}) %reduce-scatter.29.cloned.1.call-update) | async-done | bytes 1048592 | tf_op jit(solution)/shard_map/while/body/eval_jaxpr/reduce_scatter | solution.py:95
  2037.1 47.2 %all-gather.62.cloned.1.call-done = bf16[1,1024,1152]{2,1,0:T(8,128)(2,1)} async-done(((bf16[1,256,1152]{2,1,0:T(8,128)(2,1)}), bf16[1,1024,1152]{2,1,0:T(8,128)(2,1)}) %all-gather.62.cloned.1.call-update) | async-done | bytes 2359312 | tf_op jit(solution)/shard_map/while/body/eval_jaxpr/all_gather | solution.py:355
  2091.6 43.1 %all-gather.60.cloned.1.call-done = bf16[1,1024,1152]{2,1,0:T(8,128)(2,1)} async-done(((bf16[1,256,1152]{2,1,0:T(8,128)(2,1)}), bf16[1,1024,1152]{2,1,0:T(8,128)(2,1)}) %all-gather.60.cloned.1.call-update) | async-done | bytes 2359312 | tf_op jit(solution)/shard_map/while/body/eval_jaxpr/all_gather | solution.py:354
  2157.5 52.1 %all-gather.66.cloned.1.call-done = bf16[1,1152,1024]{2,1,0:T(8,128)(2,1)} async-done(((bf16[1,1152,256]{2,1,0:T(8,128)(2,1)}), bf16[1,1152,1024]{2,1,0:T(8,128)(2,1)}) %all-gather.66.cloned.1.call-update) | async-done | bytes 2359312 | tf_op jit(solution)/shard_map/while/body/eval_jaxpr/all_gather | solution.py:356
  2228.2 41.2 %reduce-scatter.27.cloned.1.call-done = f32[256,1024]{1,0:T(8,128)} async-done(((f32[1024,1024]{1,0:T(8,128)}), f32[256,1024]{1,0:T(8,128)}) %reduce-scatter.27.cloned.1.call-update) | async-done | bytes 1048592 | tf_op jit(solution)/shard_map/while/body/eval_jaxpr/reduce_scatter | solution.py:95
  2298.5 27.0 all-gather.68.cloned.1.call-done
  2371.6 60.3 %reduce-scatter.29.cloned.1.call-done = f32[256,1024]{1,0:T(8,128)} async-done(((f32[1024,1024]{1,0:T(8,128)}), f32[256,1024]{1,0:T(8,128)}) %reduce-scatter.29.cloned.1.call-update) | async-done | bytes 1048592 | tf_op jit(solution)/shard_map/while/body/eval_jaxpr/reduce_scatter | solution.py:95
  2461.4 40.6 %all-reduce.8 = (f32[2,2,1024]{2,1,0:T(2,128)S(1)}, f32[3,1024]{1,0:T(4,128)S(1)}, f32[2,64]{1,0:T(2,128)}) all-reduce(f32[2,2,1024]{2,1,0:T(2,128)S(1)} %pad_select_fusion, f32[3,1024]{1,0:T(4,128)S(1)} %constant_dynamic-update-slice_fusion, ...), channel_id=1, replica_groups=mesh['section'=2,'dp'=4,'tensor'=4] {'section','dp','tensor'}, use_global_device_ids=true, to_apply=%region_38.39 | all-reduce | flops 7296 | bytes 58368 | tf_op jit(solution)/shard_map/psum | solution.py:455
  2503.2 48.6 %reduce-scatter.21.cloned.1.call-done = f32[128,256]{1,0:T(8,128)} async-done(((f32[1024,256]{1,0:T(8,128)}), f32[128,256]{1,0:T(8,128)}) %reduce-scatter.21.cloned.1.call-update) | async-done | bytes 131088 | tf_op jit(solution)/shard_map/reduce_scatter | solution.py:443
  2551.8 45.4 %reduce-scatter.11.cloned.1.call-done = f32[256,512]{1,0:T(8,128)} async-done(((f32[1024,512]{1,0:T(8,128)}), f32[256,512]{1,0:T(8,128)}) %reduce-scatter.11.cloned.1.call-update) | async-done | bytes 524304 | tf_op jit(solution)/shard_map/reduce_scatter | solution.py:437
  2597.2 87.3 %reduce-scatter.15.cloned.1.call-done = f32[256,1152]{1,0:T(8,128)} async-done(((f32[1024,1152]{1,0:T(8,128)}), f32[256,1152]{1,0:T(8,128)}) %reduce-scatter.15.cloned.1.call-update) | async-done | bytes 1179664 | tf_op jit(solution)/shard_map/reduce_scatter | solution.py:439
  2684.5 88.7 %reduce-scatter.17.cloned.1.call-done = f32[256,1152]{1,0:T(8,128)} async-done(((f32[1024,1152]{1,0:T(8,128)}), f32[256,1152]{1,0:T(8,128)}) %reduce-scatter.17.cloned.1.call-update) | async-done | bytes 1179664 | tf_op jit(solution)/shard_map/reduce_scatter | solution.py:440
  2773.2 88.7 %reduce-scatter.19.cloned.1.call-done = f32[1152,256]{1,0:T(8,128)} async-done(((f32[1152,1024]{1,0:T(8,128)}), f32[1152,256]{1,0:T(8,128)}) %reduce-scatter.19.cloned.1.call-update) | async-done | bytes 1179664 | tf_op jit(solution)/shard_map/reduce_scatter | solution.py:441
  (765 shorter events, 820.7 us)
Async XLA Ops:
  56.7 58.3 %all-gather.50.cloned.1.call-start = ((), (), s32[]{:S(2)}) async-start(), calls=%async_computation.17 | async-start | bytes 2621440 | tf_op jit(solution)/shard_map/while/body/eval_jaxpr/all_gather | solution.py:91
  61.6 119.7 %reduce-scatter.23.cloned.1.call-start = ((), (), s32[]{:S(2)}) async-start(), calls=%async_computation.19 | async-start | bytes 5242880 | tf_op jit(solution)/shard_map/while/body/eval_jaxpr/reduce_scatter | solution.py:95
  123.4 109.4 %all-gather.56.cloned.1.call-start = ((), (), s32[]{:S(2)}) async-start(), calls=%async_computation.21 | async-start | bytes 2949120 | tf_op jit(solution)/shard_map/while/body/eval_jaxpr/all_gather | solution.py:354
  124.0 132.1 %all-gather.54.cloned.1.call-start = ((), (), s32[]{:S(2)}) async-start(), calls=%async_computation.20 | async-start | bytes 2621440 | tf_op jit(solution)/shard_map/while/body/eval_jaxpr/all_gather | solution.py:91
  185.0 123.1 %all-gather.48.cloned.1.call-start = ((), (), s32[]{:S(2)}) async-start(), calls=%async_computation.16 | async-start | bytes 2949120 | tf_op jit(solution)/shard_map/while/body/eval_jaxpr/all_gather | solution.py:356
  185.6 172.3 %all-gather.58.cloned.1.call-start = ((), (), s32[]{:S(2)}) async-start(), calls=%async_computation.22 | async-start | bytes 2949120 | tf_op jit(solution)/shard_map/while/body/eval_jaxpr/all_gather | solution.py:355
  186.3 226.5 %reduce-scatter.25.cloned.1.call-start = ((), (), s32[]{:S(2)}) async-start(), calls=%async_computation.23 | async-start | bytes 5242880 | tf_op jit(solution)/shard_map/while/body/eval_jaxpr/reduce_scatter | solution.py:95
  430.6 60.0 %all-gather.50.cloned.1.call-start = ((), (), s32[]{:S(2)}) async-start(), calls=%async_computation.17 | async-start | bytes 2621440 | tf_op jit(solution)/shard_map/while/body/eval_jaxpr/all_gather | solution.py:91
  435.6 121.5 %reduce-scatter.23.cloned.1.call-start = ((), (), s32[]{:S(2)}) async-start(), calls=%async_computation.19 | async-start | bytes 5242880 | tf_op jit(solution)/shard_map/while/body/eval_jaxpr/reduce_scatter | solution.py:95
  499.1 109.3 %all-gather.56.cloned.1.call-start = ((), (), s32[]{:S(2)}) async-start(), calls=%async_computation.21 | async-start | bytes 2949120 | tf_op jit(solution)/shard_map/while/body/eval_jaxpr/all_gather | solution.py:354
  499.7 132.3 %all-gather.54.cloned.1.call-start = ((), (), s32[]{:S(2)}) async-start(), calls=%async_computation.20 | async-start | bytes 2621440 | tf_op jit(solution)/shard_map/while/body/eval_jaxpr/all_gather | solution.py:91
  560.7 123.2 %all-gather.48.cloned.1.call-start = ((), (), s32[]{:S(2)}) async-start(), calls=%async_computation.16 | async-start | bytes 2949120 | tf_op jit(solution)/shard_map/while/body/eval_jaxpr/all_gather | solution.py:356
  561.3 172.3 %all-gather.58.cloned.1.call-start = ((), (), s32[]{:S(2)}) async-start(), calls=%async_computation.22 | async-start | bytes 2949120 | tf_op jit(solution)/shard_map/while/body/eval_jaxpr/all_gather | solution.py:355
  561.9 226.7 %reduce-scatter.25.cloned.1.call-start = ((), (), s32[]{:S(2)}) async-start(), calls=%async_computation.23 | async-start | bytes 5242880 | tf_op jit(solution)/shard_map/while/body/eval_jaxpr/reduce_scatter | solution.py:95
  806.2 60.1 %all-gather.50.cloned.1.call-start = ((), (), s32[]{:S(2)}) async-start(), calls=%async_computation.17 | async-start | bytes 2621440 | tf_op jit(solution)/shard_map/while/body/eval_jaxpr/all_gather | solution.py:91
  811.2 121.5 %reduce-scatter.23.cloned.1.call-start = ((), (), s32[]{:S(2)}) async-start(), calls=%async_computation.19 | async-start | bytes 5242880 | tf_op jit(solution)/shard_map/while/body/eval_jaxpr/reduce_scatter | solution.py:95
  874.8 109.3 %all-gather.56.cloned.1.call-start = ((), (), s32[]{:S(2)}) async-start(), calls=%async_computation.21 | async-start | bytes 2949120 | tf_op jit(solution)/shard_map/while/body/eval_jaxpr/all_gather | solution.py:354
  875.4 132.3 %all-gather.54.cloned.1.call-start = ((), (), s32[]{:S(2)}) async-start(), calls=%async_computation.20 | async-start | bytes 2621440 | tf_op jit(solution)/shard_map/while/body/eval_jaxpr/all_gather | solution.py:91
  936.4 123.4 %all-gather.48.cloned.1.call-start = ((), (), s32[]{:S(2)}) async-start(), calls=%async_computation.16 | async-start | bytes 2949120 | tf_op jit(solution)/shard_map/while/body/eval_jaxpr/all_gather | solution.py:356
  937.1 172.4 %all-gather.58.cloned.1.call-start = ((), (), s32[]{:S(2)}) async-start(), calls=%async_computation.22 | async-start | bytes 2949120 | tf_op jit(solution)/shard_map/while/body/eval_jaxpr/all_gather | solution.py:355
  937.8 226.6 %reduce-scatter.25.cloned.1.call-start = ((), (), s32[]{:S(2)}) async-start(), calls=%async_computation.23 | async-start | bytes 5242880 | tf_op jit(solution)/shard_map/while/body/eval_jaxpr/reduce_scatter | solution.py:95
  1190.5 53.5 %all-gather.62.cloned.1.call-start = ((), (), s32[]{:S(2)}) async-start(), calls=%async_computation.25 | async-start | bytes 2949120 | tf_op jit(solution)/shard_map/while/body/eval_jaxpr/all_gather | solution.py:355
  1191.3 103.0 %all-gather.60.cloned.1.call-start = ((), (), s32[]{:S(2)}) async-start(), calls=%async_computation.24 | async-start | bytes 2949120 | tf_op jit(solution)/shard_map/while/body/eval_jaxpr/all_gather | solution.py:354
  1191.9 125.2 %all-gather.64.cloned.1.call-start = ((), (), s32[]{:S(2)}) async-start(), calls=%async_computation.26 | async-start | bytes 2621440 | tf_op jit(solution)/shard_map/while/body/eval_jaxpr/all_gather | solution.py:91
  1193.9 175.3 %all-gather.66.cloned.1.call-start = ((), (), s32[]{:S(2)}) async-start(), calls=%async_computation.27 | async-start | bytes 2949120 | tf_op jit(solution)/shard_map/while/body/eval_jaxpr/all_gather | solution.py:356
  1194.6 234.4 %reduce-scatter.27.cloned.1.call-start = ((), (), s32[]{:S(2)}) async-start(), calls=%async_computation.28 | async-start | bytes 5242880 | tf_op jit(solution)/shard_map/while/body/eval_jaxpr/reduce_scatter | solution.py:95
  1386.1 69.6 %all-gather.70.cloned.1.call-start = ((), (), s32[]{:S(2)}) async-start(), calls=%async_computation.30 | async-start | bytes 2621440 | tf_op jit(solution)/shard_map/while/body/eval_jaxpr/all_gather | solution.py:91
  1433.0 52.3 %all-gather.68.cloned.1.call-start = ((), (), s32[]{:S(2)}) async-start(), calls=%async_computation.29 | async-start | bytes 1310720 | tf_op jit(solution)/shard_map/while/body/eval_jaxpr/all_gather | solution.py:352
  1433.7 157.7 %reduce-scatter.29.cloned.1.call-start = ((), (), s32[]{:S(2)}) async-start(), calls=%async_computation.31 | async-start | bytes 5242880 | tf_op jit(solution)/shard_map/while/body/eval_jaxpr/reduce_scatter | solution.py:95
  1613.4 100.9 %all-gather.60.cloned.1.call-start = ((), (), s32[]{:S(2)}) async-start(), calls=%async_computation.24 | async-start | bytes 2949120 | tf_op jit(solution)/shard_map/while/body/eval_jaxpr/all_gather | solution.py:354
  1614.2 123.1 %all-gather.64.cloned.1.call-start = ((), (), s32[]{:S(2)}) async-start(), calls=%async_computation.26 | async-start | bytes 2621440 | tf_op jit(solution)/shard_map/while/body/eval_jaxpr/all_gather | solution.py:91
  1616.1 173.1 %all-gather.66.cloned.1.call-start = ((), (), s32[]{:S(2)}) async-start(), calls=%async_computation.27 | async-start | bytes 2949120 | tf_op jit(solution)/shard_map/while/body/eval_jaxpr/all_gather | solution.py:356
  1616.7 232.3 %reduce-scatter.27.cloned.1.call-start = ((), (), s32[]{:S(2)}) async-start(), calls=%async_computation.28 | async-start | bytes 5242880 | tf_op jit(solution)/shard_map/while/body/eval_jaxpr/reduce_scatter | solution.py:95
  1806.1 69.6 %all-gather.70.cloned.1.call-start = ((), (), s32[]{:S(2)}) async-start(), calls=%async_computation.30 | async-start | bytes 2621440 | tf_op jit(solution)/shard_map/while/body/eval_jaxpr/all_gather | solution.py:91
  1853.0 52.1 %all-gather.68.cloned.1.call-start = ((), (), s32[]{:S(2)}) async-start(), calls=%async_computation.29 | async-start | bytes 1310720 | tf_op jit(solution)/shard_map/while/body/eval_jaxpr/all_gather | solution.py:352
  1853.6 157.9 %reduce-scatter.29.cloned.1.call-start = ((), (), s32[]{:S(2)}) async-start(), calls=%async_computation.31 | async-start | bytes 5242880 | tf_op jit(solution)/shard_map/while/body/eval_jaxpr/reduce_scatter | solution.py:95
  2033.6 101.1 %all-gather.60.cloned.1.call-start = ((), (), s32[]{:S(2)}) async-start(), calls=%async_computation.24 | async-start | bytes 2949120 | tf_op jit(solution)/shard_map/while/body/eval_jaxpr/all_gather | solution.py:354
  2034.3 123.1 %all-gather.64.cloned.1.call-start = ((), (), s32[]{:S(2)}) async-start(), calls=%async_computation.26 | async-start | bytes 2621440 | tf_op jit(solution)/shard_map/while/body/eval_jaxpr/all_gather | solution.py:91
  2036.3 173.2 %all-gather.66.cloned.1.call-start = ((), (), s32[]{:S(2)}) async-start(), calls=%async_computation.27 | async-start | bytes 2949120 | tf_op jit(solution)/shard_map/while/body/eval_jaxpr/all_gather | solution.py:356
  2037.1 232.3 %reduce-scatter.27.cloned.1.call-start = ((), (), s32[]{:S(2)}) async-start(), calls=%async_computation.28 | async-start | bytes 5242880 | tf_op jit(solution)/shard_map/while/body/eval_jaxpr/reduce_scatter | solution.py:95
  2226.5 69.6 %all-gather.70.cloned.1.call-start = ((), (), s32[]{:S(2)}) async-start(), calls=%async_computation.30 | async-start | bytes 2621440 | tf_op jit(solution)/shard_map/while/body/eval_jaxpr/all_gather | solution.py:91
  2273.4 52.2 %all-gather.68.cloned.1.call-start = ((), (), s32[]{:S(2)}) async-start(), calls=%async_computation.29 | async-start | bytes 1310720 | tf_op jit(solution)/shard_map/while/body/eval_jaxpr/all_gather | solution.py:352
  2274.0 157.9 %reduce-scatter.29.cloned.1.call-start = ((), (), s32[]{:S(2)}) async-start(), calls=%async_computation.31 | async-start | bytes 5242880 | tf_op jit(solution)/shard_map/while/body/eval_jaxpr/reduce_scatter | solution.py:95
  2455.6 96.2 %reduce-scatter.21.cloned.1.call-start = ((), (), s32[]{:S(2)}) async-start(), calls=%async_computation.15 | async-start | bytes 1179648 | tf_op jit(solution)/shard_map/reduce_scatter | solution.py:443
  2456.2 141.0 %reduce-scatter.11.cloned.1.call-start = ((), (), s32[]{:S(2)}) async-start(), calls=%async_computation.10 | async-start | bytes 2621440 | tf_op jit(solution)/shard_map/reduce_scatter | solution.py:437
  2459.2 225.4 %reduce-scatter.15.cloned.1.call-start = ((), (), s32[]{:S(2)}) async-start(), calls=%async_computation.12 | async-start | bytes 5898240 | tf_op jit(solution)/shard_map/reduce_scatter | solution.py:439
  2459.9 313.3 %reduce-scatter.17.cloned.1.call-start = ((), (), s32[]{:S(2)}) async-start(), calls=%async_computation.13 | async-start | bytes 5898240 | tf_op jit(solution)/shard_map/reduce_scatter | solution.py:440
  2460.7 401.2 %reduce-scatter.19.cloned.1.call-start = ((), (), s32[]{:S(2)}) async-start(), calls=%async_computation.14 | async-start | bytes 5898240 | tf_op jit(solution)/shard_map/reduce_scatter | solution.py:441
  (196 other events, 9934.2 us)
Sparse Core Ops, SparseCore 0:
  58.3 31.6 all-gather.51
  92.1 22.7 all-gather.49
  123.5 57.7 reduce-scatter.22
  182.7 49.9 all-gather.55
  234.7 21.3 all-gather.53
  257.5 50.5 all-gather.47
  309.6 48.1 all-gather.57
  369.4 43.3 reduce-scatter.24
  432.3 33.9 all-gather.51
  468.3 22.3 all-gather.49
  499.3 57.7 reduce-scatter.22
  558.5 49.9 all-gather.55
  610.6 21.3 all-gather.53
  633.4 50.5 all-gather.47
  685.4 48.1 all-gather.57
  745.2 43.3 reduce-scatter.24
  807.7 33.6 all-gather.51
  843.4 22.8 all-gather.49
  874.9 57.7 reduce-scatter.22
  934.1 49.9 all-gather.55
  986.3 21.3 all-gather.53
  1009.2 50.5 all-gather.47
  1061.3 48.1 all-gather.57
  1121.1 43.3 reduce-scatter.24
  1192.9 51.0 all-gather.61
  1245.5 48.7 all-gather.59
  1295.7 21.3 all-gather.63
  1318.6 50.5 all-gather.65
  1386.2 42.7 reduce-scatter.26
  1433.1 22.5 all-gather.69
  1457.3 27.9 all-gather.67
  1504.8 86.5 reduce-scatter.28
  1614.9 49.0 all-gather.61
  1665.6 48.7 all-gather.59
  1715.9 21.3 all-gather.63
  1738.7 50.5 all-gather.65
  1806.3 42.7 reduce-scatter.26
  1853.1 22.5 all-gather.69
  1877.2 27.9 all-gather.67
  1924.9 86.6 reduce-scatter.28
  2035.2 49.0 all-gather.61
  2085.9 48.7 all-gather.59
  2136.1 21.3 all-gather.63
  2159.0 50.5 all-gather.65
  2226.6 42.7 reduce-scatter.26
  2273.5 22.5 all-gather.69
  2297.5 27.9 all-gather.67
  2345.3 86.5 reduce-scatter.28
Sparse Core Ops, SparseCore 1:
  2458.4 26.7 reduce-scatter.12
  2489.0 62.8 reduce-scatter.20
  2554.6 42.6 reduce-scatter.10
  2600.1 84.4 reduce-scatter.14
  2687.4 85.7 reduce-scatter.16
  2776.1 85.7 reduce-scatter.18
where the time goes:
time: 2890 us; the launch traced here: 2870 us
  waiting for transfers between devices  2170 us (75%)
  matrix products  271 us (9%)
  blocking collectives  191 us (7%)
  other arithmetic  102 us (4%)
  local copies, waits for them, and re-layouts  80.8 us (3%)
    reduce_scatter x12, waiting for transfers between devices, collect(): lax.psum_scatter(partial_value, 'tensor', scatter_dimension=0, tiled=True)  576 us
    all_gather x6, waiting for transfers between devices, fetch_weights(): lax.all_gather(w_up[0], 'dp', axis=0, tiled=True)  293 us
    all_gather x6, waiting for transfers between devices, fetch_weights(): lax.all_gather(w_down[0], 'dp', axis=1, tiled=True)  290 us
    all_gather x6, waiting for transfers between devices, fetch_weights(): lax.all_gather(w_gate[0], 'dp', axis=0, tiled=True)  268 us
    all_gather x12, waiting for transfers between devices, spread(): return lax.all_gather(row_part, 'tensor', axis=0, tiled=True)  203 us
    dot_general x27, matrix products, matmul(): return jnp.dot(left_op, right_op, preferred_element_type=jnp.float32)  134 us
    all_gather x6, blocking collectives, fetch_weights(): lax.all_gather(mix_out[0], 'dp', axis=1, tiled=True)  114 us
    all_gather x6, waiting for transfers between devices, fetch_weights(): lax.all_gather(mix_in[0], 'dp', axis=0, tiled=True)  105 us
  transfers between devices with their start and end apart: 60, of which 59 were waited for; matrix products, arithmetic and copies ran while one was open for 8% of the time, Pallas kernels for 0%

commit v1 on v0

v1 whole, which is shorter than its diff:
```python
import functools

import jax
import jax.numpy as jnp
from jax import lax
from jax.experimental import pallas as pl
from jax.experimental.pallas import tpu as pltpu
from jax.sharding import PartitionSpec as P

HEADS = 16
KV_HEADS = 8

EPS = 1e-05
ROPE_BASE = 1000000.0
MASKED = -1e30

MESH = pl.DeviceIdType.MESH
ANY = pl.BlockSpec(memory_space=pl.ANY)
VM = pl.BlockSpec(memory_space=pltpu.VMEM)
DMA = pltpu.SemaphoreType.DMA
VMEM_BYTES = 62 * 1024 * 1024
BF = jnp.bfloat16
F32 = jnp.float32


def contract(left_op, right_op, left_dim, right_dim):
    return lax.dot_general(
        left_op, right_op, (((left_dim,), (right_dim,)), ((), ())), preferred_element_type=F32
    )


def contract_rows(left_op, right_op):
    return contract(left_op, right_op, 0, 0)


def norm_rows(values, gain):
    return values * lax.rsqrt(jnp.mean(values * values, axis=-1, keepdims=True) + EPS) * gain


def norm_back(values, gain, grad_in):
    row_scale = lax.rsqrt(jnp.mean(values * values, axis=-1, keepdims=True) + EPS)
    normed = values * row_scale
    feature_count = values.shape[-1]
    gain_grad = jnp.sum((grad_in * normed).reshape(-1, feature_count), axis=0)
    scaled = grad_in * gain
    value_grad = row_scale * (scaled - normed * jnp.mean(scaled * normed, axis=-1, keepdims=True))
    return (value_grad, gain_grad)


def rotation(length, head_size):
    half_size = head_size // 2
    frequency = ROPE_BASE ** (-(jnp.arange(half_size, dtype=jnp.float32) * 2.0 / head_size))
    angles = jnp.arange(length, dtype=jnp.float32)[:, None] * frequency[None, :]
    cosine_table = jnp.concatenate([jnp.cos(angles), jnp.cos(angles)], axis=1)
    sine_table = jnp.concatenate([jnp.sin(angles), jnp.sin(angles)], axis=1)
    return (cosine_table, sine_table)


def rotate(values, cosine_table, sine_table):
    half_size = values.shape[-1] // 2
    turned = jnp.concatenate([-values[..., half_size:], values[..., :half_size]], axis=-1)
    return values * cosine_table + turned * sine_table


def rotate_back(grad_in, cosine_table, sine_table):
    half_size = grad_in.shape[-1] // 2
    shifted_grad = grad_in * sine_table
    return grad_in * cosine_table + jnp.concatenate(
        [shifted_grad[..., half_size:], -shifted_grad[..., :half_size]], axis=-1
    )


def delayed(values, delay_by):
    if delay_by == 0:
        return values
    return jnp.concatenate(
        [jnp.zeros((delay_by, values.shape[1]), values.dtype), values[:-delay_by]], axis=0
    )


def advanced(values, delay_by):
    if delay_by == 0:
        return values
    return jnp.concatenate(
        [values[delay_by:], jnp.zeros((delay_by, values.shape[1]), values.dtype)], axis=0
    )


def places():
    me = lax.axis_index("tensor")
    sib = me + 1 - 2 * (me % 2)
    cross = (me + 2) % 4
    diag = (sib + 2) % 4
    return me, sib, cross, diag


def greet(sib, cross):
    barrier = pltpu.get_barrier_semaphore()
    for peer in (sib, cross):
        pl.semaphore_signal(barrier, inc=1, device_id={"tensor": peer}, device_id_type=MESH)
    pl.semaphore_wait(barrier, 2)


def remote(src, dst, send_sem, recv_sem, peer):
    return pltpu.make_async_remote_copy(
        src_ref=src, dst_ref=dst, send_sem=send_sem, recv_sem=recv_sem,
        device_id={"tensor": peer}, device_id_type=MESH,
    )


def silu_parts(gate):
    sig = 1.0 / (1.0 + jnp.exp(-gate))
    return sig, gate * sig


def gather_kernel(cfg, *refs):
    norm, n_w, n_x, trans, epilogue = cfg
    it = iter(refs)
    x_ref = next(it)
    gain_ref = next(it) if norm else None
    w_hbm = [next(it) for _ in range(n_w)]
    e_hbm = [next(it) for _ in range(n_x)]
    a_hbm = next(it)
    n_out = {"plain": n_w, "ffn": 3, "ffn_back": 2}[epilogue]
    o_hbm = [next(it) for _ in range(n_out)]
    full = next(it)
    w_v = [next(it) for _ in range(n_w)]
    e_v = [next(it) for _ in range(n_x)]
    o_v = [next(it) for _ in range(n_out)]
    in_sem, out_sem, a_sem, xs, xr, ss, sr, ls, lr = it

    me, sib, cross, diag = places()
    rows = x_ref.shape[0]
    half = rows // 2
    loads = [
        pltpu.make_async_copy(src, dst, in_sem.at[i])
        for i, (src, dst) in enumerate(zip(w_hbm + e_hbm, w_v + e_v))
    ]
    for load in loads:
        load.start()
    greet(sib, cross)

    def span(owner, sub):
        return pl.ds(pl.multiple_of(owner * rows + sub * half, half), half)

    def to_cross(i):
        return remote(full.at[span(me, i)], full.at[span(me, i)], xs.at[i], xr.at[i], cross)

    def to_sib(i):
        return remote(full.at[span(me, i)], full.at[span(me, i)], ss.at[i], sr.at[i], sib)

    def relay(i):
        return remote(full.at[span(cross, i)], full.at[span(cross, i)], ls.at[i], lr.at[i], sib)

    for i in range(2):
        part = x_ref[pl.ds(i * half, half), :]
        if norm:
            part = norm_rows(part, gain_ref[...])
        full[span(me, i), :] = part.astype(BF)
        to_cross(i).start()
        to_sib(i).start()
    for load in loads:
        load.wait()

    def step(p, carry):
        far, sub = p // 2, p % 2
        near = (1 - sub) * me + sub * sib
        first = (1 - far) * near * rows + far * (cross * rows + sub * half)
        second = (1 - far) * (near * rows + half) + far * (diag * rows + sub * half)
        pair = [pl.ds(pl.multiple_of(first, half), half), pl.ds(pl.multiple_of(second, half), half)]

        @pl.when(p == 1)
        def _():
            to_sib(0).wait_recv()
            to_sib(1).wait_recv()

        for i in range(2):

            @pl.when(p == 2 + i)
            def _():
                to_cross(i).wait_recv()
                relay(i).start()
                relay(i).wait_recv()

        a = jnp.concatenate([full[pair[0], :], full[pair[1], :]], axis=0)
        prods = [contract(a, w[...], 1, 1 if trans else 0) for w in w_v]
        if epilogue == "plain":
            values = prods
        elif epilogue == "ffn":
            sig, silu = silu_parts(prods[0])
            values = [prods[0], prods[1], silu * prods[1]]
        else:
            gate = jnp.concatenate([e_v[0][q, :] for q in pair], axis=0).astype(F32)
            up = jnp.concatenate([e_v[1][q, :] for q in pair], axis=0).astype(F32)
            sig, silu = silu_parts(gate)
            values = [prods[0] * up * sig * (1.0 + gate * (1.0 - sig)), prods[0] * silu]
        for j, value in enumerate(values):
            value = value.astype(o_v[j].dtype)
            for k in range(2):
                o_v[j][pair[k], :] = value[k * half : (k + 1) * half]
                pltpu.make_async_copy(
                    o_v[j].at[pair[k]], o_hbm[j].at[pair[k]], out_sem.at[p, k, j]
                ).start()
        for k in range(2):
            pltpu.make_async_copy(full.at[pair[k]], a_hbm.at[pair[k]], a_sem.at[p, k]).start()
        return carry

    lax.fori_loop(0, 4, step, 0)
    for i in range(2):
        to_cross(i).wait_send()
        to_sib(i).wait_send()
        relay(i).wait_send()
    for p in range(4):
        for k in range(2):
            for j in range(n_out):
                pltpu.make_async_copy(
                    o_v[j].at[pl.ds(0, half)], o_hbm[j].at[pl.ds(0, half)], out_sem.at[p, k, j]
                ).wait()
            pltpu.make_async_copy(
                full.at[pl.ds(0, half)], a_hbm.at[pl.ds(0, half)], a_sem.at[p, k]
            ).wait()


def gather_mm(x_rows, gain, weights, extras=(), trans=False, epilogue="plain", cid=0, out_type=F32):
    rows, width = x_rows.shape
    length = rows * 4
    cols = [w.shape[0] if trans else w.shape[1] for w in weights]
    if epilogue == "plain":
        outs = [(c, out_type) for c in cols]
    else:
        outs = [(cols[0], BF)] * (3 if epilogue == "ffn" else 2)
    norm = gain is not None
    cfg = (norm, len(weights), len(extras), trans, epilogue)
    operands = [x_rows] + ([gain.reshape(1, width)] if norm else []) + list(weights) + list(extras)
    flops = sum(2 * length * width * c for c in cols)
    moved = sum(w.size * 2 for w in weights) + sum(length * c * 2 for c, _ in outs) + length * width * 4
    return pl.pallas_call(
        functools.partial(gather_kernel, cfg),
        out_shape=[jax.ShapeDtypeStruct((length, width), BF)]
        + [jax.ShapeDtypeStruct((length, c), t) for c, t in outs],
        in_specs=[VM] * (2 if norm else 1) + [ANY] * (len(weights) + len(extras)),
        out_specs=[ANY] * (1 + len(outs)),
        scratch_shapes=[pltpu.VMEM((length, width), BF)]
        + [pltpu.VMEM(w.shape, BF) for w in weights]
        + [pltpu.VMEM(e.shape, e.dtype) for e in extras]
        + [pltpu.VMEM((length, c), t) for c, t in outs]
        + [DMA((len(weights) + len(extras),)), DMA((4, 2, len(outs))), DMA((4, 2))]
        + [DMA((2,))] * 6,
        compiler_params=pltpu.CompilerParams(
            collective_id=cid, has_side_effects=True, vmem_limit_bytes=VMEM_BYTES
        ),
        cost_estimate=pl.CostEstimate(flops=flops, bytes_accessed=moved * 4, transcendentals=0),
        name=f"gather{cid}",
    )(*operands)


def scatter_kernel(cfg, *refs):
    n_y, trans, epilogue = cfg
    it = iter(refs)
    y_hbm = [next(it) for _ in range(n_y)]
    w_hbm = [next(it) for _ in range(n_y)]
    resid_ref = next(it)
    if epilogue == "back":
        value_ref, gain_ref = next(it), next(it)
    out_ref = next(it)
    if epilogue == "back":
        gain_out = next(it)
    y_v = [next(it) for _ in range(n_y)]
    w_v = [next(it) for _ in range(n_y)]
    keep, own, to_s, from_s, to_c, from_c, to_o, from_o = (next(it) for _ in range(8))
    in_sem, ds, dr, cs, cr, os_, or_ = it

    me, sib, cross, diag = places()
    rows = resid_ref.shape[0]
    half = rows // 2
    loads = [
        pltpu.make_async_copy(src, dst, in_sem.at[i])
        for i, (src, dst) in enumerate(zip(y_hbm + w_hbm, y_v + w_v))
    ]
    for load in loads:
        load.start()
    greet(sib, cross)
    for load in loads:
        load.wait()

    def send_diag(i):
        return remote(to_s.at[i], from_s.at[i], ds.at[i], dr.at[i], sib)

    def send_cross(i):
        return remote(to_c.at[i], from_c.at[i], cs.at[i], cr.at[i], cross)

    send_near = remote(to_o, from_o, os_, or_, sib)

    def pass_on(i):
        send_diag(i).wait_recv()
        to_c[i] = (keep[i] + from_s[i].astype(F32)).astype(BF)
        send_cross(i).start()

    def step(p, carry):
        near, sub = p // 2, p % 2
        base = near * ((1 - sub) * sib + sub * me) * rows
        first = base + (1 - near) * (cross * rows + sub * half)
        second = base + near * half + (1 - near) * (diag * rows + sub * half)
        pair = [pl.ds(pl.multiple_of(first, half), half), pl.ds(pl.multiple_of(second, half), half)]
        total = None
        for y, w in zip(y_v, w_v):
            a = jnp.concatenate([y[pair[0], :], y[pair[1], :]], axis=0)
            prod = contract(a, w[...], 1, 1 if trans else 0)
            total = prod if total is None else total + prod

        for i in range(2):

            @pl.when(p == i)
            def _():
                keep[i] = total[:half]
                to_s[i] = total[half:].astype(BF)
                send_diag(i).start()

        @pl.when(p == 1)
        def _():
            pass_on(0)

        @pl.when(p == 2)
        def _():
            to_o[...] = total.astype(BF)
            send_near.start()
            pass_on(1)

        @pl.when(p == 3)
        def _():
            own[...] = total

        return carry

    lax.fori_loop(0, 4, step, 0)
    send_near.wait_recv()
    gain_sum = None
    for i in range(2):
        part = pl.ds(i * half, half)
        send_cross(i).wait_recv()
        total = own[part, :] + from_o[part, :].astype(F32) + from_c[i].astype(F32)
        resid = resid_ref[part, :].astype(F32)
        if epilogue == "back":
            value_grad, gain_grad = norm_back(value_ref[part, :], gain_ref[...], total)
            out_ref[part, :] = resid + value_grad
            gain_sum = gain_grad if gain_sum is None else gain_sum + gain_grad
        else:
            out_ref[part, :] = resid + total
    if epilogue == "back":
        gain_out[...] = gain_sum.reshape(gain_out.shape)
    send_near.wait_send()
    for i in range(2):
        send_diag(i).wait_send()
        send_cross(i).wait_send()


def scatter_mm(operands, weights, resid, back=None, trans=False, cid=0):
    rows, width = resid.shape
    half = rows // 2
    epilogue = "plain" if back is None else "back"
    extra = [] if back is None else [back[0], back[1].reshape(1, width)]
    out_shape = [jax.ShapeDtypeStruct((rows, width), F32)]
    if back is not None:
        out_shape.append(jax.ShapeDtypeStruct((1, width), F32))
    flops = sum(2 * y.size * width for y in operands)
    moved = sum(2 * (y.size + w.size) for y, w in zip(operands, weights)) + rows * width * 12
    result = pl.pallas_call(
        functools.partial(scatter_kernel, (len(operands), trans, epilogue)),
        out_shape=out_shape,
        in_specs=[ANY] * (2 * len(operands)) + [VM] * (1 + len(extra)),
        out_specs=[VM] * len(out_shape),
        scratch_shapes=[pltpu.VMEM(y.shape, BF) for y in operands]
        + [pltpu.VMEM(w.shape, BF) for w in weights]
        + [pltpu.VMEM((2, half, width), F32), pltpu.VMEM((rows, width), F32)]
        + [pltpu.VMEM((2, half, width), BF)] * 4
        + [pltpu.VMEM((rows, width), BF)] * 2
        + [DMA((2 * len(operands),))]
        + [DMA((2,))] * 4
        + [DMA] * 2,
        compiler_params=pltpu.CompilerParams(
            collective_id=cid, has_side_effects=True, vmem_limit_bytes=VMEM_BYTES
        ),
        cost_estimate=pl.CostEstimate(flops=flops, bytes_accessed=moved * 4, transcendentals=0),
        name=f"scatter{cid}",
    )(*operands, *weights, resid, *extra)
    return result[0] if back is None else result


def conv_core(projected, x_value, kernel):
    channels = x_value.shape[1]
    b_gate = projected[:, :channels]
    c_gate = projected[:, channels:]
    product = b_gate * x_value
    tap_count = kernel.shape[0]
    causal = jnp.zeros_like(product)
    for offset in range(tap_count):
        causal = causal + kernel[offset] * delayed(product, tap_count - 1 - offset)
    return (b_gate, c_gate, product, causal)


def conv_back(projected, x_value, kernel, grad_y):
    b_gate, c_gate, product, causal = conv_core(projected, x_value, kernel)
    grad_c = grad_y * causal
    grad_causal = grad_y * c_gate
    tap_count = kernel.shape[0]
    kernel_rows = []
    grad_product = jnp.zeros_like(product)
    for offset in range(tap_count):
        delay_by = tap_count - 1 - offset
        kernel_rows.append(jnp.sum(grad_causal * delayed(product, delay_by), axis=0))
        grad_product = grad_product + kernel[offset] * advanced(grad_causal, delay_by)
    grad_proj = jnp.concatenate([grad_product * x_value, grad_c], axis=1).astype(BF)
    grad_value = (grad_product * b_gate).astype(BF)
    return (grad_proj, grad_value, jnp.stack(kernel_rows))


def attention_inputs(projected, head_gain):
    length = projected.shape[0]
    group_width = projected.shape[1] // 2
    head_size = head_gain.shape[1]
    group_size = HEADS // KV_HEADS
    kv_local = group_width // head_size // group_size
    queries = projected[:, :group_width].reshape(length, kv_local, group_size, head_size)
    key_part = projected[:, group_width : group_width + group_width // 2].reshape(
        length, kv_local, head_size
    )
    values = projected[:, group_width + group_width // 2 :].reshape(length, kv_local, head_size)
    cosine_table, sine_table = rotation(length, head_size)
    q_rot = rotate(
        norm_rows(queries, head_gain[0]),
        cosine_table[:, None, None, :],
        sine_table[:, None, None, :],
    ).astype(BF)
    k_rot = rotate(
        norm_rows(key_part, head_gain[1]), cosine_table[:, None, :], sine_table[:, None, :]
    ).astype(BF)
    return (queries, key_part, q_rot, k_rot, values.astype(BF), cosine_table, sine_table)


def masked_scores(q_piece, k_rot, first_row, length):
    row_block = q_piece.shape[0]
    score_scale = q_piece.shape[-1] ** (-0.5)
    scores = jnp.einsum("ahgd,bhd->hgab", q_piece, k_rot, preferred_element_type=F32) * score_scale
    query_pos = first_row + jnp.arange(row_block, dtype=jnp.int32)
    key_pos = jnp.arange(length, dtype=jnp.int32)
    allowed = key_pos[None, :] <= query_pos[:, None]
    return jnp.where(allowed, scores, MASKED)


def attention_forward(parts):
    q_rot, k_rot, v_low = (parts[2], parts[3], parts[4])
    length = q_rot.shape[0]
    row_block = min(512, length)
    out_blocks = []
    total_blocks = []
    for first_row in range(0, length, row_block):
        scores = masked_scores(q_rot[first_row : first_row + row_block], k_rot, first_row, length)
        row_max = jnp.max(scores, axis=-1, keepdims=True)
        exp_scores = jnp.exp(scores - row_max)
        row_sum = jnp.sum(exp_scores, axis=-1, keepdims=True)
        weights = (exp_scores / row_sum).astype(BF)
        attended = jnp.einsum("hgab,bhd->ahgd", weights, v_low, preferred_element_type=F32)
        out_blocks.append(attended.reshape(row_block, -1))
        total_blocks.append((row_max + jnp.log(row_sum))[..., 0])
    return (jnp.concatenate(out_blocks, axis=0).astype(BF), jnp.concatenate(total_blocks, axis=-1))


def attention_back(parts, log_total, head_gain, grad_y):
    queries, key_part, q_rot, k_rot, v_low, cosine_table, sine_table = parts
    length, kv_local, group_size, head_size = queries.shape
    score_scale = head_size ** (-0.5)
    row_block = min(512, length)
    grad_low = grad_y.astype(BF).reshape(length, kv_local, group_size, head_size)
    q_grads = []
    key_grad = jnp.zeros((length, kv_local, head_size), F32)
    value_grad = jnp.zeros((length, kv_local, head_size), F32)
    for first_row in range(0, length, row_block):
        q_piece = q_rot[first_row : first_row + row_block]
        scores = masked_scores(q_piece, k_rot, first_row, length)
        probability = jnp.exp(scores - log_total[:, :, first_row : first_row + row_block, None])
        weights = probability.astype(BF)
        grad_piece = grad_low[first_row : first_row + row_block]
        grad_weights = jnp.einsum("ahgd,bhd->hgab", grad_piece, v_low, preferred_element_type=F32)
        value_grad = value_grad + jnp.einsum(
            "hgab,ahgd->bhd", weights, grad_piece, preferred_element_type=F32
        )
        grad_scores = probability * (
            grad_weights - jnp.sum(probability * grad_weights, axis=-1, keepdims=True)
        )
        grad_scores = grad_scores.astype(BF)
        q_grads.append(
            jnp.einsum("hgab,bhd->ahgd", grad_scores, k_rot, preferred_element_type=F32)
            * score_scale
        )
        key_grad = (
            key_grad
            + jnp.einsum("hgab,ahgd->bhd", grad_scores, q_piece, preferred_element_type=F32)
            * score_scale
        )
    query_grad = jnp.concatenate(q_grads, axis=0)
    query_grad = rotate_back(
        query_grad, cosine_table[:, None, None, :], sine_table[:, None, None, :]
    )
    key_grad = rotate_back(key_grad, cosine_table[:, None, :], sine_table[:, None, :])
    query_raw, q_gain_grad = norm_back(queries, head_gain[0], query_grad)
    key_raw, k_gain_grad = norm_back(key_part, head_gain[1], key_grad)
    grad_proj = jnp.concatenate(
        [
            query_raw.reshape(length, -1),
            key_raw.reshape(length, -1),
            value_grad.reshape(length, -1),
        ],
        axis=1,
    ).astype(BF)
    return (grad_proj, jnp.stack([q_gain_grad, k_gain_grad]))


SWAP = [(0, 1), (1, 0)]
WHOLE = ("section", "dp")


def gather_rows(shard):
    both = lax.all_gather(shard, WHOLE, axis=0, tiled=True)
    size = both.shape[0] // 2
    return both[:size], both[size:]


def gather_cols(shard):
    both = lax.all_gather(shard, WHOLE, axis=0, tiled=False)
    count, rows, cols = both.shape
    both = both.reshape(2, count // 2, rows, cols).transpose(0, 2, 1, 3)
    both = both.reshape(2, rows, count // 2 * cols)
    return both[0], both[1]


def body(boundary, norm_gain, mix_in, mix_out, w_gate, w_up, w_down, conv_x, conv_kernel, qk_gain):
    section = lax.axis_index("section")
    first = section == 0
    model_width = boundary.shape[3]
    channels = mix_out.shape[1]

    slots = boundary[0]
    mine = jnp.where(first, slots[0], slots[1])
    theirs = jnp.where(first, slots[1], slots[0])
    moved = lax.ppermute(theirs, "section", SWAP)
    x_low = jnp.where(first, mine, moved)
    cot = jnp.where(first, moved, mine)
    gain_other = lax.ppermute(norm_gain[0], "section", SWAP)
    gains = (
        jnp.where(first, norm_gain[0], gain_other),
        jnp.where(first, gain_other, norm_gain[0]),
    )

    w_in = gather_rows(mix_in[0])
    w_cols = lax.all_gather(conv_x, WHOLE, axis=0, tiled=True)
    w_out = gather_cols(mix_out[0])
    gate_w = gather_rows(w_gate[0])
    up_w = gather_rows(w_up[0])
    down_w = gather_cols(w_down[0])

    x_rows = x_low.astype(F32)
    a0, proj0, value0 = gather_mm(x_rows, gains[0][0], [w_in[0], w_cols], cid=0)
    b_gate, c_gate, product, causal = conv_core(proj0, value0, conv_kernel)
    y0 = (c_gate * causal).astype(BF)
    mid0 = scatter_mm([y0], [w_out[0]], x_rows, cid=1)
    m0, gate0, up0, hid0 = gather_mm(
        mid0, gains[0][1], [gate_w[0], up_w[0]], epilogue="ffn", cid=2
    )
    z_rows = scatter_mm([hid0], [down_w[0]], mid0, cid=3).astype(BF).astype(F32)
    a1, proj1 = gather_mm(z_rows, gains[1][0], [w_in[1]], cid=4)
    parts = attention_inputs(proj1, qk_gain)
    y1, log_total = attention_forward(parts)
    mid1 = scatter_mm([y1], [w_out[1]], z_rows, cid=5)
    m1, gate1, up1, hid1 = gather_mm(
        mid1, gains[1][1], [gate_w[1], up_w[1]], epilogue="ffn", cid=6
    )
    y_rows = scatter_mm([hid1], [down_w[1]], mid1, cid=7).astype(BF)

    def low_grad(left_op, right_op):
        return contract_rows(left_op, right_op).astype(BF)

    def ffn_back(dout, middle, gain, m, gate, up, hid, block, cid):
        d_full, d_gate, d_up = gather_mm(
            dout, None, [down_w[block]], [gate, up], trans=True, epilogue="ffn_back", cid=cid
        )
        grads = (low_grad(m, d_gate), low_grad(m, d_up), low_grad(hid, d_full))
        d_mid, d_gain = scatter_mm(
            [d_gate, d_up], [gate_w[block], up_w[block]], dout, (middle, gain), True, cid + 1
        )
        return d_mid, d_gain, grads

    def out_back(d_mid, block, y, cid):
        d_full, d_y = gather_mm(d_mid, None, [w_out[block]], trans=True, cid=cid)
        return d_y, low_grad(y, d_full)

    def owned(rows_first, rows_second, dim):
        return [
            lax.psum_scatter(g, "dp", scatter_dimension=dim, tiled=True)
            for g in (rows_first, rows_second)
        ]

    d_mid1, gain11, (g_gate1, g_up1, g_down1) = ffn_back(
        cot, mid1, gains[1][1], m1, gate1, up1, hid1, 1, 8
    )
    d_y1, g_out1 = out_back(d_mid1, 1, y1, 10)
    d_proj1, head_grad = attention_back(parts, log_total, qk_gain, d_y1)
    g_in1 = low_grad(a1, d_proj1)
    d_z, gain10 = scatter_mm(
        [d_proj1], [w_in[1]], d_mid1, (z_rows, gains[1][0]), True, 11
    )
    d_z = d_z.astype(BF)
    d_mid0, gain01, (g_gate0, g_up0, g_down0) = ffn_back(
        d_z, mid0, gains[0][1], m0, gate0, up0, hid0, 0, 12
    )
    d_y0, g_out0 = out_back(d_mid0, 0, y0, 14)
    d_proj0, d_value0, kernel_grad = conv_back(proj0, value0, conv_kernel, d_y0)
    g_in0 = low_grad(a0, d_proj0)
    g_cols = low_grad(a0, d_value0)
    d_x, gain00 = scatter_mm(
        [d_proj0, d_value0], [w_in[0], w_cols], d_mid0, (x_rows, gains[0][0]), True, 15
    )
    d_x = d_x.astype(BF)

    pairs = [
        owned(g_in0, g_in1, 0),
        owned(g_out0, g_out1, 1),
        owned(g_gate0, g_gate1, 0),
        owned(g_up0, g_up1, 0),
        owned(g_down0, g_down1, 1),
    ]
    weight_grads = []
    for zero, one in pairs:
        kept = jnp.where(first, zero, one)
        sent = jnp.where(first, one, zero)
        other = lax.ppermute(sent, "section", SWAP)
        weight_grads.append((kept.astype(F32) + other.astype(F32))[None])
    cols_part = lax.psum_scatter(g_cols, WHOLE, scatter_dimension=0, tiled=True).astype(F32)

    moved_out = lax.ppermute(jnp.where(first, y_rows, d_x), "section", SWAP)
    kept_out = jnp.where(first, d_x, y_rows)
    result = jnp.stack(
        [jnp.where(first, kept_out, moved_out), jnp.where(first, moved_out, kept_out)]
    )

    tensor_index = lax.axis_index("tensor")
    kernel_full = lax.dynamic_update_slice_in_dim(
        jnp.zeros((conv_kernel.shape[0], model_width), F32), kernel_grad, tensor_index * channels, 1
    )
    gains_full = jnp.concatenate([gain00, gain01, gain10, gain11], axis=0)
    gains_total, kernel_total, head_total = lax.psum(
        (gains_full, kernel_full, head_grad), ("section", "dp", "tensor")
    )
    gain_out = lax.dynamic_slice_in_dim(gains_total.reshape(2, 2, model_width), section, 1, 0)
    kernel_out = lax.dynamic_slice_in_dim(kernel_total, tensor_index * channels, channels, 1)
    return (
        result[None],
        gain_out,
        *weight_grads,
        cols_part,
        kernel_out,
        head_total,
    )


def solution(mesh):
    in_specs = (
        P("section", "dp", "tensor", None),
        P("section", None, None),
        P("section", "dp", "tensor"),
        P("section", "tensor", "dp"),
        P("section", "dp", "tensor"),
        P("section", "dp", "tensor"),
        P("section", "tensor", "dp"),
        P(("section", "dp"), "tensor"),
        P(None, "tensor"),
        P(),
    )
    out_specs = (
        P("section", "dp", "tensor", None),
        P("section", None, None),
        P("section", "dp", "tensor"),
        P("section", "tensor", "dp"),
        P("section", "dp", "tensor"),
        P("section", "dp", "tensor"),
        P("section", "tensor", "dp"),
        P(("section", "dp"), "tensor"),
        P(None, "tensor"),
        P(),
    )
    return jax.shard_map(body, mesh=mesh, in_specs=in_specs, out_specs=out_specs, check_vma=False)
```

time: 2890 us -> 1160 us (0.40)
  waiting for transfers between devices: 2170 us -> 497 us
  Pallas kernels: 0 us -> 308 us
  matrix products: 271 us -> 93.5 us
  blocking collectives: 191 us -> 83.8 us
  other arithmetic: 102 us -> 59.1 us
    all_gather x36 -> x5, waiting for transfers between devices: 1160 us -> 210 us  [the longest x3 173 us: gather_rows(): both = lax.all_gather(shard, WHOLE, axis=0, tiled=True)]
    reduce_scatter x18 -> x11, waiting for transfers between devices: 935 us -> 269 us  [the longest x10 269 us: owned(): lax.psum_scatter(g, 'dp', scatter_dimension=dim, tiled=True)]
    pallas_call x0 -> x16, Pallas kernels: none -> 308 us  [the longest x8 166 us: scatter_mm(): pl.pallas_call(functools.partial(scatter_kernel, (len(operands), trans, e...]
    dot_general x63 -> x23, matrix products: 271 us -> 93.5 us  [the longest x11 55.2 us: contract(): lax.dot_general(left_op, right_op, (((left_dim,), (right_dim,)), ((), ())...]
    all_gather x7 -> x1, blocking collectives: 150 us -> 37.2 us  [body(): w_cols = lax.all_gather(conv_x, WHOLE, axis=0, tiled=True)]
    ppermute x6 -> x8, waiting for transfers between devices: 61.3 us -> 13.8 us  [the longest x5 13.7 us: body(): other = lax.ppermute(sent, 'section', SWAP)]
    dynamic_update_slice x24 -> x1, other arithmetic: 40.5 us -> 0.02 us  [body(): lax.dynamic_update_slice_in_dim(jnp.zeros((conv_kernel.shape[0], model_wi...]
    dynamic_slice x22 -> x1, local copies, waits for them, and re-layouts: 30.9 us -> 0.6 us  [body(): lax.dynamic_slice_in_dim(gains_total.reshape(2, 2, model_width), section,...]
  transfers between devices with their start and end apart: 60 -> 24, of which waited for: 59 -> 13; matrix products, arithmetic and copies ran while one was open for 8% -> 15% of each run, Pallas kernels for 0% -> 14%
where the time goes in v1:
time: 1160 us; the launch traced here: 1150 us
  waiting for transfers between devices  497 us (43%)
  Pallas kernels  308 us (27%)
  matrix products  93.5 us (8%)
  blocking collectives  83.8 us (7%)
  local copies, waits for them, and re-layouts  83 us (7%)
  other arithmetic  59.1 us (5%)
  between operations  15.2 us (1%)
  starting transfers between devices  11.7 us (1%)
    reduce_scatter x10, waiting for transfers between devices, owned(): lax.psum_scatter(g, 'dp', scatter_dimension=dim, tiled=True)  269 us
    all_gather x3, waiting for transfers between devices, gather_rows(): both = lax.all_gather(shard, WHOLE, axis=0, tiled=True)  173 us
    pallas_call x8, Pallas kernels, scatter_mm(): pl.pallas_call(functools.partial(scatter_kernel, (len(operands), trans, e...  166 us
    pallas_call x8, Pallas kernels, gather_mm(): pl.pallas_call(functools.partial(gather_kernel, cfg), out_shape=[jax.Shap...  142 us
    dot_general x11, matrix products, contract(): lax.dot_general(left_op, right_op, (((left_dim,), (right_dim,)), ((), ())...  55.2 us
    psum x1, blocking collectives, body(): lax.psum((gains_full, kernel_full, head_grad), ('section', 'dp', 'tensor'))  46.6 us
    all_gather x1, blocking collectives, body(): w_cols = lax.all_gather(conv_x, WHOLE, axis=0, tiled=True)  37.2 us
    all_gather x2, waiting for transfers between devices, gather_cols(): both = lax.all_gather(shard, WHOLE, axis=0, tiled=False)  37 us
  transfers between devices with their start and end apart: 24, of which 13 were waited for; matrix products, arithmetic and copies ran while one was open for 15% of the time, Pallas kernels for 14%

profile of v1, /device:TPU:0, one launch (start us, length us, event | category | flops | bytes accessed | tf_op | source)
XLA Modules:
  0.0 1151.3 jit_solution(10856964905930315076)
XLA Ops:
  15.4 37.2 %all_gather.19.refs_3_ = bf16[1024,256]{1,0:T(8,128)(2,1)} all-gather(bf16[128,256]{1,0:T(8,128)(2,1)S(1)} %copy-done.51), channel_id=1, replica_groups=mesh['section'=2,'dp'=4,'tensor'=4] {'section','dp'}, dimensions={0}, use_global_device_ids=true | all-gather | bytes 589824 | tf_op jit(solution)/shard_map/all_gather | solution.py:555
  64.0 42.5 %all-gather.13.cloned.1.call-done = bf16[1,2048,512]{2,1,0:T(8,128)(2,1)} async-done(((bf16[1,256,512]{2,1,0:T(8,128)(2,1)}), bf16[1,2048,512]{2,1,0:T(8,128)(2,1)}) %all-gather.13.cloned.1.call-update) | async-done | bytes 2097168 | tf_op jit(solution)/shard_map/all_gather | solution.py:523
  109.5 17.8 %gather0.1 = (bf16[1024,1024]{1,0:T(8,128)(2,1)}, f32[1024,512]{1,0:T(8,128)}, f32[1024,256]{1,0:T(8,128)}) custom-call(f32[256,1024]{1,0:T(8,128)} %get-tuple-element.99.refs_0_.refs_2_.refs_5_, f32[1,1024]{1,0:T(1,128)} %get-tuple-element.124.refs_1_.refs_6_, bf16[1024,512]{1,0:T(8,128)(2,1)} %get-tuple-element.97.refs_2_, ...), custom_call_target="tpu_custom_call" | custom-call | flops 1610612736 | bytes 29360128 | tf_op jit(solution)/shard_map/gather0/pallas_call | solution.py:237
  131.1 18.4 %scatter1.1.refs_0_.refs_2_.refs_5_ = f32[256,1024]{1,0:T(8,128)} custom-call(bf16[1024,256]{1,0:T(8,128)(2,1)} %get-tuple-element.86.refs_0_, bf16[256,1024]{1,0:T(8,128)(2,1)} %bitcast.229, f32[256,1024]{1,0:T(8,128)} %get-tuple-element.99.refs_0_.refs_2_.refs_5_), custom_call_target="tpu_custom_call" | custom-call | flops 536870912 | bytes 16777216 | tf_op jit(solution)/shard_map/scatter1/pallas_call | solution.py:367
  149.5 37.0 %all-gather.11.cloned.1.call-done = bf16[8,1152,256]{2,1,0:T(8,128)(2,1)} async-done(((bf16[1,1152,256]{2,1,0:T(8,128)(2,1)}), bf16[8,1152,256]{2,1,0:T(8,128)(2,1)}) %all-gather.11.cloned.1.call-update) | async-done | bytes 4718608 | tf_op jit(solution)/shard_map/all_gather | solution.py:529
  186.5 18.9 %copy.148 = bf16[2,4,1152,256]{3,1,2,0:T(4,128)(2,1)S(1)} copy(bf16[2,4,1152,256]{3,2,1,0:T(8,128)(2,1)} %bitcast.211) | data formatting | bytes 9437184 | tf_op jit(solution)/shard_map/reshape | solution.py:531
  210.1 56.1 %all-gather.15.cloned.1.call-done = bf16[1,2048,1152]{2,1,0:T(8,128)(2,1)} async-done(((bf16[1,256,1152]{2,1,0:T(8,128)(2,1)}), bf16[1,2048,1152]{2,1,0:T(8,128)(2,1)}) %all-gather.15.cloned.1.call-update) | async-done | bytes 4718608 | tf_op jit(solution)/shard_map/all_gather | solution.py:523
  266.2 4.9 slice_bitcast_fusion.1
  271.1 74.7 %all-gather.17.cloned.1.call-done = bf16[1,2048,1152]{2,1,0:T(8,128)(2,1)} async-done(((bf16[1,256,1152]{2,1,0:T(8,128)(2,1)}), bf16[1,2048,1152]{2,1,0:T(8,128)(2,1)}) %all-gather.17.cloned.1.call-update) | async-done | bytes 4718608 | tf_op jit(solution)/shard_map/all_gather | solution.py:523
  345.8 4.9 slice_bitcast_fusion
  350.7 18.8 %gather2.1 = (bf16[1024,1024]{1,0:T(8,128)(2,1)}, bf16[1024,1152]{1,0:T(8,128)(2,1)}, bf16[1024,1152]{1,0:T(8,128)(2,1)}, bf16[1024,1152]{1,0:T(8,128)(2,1)}) custom-call(f32[256,1024]{1,0:T(8,128)} %scatter1.1.refs_0_.refs_2_.refs_5_, f32[1,1024]{1,0:T(1,128)} %get-tuple-element.123.refs_1_.refs_6_, bf16[1024,1152]{1,0:T(8,128)(2,1)} %get-tuple-element.95.refs_2_, ...), custom_call_target="tpu_custom_call" | custom-call | flops 4831838208 | bytes 63963136 | tf_op jit(solution)/shard_map/gather2/pallas_call | solution.py:237
  369.5 20.4 %scatter3.1 = f32[256,1024]{1,0:T(8,128)} custom-call(bf16[1024,1152]{1,0:T(8,128)(2,1)} %get-tuple-element.43.refs_0_, bf16[1152,1024]{1,0:T(8,128)(2,1)} %bitcast.227, f32[256,1024]{1,0:T(8,128)} %scatter1.1.refs_0_.refs_2_.refs_5_), custom_call_target="tpu_custom_call" | custom-call | flops 2415919104 | bytes 31457280 | tf_op jit(solution)/shard_map/scatter3/pallas_call | solution.py:367
  392.2 17.3 %gather4.1 = (bf16[1024,1024]{1,0:T(8,128)(2,1)}, f32[1024,512]{1,0:T(8,128)}) custom-call(f32[256,1024]{1,0:T(8,128)} %convert_convert_fusion.refs_0_.refs_2_.refs_3_, f32[1,1024]{1,0:T(1,128)} %get-tuple-element.122.refs_1_.refs_4_, bf16[1024,512]{1,0:T(8,128)(2,1)} %get-tuple-element.96.refs_2_.refs_1_), custom_call_target="tpu_custom_call" | custom-call | flops 1073741824 | bytes 25165824 | tf_op jit(solution)/shard_map/gather4/pallas_call | solution.py:237
  437.1 18.4 %scatter5.1.refs_0_.refs_5_.refs_2_ = f32[256,1024]{1,0:T(8,128)} custom-call(bf16[1024,256]{1,0:T(8,128)(2,1)} %pad_maximum_fusion.4.refs_0_, bf16[256,1024]{1,0:T(8,128)(2,1)} %bitcast.231, f32[256,1024]{1,0:T(8,128)} %convert_convert_fusion.refs_0_.refs_2_.refs_3_), custom_call_target="tpu_custom_call" | custom-call | flops 536870912 | bytes 16777216 | tf_op jit(solution)/shard_map/scatter5/pallas_call | solution.py:367
  455.5 18.3 %gather6.1 = (bf16[1024,1024]{1,0:T(8,128)(2,1)}, bf16[1024,1152]{1,0:T(8,128)(2,1)}, bf16[1024,1152]{1,0:T(8,128)(2,1)}, bf16[1024,1152]{1,0:T(8,128)(2,1)}) custom-call(f32[256,1024]{1,0:T(8,128)} %scatter5.1.refs_0_.refs_5_.refs_2_, f32[1,1024]{1,0:T(1,128)} %get-tuple-element.121.refs_1_.refs_6_, bf16[1024,1152]{1,0:T(8,128)(2,1)} %get-tuple-element.94.refs_2_, ...), custom_call_target="tpu_custom_call" | custom-call | flops 4831838208 | bytes 63963136 | tf_op jit(solution)/shard_map/gather6/pallas_call | solution.py:237
  473.8 19.7 %gather8.1 = (bf16[1024,1024]{1,0:T(8,128)(2,1)}, bf16[1024,1152]{1,0:T(8,128)(2,1)}, bf16[1024,1152]{1,0:T(8,128)(2,1)}) custom-call(bf16[256,1024]{1,0:T(8,128)(2,1)} %get-tuple-element.98.refs_0_.refs_4_, bf16[1152,1024]{1,0:T(8,128)(2,1)} %bitcast.225, bf16[1024,1152]{1,0:T(8,128)(2,1)} %get-tuple-element.45.refs_2_, ...), custom_call_target="tpu_custom_call" | custom-call | flops 2415919104 | bytes 45088768 | tf_op jit(solution)/shard_map/gather8/pallas_call | solution.py:237
  493.4 23.6 %scatter9.1 = (f32[256,1024]{1,0:T(8,128)}, f32[1,1024]{1,0:T(1,128)}) custom-call(bf16[1024,1152]{1,0:T(8,128)(2,1)} %get-tuple-element.47.refs_0_, bf16[1024,1152]{1,0:T(8,128)(2,1)} %get-tuple-element.48.refs_1_, bf16[1024,1152]{1,0:T(8,128)(2,1)} %get-tuple-element.94.refs_2_, bf16[1024,1152]{1,0:T(8,128)(2,1)} %get-tuple-element.92.refs_3_, ...), custom_call_target="tpu_custom_call" | custom-call | flops 4831838208 | bytes 50331648 | tf_op jit(solution)/shard_map/scatter9/pallas_call | solution.py:367
  517.0 16.4 %gather10.1 = (bf16[1024,1024]{1,0:T(8,128)(2,1)}, f32[1024,256]{1,0:T(8,128)}) custom-call(f32[256,1024]{1,0:T(8,128)} %get-tuple-element.49.refs_0_.refs_2_, bf16[256,1024]{1,0:T(8,128)(2,1)} %bitcast.232), custom_call_target="tpu_custom_call" | custom-call | flops 536870912 | bytes 20971520 | tf_op jit(solution)/shard_map/gather10/pallas_call | solution.py:237
  535.7 5.7 fusion.18
  541.4 5.3 fusion.3
  560.4 8.3 fusion
  568.7 4.8 fusion.29
  574.4 7.4 fusion.2
  584.8 3.8 broadcast_multiply_fusion
  606.1 20.0 %scatter11.1 = (f32[256,1024]{1,0:T(8,128)}, f32[1,1024]{1,0:T(1,128)}) custom-call(bf16[1024,512]{1,0:T(8,128)(2,1)} %pad_maximum_fusion.2.refs_0_, bf16[1024,512]{1,0:T(8,128)(2,1)} %get-tuple-element.96.refs_2_.refs_1_, f32[256,1024]{1,0:T(8,128)} %get-tuple-element.49.refs_0_.refs_2_, f32[256,1024]{1,0:T(8,128)} %convert_convert_fusion.refs_0_.refs_2_.refs_3_, ...), custom_call_target="tpu_custom_call" | custom-call | flops 1073741824 | bytes 20971520 | tf_op jit(solution)/shard_map/scatter11/pallas_call | solution.py:367
  628.2 17.3 %gather12.1 = (bf16[1024,1024]{1,0:T(8,128)(2,1)}, bf16[1024,1152]{1,0:T(8,128)(2,1)}, bf16[1024,1152]{1,0:T(8,128)(2,1)}) custom-call(bf16[256,1024]{1,0:T(8,128)(2,1)} %convert_element_type.138.refs_0_.refs_4_, bf16[1152,1024]{1,0:T(8,128)(2,1)} %bitcast.228, bf16[1024,1152]{1,0:T(8,128)(2,1)} %get-tuple-element.52.refs_2_, ...), custom_call_target="tpu_custom_call" | custom-call | flops 2415919104 | bytes 45088768 | tf_op jit(solution)/shard_map/gather12/pallas_call | solution.py:237
  645.6 24.5 %scatter13.1 = (f32[256,1024]{1,0:T(8,128)}, f32[1,1024]{1,0:T(1,128)}) custom-call(bf16[1024,1152]{1,0:T(8,128)(2,1)} %get-tuple-element.54.refs_0_, bf16[1024,1152]{1,0:T(8,128)(2,1)} %get-tuple-element.55.refs_1_, bf16[1024,1152]{1,0:T(8,128)(2,1)} %get-tuple-element.95.refs_2_, bf16[1024,1152]{1,0:T(8,128)(2,1)} %get-tuple-element.93.refs_3_, ...), custom_call_target="tpu_custom_call" | custom-call | flops 4831838208 | bytes 50331648 | tf_op jit(solution)/shard_map/scatter13/pallas_call | solution.py:367
  670.0 16.6 %gather14.1 = (bf16[1024,1024]{1,0:T(8,128)(2,1)}, f32[1024,256]{1,0:T(8,128)}) custom-call(f32[256,1024]{1,0:T(8,128)} %get-tuple-element.56.refs_0_.refs_4_, bf16[256,1024]{1,0:T(8,128)(2,1)} %bitcast.230), custom_call_target="tpu_custom_call" | custom-call | flops 536870912 | bytes 20971520 | tf_op jit(solution)/shard_map/gather14/pallas_call | solution.py:237
  686.6 3.1 convolution_convert_fusion.10
  689.9 4.2 convolution_convert_fusion.6
  701.7 3.2 convolution_convert_fusion.8
  705.0 6.3 convolution_convert_fusion
  711.4 6.4 convolution_convert_fusion.1
  717.9 6.7 convolution_convert_fusion.2
  724.8 6.7 convolution_convert_fusion.3
  731.6 6.7 convolution_convert_fusion.4
  738.3 6.6 convolution_convert_fusion.5
  747.0 20.7 %scatter15.1 = (f32[256,1024]{1,0:T(8,128)}, f32[1,1024]{1,0:T(1,128)}) custom-call(bf16[1024,512]{1,0:T(8,128)(2,1)} %pad_maximum_fusion.3.refs_0_, bf16[1024,256]{1,0:T(8,128)(2,1)} %get-tuple-element.83.refs_1_, bf16[1024,512]{1,0:T(8,128)(2,1)} %get-tuple-element.97.refs_2_, bf16[1024,256]{1,0:T(8,128)(2,1)} %all_gather.19.refs_3_, ...), custom_call_target="tpu_custom_call" | custom-call | flops 1610612736 | bytes 25165824 | tf_op jit(solution)/shard_map/scatter15/pallas_call | solution.py:367
  767.8 20.3 %scatter7.1 = f32[256,1024]{1,0:T(8,128)} custom-call(bf16[1024,1152]{1,0:T(8,128)(2,1)} %get-tuple-element.59.refs_0_, bf16[1152,1024]{1,0:T(8,128)(2,1)} %bitcast.226, f32[256,1024]{1,0:T(8,128)} %scatter5.1.refs_0_.refs_5_.refs_2_), custom_call_target="tpu_custom_call" | custom-call | flops 2415919104 | bytes 31457280 | tf_op jit(solution)/shard_map/scatter7/pallas_call | solution.py:367
  790.4 46.6 %all-reduce.4 = (f32[2,2,1024]{2,1,0:T(2,128)S(1)}, f32[3,1024]{1,0:T(4,128)S(1)}, f32[2,64]{1,0:T(2,128)}) all-reduce(f32[2,2,1024]{2,1,0:T(2,128)S(1)} %reshape.178, f32[3,1024]{1,0:T(4,128)S(1)} %maximum_dynamic-update-slice_fusion, ...), channel_id=1, replica_groups=mesh['section'=2,'dp'=4,'tensor'=4] {'section','dp','tensor'}, use_global_device_ids=true, to_apply=%region_10.11 | all-reduce | flops 7296 | bytes 58368 | tf_op jit(solution)/shard_map/psum | solution.py:650
  846.5 3.9 collective-permute-done.3
  851.4 29.6 %reduce-scatter.30.cloned.1.call-done = bf16[1152,256]{1,0:T(8,128)(2,1)} async-done(((bf16[1152,1024]{1,0:T(8,128)(2,1)}), bf16[1152,256]{1,0:T(8,128)(2,1)}) %reduce-scatter.30.cloned.1.call-update) | async-done | bytes 589840 | tf_op jit(solution)/shard_map/reduce_scatter | solution.py:598
  880.9 49.3 %reduce-scatter.28.cloned.1.call-done = bf16[1152,256]{1,0:T(8,128)(2,1)} async-done(((bf16[1152,1024]{1,0:T(8,128)(2,1)}), bf16[1152,256]{1,0:T(8,128)(2,1)}) %reduce-scatter.28.cloned.1.call-update) | async-done | bytes 589840 | tf_op jit(solution)/shard_map/reduce_scatter | solution.py:598
  933.7 45.9 %reduce-scatter.26.cloned.1.call-done = bf16[256,1152]{1,0:T(8,128)(2,1)} async-done(((bf16[1024,1152]{1,0:T(8,128)(2,1)}), bf16[256,1152]{1,0:T(8,128)(2,1)}) %reduce-scatter.26.cloned.1.call-update) | async-done | bytes 589840 | tf_op jit(solution)/shard_map/reduce_scatter | solution.py:598
  979.6 49.3 %reduce-scatter.24.cloned.1.call-done = bf16[256,1152]{1,0:T(8,128)(2,1)} async-done(((bf16[1024,1152]{1,0:T(8,128)(2,1)}), bf16[256,1152]{1,0:T(8,128)(2,1)}) %reduce-scatter.24.cloned.1.call-update) | async-done | bytes 589840 | tf_op jit(solution)/shard_map/reduce_scatter | solution.py:598
  1032.3 45.9 %reduce-scatter.22.cloned.1.call-done = bf16[256,1152]{1,0:T(8,128)(2,1)} async-done(((bf16[1024,1152]{1,0:T(8,128)(2,1)}), bf16[256,1152]{1,0:T(8,128)(2,1)}) %reduce-scatter.22.cloned.1.call-update) | async-done | bytes 589840 | tf_op jit(solution)/shard_map/reduce_scatter | solution.py:598
  1078.2 49.3 %reduce-scatter.20.cloned.1.call-done = bf16[256,1152]{1,0:T(8,128)(2,1)} async-done(((bf16[1024,1152]{1,0:T(8,128)(2,1)}), bf16[256,1152]{1,0:T(8,128)(2,1)}) %reduce-scatter.20.cloned.1.call-update) | async-done | bytes 589840 | tf_op jit(solution)/shard_map/reduce_scatter | solution.py:598
  1133.6 9.7 collective-permute-done.5
  (292 shorter events, 136.7 us)
Async XLA Ops:
  7.2 6.5 copy-start.12
  7.2 52.5 %all-gather.9.cloned.1.call-start = ((), (), s32[]{:S(2)}) async-start(), calls=%async_computation.11 | async-start | bytes 1179648 | tf_op jit(solution)/shard_map/all_gather | solution.py:529
  7.9 98.6 %all-gather.13.cloned.1.call-start = ((), (), s32[]{:S(2)}) async-start(), calls=%async_computation.24 | async-start | bytes 2359296 | tf_op jit(solution)/shard_map/all_gather | solution.py:523
  8.7 6.7 copy-start.58
  8.7 6.7 copy-start.57
  8.7 6.7 copy-start.51
  8.7 177.8 %all-gather.11.cloned.1.call-start = ((), (), s32[]{:S(2)}) async-start(), calls=%async_computation.12 | async-start | bytes 5308416 | tf_op jit(solution)/shard_map/all_gather | solution.py:529
  9.4 256.7 %all-gather.15.cloned.1.call-start = ((), (), s32[]{:S(2)}) async-start(), calls=%async_computation.25 | async-start | bytes 5308416 | tf_op jit(solution)/shard_map/all_gather | solution.py:523
  10.0 335.8 %all-gather.17.cloned.1.call-start = ((), (), s32[]{:S(2)}) async-start(), calls=%async_computation.26 | async-start | bytes 5308416 | tf_op jit(solution)/shard_map/all_gather | solution.py:523
  10.6 827.8 %reduce-scatter.18.cloned.1.call-start = ((), (), s32[]{:S(2)}) async-start(), calls=%async_computation.16 | async-start | bytes 655360 | tf_op jit(solution)/shard_map/reduce_scatter | solution.py:598
  10.6 45.6 %collective-permute-start.1 = (f32[2,1024]{1,0:T(2,128)}, f32[2,1024]{1,0:T(2,128)S(1)}, u32[]{:S(2)}, u32[]{:S(2)}) collective-permute-start(f32[2,1024]{1,0:T(2,128)} %bitcast.246), channel_id=1, source_target_pairs={{0,16},{16,0},{1,17},{17,1},{2,18},{18,2},{3,19},{19,3},{4,20},{20... | collective-permute-start | bytes 24584 | tf_op jit(solution)/shard_map/ppermute | solution.py:548
  13.7 43.7 %collective-permute-start = (bf16[256,1024]{1,0:T(8,128)(2,1)S(1)}, bf16[256,1024]{1,0:T(8,128)(2,1)}, u32[]{:S(2)}, u32[]{:S(2)}) collective-permute-start(bf16[256,1024]{1,0:T(8,128)(2,1)S(1)} %select_bitcast_fusion.2), channel_id=1, source_target_pairs={{0,16},{16,0},{1,17},{17,1},{2,18},{18,2},{3,19},{19,3},{4,20},{20... | collective-permute-start | bytes 1572872 | tf_op jit(solution)/shard_map/ppermute | solution.py:545
  419.4 7.3 copy-start.20
  420.2 6.6 copy-start.35
  535.7 11.1 slice-start
  560.3 278.1 %reduce-scatter.16.cloned.1.call-start = ((), (), s32[]{:S(2)}) async-start(), calls=%async_computation.15 | async-start | bytes 655360 | tf_op jit(solution)/shard_map/reduce_scatter | solution.py:598
  560.4 8.3 copy-start.38
  574.4 7.5 copy-start.22
  595.2 6.4 copy-start.10
  595.2 6.4 copy-start.11
  645.5 41.1 %copy-start.8 = (bf16[1024,256]{1,0:T(8,128)(2,1)S(1)}, bf16[1024,256]{1,0:T(8,128)(2,1)}, u32[]{:S(2)}) copy-start(bf16[1024,256]{1,0:T(8,128)(2,1)} %get-tuple-element.86.refs_0_) | copy-start | bytes 1572868
  689.8 152.1 %reduce-scatter.14.cloned.1.call-start = ((), (), s32[]{:S(2)}) async-start(), calls=%async_computation.14 | async-start | bytes 1310720 | tf_op jit(solution)/shard_map/reduce_scatter | solution.py:598
  694.1 147.8 %reduce-scatter.12.cloned.1.call-start = ((), (), s32[]{:S(2)}) async-start(), calls=%async_computation.13 | async-start | bytes 1310720 | tf_op jit(solution)/shard_map/reduce_scatter | solution.py:598
  701.7 142.5 %reduce-scatter.32.cloned.1.call-start = ((), (), s32[]{:S(2)}) async-start(), calls=%async_computation.23 | async-start | bytes 589824 | tf_op jit(solution)/shard_map/reduce_scatter | solution.py:637
  704.9 176.0 %reduce-scatter.30.cloned.1.call-start = ((), (), s32[]{:S(2)}) async-start(), calls=%async_computation.22 | async-start | bytes 2949120 | tf_op jit(solution)/shard_map/reduce_scatter | solution.py:598
  711.3 218.9 %reduce-scatter.28.cloned.1.call-start = ((), (), s32[]{:S(2)}) async-start(), calls=%async_computation.21 | async-start | bytes 2949120 | tf_op jit(solution)/shard_map/reduce_scatter | solution.py:598
  717.8 261.8 %reduce-scatter.26.cloned.1.call-start = ((), (), s32[]{:S(2)}) async-start(), calls=%async_computation.20 | async-start | bytes 2949120 | tf_op jit(solution)/shard_map/reduce_scatter | solution.py:598
  724.5 304.3 %reduce-scatter.24.cloned.1.call-start = ((), (), s32[]{:S(2)}) async-start(), calls=%async_computation.19 | async-start | bytes 2949120 | tf_op jit(solution)/shard_map/reduce_scatter | solution.py:598
  731.5 346.6 %reduce-scatter.22.cloned.1.call-start = ((), (), s32[]{:S(2)}) async-start(), calls=%async_computation.18 | async-start | bytes 2949120 | tf_op jit(solution)/shard_map/reduce_scatter | solution.py:598
  738.3 389.2 %reduce-scatter.20.cloned.1.call-start = ((), (), s32[]{:S(2)}) async-start(), calls=%async_computation.17 | async-start | bytes 2949120 | tf_op jit(solution)/shard_map/reduce_scatter | solution.py:598
  767.7 20.4 %copy-start.13 = (f32[256,1024]{1,0:T(8,128)S(1)}, f32[256,1024]{1,0:T(8,128)}, u32[]{:S(2)}) copy-start(f32[256,1024]{1,0:T(8,128)} %get-tuple-element.58) | copy-start | bytes 3145732
  788.1 50.0 %copy-start.14 = (f32[256,1024]{1,0:T(8,128)S(1)}, f32[256,1024]{1,0:T(8,128)}, u32[]{:S(2)}) copy-start(f32[256,1024]{1,0:T(8,128)} %scatter7.1) | copy-start | bytes 3145732
  789.6 48.6 %collective-permute-start.2 = (bf16[256,1024]{1,0:T(8,128)(2,1)S(1)}, bf16[256,1024]{1,0:T(8,128)(2,1)S(1)}, u32[]{:S(2)}, u32[]{:S(2)}) collective-permute-start(bf16[256,1024]{1,0:T(8,128)(2,1)S(1)} %broadcast_select_fusion.4), channel_id=1, source_target_pairs={{0,16},{16,0},{1,17},{17,1},{2,18},{18,2},{3,19},{19,3},{4,20},{20... | collective-permute-start | bytes 1572872 | tf_op jit(solution)/shard_map/ppermute | solution.py:639
  838.4 7.4 copy-start.49
  838.4 7.4 copy-start.50
  839.6 6.2 collective-permute-start.4
  841.9 8.6 copy-start.39
  841.9 8.6 copy-start.40
  843.0 7.5 collective-permute-start.3
  880.9 249.2 %copy-start.27 = (bf16[1152,256]{1,0:T(8,128)(2,1)S(1)}, bf16[1152,256]{1,0:T(8,128)(2,1)}, u32[]{:S(2)}) copy-start(bf16[1152,256]{1,0:T(8,128)(2,1)} %reduce-scatter.30.cloned.1.call-done) | copy-start | bytes 1769476
  930.2 199.9 %copy-start.28 = (bf16[1152,256]{1,0:T(8,128)(2,1)S(1)}, bf16[1152,256]{1,0:T(8,128)(2,1)}, u32[]{:S(2)}) copy-start(bf16[1152,256]{1,0:T(8,128)(2,1)} %reduce-scatter.28.cloned.1.call-done) | copy-start | bytes 1769476
  932.2 197.9 %collective-permute-start.7 = (bf16[1152,256]{1,0:T(8,128)(2,1)}, bf16[1152,256]{1,0:T(8,128)(2,1)S(1)}, u32[]{:S(2)}, u32[]{:S(2)}) collective-permute-start(bf16[1152,256]{1,0:T(8,128)(2,1)} %broadcast_select_fusion), channel_id=1, source_target_pairs={{0,16},{16,0},{1,17},{17,1},{2,18},{18,2},{3,19},{19,3},{4,20},{20... | collective-permute-start | bytes 1769480 | tf_op jit(solution)/shard_map/ppermute | solution.py:635
  1030.8 100.5 %copy-start.29 = (bf16[256,1152]{1,0:T(8,128)(2,1)S(1)}, bf16[256,1152]{1,0:T(8,128)(2,1)}, u32[]{:S(2)}) copy-start(bf16[256,1152]{1,0:T(8,128)(2,1)} %reduce-scatter.26.cloned.1.call-done) | copy-start | bytes 1769476
  1030.8 100.5 %copy-start.30 = (bf16[256,1152]{1,0:T(8,128)(2,1)S(1)}, bf16[256,1152]{1,0:T(8,128)(2,1)}, u32[]{:S(2)}) copy-start(bf16[256,1152]{1,0:T(8,128)(2,1)} %reduce-scatter.24.cloned.1.call-done) | copy-start | bytes 1769476
  1030.8 100.5 %collective-permute-start.6 = (bf16[256,1152]{1,0:T(8,128)(2,1)}, bf16[256,1152]{1,0:T(8,128)(2,1)}, u32[]{:S(2)}, u32[]{:S(2)}) collective-permute-start(bf16[256,1152]{1,0:T(8,128)(2,1)} %broadcast_select_fusion.1), channel_id=1, source_target_pairs={{0,16},{16,0},{1,17},{17,1},{2,18},{18,2},{3,19},{19,3},{4,20},{20... | collective-permute-start | bytes 1769480 | tf_op jit(solution)/shard_map/ppermute | solution.py:635
  1128.6 14.8 %copy-start.31 = (bf16[256,1152]{1,0:T(8,128)(2,1)S(1)}, bf16[256,1152]{1,0:T(8,128)(2,1)}, u32[]{:S(2)}) copy-start(bf16[256,1152]{1,0:T(8,128)(2,1)} %reduce-scatter.22.cloned.1.call-done) | copy-start | bytes 1769476
  1128.6 14.7 %copy-start.32 = (bf16[256,1152]{1,0:T(8,128)(2,1)S(1)}, bf16[256,1152]{1,0:T(8,128)(2,1)}, u32[]{:S(2)}) copy-start(bf16[256,1152]{1,0:T(8,128)(2,1)} %reduce-scatter.20.cloned.1.call-done) | copy-start | bytes 1769476
  1128.6 14.7 %collective-permute-start.5 = (bf16[256,1152]{1,0:T(8,128)(2,1)S(1)}, bf16[256,1152]{1,0:T(8,128)(2,1)S(1)}, u32[]{:S(2)}, u32[]{:S(2)}) collective-permute-start(bf16[256,1152]{1,0:T(8,128)(2,1)S(1)} %broadcast_select_fusion.2), channel_id=1, source_target_pairs={{0,16},{16,0},{1,17},{17,1},{2,18},{18,2},{3,19},{19,3},{4,20},{20... | collective-permute-start | bytes 1769480 | tf_op jit(solution)/shard_map/ppermute | solution.py:635
  (38 other events, 91.7 us)
Sparse Core Ops, SparseCore 0:
  10.1 45.9 all-gather.8
  58.2 48.2 all-gather.12
  108.6 77.8 all-gather.10
  188.4 77.6 all-gather.14
  268.1 77.6 all-gather.16
  560.4 20.8 reduce-scatter.17
  689.9 20.7 reduce-scatter.15
  713.0 25.5 reduce-scatter.13
  741.5 25.7 reduce-scatter.11
  770.5 61.3 reduce-scatter.31
  834.2 46.7 reduce-scatter.29
  883.1 47.0 reduce-scatter.27
  932.5 47.0 reduce-scatter.25
  981.8 47.0 reduce-scatter.23
  1031.0 47.0 reduce-scatter.21
  1080.3 47.0 reduce-scatter.19

commit v2 on v1

--- a/solution.py
+++ b/solution.py
@@ -94,18 +94,241 @@
     return me, sib, cross, diag
 
 
-def greet(sib, cross):
+def greet(peers):
     barrier = pltpu.get_barrier_semaphore()
-    for peer in (sib, cross):
-        pl.semaphore_signal(barrier, inc=1, device_id={"tensor": peer}, device_id_type=MESH)
-    pl.semaphore_wait(barrier, 2)
+    for peer in peers:
+        pl.semaphore_signal(barrier, inc=1, device_id=peer, device_id_type=MESH)
+    pl.semaphore_wait(barrier, len(peers))
 
 
 def remote(src, dst, send_sem, recv_sem, peer):
     return pltpu.make_async_remote_copy(
         src_ref=src, dst_ref=dst, send_sem=send_sem, recv_sem=recv_sem,
-        device_id={"tensor": peer}, device_id_type=MESH,
-    )
+        device_id=peer, device_id_type=MESH,
+    )
+
+
+class Task:
+    def __init__(self, inputs, out, axis, count, copies, sender=None):
+        self.inputs, self.out, self.axis, self.count = inputs, out, axis, count
+        self.copies, self.sender = copies, sender
+
+
+def sizes():
+    return lax.axis_size("section"), lax.axis_size("dp")
+
+
+def slots(value):
+    return jax.ShapeDtypeStruct((lax.axis_size("dp"),) + value.shape, value.dtype)
+
+
+def same(value):
+    return jax.ShapeDtypeStruct(value.shape, value.dtype)
+
+
+def z_gather(piece):
+    count = lax.axis_size("dp")
+
+    def copies(ins, out, s, d, t):
+        return [(ins[0], out.at[d], {"dp": (d + k) % count}) for k in range(1, count)]
+
+    return Task([piece], slots(piece), "dp", count - 1, copies)
+
+
+def x_gather(piece, held):
+    count = lax.axis_size("dp")
+
+    def copies(ins, out, s, d, t):
+        peer = {"section": 1 - s}
+        moves = [(ins[0], out.at[d], peer)]
+        for k in range(1, count):
+            other = (d + k) % count
+            moves.append((ins[1].at[other], out.at[other], peer))
+        return moves
+
+    return Task([piece, held], slots(piece), "section", count, copies)
+
+
+def x_half(shard):
+    out = jax.ShapeDtypeStruct(shard.shape[1:], shard.dtype)
+
+    def copies(ins, out, s, d, t):
+        return [(ins[0].at[1 - s], out, {"section": 1 - s})]
+
+    return Task([shard], out, "section", 1, copies)
+
+
+def x_swap(value):
+    def copies(ins, out, s, d, t):
+        return [(ins[0], out, {"section": 1 - s})]
+
+    return Task([value], same(value), "section", 1, copies)
+
+
+def x_rows_of(grads):
+    count = lax.axis_size("dp")
+    out = jax.ShapeDtypeStruct((count,) + grads.shape[2:], grads.dtype)
+
+    def copies(ins, out, s, d, t):
+        peer = {"section": 1 - s}
+        return [(ins[0].at[k, 1 - s], out.at[k], peer) for k in range(count)]
+
+    return Task([grads], out, "section", count, copies)
+
+
+def z_scatter(pieces):
+    count = lax.axis_size("dp")
+
+    def copies(ins, out, s, d, t):
+        moves = []
+        for k in range(1, count):
+            other = (d + k) % count
+            moves.append((ins[0].at[other], out.at[d], {"dp": other}))
+        return moves
+
+    return Task([pieces], same(pieces), "dp", count - 1, copies)
+
+
+def x_final(piece, block):
+    def copies(ins, out, s, d, t):
+        return [(ins[0], out, {"section": 1 - s})]
+
+    return Task([piece], same(piece), "section", 1, copies, sender=1 - block)
+
+
+def t_share(value):
+    out = jax.ShapeDtypeStruct((4,) + value.shape, value.dtype)
+
+    def copies(ins, out, s, d, t):
+        return [(ins[0], out.at[t], {"tensor": (t + k) % 4}) for k in range(1, 4)]
+
+    return Task([value], out, "tensor", 3, copies)
+
+
+class Background:
+    def __init__(self, tasks):
+        self.tasks = list(tasks)
+        self.inputs = [v for task in self.tasks for v in task.inputs]
+        self.outs = [task.out for task in self.tasks]
+        self.count = sum(task.count for task in self.tasks)
+        self.scratch = [DMA((max(self.count, 1),)), DMA((max(self.count, 1),))]
+
+    def bind(self, it_in, it_out):
+        self.in_refs = [next(it_in) for _ in self.inputs]
+        self.out_refs = [next(it_out) for _ in self.outs]
+
+    def peers(self, tensor):
+        _, count = sizes()
+        s, d, t = (lax.axis_index(a) for a in ("section", "dp", "tensor"))
+        axes = {task.axis for task in self.tasks}
+        found = []
+        if "section" in axes:
+            found.append({"section": 1 - s})
+        if "dp" in axes:
+            found += [{"dp": (d + k) % count} for k in range(1, count)]
+        if "tensor" in axes:
+            found += [{"tensor": (t + k) % 4} for k in range(1, 4)]
+        else:
+            found += tensor
+        return found
+
+    def plan(self, sems):
+        send, recv = sems
+        s, d, t = (lax.axis_index(a) for a in ("section", "dp", "tensor"))
+        at, i, moves = 0, 0, []
+        for task, out in zip(self.tasks, self.out_refs):
+            ins = self.in_refs[at : at + len(task.inputs)]
+            at += len(task.inputs)
+            for from_ref, to_ref, peer in task.copies(ins, out, s, d, t):
+                moves.append((remote(from_ref, to_ref, send.at[i], recv.at[i], peer), task.sender))
+                i += 1
+        return s, moves
+
+    def start(self, sems):
+        s, moves = self.plan(sems)
+        for move, sender in moves:
+            if sender is None:
+                move.start()
+            else:
+                pl.when(s == sender)(move.start)
+
+    def finish(self, sems):
+        s, moves = self.plan(sems)
+        for move, sender in moves:
+            if sender is None:
+                move.wait_recv()
+                move.wait_send()
+            else:
+                pl.when(s == sender)(move.wait_send)
+                pl.when(s == 1 - sender)(move.wait_recv)
+
+
+def exchange_kernel(bg, *refs):
+    ins = iter(refs[: len(bg.inputs)])
+    outs = iter(refs[len(bg.inputs) : len(bg.inputs) + len(bg.outs)])
+    sems = refs[len(bg.inputs) + len(bg.outs) :]
+    bg.bind(ins, outs)
+    greet(bg.peers([]))
+    bg.start(sems)
+    bg.finish(sems)
+
+
+def exchange(tasks, cid):
+    bg = Background(tasks)
+    return pl.pallas_call(
+        functools.partial(exchange_kernel, bg),
+        out_shape=bg.outs,
+        in_specs=[ANY] * len(bg.inputs),
+        out_specs=[ANY] * len(bg.outs),
+        scratch_shapes=bg.scratch,
+        compiler_params=pltpu.CompilerParams(
+            collective_id=cid, has_side_effects=True, vmem_limit_bytes=VMEM_BYTES
+        ),
+        name=f"exchange{cid}",
+    )(*bg.inputs)
+
+
+class Weight:
+    def __init__(self, kind, piece, near, far):
+        count = lax.axis_size("dp")
+        rows, cols = piece.shape
+        if kind == "cols":
+            self.shape = (2 * rows, count * cols)
+        else:
+            self.shape = (2 * count * rows, cols)
+        self.size = self.shape[0] * self.shape[1]
+        if kind == "cols" and cols % 128:
+            s, d = lax.axis_index("section"), lax.axis_index("dp")
+            near = lax.dynamic_update_index_in_dim(near, piece, d, 0)
+            both = jnp.stack([jnp.where(s == 0, near, far), jnp.where(s == 0, far, near)])
+            self.parts = [both.transpose(0, 2, 1, 3).reshape(self.shape)]
+            self.kind, self.loads = "whole", 1
+        else:
+            self.kind, self.parts, self.loads = kind, [piece, near, far], 2 * count
+
+    def copies(self, refs, dst, sem):
+        if self.kind == "whole":
+            return [pltpu.make_async_copy(refs[0], dst, sem.at[0])]
+        s, d = lax.axis_index("section"), lax.axis_index("dp")
+        count = lax.axis_size("dp")
+        rows, cols = self.parts[0].shape
+
+        def place(sec, own):
+            if self.kind == "cols":
+                top = pl.multiple_of(sec * rows, rows)
+                return dst.at[pl.ds(top, rows), pl.ds(pl.multiple_of(own * cols, cols), cols)]
+            slot = own * 2 + sec if self.kind == "rows" else sec * count + own
+            return dst.at[pl.ds(pl.multiple_of(slot * rows, rows), rows)]
+
+        moves = []
+        for k in range(count):
+            other = (d + k) % count
+            near = refs[0] if k == 0 else refs[1].at[other]
+            moves.append(pltpu.make_async_copy(near, place(s, other), sem.at[2 * k]))
+            moves.append(
+                pltpu.make_async_copy(refs[2].at[other], place(1 - s, other), sem.at[2 * k + 1])
+            )
+        return moves
 
 
 def silu_parts(gate):
@@ -113,44 +336,48 @@
     return sig, gate * sig
 
 
-def gather_kernel(cfg, *refs):
+def gather_kernel(cfg, weights, bg, *refs):
     norm, n_w, n_x, trans, epilogue = cfg
     it = iter(refs)
     x_ref = next(it)
     gain_ref = next(it) if norm else None
-    w_hbm = [next(it) for _ in range(n_w)]
+    w_hbm = [[next(it) for _ in w.parts] for w in weights]
     e_hbm = [next(it) for _ in range(n_x)]
+    bg_in = [next(it) for _ in bg.inputs]
     a_hbm = next(it)
     n_out = {"plain": n_w, "ffn": 3, "ffn_back": 2}[epilogue]
     o_hbm = [next(it) for _ in range(n_out)]
+    bg.bind(iter(bg_in), it)
     full = next(it)
     w_v = [next(it) for _ in range(n_w)]
     e_v = [next(it) for _ in range(n_x)]
     o_v = [next(it) for _ in range(n_out)]
-    in_sem, out_sem, a_sem, xs, xr, ss, sr, ls, lr = it
+    w_sem, in_sem, out_sem, a_sem, xs, xr, ss, sr, ls, lr, *bg_sems = it
 
     me, sib, cross, diag = places()
     rows = x_ref.shape[0]
     half = rows // 2
     loads = [
         pltpu.make_async_copy(src, dst, in_sem.at[i])
-        for i, (src, dst) in enumerate(zip(w_hbm + e_hbm, w_v + e_v))
+        for i, (src, dst) in enumerate(zip(e_hbm, e_v))
     ]
+    for i, w in enumerate(weights):
+        loads += w.copies(w_hbm[i], w_v[i], w_sem.at[i])
     for load in loads:
         load.start()
-    greet(sib, cross)
+    greet(bg.peers([{"tensor": sib}, {"tensor": cross}]))
 
     def span(owner, sub):
         return pl.ds(pl.multiple_of(owner * rows + sub * half, half), half)
 
     def to_cross(i):
-        return remote(full.at[span(me, i)], full.at[span(me, i)], xs.at[i], xr.at[i], cross)
+        return remote(full.at[span(me, i)], full.at[span(me, i)], xs.at[i], xr.at[i], {"tensor": cross})
 
     def to_sib(i):
-        return remote(full.at[span(me, i)], full.at[span(me, i)], ss.at[i], sr.at[i], sib)
+        return remote(full.at[span(me, i)], full.at[span(me, i)], ss.at[i], sr.at[i], {"tensor": sib})
 
     def relay(i):
-        return remote(full.at[span(cross, i)], full.at[span(cross, i)], ls.at[i], lr.at[i], sib)
+        return remote(full.at[span(cross, i)], full.at[span(cross, i)], ls.at[i], lr.at[i], {"tensor": sib})
 
     for i in range(2):
         part = x_ref[pl.ds(i * half, half), :]
@@ -159,6 +386,7 @@
         full[span(me, i), :] = part.astype(BF)
         to_cross(i).start()
         to_sib(i).start()
+    bg.start(bg_sems)
     for load in loads:
         load.wait()
 
@@ -219,77 +447,90 @@
             pltpu.make_async_copy(
                 full.at[pl.ds(0, half)], a_hbm.at[pl.ds(0, half)], a_sem.at[p, k]
             ).wait()
-
-
-def gather_mm(x_rows, gain, weights, extras=(), trans=False, epilogue="plain", cid=0, out_type=F32):
+    bg.finish(bg_sems)
+
+
+def gather_mm(x_rows, gain, weights, extras=(), trans=False, epilogue="plain", cid=0, tasks=()):
     rows, width = x_rows.shape
     length = rows * 4
     cols = [w.shape[0] if trans else w.shape[1] for w in weights]
     if epilogue == "plain":
-        outs = [(c, out_type) for c in cols]
+        outs = [(c, F32) for c in cols]
     else:
         outs = [(cols[0], BF)] * (3 if epilogue == "ffn" else 2)
     norm = gain is not None
     cfg = (norm, len(weights), len(extras), trans, epilogue)
-    operands = [x_rows] + ([gain.reshape(1, width)] if norm else []) + list(weights) + list(extras)
+    bg = Background(tasks)
+    parts = [part for w in weights for part in w.parts]
+    operands = [x_rows] + ([gain.reshape(1, width)] if norm else []) + parts + list(extras)
+    n_out = 1 + len(outs)
     flops = sum(2 * length * width * c for c in cols)
     moved = sum(w.size * 2 for w in weights) + sum(length * c * 2 for c, _ in outs) + length * width * 4
-    return pl.pallas_call(
-        functools.partial(gather_kernel, cfg),
+    result = pl.pallas_call(
+        functools.partial(gather_kernel, cfg, weights, bg),
         out_shape=[jax.ShapeDtypeStruct((length, width), BF)]
-        + [jax.ShapeDtypeStruct((length, c), t) for c, t in outs],
-        in_specs=[VM] * (2 if norm else 1) + [ANY] * (len(weights) + len(extras)),
-        out_specs=[ANY] * (1 + len(outs)),
+        + [jax.ShapeDtypeStruct((length, c), t) for c, t in outs]
+        + bg.outs,
+        in_specs=[VM] * (2 if norm else 1) + [ANY] * (len(parts) + len(extras) + len(bg.inputs)),
+        out_specs=[ANY] * (n_out + len(bg.outs)),
         scratch_shapes=[pltpu.VMEM((length, width), BF)]
         + [pltpu.VMEM(w.shape, BF) for w in weights]
         + [pltpu.VMEM(e.shape, e.dtype) for e in extras]
         + [pltpu.VMEM((length, c), t) for c, t in outs]
-        + [DMA((len(weights) + len(extras),)), DMA((4, 2, len(outs))), DMA((4, 2))]
-        + [DMA((2,))] * 6,
+        + [DMA((len(weights), max(w.loads for w in weights)))]
+        + [DMA((max(len(extras), 1),)), DMA((4, 2, len(outs))), DMA((4, 2))]
+        + [DMA((2,))] * 6
+        + bg.scratch,
         compiler_params=pltpu.CompilerParams(
             collective_id=cid, has_side_effects=True, vmem_limit_bytes=VMEM_BYTES
         ),
         cost_estimate=pl.CostEstimate(flops=flops, bytes_accessed=moved * 4, transcendentals=0),
         name=f"gather{cid}",
-    )(*operands)
-
-
-def scatter_kernel(cfg, *refs):
+    )(*operands, *bg.inputs)
+    return result[:n_out], result[n_out:]
+
+
+def scatter_kernel(cfg, weights, bg, *refs):
     n_y, trans, epilogue = cfg
     it = iter(refs)
     y_hbm = [next(it) for _ in range(n_y)]
-    w_hbm = [next(it) for _ in range(n_y)]
+    w_hbm = [[next(it) for _ in w.parts] for w in weights]
     resid_ref = next(it)
     if epilogue == "back":
         value_ref, gain_ref = next(it), next(it)
+    bg_in = [next(it) for _ in bg.inputs]
     out_ref = next(it)
     if epilogue == "back":
         gain_out = next(it)
+    bg.bind(iter(bg_in), it)
     y_v = [next(it) for _ in range(n_y)]
     w_v = [next(it) for _ in range(n_y)]
     keep, own, to_s, from_s, to_c, from_c, to_o, from_o = (next(it) for _ in range(8))
-    in_sem, ds, dr, cs, cr, os_, or_ = it
+    w_sem, in_sem, ds, dr, cs, cr, os_, or_, *bg_sems = it
 
     me, sib, cross, diag = places()
     rows = resid_ref.shape[0]
     half = rows // 2
     loads = [
         pltpu.make_async_copy(src, dst, in_sem.at[i])
-        for i, (src, dst) in enumerate(zip(y_hbm + w_hbm, y_v + w_v))
+        for i, (src, dst) in enumerate(zip(y_hbm, y_v))
     ]
+    for i, w in enumerate(weights):
+        loads += w.copies(w_hbm[i], w_v[i], w_sem.at[i])
     for load in loads:
         load.start()
-    greet(sib, cross)
+    greet(bg.peers([{"tensor": sib}, {"tensor": cross}]))
+    bg.start(bg_sems)
     for load in loads:
         load.wait()
 
     def send_diag(i):
-        return remote(to_s.at[i], from_s.at[i], ds.at[i], dr.at[i], sib)
+        return remote(to_s.at[i], from_s.at[i], ds.at[i], dr.at[i], {"tensor": sib})
 
     def send_cross(i):
-        return remote(to_c.at[i], from_c.at[i], cs.at[i], cr.at[i], cross)
-
-    send_near = remote(to_o, from_o, os_, or_, sib)
+        return remote(to_c.at[i], from_c.at[i], cs.at[i], cr.at[i], {"tensor": cross})
+
+    send_near = remote(to_o, from_o, os_, or_, {"tensor": sib})
 
     def pass_on(i):
         send_diag(i).wait_recv()
@@ -352,9 +593,10 @@
     for i in range(2):
         send_diag(i).wait_send()
         send_cross(i).wait_send()
-
-
-def scatter_mm(operands, weights, resid, back=None, trans=False, cid=0):
+    bg.finish(bg_sems)
+
+
+def scatter_mm(operands, weights, resid, back=None, trans=False, cid=0, tasks=()):
     rows, width = resid.shape
     half = rows // 2
     epilogue = "plain" if back is None else "back"
@@ -362,28 +604,34 @@
     out_shape = [jax.ShapeDtypeStruct((rows, width), F32)]
     if back is not None:
         out_shape.append(jax.ShapeDtypeStruct((1, width), F32))
+    n_out = len(out_shape)
+    bg = Background(tasks)
+    parts = [part for w in weights for part in w.parts]
     flops = sum(2 * y.size * width for y in operands)
     moved = sum(2 * (y.size + w.size) for y, w in zip(operands, weights)) + rows * width * 12
     result = pl.pallas_call(
-        functools.partial(scatter_kernel, (len(operands), trans, epilogue)),
-        out_shape=out_shape,
-        in_specs=[ANY] * (2 * len(operands)) + [VM] * (1 + len(extra)),
-        out_specs=[VM] * len(out_shape),
+        functools.partial(scatter_kernel, (len(operands), trans, epilogue), weights, bg),
+        out_shape=out_shape + bg.outs,
+        in_specs=[ANY] * (len(operands) + len(parts))
+        + [VM] * (1 + len(extra))
+        + [ANY] * len(bg.inputs),
+        out_specs=[VM] * n_out + [ANY] * len(bg.outs),
         scratch_shapes=[pltpu.VMEM(y.shape, BF) for y in operands]
         + [pltpu.VMEM(w.shape, BF) for w in weights]
         + [pltpu.VMEM((2, half, width), F32), pltpu.VMEM((rows, width), F32)]
         + [pltpu.VMEM((2, half, width), BF)] * 4
         + [pltpu.VMEM((rows, width), BF)] * 2
-        + [DMA((2 * len(operands),))]
+        + [DMA((len(weights), max(w.loads for w in weights))), DMA((len(operands),))]
         + [DMA((2,))] * 4
-        + [DMA] * 2,
+        + [DMA] * 2
+        + bg.scratch,
         compiler_params=pltpu.CompilerParams(
             collective_id=cid, has_side_effects=True, vmem_limit_bytes=VMEM_BYTES
         ),
         cost_estimate=pl.CostEstimate(flops=flops, bytes_accessed=moved * 4, transcendentals=0),
         name=f"scatter{cid}",
-    )(*operands, *weights, resid, *extra)
-    return result[0] if back is None else result
+    )(*operands, *parts, resid, *extra, *bg.inputs)
+    return result[:n_out], result[n_out:]
 
 
 def conv_core(projected, x_value, kernel):
@@ -515,147 +763,233 @@
     return (grad_proj, jnp.stack([q_gain_grad, k_gain_grad]))
 
 
-SWAP = [(0, 1), (1, 0)]
-WHOLE = ("section", "dp")
-
-
-def gather_rows(shard):
-    both = lax.all_gather(shard, WHOLE, axis=0, tiled=True)
-    size = both.shape[0] // 2
-    return both[:size], both[size:]
-
-
-def gather_cols(shard):
-    both = lax.all_gather(shard, WHOLE, axis=0, tiled=False)
-    count, rows, cols = both.shape
-    both = both.reshape(2, count // 2, rows, cols).transpose(0, 2, 1, 3)
-    both = both.reshape(2, rows, count // 2 * cols)
-    return both[0], both[1]
+def low_grad(left_op, right_op):
+    return contract_rows(left_op, right_op).astype(BF)
 
 
 def body(boundary, norm_gain, mix_in, mix_out, w_gate, w_up, w_down, conv_x, conv_kernel, qk_gain):
-    section = lax.axis_index("section")
-    first = section == 0
+    s, d, t = (lax.axis_index(a) for a in ("section", "dp", "tensor"))
+    first = s == 0
+    count = lax.axis_size("dp")
     model_width = boundary.shape[3]
     channels = mix_out.shape[1]
 
-    slots = boundary[0]
-    mine = jnp.where(first, slots[0], slots[1])
-    theirs = jnp.where(first, slots[1], slots[0])
-    moved = lax.ppermute(theirs, "section", SWAP)
-    x_low = jnp.where(first, mine, moved)
-    cot = jnp.where(first, moved, mine)
-    gain_other = lax.ppermute(norm_gain[0], "section", SWAP)
-    gains = (
-        jnp.where(first, norm_gain[0], gain_other),
-        jnp.where(first, gain_other, norm_gain[0]),
-    )
-
-    w_in = gather_rows(mix_in[0])
-    w_cols = lax.all_gather(conv_x, WHOLE, axis=0, tiled=True)
-    w_out = gather_cols(mix_out[0])
-    gate_w = gather_rows(w_gate[0])
-    up_w = gather_rows(w_up[0])
-    down_w = gather_cols(w_down[0])
+    def halves(shard):
+        rows, cols = shard.shape
+        return shard.reshape(2, rows // 2, cols)
+
+    def pick(pair, index):
+        return lax.dynamic_index_in_dim(pair, index, 0, keepdims=False)
+
+    def by_block(kept, moved):
+        return (jnp.where(first, kept, moved), jnp.where(first, moved, kept))
+
+    def blocks_of(shards, moved):
+        return [by_block(pick(shard, s), other) for shard, other in zip(shards, moved)]
+
+    seqs = boundary[0]
+    mix_shards = [halves(mix_in[0]), halves(mix_out[0])]
+    ffn_shards = [halves(w_gate[0]), halves(w_up[0]), halves(w_down[0])]
+    moved, gain_moved, *mix_moved = exchange(
+        [x_half(seqs), x_swap(norm_gain[0])] + [x_half(v) for v in mix_shards], 16
+    )
+    x_low, cot = by_block(pick(seqs, s), moved)
+    gains = by_block(norm_gain[0], gain_moved)
+    h_in, h_out = blocks_of(mix_shards, mix_moved)
+
+    z_in0, z_cols, z_out0, *ffn_moved = exchange(
+        [z_gather(v) for v in (h_in[0], conv_x, h_out[0])] + [x_half(v) for v in ffn_shards], 17
+    )
+    h_gate, h_up, h_down = blocks_of(ffn_shards, ffn_moved)
+    x_in0, x_cols, x_out0, z_gate0 = exchange(
+        [x_gather(h_in[0], z_in0), x_gather(conv_x, z_cols), x_gather(h_out[0], z_out0)]
+        + [z_gather(h_gate[0])],
+        18,
+    )
+    in0 = Weight("rows", h_in[0], z_in0, x_in0)
+    cols = Weight("conv", conv_x, z_cols, x_cols)
+    out0 = Weight("cols", h_out[0], z_out0, x_out0)
 
     x_rows = x_low.astype(F32)
-    a0, proj0, value0 = gather_mm(x_rows, gains[0][0], [w_in[0], w_cols], cid=0)
+    (a0, proj0, value0), (x_gate0, z_up0) = gather_mm(
+        x_rows, gains[0][0], [in0, cols], cid=0, tasks=[x_gather(h_gate[0], z_gate0), z_gather(h_up[0])]
+    )
+    gate_w0 = Weight("rows", h_gate[0], z_gate0, x_gate0)
     b_gate, c_gate, product, causal = conv_core(proj0, value0, conv_kernel)
     y0 = (c_gate * causal).astype(BF)
-    mid0 = scatter_mm([y0], [w_out[0]], x_rows, cid=1)
-    m0, gate0, up0, hid0 = gather_mm(
-        mid0, gains[0][1], [gate_w[0], up_w[0]], epilogue="ffn", cid=2
-    )
-    z_rows = scatter_mm([hid0], [down_w[0]], mid0, cid=3).astype(BF).astype(F32)
-    a1, proj1 = gather_mm(z_rows, gains[1][0], [w_in[1]], cid=4)
+    (mid0,), (x_up0, z_down0) = scatter_mm(
+        [y0], [out0], x_rows, cid=1, tasks=[x_gather(h_up[0], z_up0), z_gather(h_down[0])]
+    )
+    up_w0 = Weight("rows", h_up[0], z_up0, x_up0)
+    (m0, gate0, up0, hid0), (x_down0, z_in1, z_out1) = gather_mm(
+        mid0, gains[0][1], [gate_w0, up_w0], epilogue="ffn", cid=2,
+        tasks=[x_gather(h_down[0], z_down0), z_gather(h_in[1]), z_gather(h_out[1])],
+    )
+    down_w0 = Weight("cols", h_down[0], z_down0, x_down0)
+    (z_rows,), (x_in1, x_out1, z_gate1) = scatter_mm(
+        [hid0], [down_w0], mid0, cid=3,
+        tasks=[x_gather(h_in[1], z_in1), x_gather(h_out[1], z_out1), z_gather(h_gate[1])],
+    )
+    z_rows = z_rows.astype(BF).astype(F32)
+    in1 = Weight("rows", h_in[1], z_in1, x_in1)
+    out1 = Weight("cols", h_out[1], z_out1, x_out1)
+    (a1, proj1), (x_gate1, z_up1) = gather_mm(
+        z_rows, gains[1][0], [in1], cid=4, tasks=[x_gather(h_gate[1], z_gate1), z_gather(h_up[1])]
+    )
+    gate_w1 = Weight("rows", h_gate[1], z_gate1, x_gate1)
     parts = attention_inputs(proj1, qk_gain)
     y1, log_total = attention_forward(parts)
-    mid1 = scatter_mm([y1], [w_out[1]], z_rows, cid=5)
-    m1, gate1, up1, hid1 = gather_mm(
-        mid1, gains[1][1], [gate_w[1], up_w[1]], epilogue="ffn", cid=6
-    )
-    y_rows = scatter_mm([hid1], [down_w[1]], mid1, cid=7).astype(BF)
-
-    def low_grad(left_op, right_op):
-        return contract_rows(left_op, right_op).astype(BF)
-
-    def ffn_back(dout, middle, gain, m, gate, up, hid, block, cid):
-        d_full, d_gate, d_up = gather_mm(
-            dout, None, [down_w[block]], [gate, up], trans=True, epilogue="ffn_back", cid=cid
-        )
-        grads = (low_grad(m, d_gate), low_grad(m, d_up), low_grad(hid, d_full))
-        d_mid, d_gain = scatter_mm(
-            [d_gate, d_up], [gate_w[block], up_w[block]], dout, (middle, gain), True, cid + 1
-        )
-        return d_mid, d_gain, grads
-
-    def out_back(d_mid, block, y, cid):
-        d_full, d_y = gather_mm(d_mid, None, [w_out[block]], trans=True, cid=cid)
-        return d_y, low_grad(y, d_full)
-
-    def owned(rows_first, rows_second, dim):
-        return [
-            lax.psum_scatter(g, "dp", scatter_dimension=dim, tiled=True)
-            for g in (rows_first, rows_second)
-        ]
-
-    d_mid1, gain11, (g_gate1, g_up1, g_down1) = ffn_back(
-        cot, mid1, gains[1][1], m1, gate1, up1, hid1, 1, 8
-    )
-    d_y1, g_out1 = out_back(d_mid1, 1, y1, 10)
+    (mid1,), (x_up1, z_down1) = scatter_mm(
+        [y1], [out1], z_rows, cid=5, tasks=[x_gather(h_up[1], z_up1), z_gather(h_down[1])]
+    )
+    up_w1 = Weight("rows", h_up[1], z_up1, x_up1)
+    (m1, gate1, up1, hid1), (x_down1,) = gather_mm(
+        mid1, gains[1][1], [gate_w1, up_w1], epilogue="ffn", cid=6,
+        tasks=[x_gather(h_down[1], z_down1)],
+    )
+    down_w1 = Weight("cols", h_down[1], z_down1, x_down1)
+    (y_rows,), _ = scatter_mm([hid1], [down_w1], mid1, cid=7)
+    y_rows = y_rows.astype(BF)
+
+    def split_rows(grad):
+        rows, width = grad.shape
+        return grad.reshape(count, 2, rows // (2 * count), width)
+
+    def sum_rows(grad, other):
+        kept = lax.dynamic_index_in_dim(grad, s, 1, keepdims=False)
+        return (kept.astype(F32) + other.astype(F32)).astype(BF)
+
+    def split_cols(grad):
+        rows, width = grad.shape
+        return grad.reshape(2, rows // 2, width)
+
+    def sum_cols(grad, other):
+        total = (pick(grad, s).astype(F32) + other.astype(F32)).astype(BF)
+        rows, width = total.shape
+        return total.reshape(rows, count, width // count).transpose(1, 0, 2)
+
+    def gathered(kept, others):
+        own = (jnp.arange(count) == d).reshape((count,) + (1,) * (others.ndim - 1))
+        return jnp.sum(jnp.where(own, kept, others).astype(F32), axis=0)
+
+    (d_full1, d_gate1, d_up1), _ = gather_mm(
+        cot, None, [down_w1], [gate1, up1], trans=True, epilogue="ffn_back", cid=8
+    )
+    g_down1 = split_cols(low_grad(hid1, d_full1))
+    (d_mid1, gain11), (r_down1,) = scatter_mm(
+        [d_gate1, d_up1], [gate_w1, up_w1], cot, (mid1, gains[1][1]), True, 9,
+        tasks=[x_half(g_down1)],
+    )
+    g_gate1 = split_rows(low_grad(m1, d_gate1))
+    s_down1 = sum_cols(g_down1, r_down1)
+    (d_full, d_y1), (q_down1, r_gate1) = gather_mm(
+        d_mid1, None, [out1], trans=True, cid=10, tasks=[z_scatter(s_down1), x_rows_of(g_gate1)]
+    )
+    g_out1 = split_cols(low_grad(y1, d_full))
+    g_up1 = split_rows(low_grad(m1, d_up1))
+    s_gate1 = sum_rows(g_gate1, r_gate1)
     d_proj1, head_grad = attention_back(parts, log_total, qk_gain, d_y1)
-    g_in1 = low_grad(a1, d_proj1)
-    d_z, gain10 = scatter_mm(
-        [d_proj1], [w_in[1]], d_mid1, (z_rows, gains[1][0]), True, 11
+    (d_z, gain10), (q_gate1, r_up1) = scatter_mm(
+        [d_proj1], [in1], d_mid1, (z_rows, gains[1][0]), True, 11,
+        tasks=[z_scatter(s_gate1), x_rows_of(g_up1)],
     )
     d_z = d_z.astype(BF)
-    d_mid0, gain01, (g_gate0, g_up0, g_down0) = ffn_back(
-        d_z, mid0, gains[0][1], m0, gate0, up0, hid0, 0, 12
-    )
-    d_y0, g_out0 = out_back(d_mid0, 0, y0, 14)
+    g_in1 = split_rows(low_grad(a1, d_proj1))
+    s_up1 = sum_rows(g_up1, r_up1)
+    f_down1 = gathered(s_down1, q_down1).astype(BF)
+
+    (d_full0, d_gate0, d_up0), (q_up1, r_in1, r_out1) = gather_mm(
+        d_z, None, [down_w0], [gate0, up0], trans=True, epilogue="ffn_back", cid=12,
+        tasks=[z_scatter(s_up1), x_rows_of(g_in1), x_half(g_out1)],
+    )
+    g_down0 = split_cols(low_grad(hid0, d_full0))
+    s_in1, s_out1 = sum_rows(g_in1, r_in1), sum_cols(g_out1, r_out1)
+    f_gate1 = gathered(s_gate1, q_gate1).astype(BF)
+    (d_mid0, gain01), (q_in1, q_out1, r_down0, e_down1) = scatter_mm(
+        [d_gate0, d_up0], [gate_w0, up_w0], d_z, (mid0, gains[0][1]), True, 13,
+        tasks=[z_scatter(s_in1), z_scatter(s_out1), x_half(g_down0), x_final(f_down1, 1)],
+    )
+    g_gate0 = split_rows(low_grad(m0, d_gate0))
+    s_down0 = sum_cols(g_down0, r_down0)
+    f_up1 = gathered(s_up1, q_up1).astype(BF)
+    (d_full, d_y0), (q_down0, r_gate0, e_gate1) = gather_mm(
+        d_mid0, None, [out0], trans=True, cid=14,
+        tasks=[z_scatter(s_down0), x_rows_of(g_gate0), x_final(f_gate1, 1)],
+    )
+    g_up0 = split_rows(low_grad(m0, d_up0))
+    s_gate0 = sum_rows(g_gate0, r_gate0)
     d_proj0, d_value0, kernel_grad = conv_back(proj0, value0, conv_kernel, d_y0)
-    g_in0 = low_grad(a0, d_proj0)
-    g_cols = low_grad(a0, d_value0)
-    d_x, gain00 = scatter_mm(
-        [d_proj0, d_value0], [w_in[0], w_cols], d_mid0, (x_rows, gains[0][0]), True, 15
+    f_in1 = gathered(s_in1, q_in1).astype(BF)
+    f_out1 = gathered(s_out1, q_out1).astype(BF)
+    (d_x, gain00), (q_gate0, r_up0, e_up1) = scatter_mm(
+        [d_proj0, d_value0], [in0, cols], d_mid0, (x_rows, gains[0][0]), True, 15,
+        tasks=[z_scatter(s_gate0), x_rows_of(g_up0), x_final(f_up1, 1)],
     )
     d_x = d_x.astype(BF)
-
-    pairs = [
-        owned(g_in0, g_in1, 0),
-        owned(g_out0, g_out1, 1),
-        owned(g_gate0, g_gate1, 0),
-        owned(g_up0, g_up1, 0),
-        owned(g_down0, g_down1, 1),
-    ]
-    weight_grads = []
-    for zero, one in pairs:
+    g_out0 = split_cols(low_grad(y0, d_full))
+    g_in0 = split_rows(low_grad(a0, d_proj0))
+    g_cols = low_grad(a0, d_value0).reshape(2, count, conv_x.shape[0], channels)
+    s_up0 = sum_rows(g_up0, r_up0)
+    f_down0 = gathered(s_down0, q_down0).astype(BF)
+
+    small = jnp.concatenate(
+        [
+            gain00,
+            gain01,
+            gain10,
+            gain11,
+            lax.dynamic_update_slice_in_dim(
+                jnp.zeros((conv_kernel.shape[0], model_width), F32), kernel_grad, t * channels, 1
+            ),
+            jnp.pad(head_grad.reshape(1, -1), ((0, 0), (0, model_width - head_grad.size))),
+        ],
+        axis=0,
+    )
+    out_sent = jnp.where(first, y_rows, d_x)
+    q_up0, r_in0, r_cols, r_out0, small_x, out_moved, e_in1, e_out1, e_down0 = exchange(
+        [z_scatter(s_up0), x_rows_of(g_in0), x_half(g_cols), x_half(g_out0), x_swap(small)]
+        + [x_swap(out_sent), x_final(f_in1, 1), x_final(f_out1, 1), x_final(f_down0, 0)],
+        19,
+    )
+    s_in0, s_out0 = sum_rows(g_in0, r_in0), sum_cols(g_out0, r_out0)
+    s_cols = (pick(g_cols, s).astype(F32) + r_cols.astype(F32)).astype(BF)
+    f_gate0 = gathered(s_gate0, q_gate0).astype(BF)
+    f_up0 = gathered(s_up0, q_up0).astype(BF)
+    small = small + small_x
+    q_in0, q_cols, q_out0, small_z, e_gate0, e_up0 = exchange(
+        [z_scatter(v) for v in (s_in0, s_cols, s_out0)]
+        + [z_gather(small), x_final(f_gate0, 0), x_final(f_up0, 0)],
+        20,
+    )
+    f_in0 = gathered(s_in0, q_in0).astype(BF)
+    f_out0 = gathered(s_out0, q_out0).astype(BF)
+    cols_part = gathered(s_cols, q_cols)
+    small = gathered(small[None], small_z)
+    e_in0, e_out0, small_t = exchange([x_final(f_in0, 0), x_final(f_out0, 0), t_share(small)], 21)
+    own = (jnp.arange(4) == t).reshape(4, 1, 1)
+    small = jnp.sum(jnp.where(own, small[None], small_t), axis=0)
+
+    def whole(zero, zero_other, one, one_other):
         kept = jnp.where(first, zero, one)
-        sent = jnp.where(first, one, zero)
-        other = lax.ppermute(sent, "section", SWAP)
-        weight_grads.append((kept.astype(F32) + other.astype(F32))[None])
-    cols_part = lax.psum_scatter(g_cols, WHOLE, scatter_dimension=0, tiled=True).astype(F32)
-
-    moved_out = lax.ppermute(jnp.where(first, y_rows, d_x), "section", SWAP)
-    kept_out = jnp.where(first, d_x, y_rows)
-    result = jnp.stack(
-        [jnp.where(first, kept_out, moved_out), jnp.where(first, moved_out, kept_out)]
-    )
-
-    tensor_index = lax.axis_index("tensor")
-    kernel_full = lax.dynamic_update_slice_in_dim(
-        jnp.zeros((conv_kernel.shape[0], model_width), F32), kernel_grad, tensor_index * channels, 1
-    )
-    gains_full = jnp.concatenate([gain00, gain01, gain10, gain11], axis=0)
-    gains_total, kernel_total, head_total = lax.psum(
-        (gains_full, kernel_full, head_grad), ("section", "dp", "tensor")
-    )
-    gain_out = lax.dynamic_slice_in_dim(gains_total.reshape(2, 2, model_width), section, 1, 0)
-    kernel_out = lax.dynamic_slice_in_dim(kernel_total, tensor_index * channels, channels, 1)
+        moved = jnp.where(first, zero_other, one_other)
+        rows, width = kept.shape
+        lower, upper = jnp.where(first, kept, moved), jnp.where(first, moved, kept)
+        return jnp.concatenate([lower, upper], axis=0).astype(F32)[None]
+
+    result = jnp.where(first, jnp.stack([d_x, out_moved]), jnp.stack([out_moved, y_rows]))
+    gains_total = small[:4].reshape(2, 2, model_width)
+    gain_out = lax.dynamic_slice_in_dim(gains_total, s, 1, 0)
+    kernel_rows = small[4 : 4 + conv_kernel.shape[0]]
+    kernel_out = lax.dynamic_slice_in_dim(kernel_rows, t * channels, channels, 1)
+    head_total = small[-1, : qk_gain.size].reshape(qk_gain.shape)
     return (
         result[None],
         gain_out,
-        *weight_grads,
+        whole(f_in0, e_in0, f_in1, e_in1),
+        whole(f_out0, e_out0, f_out1, e_out1),
+        whole(f_gate0, e_gate0, f_gate1, e_gate1),
+        whole(f_up0, e_up0, f_up1, e_up1),
+        whole(f_down0, e_down0, f_down1, e_down1),
         cols_part,
         kernel_out,
         head_total,

time: 1160 us -> 861 us (0.74)
  waiting for transfers between devices: 497 us -> 0 us
  Pallas kernels: 308 us -> 634 us
  blocking collectives: 83.8 us -> 0 us
  local copies, waits for them, and re-layouts: 83 us -> 40.6 us
  other arithmetic: 59.1 us -> 97.8 us
  matrix products: 93.5 us -> 77 us
  between operations: 15.2 us -> 2.3 us
  starting transfers between devices: 11.7 us -> 0 us
    reduce_scatter x11 -> x0, waiting for transfers between devices: 269 us -> none  [the longest x10 269 us: owned(): lax.psum_scatter(g, 'dp', scatter_dimension=dim, tiled=True)]
    pallas_call x8 -> x14, Pallas kernels: 142 us -> 384 us  [the longest x8 234 us: gather_mm(): pl.pallas_call(functools.partial(gather_kernel, cfg, weights, bg), out_sh...]
    all_gather x5 -> x0, waiting for transfers between devices: 210 us -> none  [the longest x3 173 us: gather_rows(): both = lax.all_gather(shard, WHOLE, axis=0, tiled=True)]
    pallas_call x8, Pallas kernels: 166 us -> 250 us  [scatter_mm(): pl.pallas_call(functools.partial(scatter_kernel, (len(operands), trans, e...]
    psum x1 -> x0, blocking collectives: 46.6 us -> none  [body(): lax.psum((gains_full, kernel_full, head_grad), ('section', 'dp', 'tensor'))]
    all_gather x1 -> x0, blocking collectives: 37.2 us -> none  [body(): w_cols = lax.all_gather(conv_x, WHOLE, axis=0, tiled=True)]
    convert_element_type x2 -> x18, other arithmetic: 3.82 us -> 25 us  [the longest x6 12.6 us: sum_rows(): return (kept.astype(F32) + other.astype(F32)).astype(BF)]
    reduce_sum x0 -> x11, other arithmetic: none -> 19.8 us  [the longest x10 18.8 us: gathered(): return jnp.sum(jnp.where(own, kept, others).astype(F32), axis=0)]
  transfers between devices with their start and end apart: 24 -> 0, of which waited for: 13 -> 0; matrix products, arithmetic and copies ran while one was open for 15% -> 0% of each run, Pallas kernels for 14% -> 0%
where the time goes in v2:
time: 861 us; the launch traced here: 852 us
  Pallas kernels  634 us (74%)
  other arithmetic  97.8 us (11%)
  matrix products  77 us (9%)
  local copies, waits for them, and re-layouts  40.6 us (5%)
    pallas_call x8, Pallas kernels, scatter_mm(): pl.pallas_call(functools.partial(scatter_kernel, (len(operands), trans, e...  250 us
    pallas_call x8, Pallas kernels, gather_mm(): pl.pallas_call(functools.partial(gather_kernel, cfg, weights, bg), out_sh...  234 us
    pallas_call x6, Pallas kernels, exchange(): pl.pallas_call(functools.partial(exchange_kernel, bg), out_shape=bg.outs,...  150 us
    dot_general x11, matrix products, contract(): lax.dot_general(left_op, right_op, (((left_dim,), (right_dim,)), ((), ())...  43.2 us
    reduce_sum x10, other arithmetic, gathered(): return jnp.sum(jnp.where(own, kept, others).astype(F32), axis=0)  18.8 us

profile of v2, /device:TPU:0, one launch (start us, length us, event | category | flops | bytes accessed | tf_op | source)
XLA Modules:
  0.0 852.1 jit_solution(4624684625767602145)
XLA Ops:
  5.6 19.7 %exchange16.1 = (bf16[256,1024]{1,0:T(8,128)(2,1)}, f32[2,1024]{1,0:T(2,128)}, bf16[128,512]{1,0:T(8,128)(2,1)}, bf16[128,256]{1,0:T(8,128)(2,1)}) custom-call(bf16[2,256,1024]{2,1,0:T(8,128)(2,1)} %bitcast.316, f32[2,1024]{1,0:T(2,128)} %bitcast.346, bf16[2,128,512]{2,1,0:T(8,128)(2,1)} %bitcast.339, bf16[2,128,256]{2,1,0:T(8,128)(2,1)} %bitcast.342), custom_call_target="tpu_custom_call" | custom-call | tf_op jit(solution)/shard_map/exchange16/pallas_call | solution.py:278
  32.1 2.4 fusion.51
  34.4 26.4 %exchange17.1 = (bf16[4,128,512]{2,1,0:T(8,128)(2,1)}, bf16[4,128,256]{2,1,0:T(8,128)(2,1)}, bf16[4,128,256]{2,1,0:T(8,128)(2,1)}, bf16[128,1152]{1,0:T(8,128)(2...) custom-call(bf16[128,512]{1,0:T(8,128)(2,1)} %get-tuple-element.255.refs_0_.refs_2_, bf16[128,256]{1,0:T(8,128)(2,1)} %refs_5_.3, ...), custom_call_target="tpu_custom_call" | custom-call | tf_op jit(solution)/shard_map/exchange17/pallas_call | solution.py:278
  64.9 26.3 %exchange18.1 = (bf16[4,128,512]{2,1,0:T(8,128)(2,1)}, bf16[4,128,256]{2,1,0:T(8,128)(2,1)}, bf16[4,128,256]{2,1,0:T(8,128)(2,1)}, bf16[4,128,1152]{2,1,0:T(8,128)(2,1)}) custom-call(bf16[128,512]{1,0:T(8,128)(2,1)} %get-tuple-element.255.refs_0_.refs_2_, bf16[4,128,512]{2,1,0:T(8,128)(2,1)} %get-tuple-element.113.refs_1_.refs_3_, bf16[128,256]{1,0:T(8,128)(2,1)} %refs_5_.3, ...), custom_call_target="tpu_custom_call" | custom-call | tf_op jit(solution)/shard_map/exchange18/pallas_call | solution.py:278
  91.2 32.4 %gather0.1 = (bf16[1024,1024]{1,0:T(8,128)(2,1)}, f32[1024,512]{1,0:T(8,128)}, f32[1024,256]{1,0:T(8,128)}, bf16[4,128,1152]{2,1,0:T(8,128)(2,1)}, bf16[4,128,1152]{2,1,0:T(8,128)(2,1)}) custom-call(f32[256,1024]{1,0:T(8,128)} %get-tuple-element.225.refs_0_.refs_4_.refs_9_, f32[1,1024]{1,0:T(1,128)} %get-tuple-element.289.refs_1_.refs_10_, ...), custom_call_target="tpu_custom_call" | custom-call | flops 1610612736 | bytes 29360128 | tf_op jit(solution)/shard_map/gather0/pallas_call | solution.py:469
  127.5 31.1 %scatter1.1 = (f32[256,1024]{1,0:T(8,128)}, bf16[4,128,1152]{2,1,0:T(8,128)(2,1)}, bf16[4,576,256]{2,1,0:T(8,128)(2,1)}) custom-call(bf16[1024,256]{1,0:T(8,128)(2,1)} %get-tuple-element.221.refs_0_, bf16[128,256]{1,0:T(8,128)(2,1)} %get-tuple-element.259.refs_2_.refs_4_.refs_1_, bf16[4,128,256]{2,1,0:T(8,128)(2,1)} %get-tuple-element.115.refs_5_.refs_2_, ...), custom_call_target="tpu_custom_call" | custom-call | flops 536870912 | bytes 16777216 | tf_op jit(solution)/shard_map/scatter1/pallas_call | solution.py:612
  158.6 29.7 %gather2.1 = (bf16[1024,1024]{1,0:T(8,128)(2,1)}, bf16[1024,1152]{1,0:T(8,128)(2,1)}, bf16[1024,1152]{1,0:T(8,128)(2,1)}, bf16[1024,1152]{1,0:T(8,128)(2,1)}, bf...) custom-call(f32[256,1024]{1,0:T(8,128)} %get-tuple-element.126.refs_0_.refs_4_.refs_9_, ...), custom_call_target="tpu_custom_call" | custom-call | flops 4831838208 | bytes 63963136 | tf_op jit(solution)/shard_map/gather2/pallas_call | solution.py:469
  188.3 26.7 %scatter3.1 = (f32[256,1024]{1,0:T(8,128)}, bf16[4,128,512]{2,1,0:T(8,128)(2,1)}, bf16[4,128,256]{2,1,0:T(8,128)(2,1)}, bf16[4,128,1152]{2,1,0:T(8,128)(2,1)}) custom-call(bf16[1024,1152]{1,0:T(8,128)(2,1)} %get-tuple-element.130.refs_0_, bf16[576,256]{1,0:T(8,128)(2,1)} %get-tuple-element.244.refs_7_.refs_8_.refs_1_, ...), custom_call_target="tpu_custom_call" | custom-call | flops 2415919104 | bytes 31457280 | tf_op jit(solution)/shard_map/scatter3/pallas_call | solution.py:612
  217.3 33.3 %gather4.1 = (bf16[1024,1024]{1,0:T(8,128)(2,1)}, f32[1024,512]{1,0:T(8,128)}, bf16[4,128,1152]{2,1,0:T(8,128)(2,1)}, bf16[4,128,1152]{2,1,0:T(8,128)(2,1)}) custom-call(f32[256,1024]{1,0:T(8,128)} %convert_convert_fusion.refs_0_.refs_4_.refs_5_, f32[1,1024]{1,0:T(1,128)} %get-tuple-element.267.refs_1_.refs_6_, ...), custom_call_target="tpu_custom_call" | custom-call | flops 1073741824 | bytes 25165824 | tf_op jit(solution)/shard_map/gather4/pallas_call | solution.py:469
  259.1 2.8 fusion.65
  268.6 2.8 fusion.66
  277.9 31.6 %scatter5.1 = (f32[256,1024]{1,0:T(8,128)}, bf16[4,128,1152]{2,1,0:T(8,128)(2,1)}, bf16[4,576,256]{2,1,0:T(8,128)(2,1)}) custom-call(bf16[1024,256]{1,0:T(8,128)(2,1)} %pad_maximum_fusion.4.refs_0_, bf16[128,256]{1,0:T(8,128)(2,1)} %get-tuple-element.258.refs_11_.refs_7_.refs_1_, bf16[4,128,256]{2,1,0:T(8,128)(2,1)} %get-tuple-element.133.refs_8_.refs_2_, ...), custom_call_target="tpu_custom_call" | custom-call | flops 536870912 | bytes 16777216 | tf_op jit(solution)/shard_map/scatter5/pallas_call | solution.py:612
  309.5 30.5 %gather6.1 = (bf16[1024,1024]{1,0:T(8,128)(2,1)}, bf16[1024,1152]{1,0:T(8,128)(2,1)}, bf16[1024,1152]{1,0:T(8,128)(2,1)}, bf16[1024,1152]{1,0:T(8,128)(2,1)}, bf16[4,576,256]{2,1,0:T(8,128)(2,1)}) custom-call(f32[256,1024]{1,0:T(8,128)} %get-tuple-element.141.refs_0_.refs_9_.refs_4_, f32[1,1024]{1,0:T(1,128)} %get-tuple-element.266.refs_1_.refs_10_, ...), custom_call_target="tpu_custom_call" | custom-call | flops 4831838208 | bytes 63963136 | tf_op jit(solution)/shard_map/gather6/pallas_call | solution.py:469
  340.0 21.1 %scatter7.1 = f32[256,1024]{1,0:T(8,128)} custom-call(bf16[1024,1152]{1,0:T(8,128)(2,1)} %get-tuple-element.149.refs_0_, bf16[576,256]{1,0:T(8,128)(2,1)} %get-tuple-element.245.refs_7_.refs_8_.refs_1_, bf16[4,576,256]{2,1,0:T(8,128)(2,1)} %get-tuple-element.140.refs_9_.refs_2_, bf16[4,576,256]{2,1,0:T(8,128)(2,1)} %get-tuple-element.144.refs_3_, ...), custom_call_target="tpu_custom_call" | custom-call | flops 2415919104 | bytes 31457280 | tf_op jit(solution)/shard_map/scatter7/pallas_call | solution.py:612
  361.2 17.8 %gather8.1 = (bf16[1024,1024]{1,0:T(8,128)(2,1)}, bf16[1024,1152]{1,0:T(8,128)(2,1)}, bf16[1024,1152]{1,0:T(8,128)(2,1)}) custom-call(bf16[256,1024]{1,0:T(8,128)(2,1)} %get-tuple-element.226.refs_0_.refs_8_, bf16[576,256]{1,0:T(8,128)(2,1)} %get-tuple-element.245.refs_7_.refs_8_.refs_1_, bf16[4,576,256]{2,1,0:T(8,128)(2,1)} %get-tuple-element.140.refs_9_.refs_2_, ...), custom_call_target="tpu_custom_call" | custom-call | flops 2415919104 | bytes 45088768 | tf_op jit(solution)/shard_map/gather8/pallas_call | solution.py:469
  378.9 6.3 convolution_convert_fusion.5
  385.3 33.2 %scatter9.1 = (f32[256,1024]{1,0:T(8,128)}, f32[1,1024]{1,0:T(1,128)}, bf16[576,1024]{1,0:T(8,128)(2,1)}) custom-call(bf16[1024,1152]{1,0:T(8,128)(2,1)} %get-tuple-element.147.refs_0_, bf16[1024,1152]{1,0:T(8,128)(2,1)} %get-tuple-element.148.refs_1_, bf16[128,1152]{1,0:T(8,128)(2,1)} %get-tuple-element.288.refs_9_.refs_5_.refs_2_, ...), custom_call_target="tpu_custom_call" | custom-call | flops 4831838208 | bytes 50331648 | tf_op jit(solution)/shard_map/scatter9/pallas_call | solution.py:612
  418.5 6.8 convolution_convert_fusion.3
  425.3 4.3 convolution_convert_fusion.4
  432.8 30.6 %gather10.1 = (bf16[1024,1024]{1,0:T(8,128)(2,1)}, f32[1024,256]{1,0:T(8,128)}, bf16[4,576,256]{2,1,0:T(8,128)(2,1)}, bf16[4,128,1152]{2,1,0:T(8,128)(2,1)}) custom-call(f32[256,1024]{1,0:T(8,128)} %get-tuple-element.151.refs_0_.refs_4_, bf16[128,256]{1,0:T(8,128)(2,1)} %get-tuple-element.258.refs_11_.refs_7_.refs_1_, ...), custom_call_target="tpu_custom_call" | custom-call | flops 536870912 | bytes 20971520 | tf_op jit(solution)/shard_map/gather10/pallas_call | solution.py:469
  463.5 3.0 select_reduce_fusion.5.refs_14_
  468.0 2.7 fusion.22.refs_7_
  471.1 4.8 fusion.24
  475.9 4.8 fusion.35
  481.6 5.2 fusion
  486.8 4.7 fusion.2
  494.6 5.2 fusion.3
  499.8 4.9 fusion.5
  517.6 2.5 copy.107
  520.2 2.4 multiply_reduce_fusion
  527.5 30.8 %scatter11.1 = (f32[256,1024]{1,0:T(8,128)}, f32[1,1024]{1,0:T(1,128)}, bf16[4,128,1152]{2,1,0:T(8,128)(2,1)}, bf16[4,128,1152]{2,1,0:T(8,128)(2,1)}) custom-call(bf16[1024,512]{1,0:T(8,128)(2,1)} %pad_maximum_fusion.2.refs_0_, bf16[128,512]{1,0:T(8,128)(2,1)} %get-tuple-element.254.refs_10_.refs_5_.refs_2_.refs_1_, ...), custom_call_target="tpu_custom_call" | custom-call | flops 1073741824 | bytes 20971520 | tf_op jit(solution)/shard_map/scatter11/pallas_call | solution.py:612
  558.3 3.0 fusion.21.refs_6_
  562.2 24.8 %gather12.1 = (bf16[1024,1024]{1,0:T(8,128)(2,1)}, bf16[1024,1152]{1,0:T(8,128)(2,1)}, bf16[1024,1152]{1,0:T(8,128)(2,1)}, bf16[4,128,1152]{2,1,0:T(8,128)(2,1)}...) custom-call(bf16[256,1024]{1,0:T(8,128)(2,1)} %convert_element_type.323.refs_0_.refs_8_, ...), custom_call_target="tpu_custom_call" | custom-call | flops 2415919104 | bytes 45088768 | tf_op jit(solution)/shard_map/gather12/pallas_call | solution.py:469
  587.1 3.9 select_reduce_fusion.3
  591.0 4.0 convolution_convert_fusion.2
  597.0 39.8 %scatter13.1 = (f32[256,1024]{1,0:T(8,128)}, f32[1,1024]{1,0:T(1,128)}, bf16[4,128,512]{2,1,0:T(8,128)(2,1)}, bf16[4,128,256]{2,1,0:T(8,128)(2,1)}, bf16[576,1024]{1,0:T(8,128)(2,1)}, /*index=5*/bf16[576,256]{1,0:T(8,128)(2,1)}) custom-call(bf16[1024,1152]{1,0:T(8,128)(2,1)} %get-tuple-element.162.refs_0_, bf16[1024,1152]{1,0:T(8,128)(2,1)} %get-tuple-element.163.refs_1_, ...), custom_call_target="tpu_custom_call" | custom-call | flops 4831838208 | bytes 50331648 | tf_op jit(solution)/shard_map/scatter13/pallas_call | solution.py:612
  636.8 6.8 convolution_convert_fusion
  643.7 4.3 convolution_convert_fusion.1
  651.1 35.1 %gather14.1 = (bf16[1024,1024]{1,0:T(8,128)(2,1)}, f32[1024,256]{1,0:T(8,128)}, bf16[4,576,256]{2,1,0:T(8,128)(2,1)}, bf16[4,128,1152]{2,1,0:T(8,128)(2,1)}, bf16[128,1152]{1,0:T(8,128)(2,1)}) custom-call(f32[256,1024]{1,0:T(8,128)} %get-tuple-element.168.refs_0_.refs_8_, bf16[128,256]{1,0:T(8,128)(2,1)} %get-tuple-element.259.refs_2_.refs_4_.refs_1_, ...), custom_call_target="tpu_custom_call" | custom-call | flops 536870912 | bytes 20971520 | tf_op jit(solution)/shard_map/gather14/pallas_call | solution.py:469
  686.2 2.6 select_reduce_fusion.2.refs_8_
  688.9 3.1 convolution_convert_fusion.8
  703.1 35.9 %scatter15.1 = (f32[256,1024]{1,0:T(8,128)}, f32[1,1024]{1,0:T(1,128)}, bf16[4,128,1152]{2,1,0:T(8,128)(2,1)}, bf16[4,128,1152]{2,1,0:T(8,128)(2,1)}, bf16[128,1152]{1,0:T(8,128)(2,1)}) custom-call(bf16[1024,512]{1,0:T(8,128)(2,1)} %pad_maximum_fusion.3.refs_0_, bf16[1024,256]{1,0:T(8,128)(2,1)} %copy-done.48, ...), custom_call_target="tpu_custom_call" | custom-call | flops 1610612736 | bytes 25165824 | tf_op jit(solution)/shard_map/scatter15/pallas_call | solution.py:612
  741.3 2.7 fusion.18.refs_0_
  744.8 44.4 %exchange19.1 = (bf16[4,128,1152]{2,1,0:T(8,128)(2,1)}, bf16[4,128,512]{2,1,0:T(8,128)(2,1)}, bf16[4,128,256]{2,1,0:T(8,128)(2,1)}, bf16[128,1024]{1,0:T(8,128)(...) custom-call(bf16[4,128,1152]{2,1,0:T(8,128)(2,1)} %fusion.18.refs_0_, ...), custom_call_target="tpu_custom_call" | custom-call | tf_op jit(solution)/shard_map/exchange19/pallas_call | solution.py:278
  791.2 3.5 select_reduce_fusion
  800.2 2.4 maximum_select_fusion
  803.8 25.7 %exchange20.1 = (bf16[4,128,512]{2,1,0:T(8,128)(2,1)}, bf16[4,128,256]{2,1,0:T(8,128)(2,1)}, bf16[4,128,256]{2,1,0:T(8,128)(2,1)}, f32[4,8,1024]{2,1,0:T(8,128)}...) custom-call(bf16[4,128,512]{2,1,0:T(8,128)(2,1)} %fusion.43.refs_0_, bf16[4,128,256]{2,1,0:T(8,128)(2,1)} %fusion.49.refs_1_, ...), custom_call_target="tpu_custom_call" | custom-call | tf_op jit(solution)/shard_map/exchange20/pallas_call | solution.py:278
  835.7 7.5 exchange21.1
  (362 shorter events, 113.6 us)
Async XLA Ops:
  0.6 24.6 %copy-start.93 = (f32[1,2,1024]{2,1,0:T(2,128)S(1)}, f32[1,2,1024]{2,1,0:T(2,128)}, u32[]{:S(2)}) copy-start(f32[1,2,1024]{2,1,0:T(2,128)} %param.11) | copy-start | bytes 24580
  0.7 25.9 %copy-start.84 = (bf16[1,256,256]{2,1,0:T(8,128)(2,1)S(1)}, bf16[1,256,256]{2,1,0:T(8,128)(2,1)}, u32[]{:S(2)}) copy-start(bf16[1,256,256]{2,1,0:T(8,128)(2,1)} %param.13) | copy-start | bytes 393220
  0.7 27.4 %copy-start.74 = (bf16[1,256,512]{2,1,0:T(8,128)(2,1)S(1)}, bf16[1,256,512]{2,1,0:T(8,128)(2,1)}, u32[]{:S(2)}) copy-start(bf16[1,256,512]{2,1,0:T(8,128)(2,1)} %param.12) | copy-start | bytes 786436
  2.9 122.6 %copy-start.95 = (f32[1,256]{1,0:T(1,128)}, f32[1,256]{1,0:T(1,128)S(1)}, u32[]{:S(2)}) copy-start(f32[1,256]{1,0:T(1,128)S(1)} %get-tuple-element.270) | copy-start | bytes 3076
  2.9 122.6 %copy-start.97 = (f32[1,256]{1,0:T(1,128)}, f32[1,256]{1,0:T(1,128)S(1)}, u32[]{:S(2)}) copy-start(f32[1,256]{1,0:T(1,128)S(1)} %get-tuple-element.271) | copy-start | bytes 3076
  2.9 122.6 %copy-start.99 = (f32[1,256]{1,0:T(1,128)}, f32[1,256]{1,0:T(1,128)S(1)}, u32[]{:S(2)}) copy-start(f32[1,256]{1,0:T(1,128)S(1)} %get-tuple-element.272) | copy-start | bytes 3076
  30.6 222.9 %copy-start.24 = (f32[1024,64]{0,1:T(8,128)}, f32[1024,64]{0,1:T(8,128)S(1)}, u32[]{:S(2)}) copy-start(f32[1024,64]{0,1:T(8,128)S(1)} %get-tuple-element.263) | copy-start | bytes 786436
  32.1 28.7 %copy-start.55 = (bf16[1,256,1152]{2,1,0:T(8,128)(2,1)S(1)}, bf16[1,256,1152]{2,1,0:T(8,128)(2,1)}, u32[]{:S(2)}) copy-start(bf16[1,256,1152]{2,1,0:T(8,128)(2,1)} %param.14) | copy-start | bytes 1769476
  251.9 20.7 %copy-start.35 = (bf16[1024,128]{0,1:T(8,128)(2,1)}, bf16[1024,128]{0,1:T(8,128)(2,1)S(1)}, u32[]{:S(2)}) copy-start(bf16[1024,128]{0,1:T(8,128)(2,1)S(1)} %copy.92) | copy-start | bytes 786436
  268.6 7.8 copy-start.41
  418.4 6.9 copy-start.109
  418.5 6.9 copy-start.113
  475.9 5.7 copy-start.36
  486.8 4.7 copy-start.39
  514.8 5.4 copy-start.18
  514.8 5.4 copy-start.19
  562.2 24.8 %copy-start.6 = (bf16[4,128,1152]{2,1,0:T(8,128)(2,1)S(1)}, bf16[4,128,1152]{2,1,0:T(8,128)(2,1)}, u32[]{:S(2)}) copy-start(bf16[4,128,1152]{2,1,0:T(8,128)(2,1)} %fusion.22.refs_7_) | copy-start | bytes 3538948
  591.0 4.9 copy-start.29
  591.0 4.9 copy-start.89
  636.8 6.8 copy-start.106
  636.8 6.8 copy-start.112
  643.6 5.1 copy-start.53
  643.6 5.0 copy-start.77
  643.7 5.9 copy-start.72
  686.2 5.8 copy-start.3
  686.2 5.8 copy-start.11
  686.2 5.8 copy-start.20
  686.2 5.8 copy-start.63
  703.1 35.9 %copy-start.22 = (f32[256,1024]{1,0:T(8,128)S(1)}, f32[256,1024]{1,0:T(8,128)}, u32[]{:S(2)}) copy-start(f32[256,1024]{1,0:T(8,128)} %scatter7.1) | copy-start | bytes 3145732
  744.8 44.4 %copy-start.33 = (bf16[576,256]{1,0:T(8,128)(2,1)S(1)}, bf16[576,256]{1,0:T(8,128)(2,1)}, u32[]{:S(2)}) copy-start(bf16[576,256]{1,0:T(8,128)(2,1)} %select_reduce_fusion.2.refs_8_) | copy-start | bytes 884740
  744.8 46.4 %copy-start.8 = (bf16[4,128,1152]{2,1,0:T(8,128)(2,1)S(1)}, bf16[4,128,1152]{2,1,0:T(8,128)(2,1)}, u32[]{:S(2)}) copy-start(bf16[4,128,1152]{2,1,0:T(8,128)(2,1)} %fusion.19.refs_11_) | copy-start | bytes 3538948
  791.2 4.7 copy-start.87
  794.7 4.9 copy-start.79
  794.7 4.9 copy-start.94
  794.7 5.5 copy-start.50
  795.9 6.8 copy-start.58
  795.9 6.8 copy-start.59
  802.6 26.9 %copy-start.45 = (bf16[4,128,256]{2,1,0:T(8,128)(2,1)S(1)}, bf16[4,128,256]{2,1,0:T(8,128)(2,1)}, u32[]{:S(2)}) copy-start(bf16[4,128,256]{2,1,0:T(8,128)(2,1)} %fusion.49.refs_1_) | copy-start | bytes 786436
  802.6 28.8 %copy-start.30 = (bf16[128,1152]{1,0:T(8,128)(2,1)S(1)}, bf16[128,1152]{1,0:T(8,128)(2,1)}, u32[]{:S(2)}) copy-start(bf16[128,1152]{1,0:T(8,128)(2,1)} %get-tuple-element.215.refs_13_) | copy-start | bytes 884740
  802.6 28.8 %copy-start.32 = (bf16[128,1152]{1,0:T(8,128)(2,1)S(1)}, bf16[128,1152]{1,0:T(8,128)(2,1)}, u32[]{:S(2)}) copy-start(bf16[128,1152]{1,0:T(8,128)(2,1)} %get-tuple-element.213.refs_5_) | copy-start | bytes 884740
  803.8 28.8 %copy-start.31 = (bf16[128,1152]{1,0:T(8,128)(2,1)S(1)}, bf16[128,1152]{1,0:T(8,128)(2,1)}, u32[]{:S(2)}) copy-start(bf16[128,1152]{1,0:T(8,128)(2,1)} %get-tuple-element.214.refs_4_) | copy-start | bytes 884740
  803.8 28.8 %copy-start.34 = (bf16[128,1152]{1,0:T(8,128)(2,1)S(1)}, bf16[128,1152]{1,0:T(8,128)(2,1)}, u32[]{:S(2)}) copy-start(bf16[128,1152]{1,0:T(8,128)(2,1)} %get-tuple-element.216.refs_6_) | copy-start | bytes 884740
  832.5 10.7 %copy-start.71 = (bf16[128,256]{1,0:T(8,128)(2,1)S(1)}, bf16[128,256]{1,0:T(8,128)(2,1)}, u32[]{:S(2)}) copy-start(bf16[128,256]{1,0:T(8,128)(2,1)} %select_reduce_fusion.9.refs_7_) | copy-start | bytes 196612
  832.5 10.7 %copy-start.92 = (bf16[128,256]{1,0:T(8,128)(2,1)S(1)}, bf16[128,256]{1,0:T(8,128)(2,1)}, u32[]{:S(2)}) copy-start(bf16[128,256]{1,0:T(8,128)(2,1)} %get-tuple-element.200) | copy-start | bytes 196612
  832.5 11.6 %copy-start.56 = (bf16[128,512]{1,0:T(8,128)(2,1)S(1)}, bf16[128,512]{1,0:T(8,128)(2,1)}, u32[]{:S(2)}) copy-start(bf16[128,512]{1,0:T(8,128)(2,1)} %select_reduce_fusion.7.refs_6_) | copy-start | bytes 393220
  832.6 11.6 %copy-start.91 = (bf16[128,512]{1,0:T(8,128)(2,1)S(1)}, bf16[128,512]{1,0:T(8,128)(2,1)}, u32[]{:S(2)}) copy-start(bf16[128,512]{1,0:T(8,128)(2,1)} %get-tuple-element.198) | copy-start | bytes 393220
  832.6 12.6 %copy-start.105 = (pred[4]{0:T(512)(128)(4,1)S(1)}, pred[4]{0:T(512)(128)(4,1)}, u32[]{:S(2)}) copy-start(pred[4]{0:T(512)(128)(4,1)} %iota_compare_fusion.2) | copy-start | bytes 16
  833.4 16.3 %copy-start.57 = (bf16[1,128,1152]{2,1,0:T(8,128)(2,1)S(1)}, bf16[1,128,1152]{2,1,0:T(8,128)(2,1)}, u32[]{:S(2)}) copy-start(bf16[1,128,1152]{2,1,0:T(8,128)(2,1)} %get-tuple-element.232) | copy-start | bytes 884740
  (66 other events, 181.9 us)

commit v3 on v2

v3 whole, which is shorter than its diff:
```python
import functools

import jax
import jax.numpy as jnp
from jax import lax
from jax.experimental import pallas as pl
from jax.experimental.pallas import tpu as pltpu
from jax.sharding import PartitionSpec as P

HEADS = 16
KV_HEADS = 8

EPS = 1e-05
ROPE_BASE = 1000000.0
MASKED = -1e30

MESH = pl.DeviceIdType.MESH
ANY = pl.BlockSpec(memory_space=pl.ANY)
VM = pl.BlockSpec(memory_space=pltpu.VMEM)
DMA = pltpu.SemaphoreType.DMA
VMEM_BYTES = 62 * 1024 * 1024
BF = jnp.bfloat16
F32 = jnp.float32


def contract(left_op, right_op, left_dim, right_dim):
    return lax.dot_general(
        left_op, right_op, (((left_dim,), (right_dim,)), ((), ())), preferred_element_type=F32
    )


def norm_rows(values, gain):
    return values * lax.rsqrt(jnp.mean(values * values, axis=-1, keepdims=True) + EPS) * gain


def norm_back(values, gain, grad_in):
    row_scale = lax.rsqrt(jnp.mean(values * values, axis=-1, keepdims=True) + EPS)
    normed = values * row_scale
    feature_count = values.shape[-1]
    gain_grad = jnp.sum((grad_in * normed).reshape(-1, feature_count), axis=0)
    scaled = grad_in * gain
    value_grad = row_scale * (scaled - normed * jnp.mean(scaled * normed, axis=-1, keepdims=True))
    return (value_grad, gain_grad)


def rotation(length, head_size):
    half_size = head_size // 2
    frequency = ROPE_BASE ** (-(jnp.arange(half_size, dtype=jnp.float32) * 2.0 / head_size))
    angles = jnp.arange(length, dtype=jnp.float32)[:, None] * frequency[None, :]
    cosine_table = jnp.concatenate([jnp.cos(angles), jnp.cos(angles)], axis=1)
    sine_table = jnp.concatenate([jnp.sin(angles), jnp.sin(angles)], axis=1)
    return (cosine_table, sine_table)


def delayed(values, delay_by):
    if delay_by == 0:
        return values
    return jnp.concatenate(
        [jnp.zeros((delay_by, values.shape[1]), values.dtype), values[:-delay_by]], axis=0
    )


def advanced(values, delay_by):
    if delay_by == 0:
        return values
    return jnp.concatenate(
        [values[delay_by:], jnp.zeros((delay_by, values.shape[1]), values.dtype)], axis=0
    )


def places():
    me = lax.axis_index("tensor")
    sib = me + 1 - 2 * (me % 2)
    cross = (me + 2) % 4
    diag = (sib + 2) % 4
    return me, sib, cross, diag


def greet(peers):
    barrier = pltpu.get_barrier_semaphore()
    for peer in peers:
        pl.semaphore_signal(barrier, inc=1, device_id=peer, device_id_type=MESH)
    pl.semaphore_wait(barrier, len(peers))


def remote(src, dst, send_sem, recv_sem, peer):
    return pltpu.make_async_remote_copy(
        src_ref=src, dst_ref=dst, send_sem=send_sem, recv_sem=recv_sem,
        device_id=peer, device_id_type=MESH,
    )


class Task:
    def __init__(self, inputs, out, axis, moves, count, final=None, room=()):
        self.inputs, self.out, self.axis, self.count = inputs, out, axis, count
        self.make, self.final, self.room = moves, final, list(room)
        self.scratch = [DMA((count,)), DMA((count,)), DMA((2 + dp_size(),))] + self.room

    def bind(self, ins, out, scratch):
        self.ins, self.out_ref = ins, out
        self.send_sem, self.recv_sem, self.local_sem, *self.bufs = scratch

    def at(self):
        return tuple(lax.axis_index(a) for a in ("section", "dp", "tensor"))

    def local(self, src, dst, i):
        return pltpu.make_async_copy(src, dst, self.local_sem.at[i])

    def load(self):
        pass

    def pairs(self):
        remotes, locals_ = self.make(self, *self.at())
        far = [
            [(cond, remote(src, dst, self.send_sem.at[i], self.recv_sem.at[i], peer))
             for cond, src in sources]
            for i, (sources, dst, peer) in enumerate(remotes)
        ]
        near = [
            [(cond, self.local(src, dst, i)) for cond, src in sources]
            for i, (sources, dst) in enumerate(locals_)
        ]
        return far, near

    def send(self):
        far, near = self.pairs()
        s = lax.axis_index("section")
        for variants in far:
            for cond, move in variants:
                if self.final is not None:
                    cond = s == 1 - self.final
                if cond is None:
                    move.start()
                else:
                    pl.when(cond)(move.start)
        for variants in near:
            for cond, move in variants:
                if cond is None:
                    move.start()
                else:
                    pl.when(cond)(move.start)

    def wait(self):
        far, near = self.pairs()
        s = lax.axis_index("section")
        for variants in far:
            move = variants[0][1]
            if self.final is None:
                move.wait_recv()
                move.wait_send()
            else:
                pl.when(s == 1 - self.final)(move.wait_send)
                pl.when(s == self.final)(move.wait_recv)
        for variants in near:
            variants[0][1].wait()


def dp_size():
    return lax.axis_size("dp")


def like(shape, value):
    return jax.ShapeDtypeStruct(shape, value.dtype)


def z_gather(piece):
    count = dp_size()

    def moves(task, s, d, t):
        far = [([(None, task.ins[0])], task.out_ref.at[d], {"dp": (d + k) % count}) for k in range(1, count)]
        return far, [([(None, task.ins[0])], task.out_ref.at[d])]

    return Task([piece], like((count,) + piece.shape, piece), "dp", moves, count - 1)


def z_gather_half(shard, moved, block):
    count = dp_size()

    def moves(task, s, d, t):
        sources = [(s == block, task.ins[0].at[block]), (s == 1 - block, task.ins[1])]
        far = [(sources, task.out_ref.at[d], {"dp": (d + k) % count}) for k in range(1, count)]
        return far, [(sources, task.out_ref.at[d])]

    return Task([shard, moved], like((count,) + shard.shape[1:], shard), "dp", moves, count - 1)


def x_move(value, index=None):
    def moves(task, s, d, t):
        src = task.ins[0] if index is None else task.ins[0].at[1 - s]
        return [([(None, src)], task.out_ref, {"section": 1 - s})], []

    out = value.out if isinstance(value, Task) else value
    shape = out.shape if index is None else out.shape[1:]
    return Task([value], jax.ShapeDtypeStruct(shape, out.dtype), "section", moves, 1)


def x_half(shard):
    return x_move(shard, 0)


def x_rows_of(grads):
    count = dp_size()

    def moves(task, s, d, t):
        return [
            ([(None, task.ins[0].at[k, 1 - s])], task.out_ref.at[k], {"section": 1 - s})
            for k in range(count)
        ], []

    return Task([grads], like((count,) + grads.shape[2:], grads), "section", moves, count)


def t_share(value):
    def moves(task, s, d, t):
        far = [([(None, task.ins[0])], task.out_ref.at[t], {"tensor": (t + k) % 4}) for k in range(1, 4)]
        return far, [([(None, task.ins[0])], task.out_ref.at[t])]

    return Task([value], like((4,) + value.shape, value), "tensor", moves, 3)


class SumScatter(Task):
    def __init__(self, kind, grads, received):
        count = dp_size()
        if kind == "cols":
            rows, width = grads.shape[1:]
            cols, held = width // count, (rows, width)
        else:
            rows, cols = grads.shape[2:]
            held = (count, rows, cols)
        self.kind, self.cols, self.n = kind, cols, count

        def moves(task, s, d, t):
            total = task.bufs[2]
            far = []
            for k in range(1, count):
                other = (d + k) % count
                far.append(([(None, total.at[other])], task.out_ref.at[d], {"dp": other}))
            return far, [([(None, total.at[d])], task.out_ref.at[d])]

        room = [pltpu.VMEM(held, BF)] * 2 + [pltpu.VMEM((count, rows, cols), BF)]
        super().__init__(
            [grads, received], like((count, rows, cols), grads), "dp", moves, count - 1, room=room
        )

    def loads(self):
        s = lax.axis_index("section")
        kept, got = self.bufs[:2]
        if self.kind == "rows":
            moves = [self.local(self.ins[0].at[k, s], kept.at[k], 2 + k) for k in range(self.n)]
        else:
            moves = [self.local(self.ins[0].at[s], kept, 2)]
        return moves + [self.local(self.ins[1], got, 1)]

    def load(self):
        for move in self.loads():
            move.start()

    def send(self):
        for move in self.loads():
            move.wait()
        kept, got, total = self.bufs
        for k in range(self.n):
            if self.kind == "cols":
                part = (slice(None), slice(k * self.cols, (k + 1) * self.cols))
            else:
                part = k
            total[k] = (kept[part].astype(F32) + got[part].astype(F32)).astype(BF)
        super().send()


class Finish(Task):
    def __init__(self, pieces, block):
        out = pieces.out if isinstance(pieces, Task) else pieces
        count, rows, cols = out.shape
        self.n = count

        def moves(task, s, d, t):
            total = task.bufs[1]
            far = [([(None, total)], task.out_ref.at[s], {"section": 1 - s})]
            return far, [([(None, total)], task.out_ref.at[s])]

        room = [pltpu.VMEM((count, rows, cols), BF), pltpu.VMEM((rows, cols), BF)]
        super().__init__(
            [pieces], like((2, rows, cols), out), "section", moves, 1, final=block, room=room
        )

    def load(self):
        self.local(self.ins[0], self.bufs[0], 1).start()

    def send(self):
        self.local(self.ins[0], self.bufs[0], 1).wait()
        held, total = self.bufs
        acc = held[0].astype(F32)
        for k in range(1, self.n):
            acc = acc + held[k].astype(F32)
        total[...] = acc.astype(BF)
        super().send()


class Background:
    def __init__(self, tasks):
        self.tasks = list(tasks)
        self.inputs = [v for task in self.tasks for v in task.inputs if not isinstance(v, Task)]
        self.outs = [task.out for task in self.tasks]
        self.scratch = [room for task in self.tasks for room in task.scratch]

    def bind(self, it_in, it_out):
        self.in_refs = [next(it_in) for _ in self.inputs]
        self.out_refs = [next(it_out) for _ in self.outs]

    def hold(self, scratch):
        scratch, ins = iter(scratch), iter(self.in_refs)
        for task, out in zip(self.tasks, self.out_refs):
            task.out_ref = out
        for task, out in zip(self.tasks, self.out_refs):
            refs = [v.out_ref if isinstance(v, Task) else next(ins) for v in task.inputs]
            task.bind(refs, out, [next(scratch) for _ in task.scratch])

    def peers(self, tensor):
        count = dp_size()
        s, d, t = (lax.axis_index(a) for a in ("section", "dp", "tensor"))
        axes = {task.axis for task in self.tasks}
        found = []
        if "section" in axes:
            found.append({"section": 1 - s})
        if "dp" in axes:
            found += [{"dp": (d + k) % count} for k in range(1, count)]
        if "tensor" in axes:
            found += [{"tensor": (t + k) % 4} for k in range(1, 4)]
        else:
            found += tensor
        return found

    def load(self):
        for task in self.tasks:
            task.load()

    def start(self):
        for task in sorted(self.tasks, key=lambda v: isinstance(v, (SumScatter, Finish))):
            task.send()

    def finish(self):
        for task in self.tasks:
            task.wait()

    def open(self, scratch):
        self.hold(scratch)
        if self.tasks:
            self.load()
            greet(self.peers([]))
            self.start()

    def close(self):
        self.finish()

    def params(self, cid):
        if not self.tasks:
            return pltpu.CompilerParams(vmem_limit_bytes=VMEM_BYTES)
        return pltpu.CompilerParams(
            collective_id=cid, has_side_effects=True, vmem_limit_bytes=VMEM_BYTES
        )


def exchange_kernel(bg, program, *refs):
    ins = iter(refs[: len(bg.inputs)])
    outs = iter(refs[len(bg.inputs) : len(bg.inputs) + len(bg.outs)])
    bg.bind(ins, outs)
    bg.hold(refs[len(bg.inputs) + len(bg.outs) :])
    for act, task in program:
        if act == "load":
            task.load()
    greet(bg.peers([]))
    for act, task in program:
        if act == "reload":
            task.load()
        elif act == "send":
            task.send()
        elif act == "wait":
            task.wait()


def exchange(tasks, program, cid):
    bg = Background(tasks)
    return pl.pallas_call(
        functools.partial(exchange_kernel, bg, program),
        out_shape=bg.outs,
        in_specs=[ANY] * len(bg.inputs),
        out_specs=[ANY] * len(bg.outs),
        scratch_shapes=bg.scratch,
        compiler_params=bg.params(cid),
        name=f"exchange{cid}",
    )(*bg.inputs)


class Weight:
    def __init__(self, kind, near, far):
        count, rows, cols = near.shape
        if kind == "cols":
            self.shape = (2 * rows, count * cols)
        else:
            self.shape = (2 * count * rows, cols)
        self.size = self.shape[0] * self.shape[1]
        if kind == "cols" and cols % 128:
            s = lax.axis_index("section")
            both = jnp.stack([jnp.where(s == 0, near, far), jnp.where(s == 0, far, near)])
            self.parts = [both.transpose(0, 2, 1, 3).reshape(self.shape)]
            self.kind, self.loads = "whole", 1
        else:
            self.kind, self.parts, self.loads = kind, [near, far], 2 * count

    def copies(self, refs, dst, sem):
        if self.kind == "whole":
            return [pltpu.make_async_copy(refs[0], dst, sem.at[0])]
        s = lax.axis_index("section")
        count, rows, cols = self.parts[0].shape

        def place(sec, own):
            if self.kind == "cols":
                top = pl.multiple_of(sec * rows, rows)
                return dst.at[pl.ds(top, rows), pl.ds(own * cols, cols)]
            slot = own * 2 + sec if self.kind == "rows" else sec * count + own
            return dst.at[pl.ds(pl.multiple_of(slot * rows, rows), rows)]

        moves = []
        for k in range(count):
            for i, sec in enumerate((s, 1 - s)):
                moves.append(pltpu.make_async_copy(refs[i].at[k], place(sec, k), sem.at[2 * k + i]))
        return moves


def grad_chunk(cols):
    return 384 if cols % 384 == 0 else 256


def grad_copies(dst_v, dst_hbm, sem):
    chunk = grad_chunk(dst_v.shape[0])
    return [
        pltpu.make_async_copy(
            dst_v.at[pl.ds(i * chunk, chunk)], dst_hbm.at[pl.ds(i * chunk, chunk)], sem.at[i]
        )
        for i in range(dst_v.shape[0] // chunk)
    ]


def grad_products(left, right, dst_v, dst_hbm, sem):
    cols = left.shape[1]
    chunk = grad_chunk(cols)

    def step(i, carry):
        part = pl.ds(pl.multiple_of(i * chunk, chunk), chunk)
        dst_v[part, :] = contract(left[:, part], right[...], 0, 0).astype(BF)
        pltpu.make_async_copy(dst_v.at[part], dst_hbm.at[part], sem.at[i]).start()
        return carry

    lax.fori_loop(0, cols // chunk, step, 0)


def silu_parts(gate):
    sig = 1.0 / (1.0 + jnp.exp(-gate))
    return sig, gate * sig


def gather_kernel(cfg, weights, bg, *refs):
    norm, n_w, n_x, trans, epilogue, with_grad = cfg
    it = iter(refs)
    x_ref = next(it)
    gain_ref = next(it) if norm else None
    w_hbm = [[next(it) for _ in w.parts] for w in weights]
    e_hbm = [next(it) for _ in range(n_x)]
    left_hbm = next(it) if with_grad else None
    bg_in = [next(it) for _ in bg.inputs]
    a_hbm = next(it)
    n_out = {"plain": n_w, "ffn": 3, "ffn_back": 2}[epilogue]
    o_hbm = [next(it) for _ in range(n_out)]
    grad_hbm = next(it) if with_grad else None
    bg.bind(iter(bg_in), it)
    full = next(it)
    w_v = [next(it) for _ in range(n_w)]
    e_v = [next(it) for _ in range(n_x)]
    o_v = [next(it) for _ in range(n_out)]
    if with_grad:
        left, grad_v, left_sem, grad_sem = (next(it) for _ in range(4))
        left_load = pltpu.make_async_copy(left_hbm, left, left_sem)
    w_sem, in_sem, out_sem, a_sem, xs, xr, ss, sr, ls, lr, *bg_room = it
    bg.hold(bg_room)

    me, sib, cross, diag = places()
    rows = x_ref.shape[0]
    half = rows // 2
    loads = [
        pltpu.make_async_copy(src, dst, in_sem.at[i])
        for i, (src, dst) in enumerate(zip(e_hbm, e_v))
    ]
    for i, w in enumerate(weights):
        loads += w.copies(w_hbm[i], w_v[i], w_sem.at[i])
    for load in loads:
        load.start()
    if with_grad:
        left_load.start()
    bg.load()
    greet(bg.peers([{"tensor": sib}, {"tensor": cross}]))

    def span(owner, sub):
        return pl.ds(pl.multiple_of(owner * rows + sub * half, half), half)

    def to_cross(i):
        return remote(full.at[span(me, i)], full.at[span(me, i)], xs.at[i], xr.at[i], {"tensor": cross})

    def to_sib(i):
        return remote(full.at[span(me, i)], full.at[span(me, i)], ss.at[i], sr.at[i], {"tensor": sib})

    def relay(i):
        return remote(full.at[span(cross, i)], full.at[span(cross, i)], ls.at[i], lr.at[i], {"tensor": sib})

    for i in range(2):
        part = x_ref[pl.ds(i * half, half), :]
        if norm:
            part = norm_rows(part, gain_ref[...])
        full[span(me, i), :] = part.astype(BF)
        to_cross(i).start()
        to_sib(i).start()
    bg.start()
    for load in loads:
        load.wait()

    def step(p, carry):
        far, sub = p // 2, p % 2
        near = (1 - sub) * me + sub * sib
        first = (1 - far) * near * rows + far * (cross * rows + sub * half)
        second = (1 - far) * (near * rows + half) + far * (diag * rows + sub * half)
        pair = [pl.ds(pl.multiple_of(first, half), half), pl.ds(pl.multiple_of(second, half), half)]

        @pl.when(p == 1)
        def _():
            to_sib(0).wait_recv()
            to_sib(1).wait_recv()

        for i in range(2):

            @pl.when(p == 2 + i)
            def _():
                to_cross(i).wait_recv()
                relay(i).start()
                relay(i).wait_recv()

        a = jnp.concatenate([full[pair[0], :], full[pair[1], :]], axis=0)
        prods = [contract(a, w[...], 1, 1 if trans else 0) for w in w_v]
        if epilogue == "plain":
            values = prods
        elif epilogue == "ffn":
            sig, silu = silu_parts(prods[0])
            values = [prods[0], prods[1], silu * prods[1]]
        else:
            gate = jnp.concatenate([e_v[0][q, :] for q in pair], axis=0).astype(F32)
            up = jnp.concatenate([e_v[1][q, :] for q in pair], axis=0).astype(F32)
            sig, silu = silu_parts(gate)
            values = [prods[0] * up * sig * (1.0 + gate * (1.0 - sig)), prods[0] * silu]
        for j, value in enumerate(values):
            value = value.astype(o_v[j].dtype)
            for k in range(2):
                o_v[j][pair[k], :] = value[k * half : (k + 1) * half]
                pltpu.make_async_copy(
                    o_v[j].at[pair[k]], o_hbm[j].at[pair[k]], out_sem.at[p, k, j]
                ).start()
        for k in range(2):
            pltpu.make_async_copy(full.at[pair[k]], a_hbm.at[pair[k]], a_sem.at[p, k]).start()
        return carry

    lax.fori_loop(0, 4, step, 0)
    if with_grad:
        left_load.wait()
        grad_products(left, full, grad_v, grad_hbm, grad_sem)
        for copy in grad_copies(grad_v, grad_hbm, grad_sem):
            copy.wait()
    for i in range(2):
        to_cross(i).wait_send()
        to_sib(i).wait_send()
        relay(i).wait_send()
    for p in range(4):
        for k in range(2):
            for j in range(n_out):
                pltpu.make_async_copy(
                    o_v[j].at[pl.ds(0, half)], o_hbm[j].at[pl.ds(0, half)], out_sem.at[p, k, j]
                ).wait()
            pltpu.make_async_copy(
                full.at[pl.ds(0, half)], a_hbm.at[pl.ds(0, half)], a_sem.at[p, k]
            ).wait()
    bg.finish()


def gather_mm(x_rows, gain, weights, extras=(), trans=False, epilogue="plain", cid=0, tasks=(), left=None):
    rows, width = x_rows.shape
    length = rows * 4
    cols = [w.shape[0] if trans else w.shape[1] for w in weights]
    if epilogue == "plain":
        outs = [(c, F32) for c in cols]
    else:
        outs = [(cols[0], BF)] * (3 if epilogue == "ffn" else 2)
    norm = gain is not None
    cfg = (norm, len(weights), len(extras), trans, epilogue, left is not None)
    bg = Background(tasks)
    parts = [part for w in weights for part in w.parts]
    operands = [x_rows] + ([gain.reshape(1, width)] if norm else []) + parts + list(extras)
    n_out = 1 + len(outs)
    grad_out, grad_room = [], []
    if left is not None:
        operands.append(left)
        grad_out = [jax.ShapeDtypeStruct((left.shape[1], width), BF)]
        grad_room = [pltpu.VMEM(left.shape, BF), pltpu.VMEM((left.shape[1], width), BF), DMA]
        grad_room.append(DMA((left.shape[1] // grad_chunk(left.shape[1]),)))
        n_out += 1
    flops = sum(2 * length * width * c for c in cols)
    moved = sum(w.size * 2 for w in weights) + sum(length * c * 2 for c, _ in outs) + length * width * 4
    result = pl.pallas_call(
        functools.partial(gather_kernel, cfg, weights, bg),
        out_shape=[jax.ShapeDtypeStruct((length, width), BF)]
        + [jax.ShapeDtypeStruct((length, c), t) for c, t in outs]
        + grad_out
        + bg.outs,
        in_specs=[VM] * (2 if norm else 1)
        + [ANY] * (len(operands) - (2 if norm else 1) + len(bg.inputs)),
        out_specs=[ANY] * (n_out + len(bg.outs)),
        scratch_shapes=[pltpu.VMEM((length, width), BF)]
        + [pltpu.VMEM(w.shape, BF) for w in weights]
        + [pltpu.VMEM(e.shape, e.dtype) for e in extras]
        + [pltpu.VMEM((length, c), t) for c, t in outs]
        + grad_room
        + [DMA((len(weights), max(w.loads for w in weights)))]
        + [DMA((max(len(extras), 1),)), DMA((4, 2, len(outs))), DMA((4, 2))]
        + [DMA((2,))] * 6
        + bg.scratch,
        compiler_params=pltpu.CompilerParams(
            collective_id=cid, has_side_effects=True, vmem_limit_bytes=VMEM_BYTES
        ),
        cost_estimate=pl.CostEstimate(flops=flops, bytes_accessed=moved * 4, transcendentals=0),
        name=f"gather{cid}",
    )(*operands, *bg.inputs)
    return result[:n_out], result[n_out:]


def scatter_kernel(cfg, weights, bg, *refs):
    n_y, trans, epilogue, with_grad = cfg
    it = iter(refs)
    y_hbm = [next(it) for _ in range(n_y)]
    w_hbm = [[next(it) for _ in w.parts] for w in weights]
    resid_ref = next(it)
    if epilogue == "back":
        value_ref, gain_ref = next(it), next(it)
    left_hbm = next(it) if with_grad else None
    bg_in = [next(it) for _ in bg.inputs]
    out_ref = next(it)
    if epilogue == "back":
        gain_out = next(it)
    grad_hbm = [next(it) for _ in range(n_y)] if with_grad else []
    bg.bind(iter(bg_in), it)
    y_v = [next(it) for _ in range(n_y)]
    w_v = [next(it) for _ in range(n_y)]
    keep, own, to_s, from_s, to_c, from_c, to_o, from_o = (next(it) for _ in range(8))
    if with_grad:
        left, left_sem, grad_sem = (next(it) for _ in range(3))
        grad_v = [next(it) for _ in range(n_y)]
        left_load = pltpu.make_async_copy(left_hbm, left, left_sem)
    w_sem, in_sem, ds, dr, cs, cr, os_, or_, *bg_room = it
    bg.hold(bg_room)

    me, sib, cross, diag = places()
    rows = resid_ref.shape[0]
    half = rows // 2
    loads = [
        pltpu.make_async_copy(src, dst, in_sem.at[i])
        for i, (src, dst) in enumerate(zip(y_hbm, y_v))
    ]
    for i, w in enumerate(weights):
        loads += w.copies(w_hbm[i], w_v[i], w_sem.at[i])
    for load in loads:
        load.start()
    if with_grad:
        left_load.start()
    bg.load()
    greet(bg.peers([{"tensor": sib}, {"tensor": cross}]))
    bg.start()
    for load in loads:
        load.wait()

    def send_diag(i):
        return remote(to_s.at[i], from_s.at[i], ds.at[i], dr.at[i], {"tensor": sib})

    def send_cross(i):
        return remote(to_c.at[i], from_c.at[i], cs.at[i], cr.at[i], {"tensor": cross})

    send_near = remote(to_o, from_o, os_, or_, {"tensor": sib})

    def pass_on(i):
        send_diag(i).wait_recv()
        to_c[i] = (keep[i] + from_s[i].astype(F32)).astype(BF)
        send_cross(i).start()

    def step(p, carry):
        near, sub = p // 2, p % 2
        base = near * ((1 - sub) * sib + sub * me) * rows
        first = base + (1 - near) * (cross * rows + sub * half)
        second = base + near * half + (1 - near) * (diag * rows + sub * half)
        pair = [pl.ds(pl.multiple_of(first, half), half), pl.ds(pl.multiple_of(second, half), half)]
        total = None
        for y, w in zip(y_v, w_v):
            a = jnp.concatenate([y[pair[0], :], y[pair[1], :]], axis=0)
            prod = contract(a, w[...], 1, 1 if trans else 0)
            total = prod if total is None else total + prod

        for i in range(2):

            @pl.when(p == i)
            def _():
                keep[i] = total[:half]
                to_s[i] = total[half:].astype(BF)
                send_diag(i).start()

        @pl.when(p == 1)
        def _():
            pass_on(0)

        @pl.when(p == 2)
        def _():
            to_o[...] = total.astype(BF)
            send_near.start()
            pass_on(1)

        @pl.when(p == 3)
        def _():
            own[...] = total

        return carry

    lax.fori_loop(0, 4, step, 0)
    if with_grad:
        left_load.wait()
        for j in range(n_y):
            grad_products(left, y_v[j], grad_v[j], grad_hbm[j], grad_sem.at[j])
    send_near.wait_recv()
    gain_sum = None
    for i in range(2):
        part = pl.ds(i * half, half)
        send_cross(i).wait_recv()
        total = own[part, :] + from_o[part, :].astype(F32) + from_c[i].astype(F32)
        resid = resid_ref[part, :].astype(F32)
        if epilogue == "back":
            value_grad, gain_grad = norm_back(value_ref[part, :], gain_ref[...], total)
            out_ref[part, :] = resid + value_grad
            gain_sum = gain_grad if gain_sum is None else gain_sum + gain_grad
        else:
            out_ref[part, :] = resid + total
    if epilogue == "back":
        gain_out[...] = gain_sum.reshape(gain_out.shape)
    send_near.wait_send()
    for i in range(2):
        send_diag(i).wait_send()
        send_cross(i).wait_send()
    for j in range(n_y if with_grad else 0):
        for copy in grad_copies(grad_v[j], grad_hbm[j], grad_sem.at[j]):
            copy.wait()
    bg.finish()


def scatter_mm(operands, weights, resid, back=None, trans=False, cid=0, tasks=(), left=None):
    rows, width = resid.shape
    half = rows // 2
    epilogue = "plain" if back is None else "back"
    extra = [] if back is None else [back[0], back[1].reshape(1, width)]
    out_shape = [jax.ShapeDtypeStruct((rows, width), F32)]
    if back is not None:
        out_shape.append(jax.ShapeDtypeStruct((1, width), F32))
    n_out = len(out_shape)
    grad_out, grad_room, operand_left = [], [], []
    if left is not None:
        operand_left = [left]
        chunks = left.shape[1] // grad_chunk(left.shape[1])
        grad_out = [jax.ShapeDtypeStruct((left.shape[1], y.shape[1]), BF) for y in operands]
        grad_room = [pltpu.VMEM(left.shape, BF), DMA, DMA((len(operands), chunks))]
        grad_room += [pltpu.VMEM(g.shape, BF) for g in grad_out]
    bg = Background(tasks)
    parts = [part for w in weights for part in w.parts]
    flops = sum(2 * y.size * width for y in operands)
    moved = sum(2 * (y.size + w.size) for y, w in zip(operands, weights)) + rows * width * 12
    result = pl.pallas_call(
        functools.partial(scatter_kernel, (len(operands), trans, epilogue, left is not None), weights, bg),
        out_shape=out_shape + grad_out + bg.outs,
        in_specs=[ANY] * (len(operands) + len(parts))
        + [VM] * (1 + len(extra))
        + [ANY] * (len(operand_left) + len(bg.inputs)),
        out_specs=[VM] * n_out + [ANY] * (len(grad_out) + len(bg.outs)),
        scratch_shapes=[pltpu.VMEM(y.shape, BF) for y in operands]
        + [pltpu.VMEM(w.shape, BF) for w in weights]
        + [pltpu.VMEM((2, half, width), F32), pltpu.VMEM((rows, width), F32)]
        + [pltpu.VMEM((2, half, width), BF)] * 4
        + [pltpu.VMEM((rows, width), BF)] * 2
        + grad_room
        + [DMA((len(weights), max(w.loads for w in weights))), DMA((len(operands),))]
        + [DMA((2,))] * 4
        + [DMA] * 2
        + bg.scratch,
        compiler_params=pltpu.CompilerParams(
            collective_id=cid, has_side_effects=True, vmem_limit_bytes=VMEM_BYTES
        ),
        cost_estimate=pl.CostEstimate(flops=flops, bytes_accessed=moved * 4, transcendentals=0),
        name=f"scatter{cid}",
    )(*operands, *parts, resid, *extra, *operand_left, *bg.inputs)
    n_out += len(grad_out)
    return result[:n_out], result[n_out:]


def conv_core(projected, x_value, kernel):
    channels = x_value.shape[1]
    b_gate = projected[:, :channels]
    c_gate = projected[:, channels:]
    product = b_gate * x_value
    tap_count = kernel.shape[0]
    causal = jnp.zeros_like(product)
    for offset in range(tap_count):
        causal = causal + kernel[offset] * delayed(product, tap_count - 1 - offset)
    return (b_gate, c_gate, product, causal)


def conv_back(projected, x_value, kernel, grad_y):
    b_gate, c_gate, product, causal = conv_core(projected, x_value, kernel)
    grad_c = grad_y * causal
    grad_causal = grad_y * c_gate
    tap_count = kernel.shape[0]
    kernel_rows = []
    grad_product = jnp.zeros_like(product)
    for offset in range(tap_count):
        delay_by = tap_count - 1 - offset
        kernel_rows.append(jnp.sum(grad_causal * delayed(product, delay_by), axis=0))
        grad_product = grad_product + kernel[offset] * advanced(grad_causal, delay_by)
    grad_proj = jnp.concatenate([grad_product * x_value, grad_c], axis=1).astype(BF)
    grad_value = (grad_product * b_gate).astype(BF)
    return (grad_proj, grad_value, jnp.stack(kernel_rows))


def head_mean(values, head_size):
    width = values.shape[1]
    row = lax.broadcasted_iota(jnp.int32, (width, width), 0) // head_size
    col = lax.broadcasted_iota(jnp.int32, (width, width), 1) // head_size
    group = jnp.where(row == col, 1.0 / head_size, 0.0).astype(F32)
    return lax.dot_general(
        values, group, (((1,), (0,)), ((), ())),
        precision=lax.Precision.HIGHEST, preferred_element_type=F32,
    )


def turn(values, head_size, back):
    width, half = values.shape[1], head_size // 2
    lane = lax.broadcasted_iota(jnp.int32, values.shape, 1) % head_size
    upper = pltpu.roll(values, width - half, 1)
    lower = pltpu.roll(values, half, 1)
    return jnp.where(lane < half, upper, -lower) if back else jnp.where(lane < half, -upper, lower)


def head_norm(values, gain, head_size):
    return values * lax.rsqrt(head_mean(values * values, head_size) + EPS) * gain


def head_norm_back(values, gain, grad_in, head_size):
    row_scale = lax.rsqrt(head_mean(values * values, head_size) + EPS)
    normed = values * row_scale
    gain_grad = jnp.sum(grad_in * normed, axis=0, keepdims=True)
    scaled = grad_in * gain
    return row_scale * (scaled - normed * head_mean(scaled * normed, head_size)), gain_grad


ROW_BLOCK = 256


def block_weights(q_rows, k_rows, first_row):
    rows, length = q_rows.shape[0], k_rows.shape[0]
    scores = contract(q_rows, k_rows, 1, 1) * (q_rows.shape[1] ** -0.5)
    query = first_row + lax.broadcasted_iota(jnp.int32, (rows, length), 0)
    key = lax.broadcasted_iota(jnp.int32, (rows, length), 1)
    scores = jnp.where(key <= query, scores, MASKED)
    exps = jnp.exp(scores - jnp.max(scores, axis=1, keepdims=True))
    return exps * (1.0 / jnp.sum(exps, axis=1, keepdims=True))


def attend_kernel(dims, bg, *refs):
    length, heads, kv_heads, size = dims
    it = iter(refs)
    proj, gain, cos, sin = (next(it) for _ in range(4))
    bg_in = [next(it) for _ in bg.inputs]
    y_out, q_out, k_out = (next(it) for _ in range(3))
    bg.bind(iter(bg_in), it)
    q_h, k_h, v_h, y_h, *room = it
    bg.open(room)
    q_cols, k_cols = heads * size, kv_heads * size

    def prepare(p, carry):
        rows = pl.ds(pl.multiple_of(p * ROW_BLOCK, ROW_BLOCK), ROW_BLOCK)
        c, n = cos[rows, :], sin[rows, :]
        q = head_norm(proj[rows, :q_cols], gain[0:1, :], size)
        q = (q * c + turn(q, size, False) * n).astype(BF)
        k = head_norm(proj[rows, q_cols : q_cols + k_cols], gain[1:2, :k_cols], size)
        k = (k * c[:, :k_cols] + turn(k, size, False) * n[:, :k_cols]).astype(BF)
        q_out[rows, :] = q
        k_out[rows, :] = k
        for h in range(heads):
            q_h[h, rows, :] = q[:, h * size : (h + 1) * size]
        v = proj[rows, q_cols + k_cols :].astype(BF)
        for g in range(kv_heads):
            k_h[g, rows, :] = k[:, g * size : (g + 1) * size]
            v_h[g, rows, :] = v[:, g * size : (g + 1) * size]
        return carry

    lax.fori_loop(0, length // ROW_BLOCK, prepare, 0)

    def head(h, carry):
        g = h // (heads // kv_heads)
        for i in range(length // ROW_BLOCK):
            rows, seen = pl.ds(i * ROW_BLOCK, ROW_BLOCK), pl.ds(0, (i + 1) * ROW_BLOCK)
            weights = block_weights(q_h[h, rows, :], k_h[g, seen, :], i * ROW_BLOCK)
            y_h[h, rows, :] = contract(weights.astype(BF), v_h[g, seen, :], 1, 0).astype(BF)
        return carry

    lax.fori_loop(0, heads, head, 0)
    y_out[...] = jnp.concatenate([y_h[h] for h in range(heads)], axis=1)
    bg.close()


def attend_back_kernel(dims, bg, *refs):
    length, heads, kv_heads, size = dims
    it = iter(refs)
    proj, q_rot, k_rot, dy, gain, cos, sin = (next(it) for _ in range(7))
    bg_in = [next(it) for _ in bg.inputs]
    d_proj, q_gain, k_gain = (next(it) for _ in range(3))
    bg.bind(iter(bg_in), it)
    q_h, k_h, v_h, dy_h, dq_h, dk_h, dv_h, *room = it
    bg.open(room)
    q_cols, k_cols = heads * size, kv_heads * size
    scale = size**-0.5

    def prepare(p, carry):
        rows = pl.ds(pl.multiple_of(p * ROW_BLOCK, ROW_BLOCK), ROW_BLOCK)
        low = dy[rows, :].astype(BF)
        q, k, v = q_rot[rows, :], k_rot[rows, :], proj[rows, q_cols + k_cols :].astype(BF)
        for h in range(heads):
            q_h[h, rows, :] = q[:, h * size : (h + 1) * size]
            dy_h[h, rows, :] = low[:, h * size : (h + 1) * size]
        for g in range(kv_heads):
            k_h[g, rows, :] = k[:, g * size : (g + 1) * size]
            v_h[g, rows, :] = v[:, g * size : (g + 1) * size]
        return carry

    lax.fori_loop(0, length // ROW_BLOCK, prepare, 0)
    dk_h[...] = jnp.zeros_like(dk_h)
    dv_h[...] = jnp.zeros_like(dv_h)

    def head(h, carry):
        g = h // (heads // kv_heads)
        for i in range(length // ROW_BLOCK):
            rows, seen = pl.ds(i * ROW_BLOCK, ROW_BLOCK), pl.ds(0, (i + 1) * ROW_BLOCK)
            q, low, k = q_h[h, rows, :], dy_h[h, rows, :], k_h[g, seen, :]
            prob = block_weights(q, k, i * ROW_BLOCK)
            d_weights = contract(low, v_h[g, seen, :], 1, 1)
            dv_h[g, seen, :] += contract(prob.astype(BF), low, 0, 0)
            inner = jnp.sum(prob * d_weights, axis=1, keepdims=True)
            d_scores = (prob * (d_weights - inner)).astype(BF)
            dq_h[h, rows, :] = contract(d_scores, k, 1, 0) * scale
            dk_h[g, seen, :] += contract(d_scores, q, 0, 0) * scale
        return carry

    lax.fori_loop(0, heads, head, 0)
    q_gain[...] = jnp.zeros_like(q_gain)
    k_gain[...] = jnp.zeros_like(k_gain)

    def finish(p, carry):
        rows = pl.ds(pl.multiple_of(p * ROW_BLOCK, ROW_BLOCK), ROW_BLOCK)
        c, n = cos[rows, :], sin[rows, :]
        dq = jnp.concatenate([dq_h[h, rows, :] for h in range(heads)], axis=1)
        dk = jnp.concatenate([dk_h[g, rows, :] for g in range(kv_heads)], axis=1)
        dv = jnp.concatenate([dv_h[g, rows, :] for g in range(kv_heads)], axis=1)
        dq = dq * c + turn(dq * n, size, True)
        dk = dk * c[:, :k_cols] + turn(dk * n[:, :k_cols], size, True)
        dq, q_sum = head_norm_back(proj[rows, :q_cols], gain[0:1, :], dq, size)
        dk, k_sum = head_norm_back(
            proj[rows, q_cols : q_cols + k_cols], gain[1:2, :k_cols], dk, size
        )
        q_gain[...] += q_sum
        k_gain[...] += k_sum
        d_proj[rows, :q_cols] = dq.astype(BF)
        d_proj[rows, q_cols : q_cols + k_cols] = dk.astype(BF)
        d_proj[rows, q_cols + k_cols :] = dv.astype(BF)
        return carry

    lax.fori_loop(0, length // ROW_BLOCK, finish, 0)
    bg.close()


def attention_dims(proj, qk_gain):
    length, width = proj.shape
    size = qk_gain.shape[1]
    heads = width // 2 // size
    return length, heads, heads // (HEADS // KV_HEADS), size


def attention_tables(width, length, qk_gain):
    size = qk_gain.shape[1]
    heads = width // 2 // size
    cosine_table, sine_table = rotation(length, size)
    return [jnp.tile(v, (1, heads)) for v in (qk_gain, cosine_table, sine_table)]


def attend(proj, qk_gain, tables, cid, tasks=()):
    dims = attention_dims(proj, qk_gain)
    length, heads, kv_heads, size = dims
    bg = Background(tasks)
    out = [jax.ShapeDtypeStruct((length, heads * size), BF)] * 2
    out.append(jax.ShapeDtypeStruct((length, kv_heads * size), BF))
    result = pl.pallas_call(
        functools.partial(attend_kernel, dims, bg),
        out_shape=out + bg.outs,
        in_specs=[VM] * 4 + [ANY] * len(bg.inputs),
        out_specs=[VM] * 3 + [ANY] * len(bg.outs),
        scratch_shapes=[
            pltpu.VMEM((n, length, size), BF) for n in (heads, kv_heads, kv_heads, heads)
        ]
        + bg.scratch,
        compiler_params=bg.params(cid),
        name=f"attend{cid}",
    )(proj, *tables, *bg.inputs)
    return result[:3], result[3:]


def attend_back(proj, rotated, d_y, qk_gain, tables, cid, tasks=()):
    dims = attention_dims(proj, qk_gain)
    length, heads, kv_heads, size = dims
    bg = Background(tasks)
    out = [
        jax.ShapeDtypeStruct(proj.shape, BF),
        jax.ShapeDtypeStruct((1, heads * size), F32),
        jax.ShapeDtypeStruct((1, kv_heads * size), F32),
    ]
    shapes = [(heads, BF), (kv_heads, BF), (kv_heads, BF), (heads, BF), (heads, F32)]
    shapes += [(kv_heads, F32)] * 2
    (d_proj, q_gain, k_gain), rest = (lambda r: (r[:3], r[3:]))(
        pl.pallas_call(
            functools.partial(attend_back_kernel, dims, bg),
            out_shape=out + bg.outs,
            in_specs=[VM] * 7 + [ANY] * len(bg.inputs),
            out_specs=[VM] * 3 + [ANY] * len(bg.outs),
            scratch_shapes=[pltpu.VMEM((n, length, size), kind) for n, kind in shapes]
            + bg.scratch,
            compiler_params=bg.params(cid),
            name=f"attend_back{cid}",
        )(proj, *rotated, d_y, *tables, *bg.inputs)
    )
    head_grad = jnp.stack(
        [jnp.sum(v.reshape(-1, size), axis=0) for v in (q_gain, k_gain)]
    )
    return (d_proj, head_grad), rest


def body(boundary, norm_gain, mix_in, mix_out, w_gate, w_up, w_down, conv_x, conv_kernel, qk_gain):
    s, d, t = (lax.axis_index(a) for a in ("section", "dp", "tensor"))
    first = s == 0
    count = dp_size()
    model_width = boundary.shape[3]
    channels = mix_out.shape[1]

    def halves(shard):
        rows, cols = shard.shape
        return shard.reshape(2, rows // 2, cols)

    def pick(pair, index):
        return lax.dynamic_index_in_dim(pair, index, 0, keepdims=False)

    def by_block(kept, moved):
        return (jnp.where(first, kept, moved), jnp.where(first, moved, kept))

    seqs = boundary[0]
    sh_in, sh_out, sh_gate, sh_up, sh_down = (
        halves(v[0]) for v in (mix_in, mix_out, w_gate, w_up, w_down)
    )
    t_in, t_out, t_gate, t_seq, t_up, t_down = (
        x_half(v) for v in (sh_in, sh_out, sh_gate, seqs, sh_up, sh_down)
    )
    t_gain, zt_cols = x_move(norm_gain[0]), z_gather(conv_x)
    zt_in, zt_out, zt_gate = (
        z_gather_half(a, b, 0) for a, b in ((sh_in, t_in), (sh_out, t_out), (sh_gate, t_gate))
    )
    xt_cols, xt_in, xt_out = x_move(zt_cols), x_move(zt_in), x_move(zt_out)
    program = [("send", v) for v in (t_in, t_out, zt_cols, t_gate, t_gain, t_seq)]
    program += [("wait", t_in), ("send", zt_in), ("wait", t_out), ("send", zt_out)]
    program += [("send", t_up), ("wait", t_gate), ("send", zt_gate)]
    program += [("wait", zt_cols), ("send", xt_cols), ("wait", zt_in), ("send", xt_in)]
    program += [("wait", zt_out), ("send", xt_out), ("send", t_down)]
    rest = [t_gain, t_seq, t_up, t_down, zt_gate, xt_cols, xt_in, xt_out]
    program += [("wait", v) for v in rest]
    order = [t_in, t_out, t_gate, t_seq, t_up, t_down, t_gain]
    order += [zt_cols, zt_in, zt_out, zt_gate, xt_cols, xt_in, xt_out]
    (m_in, m_out, m_gate, m_seq, m_up, m_down, m_gain), (
        z_cols, z_in0, z_out0, z_gate0, x_cols, x_in0, x_out0
    ) = (lambda r: (r[:7], r[7:]))(exchange(order, program, 16))

    x_low, cot = by_block(pick(seqs, s), m_seq)
    gains = by_block(norm_gain[0], m_gain)
    in0, cols = Weight("rows", z_in0, x_in0), Weight("conv", z_cols, x_cols)
    out0 = Weight("cols", z_out0, x_out0)
    tables = attention_tables(2 * channels, boundary.shape[2] * 4, qk_gain)

    x_rows = x_low.astype(F32)
    (a0, proj0, value0), (x_gate0, z_up0) = gather_mm(
        x_rows, gains[0][0], [in0, cols], cid=0,
        tasks=[x_move(z_gate0), z_gather_half(sh_up, m_up, 0)],
    )
    gate_w0 = Weight("rows", z_gate0, x_gate0)
    b_gate, c_gate, product, causal = conv_core(proj0, value0, conv_kernel)
    y0 = (c_gate * causal).astype(BF)
    (mid0,), (x_up0, z_down0) = scatter_mm(
        [y0], [out0], x_rows, cid=1, tasks=[x_move(z_up0), z_gather_half(sh_down, m_down, 0)]
    )
    up_w0 = Weight("rows", z_up0, x_up0)
    (m0, gate0, up0, hid0), (x_down0, z_in1, z_out1) = gather_mm(
        mid0, gains[0][1], [gate_w0, up_w0], epilogue="ffn", cid=2,
        tasks=[x_move(z_down0), z_gather_half(sh_in, m_in, 1), z_gather_half(sh_out, m_out, 1)],
    )
    down_w0 = Weight("cols", z_down0, x_down0)
    (z_rows,), (x_in1, x_out1, z_gate1) = scatter_mm(
        [hid0], [down_w0], mid0, cid=3,
        tasks=[x_move(z_in1), x_move(z_out1), z_gather_half(sh_gate, m_gate, 1)],
    )
    z_rows = z_rows.astype(BF).astype(F32)
    in1, out1 = Weight("rows", z_in1, x_in1), Weight("cols", z_out1, x_out1)
    (a1, proj1), (x_gate1, z_up1) = gather_mm(
        z_rows, gains[1][0], [in1], cid=4,
        tasks=[x_move(z_gate1), z_gather_half(sh_up, m_up, 1)],
    )
    gate_w1 = Weight("rows", z_gate1, x_gate1)
    (y1, *rotated), (x_up1, z_down1) = attend(
        proj1, qk_gain, tables, 22, tasks=[x_move(z_up1), z_gather_half(sh_down, m_down, 1)]
    )
    up_w1 = Weight("rows", z_up1, x_up1)
    (mid1,), (x_down1,) = scatter_mm([y1], [out1], z_rows, cid=5, tasks=[x_move(z_down1)])
    down_w1 = Weight("cols", z_down1, x_down1)
    (m1, gate1, up1, hid1), _ = gather_mm(
        mid1, gains[1][1], [gate_w1, up_w1], epilogue="ffn", cid=6
    )
    (y_rows,), _ = scatter_mm([hid1], [down_w1], mid1, cid=7)
    y_rows = y_rows.astype(BF)

    def split_rows(grad):
        rows, width = grad.shape
        return grad.reshape(count, 2, rows // (2 * count), width)

    def sum_rows(grad, other):
        return SumScatter("rows", grad, other)

    def sum_cols(grad, other):
        return SumScatter("cols", grad, other)

    (_, d_gate1, d_up1, g_down1), _ = gather_mm(
        cot, None, [down_w1], [gate1, up1], trans=True, epilogue="ffn_back", cid=8, left=hid1
    )
    g_down1 = halves(g_down1)
    (d_mid1, gain11, g_gate1, g_up1), (r_down1,) = scatter_mm(
        [d_gate1, d_up1], [gate_w1, up_w1], cot, (mid1, gains[1][1]), True, 9, left=m1,
        tasks=[x_half(g_down1)],
    )
    g_gate1, g_up1 = split_rows(g_gate1), split_rows(g_up1)
    (_, d_y1, g_out1), (q_down1, r_gate1) = gather_mm(
        d_mid1, None, [out1], trans=True, cid=10, left=y1,
        tasks=[sum_cols(g_down1, r_down1), x_rows_of(g_gate1)],
    )
    g_out1 = halves(g_out1)
    (d_proj1, head_grad), (q_gate1, r_up1) = attend_back(
        proj1, rotated, d_y1, qk_gain, tables, 23,
        tasks=[sum_rows(g_gate1, r_gate1), x_rows_of(g_up1)],
    )
    (d_z, gain10, g_in1), (q_up1, r_out1, e_down1) = scatter_mm(
        [d_proj1], [in1], d_mid1, (z_rows, gains[1][0]), True, 11, left=a1,
        tasks=[sum_rows(g_up1, r_up1), x_half(g_out1), Finish(q_down1, 1)],
    )
    g_in1 = split_rows(g_in1)
    d_z = d_z.astype(BF)

    (_, d_gate0, d_up0, g_down0), (q_out1, r_in1, e_gate1) = gather_mm(
        d_z, None, [down_w0], [gate0, up0], trans=True, epilogue="ffn_back", cid=12, left=hid0,
        tasks=[sum_cols(g_out1, r_out1), x_rows_of(g_in1), Finish(q_gate1, 1)],
    )
    g_down0 = halves(g_down0)
    (d_mid0, gain01, g_gate0, g_up0), (q_in1, r_down0, e_up1) = scatter_mm(
        [d_gate0, d_up0], [gate_w0, up_w0], d_z, (mid0, gains[0][1]), True, 13, left=m0,
        tasks=[sum_rows(g_in1, r_in1), x_half(g_down0), Finish(q_up1, 1)],
    )
    g_gate0, g_up0 = split_rows(g_gate0), split_rows(g_up0)
    (_, d_y0, g_out0), (q_down0, r_gate0, e_out1) = gather_mm(
        d_mid0, None, [out0], trans=True, cid=14, left=y0,
        tasks=[sum_cols(g_down0, r_down0), x_rows_of(g_gate0), Finish(q_out1, 1)],
    )
    g_out0 = halves(g_out0)
    d_proj0, d_value0, kernel_grad = conv_back(proj0, value0, conv_kernel, d_y0)
    (d_x, gain00, g_in0, g_cols), (q_gate0, r_up0, e_in1) = scatter_mm(
        [d_proj0, d_value0], [in0, cols], d_mid0, (x_rows, gains[0][0]), True, 15, left=a0,
        tasks=[sum_rows(g_gate0, r_gate0), x_rows_of(g_up0), Finish(q_in1, 1)],
    )
    d_x = d_x.astype(BF)
    g_in0 = split_rows(g_in0)
    g_cols = g_cols.reshape(2, count, conv_x.shape[0], channels)

    small = jnp.concatenate(
        [
            gain00,
            gain01,
            gain10,
            gain11,
            lax.dynamic_update_slice_in_dim(
                jnp.zeros((conv_kernel.shape[0], model_width), F32), kernel_grad, t * channels, 1
            ),
            jnp.pad(head_grad.reshape(1, -1), ((0, 0), (0, model_width - head_grad.size))),
        ],
        axis=0,
    )
    s_up = sum_rows(g_up0, r_up0)
    t_in0, t_cols, t_out0 = x_rows_of(g_in0), x_half(g_cols), x_half(g_out0)
    s_in, s_out = sum_rows(g_in0, t_in0), sum_cols(g_out0, t_out0)
    s_cols = SumScatter("slots", g_cols, t_cols)
    f_gate, f_down, f_up = Finish(q_gate0, 0), Finish(q_down0, 0), Finish(s_up, 0)
    f_in, f_out = Finish(s_in, 0), Finish(s_out, 0)
    t_small, t_result = x_move(small), x_move(jnp.where(first, y_rows, d_x))
    program = [("load", v) for v in (s_up, f_gate, f_down)]
    program += [("send", v) for v in (t_in0, t_small, t_cols, t_out0, s_up, t_result)]
    program += [("send", f_down), ("send", f_gate)]
    program += [("wait", t_in0), ("reload", s_in), ("send", s_in)]
    program += [("wait", t_cols), ("reload", s_cols), ("wait", t_out0), ("reload", s_out)]
    program += [("send", s_out), ("send", s_cols)]
    program += [("wait", s_up), ("reload", f_up), ("send", f_up)]
    program += [("wait", s_in), ("reload", f_in), ("send", f_in)]
    program += [("wait", s_out), ("reload", f_out), ("send", f_out)]
    rest = [s_cols, t_small, t_result, f_gate, f_down, f_up, f_in, f_out]
    program += [("wait", v) for v in rest]
    order = [t_in0, t_cols, t_out0, s_up, s_in, s_out, s_cols, f_gate, f_down, f_up, f_in, f_out]
    order += [t_small, t_result]
    *_, q_cols, e_gate0, e_down0, e_up0, e_in0, e_out0, small_x, out_moved = exchange(
        order, program, 17
    )
    small = small + small_x
    t_z = z_gather(small)
    (small_z,) = exchange([t_z], [("send", t_z), ("wait", t_z)], 18)
    small = jnp.sum(small_z, axis=0)
    t_t = t_share(small)
    (small_t,) = exchange([t_t], [("send", t_t), ("wait", t_t)], 19)
    small = jnp.sum(small_t, axis=0)

    def whole(zero, one):
        kept = jnp.where(first, zero, one)
        return kept.reshape(1, -1, kept.shape[-1]).astype(F32)

    result = jnp.where(first, jnp.stack([d_x, out_moved]), jnp.stack([out_moved, y_rows]))
    gains_total = small[:4].reshape(2, 2, model_width)
    gain_out = lax.dynamic_slice_in_dim(gains_total, s, 1, 0)
    kernel_rows = small[4 : 4 + conv_kernel.shape[0]]
    kernel_out = lax.dynamic_slice_in_dim(kernel_rows, t * channels, channels, 1)
    head_total = small[-1, : qk_gain.size].reshape(qk_gain.shape)
    return (
        result[None],
        gain_out,
        whole(e_in0, e_in1),
        whole(e_out0, e_out1),
        whole(e_gate0, e_gate1),
        whole(e_up0, e_up1),
        whole(e_down0, e_down1),
        jnp.sum(q_cols.astype(F32), axis=0),
        kernel_out,
        head_total,
    )


def solution(mesh):
    in_specs = (
        P("section", "dp", "tensor", None),
        P("section", None, None),
        P("section", "dp", "tensor"),
        P("section", "tensor", "dp"),
        P("section", "dp", "tensor"),
        P("section", "dp", "tensor"),
        P("section", "tensor", "dp"),
        P(("section", "dp"), "tensor"),
        P(None, "tensor"),
        P(),
    )
    out_specs = (
        P("section", "dp", "tensor", None),
        P("section", None, None),
        P("section", "dp", "tensor"),
        P("section", "tensor", "dp"),
        P("section", "dp", "tensor"),
        P("section", "dp", "tensor"),
        P("section", "tensor", "dp"),
        P(("section", "dp"), "tensor"),
        P(None, "tensor"),
        P(),
    )
    return jax.shard_map(body, mesh=mesh, in_specs=in_specs, out_specs=out_specs, check_vma=False)
```

time: 861 us -> 723 us (0.84)
  matrix products: 77 us -> 0 us
  other arithmetic: 97.8 us -> 32.3 us
  Pallas kernels: 634 us -> 668 us
  local copies, waits for them, and re-layouts: 40.6 us -> 10.9 us
    dot_general x23 -> x0, matrix products: 77 us -> none  [the longest x11 43.2 us: contract(): lax.dot_general(left_op, right_op, (((left_dim,), (right_dim,)), ((), ())...]
    pallas_call x6, Pallas kernels: 150 us -> 206 us  [the longest x4 140 us: exchange(): pl.pallas_call(functools.partial(exchange_kernel, bg, program), out_shape...]
    convert_element_type x22 -> x5, other arithmetic: 34.3 us -> 4.86 us  [whole(): return kept.reshape(1, -1, kept.shape[-1]).astype(F32)]
    reduce_sum x18 -> x5, other arithmetic: 24.9 us -> 3.24 us  [the longest x1 1.53 us: body(): small = jnp.sum(small_z, axis=0)]
    pallas_call x8, Pallas kernels: 250 us -> 237 us  [scatter_mm(): pl.pallas_call(functools.partial(scatter_kernel, (len(operands), trans, e...]
    unnamed x228 -> x50, local copies, waits for them, and re-layouts: 13.8 us -> 1.95 us
    concatenate x8 -> x2, other arithmetic: 9.99 us -> 0.04 us  [the longest x1 0.02 us: rotation(): cosine_table = jnp.concatenate([jnp.cos(angles), jnp.cos(angles)], axis=1)]
where the time goes in v3:
time: 723 us; the launch traced here: 713 us
  Pallas kernels  668 us (92%)
  other arithmetic  32.3 us (4%)
  local copies, waits for them, and re-layouts  10.9 us (2%)
    pallas_call x8, Pallas kernels, scatter_mm(): pl.pallas_call(functools.partial(scatter_kernel, (len(operands), trans, e...  237 us
    pallas_call x8, Pallas kernels, gather_mm(): pl.pallas_call(functools.partial(gather_kernel, cfg, weights, bg), out_sh...  226 us
    pallas_call x4, Pallas kernels, exchange(): pl.pallas_call(functools.partial(exchange_kernel, bg, program), out_shape...  140 us
    pallas_call x1, Pallas kernels, attend_back(): pl.pallas_call(functools.partial(attend_back_kernel, dims, bg), out_shape...  33.6 us
    pallas_call x1, Pallas kernels, attend(): pl.pallas_call(functools.partial(attend_kernel, dims, bg), out_shape=out...  32.1 us

profile of v3, /device:TPU:0, one launch (start us, length us, event | category | flops | bytes accessed | tf_op | source)
XLA Modules:
  0.0 713.0 jit_solution(9888631601617950935)
XLA Ops:
  0.7 65.6 %exchange16.1 = (bf16[128,512]{1,0:T(8,128)(2,1)}, bf16[128,256]{1,0:T(8,128)(2,1)}, bf16[128,1152]{1,0:T(8,128)(2,1)}, bf16[256,1024]{1,0:T(8,128)(2,1)}, bf16[...) custom-call(bf16[2,128,512]{2,1,0:T(8,128)(2,1)} %bitcast.103, ...), custom_call_target="tpu_custom_call" | custom-call | tf_op jit(solution)/shard_map/exchange16/pallas_call | solution.py:384
  66.3 2.3 bitcast_select_fusion
  69.2 29.7 %gather0.1 = (bf16[1024,1024]{1,0:T(8,128)(2,1)}, f32[1024,512]{1,0:T(8,128)}, f32[1024,256]{1,0:T(8,128)}, bf16[4,128,1152]{2,1,0:T(8,128)(2,1)}, bf16[4,128,1152]{2,1,0:T(8,128)(2,1)}) custom-call(f32[256,1024]{1,0:T(8,128)} %get-tuple-element.227.refs_0_.refs_3_.refs_7_, f32[1,1024]{1,0:T(1,128)} %get-tuple-element.234.refs_1_.refs_8_, ...), custom_call_target="tpu_custom_call" | custom-call | flops 1610612736 | bytes 29360128 | tf_op jit(solution)/shard_map/gather0/pallas_call | solution.py:614
  99.0 1.8 slice_multiply_fusion
  101.2 1.6 multiply_convert_fusion.3
  102.8 31.1 %scatter1.1 = (f32[256,1024]{1,0:T(8,128)}, bf16[4,128,1152]{2,1,0:T(8,128)(2,1)}, bf16[4,576,256]{2,1,0:T(8,128)(2,1)}) custom-call(bf16[1024,256]{1,0:T(8,128)(2,1)} %get-tuple-element.224.refs_0_.refs_3_, bf16[4,128,256]{2,1,0:T(8,128)(2,1)} %get-tuple-element.124.refs_1_, bf16[4,128,256]{2,1,0:T(8,128)(2,1)} %get-tuple-element.125.refs_2_, ...), custom_call_target="tpu_custom_call" | custom-call | flops 536870912 | bytes 16777216 | tf_op jit(solution)/shard_map/scatter1/pallas_call | solution.py:784
  133.9 30.1 %gather2.1 = (bf16[1024,1024]{1,0:T(8,128)(2,1)}, bf16[1024,1152]{1,0:T(8,128)(2,1)}, bf16[1024,1152]{1,0:T(8,128)(2,1)}, bf16[1024,1152]{1,0:T(8,128)(2,1)}, bf...) custom-call(f32[256,1024]{1,0:T(8,128)} %get-tuple-element.128.refs_0_.refs_3_.refs_7_, ...), custom_call_target="tpu_custom_call" | custom-call | flops 4831838208 | bytes 63963136 | tf_op jit(solution)/shard_map/gather2/pallas_call | solution.py:614
  164.0 25.8 %scatter3.1 = (f32[256,1024]{1,0:T(8,128)}, bf16[4,128,512]{2,1,0:T(8,128)(2,1)}, bf16[4,128,256]{2,1,0:T(8,128)(2,1)}, bf16[4,128,1152]{2,1,0:T(8,128)(2,1)}) custom-call(bf16[1024,1152]{1,0:T(8,128)(2,1)} %get-tuple-element.134.refs_0_.refs_5_, bf16[4,576,256]{2,1,0:T(8,128)(2,1)} %get-tuple-element.131.refs_6_.refs_1_, ...), custom_call_target="tpu_custom_call" | custom-call | flops 2415919104 | bytes 31457280 | tf_op jit(solution)/shard_map/scatter3/pallas_call | solution.py:784
  189.7 2.3 convert_convert_fusion.refs_0_.refs_3_.refs_4_
  192.7 34.4 %gather4.1 = (bf16[1024,1024]{1,0:T(8,128)(2,1)}, f32[1024,512]{1,0:T(8,128)}, bf16[4,128,1152]{2,1,0:T(8,128)(2,1)}, bf16[4,128,1152]{2,1,0:T(8,128)(2,1)}) custom-call(f32[256,1024]{1,0:T(8,128)} %convert_convert_fusion.refs_0_.refs_3_.refs_4_, f32[1,1024]{1,0:T(1,128)} %get-tuple-element.232.refs_1_.refs_5_, ...), custom_call_target="tpu_custom_call" | custom-call | flops 1073741824 | bytes 25165824 | tf_op jit(solution)/shard_map/gather4/pallas_call | solution.py:614
  227.1 0.7 tile.13.refs_1_.refs_4_
  228.5 1.3 copy.20.refs_2_.refs_5_
  229.9 1.4 copy.21.refs_3_.refs_6_
  231.3 32.1 %attend22.1 = (bf16[1024,256]{1,0:T(8,128)(2,1)}, bf16[1024,256]{1,0:T(8,128)(2,1)}, bf16[1024,128]{1,0:T(8,128)(2,1)}, bf16[4,128,1152]{2,1,0:T(8,128)(2,1)}, bf16[4,576,256]{2,1,0:T(8,128)(2,1)}) custom-call(f32[1024,512]{1,0:T(8,128)} %get-tuple-element.142.refs_0_, f32[2,256]{1,0:T(2,128)} %tile.13.refs_1_.refs_4_, f32[1024,256]{1,0:T(8,128)} %copy.20.refs_2_.refs_5_, ...), custom_call_target="tpu_custom_call" | custom-call | tf_op jit(solution)/shard_map/attend22/pallas_call | solution.py:1015
  263.4 30.2 %scatter5.1 = (f32[256,1024]{1,0:T(8,128)}, bf16[4,576,256]{2,1,0:T(8,128)(2,1)}) custom-call(bf16[1024,256]{1,0:T(8,128)(2,1)} %get-tuple-element.147.refs_0_.refs_3_, bf16[4,128,256]{2,1,0:T(8,128)(2,1)} %get-tuple-element.137.refs_5_.refs_1_, bf16[4,128,256]{2,1,0:T(8,128)(2,1)} %get-tuple-element.148.refs_2_, ...), custom_call_target="tpu_custom_call" | custom-call | flops 536870912 | bytes 16777216 | tf_op jit(solution)/shard_map/scatter5/pallas_call | solution.py:784
  293.6 19.4 %gather6.1 = (bf16[1024,1024]{1,0:T(8,128)(2,1)}, bf16[1024,1152]{1,0:T(8,128)(2,1)}, bf16[1024,1152]{1,0:T(8,128)(2,1)}, bf16[1024,1152]{1,0:T(8,128)(2,1)}) custom-call(f32[256,1024]{1,0:T(8,128)} %get-tuple-element.150.refs_0_.refs_7_.refs_3_, f32[1,1024]{1,0:T(1,128)} %get-tuple-element.231.refs_1_.refs_8_, ...), custom_call_target="tpu_custom_call" | custom-call | flops 4831838208 | bytes 63963136 | tf_op jit(solution)/shard_map/gather6/pallas_call | solution.py:614
  313.1 22.5 %gather8.1 = (bf16[1024,1024]{1,0:T(8,128)(2,1)}, bf16[1024,1152]{1,0:T(8,128)(2,1)}, bf16[1024,1152]{1,0:T(8,128)(2,1)}, bf16[1152,1024]{1,0:T(8,128)(2,1)}) custom-call(bf16[256,1024]{1,0:T(8,128)(2,1)} %get-tuple-element.226.refs_0_.refs_6_, bf16[4,576,256]{2,1,0:T(8,128)(2,1)} %get-tuple-element.146.refs_4_.refs_1_, ...), custom_call_target="tpu_custom_call" | custom-call | flops 2415919104 | bytes 45088768 | tf_op jit(solution)/shard_map/gather8/pallas_call | solution.py:614
  335.6 32.4 %scatter9.1 = (f32[256,1024]{1,0:T(8,128)}, f32[1,1024]{1,0:T(1,128)}, bf16[1024,1152]{1,0:T(8,128)(2,1)}, bf16[1024,1152]{1,0:T(8,128)(2,1)}, bf16[576,1024]{1,0:T(8,128)(2,1)}) custom-call(bf16[1024,1152]{1,0:T(8,128)(2,1)} %get-tuple-element.156.refs_0_, bf16[1024,1152]{1,0:T(8,128)(2,1)} %get-tuple-element.157.refs_1_, ...), custom_call_target="tpu_custom_call" | custom-call | flops 4831838208 | bytes 50331648 | tf_op jit(solution)/shard_map/scatter9/pallas_call | solution.py:784
  368.0 30.5 %gather10.1 = (bf16[1024,1024]{1,0:T(8,128)(2,1)}, f32[1024,256]{1,0:T(8,128)}, bf16[256,1024]{1,0:T(8,128)(2,1)}, bf16[4,576,256]{2,1,0:T(8,128)(2,1)}, bf16[4,128,1152]{2,1,0:T(8,128)(2,1)}) custom-call(f32[256,1024]{1,0:T(8,128)} %get-tuple-element.160.refs_0_.refs_3_, bf16[4,128,256]{2,1,0:T(8,128)(2,1)} %get-tuple-element.137.refs_5_.refs_1_, ...), custom_call_target="tpu_custom_call" | custom-call | flops 536870912 | bytes 20971520 | tf_op jit(solution)/shard_map/gather10/pallas_call | solution.py:614
  398.5 33.6 %attend_back23.1 = (bf16[1024,512]{1,0:T(8,128)(2,1)}, f32[1,256]{1,0:T(1,128)}, f32[1,128]{1,0:T(1,128)}, bf16[4,128,1152]{2,1,0:T(8,128)(2,1)}, bf16[4,128,1152]{2,1,0:T(8,128)(2,1)}) custom-call(f32[1024,512]{1,0:T(8,128)} %get-tuple-element.142.refs_0_, bf16[1024,256]{1,0:T(8,128)(2,1)} %get-tuple-element.144.refs_1_, ...), custom_call_target="tpu_custom_call" | custom-call | tf_op jit(solution)/shard_map/attend_back23/pallas_call | solution.py:1042
  432.2 26.0 %scatter11.1 = (f32[256,1024]{1,0:T(8,128)}, f32[1,1024]{1,0:T(1,128)}, bf16[1024,512]{1,0:T(8,128)(2,1)}, bf16[4,128,1152]{2,1,0:T(8,128)(2,1)}, bf16[128,1024]...) custom-call(bf16[1024,512]{1,0:T(8,128)(2,1)} %get-tuple-element.166.refs_0_, ...), custom_call_target="tpu_custom_call" | custom-call | flops 1073741824 | bytes 20971520 | tf_op jit(solution)/shard_map/scatter11/pallas_call | solution.py:784
  458.1 2.1 convert_element_type.104.refs_0_.refs_6_
  460.2 26.7 %gather12.1 = (bf16[1024,1024]{1,0:T(8,128)(2,1)}, bf16[1024,1152]{1,0:T(8,128)(2,1)}, bf16[1024,1152]{1,0:T(8,128)(2,1)}, bf16[1152,1024]{1,0:T(8,128)(2,1)}, b...) custom-call(bf16[256,1024]{1,0:T(8,128)(2,1)} %convert_element_type.104.refs_0_.refs_6_, ...), custom_call_target="tpu_custom_call" | custom-call | flops 2415919104 | bytes 45088768 | tf_op jit(solution)/shard_map/gather12/pallas_call | solution.py:614
  487.0 37.1 %scatter13.1 = (f32[256,1024]{1,0:T(8,128)}, f32[1,1024]{1,0:T(1,128)}, bf16[1024,1152]{1,0:T(8,128)(2,1)}, bf16[1024,1152]{1,0:T(8,128)(2,1)}, bf16[4,128,512]{...) custom-call(bf16[1024,1152]{1,0:T(8,128)(2,1)} %get-tuple-element.177.refs_0_, ...), custom_call_target="tpu_custom_call" | custom-call | flops 4831838208 | bytes 50331648 | tf_op jit(solution)/shard_map/scatter13/pallas_call | solution.py:784
  524.1 32.4 %gather14.1 = (bf16[1024,1024]{1,0:T(8,128)(2,1)}, f32[1024,256]{1,0:T(8,128)}, bf16[256,1024]{1,0:T(8,128)(2,1)}, bf16[4,576,256]{2,1,0:T(8,128)(2,1)}, bf16[4,...) custom-call(f32[256,1024]{1,0:T(8,128)} %get-tuple-element.183.refs_0_.refs_6_, ...), custom_call_target="tpu_custom_call" | custom-call | flops 536870912 | bytes 20971520 | tf_op jit(solution)/shard_map/gather14/pallas_call | solution.py:614
  556.5 2.3 multiply_reduce_fusion.2
  559.0 1.4 copy-done.1
  560.4 1.2 multiply_convert_fusion
  561.8 1.1 pad_maximum_fusion.refs_0_
  562.9 33.6 %scatter15.1 = (f32[256,1024]{1,0:T(8,128)}, f32[1,1024]{1,0:T(1,128)}, bf16[1024,512]{1,0:T(8,128)(2,1)}, bf16[1024,256]{1,0:T(8,128)(2,1)}, bf16[4,128,1152]{2...) custom-call(bf16[1024,512]{1,0:T(8,128)(2,1)} %pad_maximum_fusion.refs_0_, ...), custom_call_target="tpu_custom_call" | custom-call | flops 1610612736 | bytes 25165824 | tf_op jit(solution)/shard_map/scatter15/pallas_call | solution.py:784
  598.7 1.3 concatenate.50.refs_10_
  600.1 20.5 %scatter7.1 = f32[256,1024]{1,0:T(8,128)} custom-call(bf16[1024,1152]{1,0:T(8,128)(2,1)} %get-tuple-element.155.refs_5_.refs_0_, bf16[4,576,256]{2,1,0:T(8,128)(2,1)} %get-tuple-element.146.refs_4_.refs_1_, bf16[4,576,256]{2,1,0:T(8,128)(2,1)} %get-tuple-element.149.refs_2_, f32[256,1024]{1,0:T(8,128)} %get-tuple-element.150.refs_0_.refs_7_.refs_3_), custom_call_target="tpu_custom_call" | custom-call | flops 2415919104 | bytes 31457280 | tf_op jit(solution)/shard_map/scatter7/pallas_call | solution.py:784
  620.6 2.2 broadcast_select_fusion.3.refs_11_
  622.8 64.0 %exchange17.1 = (bf16[4,128,512]{2,1,0:T(8,128)(2,1)}, bf16[4,128,256]{2,1,0:T(8,128)(2,1)}, bf16[128,1024]{1,0:T(8,128)(2,1)}, bf16[4,128,1152]{2,1,0:T(8,128)(...) custom-call(bf16[4,2,128,512]{3,2,1,0:T(8,128)(2,1)} %bitcast.83, ...), custom_call_target="tpu_custom_call" | custom-call | tf_op jit(solution)/shard_map/exchange17/pallas_call | solution.py:384
  686.8 1.4 convert_bitcast_fusion
  688.3 1.1 maximum_select_fusion
  690.0 6.1 exchange18.1
  696.2 1.5 reduce_sum.77.refs_0_
  697.7 4.5 exchange19.1
  702.2 1.0 reduce_sum.78
  703.8 1.0 broadcast_select_fusion.4
  704.8 0.9 bitcast_convert_fusion.3
  705.7 0.9 broadcast_select_fusion.5
  706.6 0.7 bitcast_convert_fusion.4
  707.5 1.1 bitcast_convert_fusion.2
  708.6 1.1 bitcast_convert_fusion.1
  709.8 1.1 bitcast_convert_fusion
  710.9 0.7 convert_reduce_fusion
  (85 shorter events, 7.8 us)
Async XLA Ops:
  0.6 65.6 %copy-start.4 = (bf16[1,2,256,1024]{3,2,1,0:T(8,128)(2,1)S(1)}, bf16[1,2,256,1024]{3,2,1,0:T(8,128)(2,1)}, u32[]{:S(2)}) copy-start(bf16[1,2,256,1024]{3,2,1,0:T(8,128)(2,1)} %param.10) | copy-start | bytes 3145732
  66.2 2.3 copy-start.15
  66.3 2.3 copy-start.17
  98.9 1.9 copy-start.21
  98.9 2.2 copy-start
  192.1 35.0 %copy-start.22 = (f32[2,64]{1,0:T(2,128)S(1)}, f32[2,64]{1,0:T(2,128)}, u32[]{:S(2)}) copy-start(f32[2,64]{1,0:T(2,128)} %param.19) | copy-start | bytes 1540
  558.8 1.6 copy-start.1
  560.4 1.2 copy-start.2
  562.9 34.2 %copy-start.24 = (f32[1,128]{1,0:T(1,128)S(1)}, f32[1,128]{1,0:T(1,128)}, u32[]{:S(2)}) copy-start(f32[1,128]{1,0:T(1,128)} %get-tuple-element.204) | copy-start | bytes 1540
  562.9 34.9 %copy-start.23 = (f32[1,256]{1,0:T(1,128)S(1)}, f32[1,256]{1,0:T(1,128)}, u32[]{:S(2)}) copy-start(f32[1,256]{1,0:T(1,128)} %get-tuple-element.203) | copy-start | bytes 3076
  562.9 35.8 %copy-start.18 = (f32[1,1024]{1,0:T(1,128)S(1)}, f32[1,1024]{1,0:T(1,128)}, u32[]{:S(2)}) copy-start(f32[1,1024]{1,0:T(1,128)} %get-tuple-element.202) | copy-start | bytes 12292
  562.9 35.8 %copy-start.19 = (f32[1,1024]{1,0:T(1,128)S(1)}, f32[1,1024]{1,0:T(1,128)}, u32[]{:S(2)}) copy-start(f32[1,1024]{1,0:T(1,128)} %get-tuple-element.201) | copy-start | bytes 12292
  562.9 35.8 %copy-start.20 = (f32[1,1024]{1,0:T(1,128)S(1)}, f32[1,1024]{1,0:T(1,128)}, u32[]{:S(2)}) copy-start(f32[1,1024]{1,0:T(1,128)} %get-tuple-element.200) | copy-start | bytes 12292
  600.1 20.5 %copy-start.3 = (f32[256,1024]{1,0:T(8,128)S(1)}, f32[256,1024]{1,0:T(8,128)}, u32[]{:S(2)}) copy-start(f32[256,1024]{1,0:T(8,128)} %get-tuple-element.192) | copy-start | bytes 3145732
  686.8 1.5 copy-start.11
  688.2 1.2 copy-start.12
  688.2 1.2 copy-start.16
  688.3 15.6 %copy-start.14 = (bf16[2,128,512]{2,1,0:T(8,128)(2,1)S(1)}, bf16[2,128,512]{2,1,0:T(8,128)(2,1)}, u32[]{:S(2)}) copy-start(bf16[2,128,512]{2,1,0:T(8,128)(2,1)} %get-tuple-element.208) | copy-start | bytes 786436
  689.4 17.9 %copy-start.7 = (bf16[2,128,1152]{2,1,0:T(8,128)(2,1)S(1)}, bf16[2,128,1152]{2,1,0:T(8,128)(2,1)}, u32[]{:S(2)}) copy-start(bf16[2,128,1152]{2,1,0:T(8,128)(2,1)} %get-tuple-element.212) | copy-start | bytes 1769476
  689.4 17.9 %copy-start.8 = (bf16[2,128,1152]{2,1,0:T(8,128)(2,1)S(1)}, bf16[2,128,1152]{2,1,0:T(8,128)(2,1)}, u32[]{:S(2)}) copy-start(bf16[2,128,1152]{2,1,0:T(8,128)(2,1)} %get-tuple-element.214) | copy-start | bytes 1769476
  689.4 17.9 %copy-start.9 = (bf16[2,128,1152]{2,1,0:T(8,128)(2,1)S(1)}, bf16[2,128,1152]{2,1,0:T(8,128)(2,1)}, u32[]{:S(2)}) copy-start(bf16[2,128,1152]{2,1,0:T(8,128)(2,1)} %get-tuple-element.211) | copy-start | bytes 1769476
  702.2 5.1 copy-start.10
  707.5 2.2 copy-start.5
  707.5 2.2 copy-start.6
  709.7 1.2 copy-start.13

commit v4 on v3

--- a/solution.py
+++ b/solution.py
@@ -91,6 +91,8 @@
 
 
 class Task:
+    summed = False
+
     def __init__(self, inputs, out, axis, moves, count, final=None, room=()):
         self.inputs, self.out, self.axis, self.count = inputs, out, axis, count
         self.make, self.final, self.room = moves, final, list(room)
@@ -194,6 +196,14 @@
     return Task([value], jax.ShapeDtypeStruct(shape, out.dtype), "section", moves, 1)
 
 
+def x_part(value, lo, hi):
+    def moves(task, s, d, t):
+        part = pl.ds(lo, hi - lo)
+        return [([(None, task.ins[0].at[part])], task.out_ref, {"section": 1 - s})], []
+
+    return Task([value], like((hi - lo,) + value.shape[1:], value), "section", moves, 1)
+
+
 def x_half(shard):
     return x_move(shard, 0)
 
@@ -210,15 +220,9 @@
     return Task([grads], like((count,) + grads.shape[2:], grads), "section", moves, count)
 
 
-def t_share(value):
-    def moves(task, s, d, t):
-        far = [([(None, task.ins[0])], task.out_ref.at[t], {"tensor": (t + k) % 4}) for k in range(1, 4)]
-        return far, [([(None, task.ins[0])], task.out_ref.at[t])]
-
-    return Task([value], like((4,) + value.shape, value), "tensor", moves, 3)
-
-
 class SumScatter(Task):
+    summed = True
+
     def __init__(self, kind, grads, received):
         count = dp_size()
         if kind == "cols":
@@ -269,6 +273,8 @@
 
 
 class Finish(Task):
+    summed = True
+
     def __init__(self, pieces, block):
         out = pieces.out if isinstance(pieces, Task) else pieces
         count, rows, cols = out.shape
@@ -294,6 +300,45 @@
         for k in range(1, self.n):
             acc = acc + held[k].astype(F32)
         total[...] = acc.astype(BF)
+        super().send()
+
+
+class SumShare(Task):
+    summed = True
+
+    def __init__(self, terms, axis, slotted=False):
+        first = terms[0].out if isinstance(terms[0], Task) else terms[0]
+        shape = first.shape[1:] if slotted else first.shape
+        count = dp_size() if axis == "dp" else 4
+        self.slotted, self.n = slotted, len(terms)
+
+        def moves(task, s, d, t):
+            total, me = task.bufs[-1], d if axis == "dp" else t
+            far = [
+                ([(None, total)], task.out_ref.at[me], {axis: (me + k) % count})
+                for k in range(1, count)
+            ]
+            return far, [([(None, total)], task.out_ref.at[me])]
+
+        room = [pltpu.VMEM(first.shape, F32) for _ in terms] + [pltpu.VMEM(shape, F32)]
+        super().__init__(
+            terms, jax.ShapeDtypeStruct((count,) + shape, F32), axis, moves, count - 1, room=room
+        )
+
+    def send(self):
+        loads = [self.local(self.ins[i], self.bufs[i], 1 + i) for i in range(self.n)]
+        for load in loads:
+            load.start()
+        for load in loads:
+            load.wait()
+        if self.slotted:
+            parts = [self.bufs[0][k] for k in range(self.bufs[0].shape[0])]
+        else:
+            parts = [buf[...] for buf in self.bufs[: self.n]]
+        acc = parts[0]
+        for part in parts[1:]:
+            acc = acc + part
+        self.bufs[-1][...] = acc
         super().send()
 
 
@@ -335,9 +380,10 @@
         for task in self.tasks:
             task.load()
 
-    def start(self):
-        for task in sorted(self.tasks, key=lambda v: isinstance(v, (SumScatter, Finish))):
-            task.send()
+    def start(self, summed):
+        for task in self.tasks:
+            if task.summed == summed:
+                task.send()
 
     def finish(self):
         for task in self.tasks:
@@ -348,7 +394,8 @@
         if self.tasks:
             self.load()
             greet(self.peers([]))
-            self.start()
+            self.start(False)
+            self.start(True)
 
     def close(self):
         self.finish()
@@ -393,8 +440,9 @@
 
 
 class Weight:
-    def __init__(self, kind, near, far):
+    def __init__(self, kind, near, *far):
         count, rows, cols = near.shape
+        self.rows, self.cols = rows, cols
         if kind == "cols":
             self.shape = (2 * rows, count * cols)
         else:
@@ -402,17 +450,19 @@
         self.size = self.shape[0] * self.shape[1]
         if kind == "cols" and cols % 128:
             s = lax.axis_index("section")
+            far = jnp.concatenate(far, axis=0)
             both = jnp.stack([jnp.where(s == 0, near, far), jnp.where(s == 0, far, near)])
             self.parts = [both.transpose(0, 2, 1, 3).reshape(self.shape)]
             self.kind, self.loads = "whole", 1
         else:
-            self.kind, self.parts, self.loads = kind, [near, far], 2 * count
+            self.kind, self.parts, self.loads = kind, [near, *far], 2 * count
+            self.far_at = [(i + 1, k) for i, f in enumerate(far) for k in range(f.shape[0])]
 
     def copies(self, refs, dst, sem):
         if self.kind == "whole":
             return [pltpu.make_async_copy(refs[0], dst, sem.at[0])]
         s = lax.axis_index("section")
-        count, rows, cols = self.parts[0].shape
+        rows, cols, count = self.rows, self.cols, len(self.far_at)
 
         def place(sec, own):
             if self.kind == "cols":
@@ -422,9 +472,12 @@
             return dst.at[pl.ds(pl.multiple_of(slot * rows, rows), rows)]
 
         moves = []
-        for k in range(count):
-            for i, sec in enumerate((s, 1 - s)):
-                moves.append(pltpu.make_async_copy(refs[i].at[k], place(sec, k), sem.at[2 * k + i]))
+        for k, (i, far) in enumerate(self.far_at):
+            near = refs[0].at[k]
+            moves.append(pltpu.make_async_copy(near, place(s, k), sem.at[2 * k]))
+            moves.append(
+                pltpu.make_async_copy(refs[i].at[far], place(1 - s, k), sem.at[2 * k + 1])
+            )
         return moves
 
 
@@ -461,26 +514,31 @@
 
 
 def gather_kernel(cfg, weights, bg, *refs):
-    norm, n_w, n_x, trans, epilogue, with_grad = cfg
+    norm, n_w, n_x, trans, epilogue, n_left, grads = cfg
     it = iter(refs)
     x_ref = next(it)
     gain_ref = next(it) if norm else None
     w_hbm = [[next(it) for _ in w.parts] for w in weights]
     e_hbm = [next(it) for _ in range(n_x)]
-    left_hbm = next(it) if with_grad else None
+    left_hbm = [next(it) for _ in range(n_left)]
     bg_in = [next(it) for _ in bg.inputs]
     a_hbm = next(it)
     n_out = {"plain": n_w, "ffn": 3, "ffn_back": 2}[epilogue]
     o_hbm = [next(it) for _ in range(n_out)]
-    grad_hbm = next(it) if with_grad else None
+    grad_hbm = [next(it) for _ in grads]
     bg.bind(iter(bg_in), it)
     full = next(it)
     w_v = [next(it) for _ in range(n_w)]
     e_v = [next(it) for _ in range(n_x)]
     o_v = [next(it) for _ in range(n_out)]
-    if with_grad:
-        left, grad_v, left_sem, grad_sem = (next(it) for _ in range(4))
-        left_load = pltpu.make_async_copy(left_hbm, left, left_sem)
+    left_v = [next(it) for _ in range(n_left)]
+    grad_v = [next(it) for _ in grads]
+    grad_sem = [next(it) for _ in grads]
+    left_sem = next(it)
+    left_loads = [
+        pltpu.make_async_copy(src, dst, left_sem.at[i])
+        for i, (src, dst) in enumerate(zip(left_hbm, left_v))
+    ]
     w_sem, in_sem, out_sem, a_sem, xs, xr, ss, sr, ls, lr, *bg_room = it
     bg.hold(bg_room)
 
@@ -495,10 +553,11 @@
         loads += w.copies(w_hbm[i], w_v[i], w_sem.at[i])
     for load in loads:
         load.start()
-    if with_grad:
-        left_load.start()
+    for load in left_loads:
+        load.start()
     bg.load()
     greet(bg.peers([{"tensor": sib}, {"tensor": cross}]))
+    bg.start(False)
 
     def span(owner, sub):
         return pl.ds(pl.multiple_of(owner * rows + sub * half, half), half)
@@ -519,7 +578,7 @@
         full[span(me, i), :] = part.astype(BF)
         to_cross(i).start()
         to_sib(i).start()
-    bg.start()
+    bg.start(True)
     for load in loads:
         load.wait()
 
@@ -567,10 +626,13 @@
         return carry
 
     lax.fori_loop(0, 4, step, 0)
-    if with_grad:
-        left_load.wait()
-        grad_products(left, full, grad_v, grad_hbm, grad_sem)
-        for copy in grad_copies(grad_v, grad_hbm, grad_sem):
+    for load in left_loads:
+        load.wait()
+    for j, (i, right) in enumerate(grads):
+        right_v = full if right is None else o_v[right]
+        grad_products(left_v[i], right_v, grad_v[j], grad_hbm[j], grad_sem[j])
+    for j in range(len(grads)):
+        for copy in grad_copies(grad_v[j], grad_hbm[j], grad_sem[j]):
             copy.wait()
     for i in range(2):
         to_cross(i).wait_send()
@@ -588,7 +650,7 @@
     bg.finish()
 
 
-def gather_mm(x_rows, gain, weights, extras=(), trans=False, epilogue="plain", cid=0, tasks=(), left=None):
+def gather_mm(x_rows, gain, weights, extras=(), trans=False, epilogue="plain", cid=0, tasks=(), lefts=(), grads=()):
     rows, width = x_rows.shape
     length = rows * 4
     cols = [w.shape[0] if trans else w.shape[1] for w in weights]
@@ -597,18 +659,20 @@
     else:
         outs = [(cols[0], BF)] * (3 if epilogue == "ffn" else 2)
     norm = gain is not None
-    cfg = (norm, len(weights), len(extras), trans, epilogue, left is not None)
+    cfg = (norm, len(weights), len(extras), trans, epilogue, len(lefts), tuple(grads))
     bg = Background(tasks)
     parts = [part for w in weights for part in w.parts]
     operands = [x_rows] + ([gain.reshape(1, width)] if norm else []) + parts + list(extras)
     n_out = 1 + len(outs)
-    grad_out, grad_room = [], []
-    if left is not None:
-        operands.append(left)
-        grad_out = [jax.ShapeDtypeStruct((left.shape[1], width), BF)]
-        grad_room = [pltpu.VMEM(left.shape, BF), pltpu.VMEM((left.shape[1], width), BF), DMA]
-        grad_room.append(DMA((left.shape[1] // grad_chunk(left.shape[1]),)))
-        n_out += 1
+    operands += lefts
+    grad_out = [
+        jax.ShapeDtypeStruct((lefts[i].shape[1], width if j is None else outs[j][0]), BF)
+        for i, j in grads
+    ]
+    grad_room = [pltpu.VMEM(v.shape, BF) for v in list(lefts) + grad_out]
+    grad_room += [DMA((g.shape[0] // grad_chunk(g.shape[0]),)) for g in grad_out]
+    grad_room.append(DMA((max(len(lefts), 1),)))
+    n_out += len(grad_out)
     flops = sum(2 * length * width * c for c in cols)
     moved = sum(w.size * 2 for w in weights) + sum(length * c * 2 for c, _ in outs) + length * width * 4
     result = pl.pallas_call(
@@ -678,7 +742,7 @@
         left_load.start()
     bg.load()
     greet(bg.peers([{"tensor": sib}, {"tensor": cross}]))
-    bg.start()
+    bg.start(False)
     for load in loads:
         load.wait()
 
@@ -694,6 +758,8 @@
         send_diag(i).wait_recv()
         to_c[i] = (keep[i] + from_s[i].astype(F32)).astype(BF)
         send_cross(i).start()
+
+    bg.start(True)
 
     def step(p, carry):
         near, sub = p // 2, p % 2
@@ -926,11 +992,13 @@
 def attend_back_kernel(dims, bg, *refs):
     length, heads, kv_heads, size = dims
     it = iter(refs)
-    proj, q_rot, k_rot, dy, gain, cos, sin = (next(it) for _ in range(7))
+    proj, q_rot, k_rot, dy, gain, cos, sin, left_hbm = (next(it) for _ in range(8))
     bg_in = [next(it) for _ in bg.inputs]
-    d_proj, q_gain, k_gain = (next(it) for _ in range(3))
+    d_proj, q_gain, k_gain, grad_hbm = (next(it) for _ in range(4))
     bg.bind(iter(bg_in), it)
-    q_h, k_h, v_h, dy_h, dq_h, dk_h, dv_h, *room = it
+    q_h, k_h, v_h, dy_h, dq_h, dk_h, dv_h, left, grad_v, left_sem, grad_sem, *room = it
+    left_load = pltpu.make_async_copy(left_hbm, left, left_sem)
+    left_load.start()
     bg.open(room)
     q_cols, k_cols = heads * size, kv_heads * size
     scale = size**-0.5
@@ -989,6 +1057,10 @@
         return carry
 
     lax.fori_loop(0, length // ROW_BLOCK, finish, 0)
+    left_load.wait()
+    grad_products(left, d_proj, grad_v, grad_hbm, grad_sem)
+    for copy in grad_copies(grad_v, grad_hbm, grad_sem):
+        copy.wait()
     bg.close()
 
 
@@ -1027,33 +1099,34 @@
     return result[:3], result[3:]
 
 
-def attend_back(proj, rotated, d_y, qk_gain, tables, cid, tasks=()):
+def attend_back(proj, rotated, d_y, qk_gain, tables, left, cid, tasks=()):
     dims = attention_dims(proj, qk_gain)
     length, heads, kv_heads, size = dims
     bg = Background(tasks)
+    grad = (left.shape[1], proj.shape[1])
     out = [
         jax.ShapeDtypeStruct(proj.shape, BF),
         jax.ShapeDtypeStruct((1, heads * size), F32),
         jax.ShapeDtypeStruct((1, kv_heads * size), F32),
+        jax.ShapeDtypeStruct(grad, BF),
     ]
     shapes = [(heads, BF), (kv_heads, BF), (kv_heads, BF), (heads, BF), (heads, F32)]
     shapes += [(kv_heads, F32)] * 2
-    (d_proj, q_gain, k_gain), rest = (lambda r: (r[:3], r[3:]))(
-        pl.pallas_call(
-            functools.partial(attend_back_kernel, dims, bg),
-            out_shape=out + bg.outs,
-            in_specs=[VM] * 7 + [ANY] * len(bg.inputs),
-            out_specs=[VM] * 3 + [ANY] * len(bg.outs),
-            scratch_shapes=[pltpu.VMEM((n, length, size), kind) for n, kind in shapes]
-            + bg.scratch,
-            compiler_params=bg.params(cid),
-            name=f"attend_back{cid}",
-        )(proj, *rotated, d_y, *tables, *bg.inputs)
-    )
-    head_grad = jnp.stack(
-        [jnp.sum(v.reshape(-1, size), axis=0) for v in (q_gain, k_gain)]
-    )
-    return (d_proj, head_grad), rest
+    result = pl.pallas_call(
+        functools.partial(attend_back_kernel, dims, bg),
+        out_shape=out + bg.outs,
+        in_specs=[VM] * 7 + [ANY] * (1 + len(bg.inputs)),
+        out_specs=[VM] * 3 + [ANY] * (1 + len(bg.outs)),
+        scratch_shapes=[pltpu.VMEM((n, length, size), kind) for n, kind in shapes]
+        + [pltpu.VMEM(left.shape, BF), pltpu.VMEM(grad, BF), DMA]
+        + [DMA((grad[0] // grad_chunk(grad[0]),))]
+        + bg.scratch,
+        compiler_params=bg.params(cid),
+        name=f"attend_back{cid}",
+    )(proj, *rotated, d_y, *tables, left, *bg.inputs)
+    d_proj, q_gain, k_gain, d_left = result[:4]
+    head_grad = jnp.stack([jnp.sum(v.reshape(-1, size), axis=0) for v in (q_gain, k_gain)])
+    return (d_proj, head_grad, d_left), result[4:]
 
 
 def body(boundary, norm_gain, mix_in, mix_out, w_gate, w_up, w_down, conv_x, conv_kernel, qk_gain):
@@ -1136,13 +1209,14 @@
         proj1, qk_gain, tables, 22, tasks=[x_move(z_up1), z_gather_half(sh_down, m_down, 1)]
     )
     up_w1 = Weight("rows", z_up1, x_up1)
-    (mid1,), (x_down1,) = scatter_mm([y1], [out1], z_rows, cid=5, tasks=[x_move(z_down1)])
-    down_w1 = Weight("cols", z_down1, x_down1)
-    (m1, gate1, up1, hid1), _ = gather_mm(
-        mid1, gains[1][1], [gate_w1, up_w1], epilogue="ffn", cid=6
-    )
-    (y_rows,), _ = scatter_mm([hid1], [down_w1], mid1, cid=7)
-    y_rows = y_rows.astype(BF)
+    (mid1,), (x_down1,) = scatter_mm(
+        [y1], [out1], z_rows, cid=5, tasks=[x_part(z_down1, 0, count // 2)]
+    )
+    (m1, gate1, up1, hid1), (x_down1b,) = gather_mm(
+        mid1, gains[1][1], [gate_w1, up_w1], epilogue="ffn", cid=6,
+        tasks=[x_part(z_down1, count // 2, count)],
+    )
+    down_w1 = Weight("cols", z_down1, x_down1, x_down1b)
 
     def split_rows(grad):
         rows, width = grad.shape
@@ -1154,50 +1228,53 @@
     def sum_cols(grad, other):
         return SumScatter("cols", grad, other)
 
-    (_, d_gate1, d_up1, g_down1), _ = gather_mm(
-        cot, None, [down_w1], [gate1, up1], trans=True, epilogue="ffn_back", cid=8, left=hid1
-    )
-    g_down1 = halves(g_down1)
-    (d_mid1, gain11, g_gate1, g_up1), (r_down1,) = scatter_mm(
-        [d_gate1, d_up1], [gate_w1, up_w1], cot, (mid1, gains[1][1]), True, 9, left=m1,
-        tasks=[x_half(g_down1)],
-    )
-    g_gate1, g_up1 = split_rows(g_gate1), split_rows(g_up1)
-    (_, d_y1, g_out1), (q_down1, r_gate1) = gather_mm(
-        d_mid1, None, [out1], trans=True, cid=10, left=y1,
+    ffn_grads = [(0, None), (1, 0), (1, 1)]
+    (_, d_gate1, d_up1, g_down1, g_gate1, g_up1), _ = gather_mm(
+        cot, None, [down_w1], [gate1, up1], trans=True, epilogue="ffn_back", cid=8,
+        lefts=[hid1, m1], grads=ffn_grads,
+    )
+    g_down1, g_gate1, g_up1 = halves(g_down1), split_rows(g_gate1), split_rows(g_up1)
+    (y_rows,), (r_down1,) = scatter_mm([hid1], [down_w1], mid1, cid=7, tasks=[x_half(g_down1)])
+    y_rows = y_rows.astype(BF)
+    (d_mid1, gain11), (q_down1, r_gate1) = scatter_mm(
+        [d_gate1, d_up1], [gate_w1, up_w1], cot, (mid1, gains[1][1]), True, 9,
         tasks=[sum_cols(g_down1, r_down1), x_rows_of(g_gate1)],
     )
+    (_, d_y1, g_out1), (q_gate1, r_up1) = gather_mm(
+        d_mid1, None, [out1], trans=True, cid=10, lefts=[y1], grads=[(0, None)],
+        tasks=[sum_rows(g_gate1, r_gate1), x_rows_of(g_up1)],
+    )
     g_out1 = halves(g_out1)
-    (d_proj1, head_grad), (q_gate1, r_up1) = attend_back(
-        proj1, rotated, d_y1, qk_gain, tables, 23,
-        tasks=[sum_rows(g_gate1, r_gate1), x_rows_of(g_up1)],
-    )
-    (d_z, gain10, g_in1), (q_up1, r_out1, e_down1) = scatter_mm(
-        [d_proj1], [in1], d_mid1, (z_rows, gains[1][0]), True, 11, left=a1,
+    (d_proj1, head_grad, g_in1), (q_up1, r_out1, e_down1) = attend_back(
+        proj1, rotated, d_y1, qk_gain, tables, a1, 23,
         tasks=[sum_rows(g_up1, r_up1), x_half(g_out1), Finish(q_down1, 1)],
     )
     g_in1 = split_rows(g_in1)
+    (d_z, gain10), (q_out1, r_in1, e_gate1) = scatter_mm(
+        [d_proj1], [in1], d_mid1, (z_rows, gains[1][0]), True, 11,
+        tasks=[sum_cols(g_out1, r_out1), x_rows_of(g_in1), Finish(q_gate1, 1)],
+    )
     d_z = d_z.astype(BF)
 
-    (_, d_gate0, d_up0, g_down0), (q_out1, r_in1, e_gate1) = gather_mm(
-        d_z, None, [down_w0], [gate0, up0], trans=True, epilogue="ffn_back", cid=12, left=hid0,
-        tasks=[sum_cols(g_out1, r_out1), x_rows_of(g_in1), Finish(q_gate1, 1)],
-    )
-    g_down0 = halves(g_down0)
-    (d_mid0, gain01, g_gate0, g_up0), (q_in1, r_down0, e_up1) = scatter_mm(
-        [d_gate0, d_up0], [gate_w0, up_w0], d_z, (mid0, gains[0][1]), True, 13, left=m0,
-        tasks=[sum_rows(g_in1, r_in1), x_half(g_down0), Finish(q_up1, 1)],
-    )
-    g_gate0, g_up0 = split_rows(g_gate0), split_rows(g_up0)
-    (_, d_y0, g_out0), (q_down0, r_gate0, e_out1) = gather_mm(
-        d_mid0, None, [out0], trans=True, cid=14, left=y0,
-        tasks=[sum_cols(g_down0, r_down0), x_rows_of(g_gate0), Finish(q_out1, 1)],
+    (_, d_gate0, d_up0, g_down0, g_gate0, g_up0), (q_in1, e_up1, e_out1) = gather_mm(
+        d_z, None, [down_w0], [gate0, up0], trans=True, epilogue="ffn_back", cid=12,
+        lefts=[hid0, m0], grads=ffn_grads,
+        tasks=[sum_rows(g_in1, r_in1), Finish(q_up1, 1), Finish(q_out1, 1)],
+    )
+    g_down0, g_gate0, g_up0 = halves(g_down0), split_rows(g_gate0), split_rows(g_up0)
+    (d_mid0, gain01), (r_down0, e_in1) = scatter_mm(
+        [d_gate0, d_up0], [gate_w0, up_w0], d_z, (mid0, gains[0][1]), True, 13,
+        tasks=[x_half(g_down0), Finish(q_in1, 1)],
+    )
+    (_, d_y0, g_out0), (q_down0, r_gate0) = gather_mm(
+        d_mid0, None, [out0], trans=True, cid=14, lefts=[y0], grads=[(0, None)],
+        tasks=[sum_cols(g_down0, r_down0), x_rows_of(g_gate0)],
     )
     g_out0 = halves(g_out0)
     d_proj0, d_value0, kernel_grad = conv_back(proj0, value0, conv_kernel, d_y0)
-    (d_x, gain00, g_in0, g_cols), (q_gate0, r_up0, e_in1) = scatter_mm(
+    (d_x, gain00, g_in0, g_cols), (q_gate0, r_up0) = scatter_mm(
         [d_proj0, d_value0], [in0, cols], d_mid0, (x_rows, gains[0][0]), True, 15, left=a0,
-        tasks=[sum_rows(g_gate0, r_gate0), x_rows_of(g_up0), Finish(q_in1, 1)],
+        tasks=[sum_rows(g_gate0, r_gate0), x_rows_of(g_up0)],
     )
     d_x = d_x.astype(BF)
     g_in0 = split_rows(g_in0)
@@ -1223,28 +1300,25 @@
     f_gate, f_down, f_up = Finish(q_gate0, 0), Finish(q_down0, 0), Finish(s_up, 0)
     f_in, f_out = Finish(s_in, 0), Finish(s_out, 0)
     t_small, t_result = x_move(small), x_move(jnp.where(first, y_rows, d_x))
+    z_small = SumShare([small, t_small], "dp")
+    tp_small = SumShare([z_small], "tensor", slotted=True)
     program = [("load", v) for v in (s_up, f_gate, f_down)]
     program += [("send", v) for v in (t_in0, t_small, t_cols, t_out0, s_up, t_result)]
     program += [("send", f_down), ("send", f_gate)]
     program += [("wait", t_in0), ("reload", s_in), ("send", s_in)]
     program += [("wait", t_cols), ("reload", s_cols), ("wait", t_out0), ("reload", s_out)]
-    program += [("send", s_out), ("send", s_cols)]
+    program += [("send", s_out), ("send", s_cols), ("wait", t_small), ("send", z_small)]
     program += [("wait", s_up), ("reload", f_up), ("send", f_up)]
     program += [("wait", s_in), ("reload", f_in), ("send", f_in)]
+    program += [("wait", z_small), ("send", tp_small)]
     program += [("wait", s_out), ("reload", f_out), ("send", f_out)]
-    rest = [s_cols, t_small, t_result, f_gate, f_down, f_up, f_in, f_out]
+    rest = [s_cols, tp_small, t_result, f_gate, f_down, f_up, f_in, f_out]
     program += [("wait", v) for v in rest]
     order = [t_in0, t_cols, t_out0, s_up, s_in, s_out, s_cols, f_gate, f_down, f_up, f_in, f_out]
-    order += [t_small, t_result]
-    *_, q_cols, e_gate0, e_down0, e_up0, e_in0, e_out0, small_x, out_moved = exchange(
+    order += [t_small, z_small, tp_small, t_result]
+    *_, q_cols, e_gate0, e_down0, e_up0, e_in0, e_out0, _, _, small_t, out_moved = exchange(
         order, program, 17
     )
-    small = small + small_x
-    t_z = z_gather(small)
-    (small_z,) = exchange([t_z], [("send", t_z), ("wait", t_z)], 18)
-    small = jnp.sum(small_z, axis=0)
-    t_t = t_share(small)
-    (small_t,) = exchange([t_t], [("send", t_t), ("wait", t_t)], 19)
     small = jnp.sum(small_t, axis=0)
 
     def whole(zero, one):

time: 723 us -> 706 us (0.976)
  Pallas kernels: 668 us -> 656 us
    pallas_call x4 -> x2, Pallas kernels: 140 us -> 128 us  [exchange(): pl.pallas_call(functools.partial(exchange_kernel, bg, program), out_shape...]
    pallas_call x8, Pallas kernels: 226 us -> 237 us  [gather_mm(): pl.pallas_call(functools.partial(gather_kernel, cfg, weights, bg), out_sh...]
    pallas_call x8, Pallas kernels: 237 us -> 228 us  [scatter_mm(): pl.pallas_call(functools.partial(scatter_kernel, (len(operands), trans, e...]
where the time goes in v4:
time: 706 us; the launch traced here: 696 us
  Pallas kernels  656 us (93%)
  other arithmetic  27.3 us (4%)
  local copies, waits for them, and re-layouts  10.8 us (2%)
    pallas_call x8, Pallas kernels, gather_mm(): pl.pallas_call(functools.partial(gather_kernel, cfg, weights, bg), out_sh...  237 us
    pallas_call x8, Pallas kernels, scatter_mm(): pl.pallas_call(functools.partial(scatter_kernel, (len(operands), trans, e...  228 us
    pallas_call x2, Pallas kernels, exchange(): pl.pallas_call(functools.partial(exchange_kernel, bg, program), out_shape...  128 us
    pallas_call x1, Pallas kernels, attend(): pl.pallas_call(functools.partial(attend_kernel, dims, bg), out_shape=out...  32.1 us
    pallas_call x1, Pallas kernels, attend_back(): pl.pallas_call(functools.partial(attend_back_kernel, dims, bg), out_shape...  30 us

profile of v4, /device:TPU:0, one launch (start us, length us, event | category | flops | bytes accessed | tf_op | source)
XLA Modules:
  0.0 695.6 jit_solution(13495317503254712576)
XLA Ops:
  0.7 65.6 %exchange16.1 = (bf16[128,512]{1,0:T(8,128)(2,1)}, bf16[128,256]{1,0:T(8,128)(2,1)}, bf16[128,1152]{1,0:T(8,128)(2,1)}, bf16[256,1024]{1,0:T(8,128)(2,1)}, bf16[...) custom-call(bf16[2,128,512]{2,1,0:T(8,128)(2,1)} %bitcast.101, ...), custom_call_target="tpu_custom_call" | custom-call | tf_op jit(solution)/shard_map/exchange16/pallas_call | solution.py:431
  66.3 2.3 bitcast_select_fusion
  68.6 0.6 fusion.4
  69.2 29.4 %gather0.1 = (bf16[1024,1024]{1,0:T(8,128)(2,1)}, f32[1024,512]{1,0:T(8,128)}, f32[1024,256]{1,0:T(8,128)}, bf16[4,128,1152]{2,1,0:T(8,128)(2,1)}, bf16[4,128,1152]{2,1,0:T(8,128)(2,1)}) custom-call(f32[256,1024]{1,0:T(8,128)} %get-tuple-element.231.refs_0_.refs_3_.refs_7_, f32[1,1024]{1,0:T(1,128)} %get-tuple-element.238.refs_1_.refs_8_, ...), custom_call_target="tpu_custom_call" | custom-call | flops 1610612736 | bytes 29360128 | tf_op jit(solution)/shard_map/gather0/pallas_call | solution.py:678
  98.7 1.8 slice_multiply_fusion
  100.9 1.6 multiply_convert_fusion.3
  102.5 31.1 %scatter1.1 = (f32[256,1024]{1,0:T(8,128)}, bf16[4,128,1152]{2,1,0:T(8,128)(2,1)}, bf16[4,576,256]{2,1,0:T(8,128)(2,1)}) custom-call(bf16[1024,256]{1,0:T(8,128)(2,1)} %get-tuple-element.228.refs_0_.refs_3_, bf16[4,128,256]{2,1,0:T(8,128)(2,1)} %get-tuple-element.126.refs_1_, bf16[4,128,256]{2,1,0:T(8,128)(2,1)} %get-tuple-element.127.refs_2_, ...), custom_call_target="tpu_custom_call" | custom-call | flops 536870912 | bytes 16777216 | tf_op jit(solution)/shard_map/scatter1/pallas_call | solution.py:850
  133.6 29.7 %gather2.1 = (bf16[1024,1024]{1,0:T(8,128)(2,1)}, bf16[1024,1152]{1,0:T(8,128)(2,1)}, bf16[1024,1152]{1,0:T(8,128)(2,1)}, bf16[1024,1152]{1,0:T(8,128)(2,1)}, bf...) custom-call(f32[256,1024]{1,0:T(8,128)} %get-tuple-element.130.refs_0_.refs_3_.refs_7_, ...), custom_call_target="tpu_custom_call" | custom-call | flops 4831838208 | bytes 63963136 | tf_op jit(solution)/shard_map/gather2/pallas_call | solution.py:678
  163.4 25.7 %scatter3.1 = (f32[256,1024]{1,0:T(8,128)}, bf16[4,128,512]{2,1,0:T(8,128)(2,1)}, bf16[4,128,256]{2,1,0:T(8,128)(2,1)}, bf16[4,128,1152]{2,1,0:T(8,128)(2,1)}) custom-call(bf16[1024,1152]{1,0:T(8,128)(2,1)} %get-tuple-element.136.refs_0_.refs_5_, bf16[4,576,256]{2,1,0:T(8,128)(2,1)} %get-tuple-element.133.refs_6_.refs_1_, ...), custom_call_target="tpu_custom_call" | custom-call | flops 2415919104 | bytes 31457280 | tf_op jit(solution)/shard_map/scatter3/pallas_call | solution.py:850
  189.1 2.3 convert_convert_fusion.refs_0_.refs_3_.refs_4_
  191.4 0.6 fusion.3
  192.0 34.1 %gather4.1 = (bf16[1024,1024]{1,0:T(8,128)(2,1)}, f32[1024,512]{1,0:T(8,128)}, bf16[4,128,1152]{2,1,0:T(8,128)(2,1)}, bf16[4,128,1152]{2,1,0:T(8,128)(2,1)}) custom-call(f32[256,1024]{1,0:T(8,128)} %convert_convert_fusion.refs_0_.refs_3_.refs_4_, f32[1,1024]{1,0:T(1,128)} %get-tuple-element.236.refs_1_.refs_5_, ...), custom_call_target="tpu_custom_call" | custom-call | flops 1073741824 | bytes 25165824 | tf_op jit(solution)/shard_map/gather4/pallas_call | solution.py:678
  226.2 0.7 tile.13.refs_1_.refs_4_
  227.5 1.3 copy.20.refs_2_.refs_5_
  229.0 1.3 copy.21.refs_3_.refs_6_
  230.3 32.1 %attend22.1 = (bf16[1024,256]{1,0:T(8,128)(2,1)}, bf16[1024,256]{1,0:T(8,128)(2,1)}, bf16[1024,128]{1,0:T(8,128)(2,1)}, bf16[4,128,1152]{2,1,0:T(8,128)(2,1)}, bf16[4,576,256]{2,1,0:T(8,128)(2,1)}) custom-call(f32[1024,512]{1,0:T(8,128)} %get-tuple-element.144.refs_0_, f32[2,256]{1,0:T(2,128)} %tile.13.refs_1_.refs_4_, f32[1024,256]{1,0:T(8,128)} %copy.20.refs_2_.refs_5_, ...), custom_call_target="tpu_custom_call" | custom-call | tf_op jit(solution)/shard_map/attend22/pallas_call | solution.py:1087
  262.4 19.5 %scatter5.1 = (f32[256,1024]{1,0:T(8,128)}, bf16[2,576,256]{2,1,0:T(8,128)(2,1)}) custom-call(bf16[1024,256]{1,0:T(8,128)(2,1)} %get-tuple-element.149.refs_0_.refs_3_, bf16[4,128,256]{2,1,0:T(8,128)(2,1)} %get-tuple-element.139.refs_5_.refs_1_, bf16[4,128,256]{2,1,0:T(8,128)(2,1)} %get-tuple-element.150.refs_2_, ...), custom_call_target="tpu_custom_call" | custom-call | flops 536870912 | bytes 16777216 | tf_op jit(solution)/shard_map/scatter5/pallas_call | solution.py:850
  282.0 19.3 %gather6.1 = (bf16[1024,1024]{1,0:T(8,128)(2,1)}, bf16[1024,1152]{1,0:T(8,128)(2,1)}, bf16[1024,1152]{1,0:T(8,128)(2,1)}, bf16[1024,1152]{1,0:T(8,128)(2,1)}, bf16[2,576,256]{2,1,0:T(8,128)(2,1)}) custom-call(f32[256,1024]{1,0:T(8,128)} %get-tuple-element.152.refs_0_.refs_4_.refs_7_, f32[1,1024]{1,0:T(1,128)} %get-tuple-element.235.refs_1_.refs_8_, ...), custom_call_target="tpu_custom_call" | custom-call | flops 4831838208 | bytes 63963136 | tf_op jit(solution)/shard_map/gather6/pallas_call | solution.py:678
  301.3 29.8 %gather8.1 = (bf16[1024,1024]{1,0:T(8,128)(2,1)}, bf16[1024,1152]{1,0:T(8,128)(2,1)}, bf16[1024,1152]{1,0:T(8,128)(2,1)}, bf16[1152,1024]{1,0:T(8,128)(2,1)}, bf...) custom-call(bf16[256,1024]{1,0:T(8,128)(2,1)} %get-tuple-element.230.refs_0_.refs_6_, ...), custom_call_target="tpu_custom_call" | custom-call | flops 2415919104 | bytes 45088768 | tf_op jit(solution)/shard_map/gather8/pallas_call | solution.py:678
  331.2 31.1 %scatter7.1 = (f32[256,1024]{1,0:T(8,128)}, bf16[576,1024]{1,0:T(8,128)(2,1)}) custom-call(bf16[1024,1152]{1,0:T(8,128)(2,1)} %get-tuple-element.158.refs_6_.refs_0_, bf16[4,576,256]{2,1,0:T(8,128)(2,1)} %get-tuple-element.148.refs_4_.refs_6_.refs_1_, bf16[2,576,256]{2,1,0:T(8,128)(2,1)} %get-tuple-element.151.refs_2_, ...), custom_call_target="tpu_custom_call" | custom-call | flops 2415919104 | bytes 31457280 | tf_op jit(solution)/shard_map/scatter7/pallas_call | solution.py:850
  362.2 31.5 %scatter9.1 = (f32[256,1024]{1,0:T(8,128)}, f32[1,1024]{1,0:T(1,128)}, bf16[4,576,256]{2,1,0:T(8,128)(2,1)}, bf16[4,128,1152]{2,1,0:T(8,128)(2,1)}) custom-call(bf16[1024,1152]{1,0:T(8,128)(2,1)} %get-tuple-element.160.refs_0_, bf16[1024,1152]{1,0:T(8,128)(2,1)} %get-tuple-element.161.refs_1_, bf16[4,128,1152]{2,1,0:T(8,128)(2,1)} %get-tuple-element.143.refs_4_.refs_2_, ...), custom_call_target="tpu_custom_call" | custom-call | flops 4831838208 | bytes 50331648 | tf_op jit(solution)/shard_map/scatter9/pallas_call | solution.py:850
  393.8 32.6 %gather10.1 = (bf16[1024,1024]{1,0:T(8,128)(2,1)}, f32[1024,256]{1,0:T(8,128)}, bf16[256,1024]{1,0:T(8,128)(2,1)}, bf16[4,128,1152]{2,1,0:T(8,128)(2,1)}, bf16[4,128,1152]{2,1,0:T(8,128)(2,1)}) custom-call(f32[256,1024]{1,0:T(8,128)} %get-tuple-element.165.refs_0_.refs_3_, bf16[4,128,256]{2,1,0:T(8,128)(2,1)} %get-tuple-element.139.refs_5_.refs_1_, ...), custom_call_target="tpu_custom_call" | custom-call | flops 536870912 | bytes 20971520 | tf_op jit(solution)/shard_map/gather10/pallas_call | solution.py:678
  426.4 30.0 %attend_back23.1 = (bf16[1024,512]{1,0:T(8,128)(2,1)}, f32[1,256]{1,0:T(1,128)}, f32[1,128]{1,0:T(1,128)}, bf16[1024,512]{1,0:T(8,128)(2,1)}, bf16[4,128,1152]{2...) custom-call(f32[1024,512]{1,0:T(8,128)} %get-tuple-element.144.refs_0_, ...), custom_call_target="tpu_custom_call" | custom-call | tf_op jit(solution)/shard_map/attend_back23/pallas_call | solution.py:1115
  456.4 22.4 %scatter11.1 = (f32[256,1024]{1,0:T(8,128)}, f32[1,1024]{1,0:T(1,128)}, bf16[4,128,256]{2,1,0:T(8,128)(2,1)}, bf16[4,128,512]{2,1,0:T(8,128)(2,1)}, bf16[2,128,1152]{2,1,0:T(8,128)(2,1)}) custom-call(bf16[1024,512]{1,0:T(8,128)(2,1)} %get-tuple-element.173.refs_0_, bf16[4,128,512]{2,1,0:T(8,128)(2,1)} %get-tuple-element.138.refs_4_.refs_2_.refs_1_, ...), custom_call_target="tpu_custom_call" | custom-call | flops 1073741824 | bytes 20971520 | tf_op jit(solution)/shard_map/scatter11/pallas_call | solution.py:850
  478.8 2.1 convert_element_type.104.refs_0_.refs_6_
  480.9 29.4 %gather12.1 = (bf16[1024,1024]{1,0:T(8,128)(2,1)}, bf16[1024,1152]{1,0:T(8,128)(2,1)}, bf16[1024,1152]{1,0:T(8,128)(2,1)}, bf16[1152,1024]{1,0:T(8,128)(2,1)}, b...) custom-call(bf16[256,1024]{1,0:T(8,128)(2,1)} %convert_element_type., ...), custom_call_target="tpu_custom_call" | custom-call | flops 2415919104 | bytes 45088768 | tf_op jit(solution)/shard_map/gather12/pallas_call | solution.py:678
  510.3 34.2 %scatter13.1 = (f32[256,1024]{1,0:T(8,128)}, f32[1,1024]{1,0:T(1,128)}, bf16[576,1024]{1,0:T(8,128)(2,1)}, bf16[2,128,512]{2,1,0:T(8,128)(2,1)}) custom-call(bf16[1024,1152]{1,0:T(8,128)(2,1)} %get-tuple-element.184.refs_0_, bf16[1024,1152]{1,0:T(8,128)(2,1)} %get-tuple-element.185.refs_1_, bf16[4,128,1152]{2,1,0:T(8,128)(2,1)} %get-tuple-element.122.refs_6_.refs_2_, ...), custom_call_target="tpu_custom_call" | custom-call | flops 4831838208 | bytes 50331648 | tf_op jit(solution)/shard_map/scatter13/pallas_call | solution.py:850
  544.5 32.8 %gather14.1 = (bf16[1024,1024]{1,0:T(8,128)(2,1)}, f32[1024,256]{1,0:T(8,128)}, bf16[256,1024]{1,0:T(8,128)(2,1)}, bf16[4,576,256]{2,1,0:T(8,128)(2,1)}, bf16[4,128,1152]{2,1,0:T(8,128)(2,1)}) custom-call(f32[256,1024]{1,0:T(8,128)} %get-tuple-element.188.refs_0_.refs_6_, bf16[4,128,256]{2,1,0:T(8,128)(2,1)} %get-tuple-element.126.refs_1_, ...), custom_call_target="tpu_custom_call" | custom-call | flops 536870912 | bytes 20971520 | tf_op jit(solution)/shard_map/gather14/pallas_call | solution.py:678
  577.4 2.3 multiply_reduce_fusion.2
  579.8 1.4 copy-done.1
  581.3 1.2 multiply_convert_fusion
  582.7 1.1 pad_maximum_fusion.refs_0_
  583.7 32.5 %scatter15.1 = (f32[256,1024]{1,0:T(8,128)}, f32[1,1024]{1,0:T(1,128)}, bf16[1024,512]{1,0:T(8,128)(2,1)}, bf16[1024,256]{1,0:T(8,128)(2,1)}, bf16[4,128,1152]{2...) custom-call(bf16[1024,512]{1,0:T(8,128)(2,1)} %pad_maximum_fusion.refs_0_, bf16[1024,256]{1,0:T(8,128)(2,1)} %get-tuple-element.226.refs_1_, ...), custom_call_target="tpu_custom_call" | custom-call | flops 1610612736 | bytes 25165824 | tf_op jit(solution)/shard_map/scatter15/pallas_call | solution.py:850
  616.8 0.7 reduce.10
  617.6 0.7 reduce.11
  618.5 1.3 concatenate.50.refs_10_.refs_11_
  619.8 2.2 broadcast_select_fusion.3.refs_12_
  622.0 62.9 %exchange17.1 = (bf16[4,128,512]{2,1,0:T(8,128)(2,1)}, bf16[4,128,256]{2,1,0:T(8,128)(2,1)}, bf16[128,1024]{1,0:T(8,128)(2,1)}, bf16[4,128,1152]{2,1,0:T(8,128)(...) custom-call(bf16[4,2,128,512]{3,2,1,0:T(8,128)(2,1)} %bitcast.79, ...), custom_call_target="tpu_custom_call" | custom-call | tf_op jit(solution)/shard_map/exchange17/pallas_call | solution.py:431
  684.9 1.4 convert_bitcast_fusion
  686.5 1.1 maximum_select_fusion
  687.7 0.6 constant_dynamic-slice_fusion.1
  688.3 0.9 bitcast_convert_fusion.3
  689.2 0.7 bitcast_convert_fusion.4
  690.1 1.1 bitcast_convert_fusion.2
  691.2 1.1 bitcast_convert_fusion.1
  692.3 1.1 bitcast_convert_fusion
  693.4 0.7 convert_reduce_fusion
  694.7 0.6 reshape_squeeze.23
  (85 shorter events, 3.4 us)
Async XLA Ops:
  0.6 65.6 %copy-start.4 = (bf16[1,2,256,1024]{3,2,1,0:T(8,128)(2,1)S(1)}, bf16[1,2,256,1024]{3,2,1,0:T(8,128)(2,1)}, u32[]{:S(2)}) copy-start(bf16[1,2,256,1024]{3,2,1,0:T(8,128)(2,1)} %param.10) | copy-start | bytes 3145732
  66.2 2.3 copy-start.18
  66.3 2.3 copy-start.19
  98.6 1.9 copy-start.23
  98.6 2.2 copy-start
  191.4 34.7 %copy-start.24 = (f32[2,64]{1,0:T(2,128)S(1)}, f32[2,64]{1,0:T(2,128)}, u32[]{:S(2)}) copy-start(f32[2,64]{1,0:T(2,128)} %param.19) | copy-start | bytes 1540
  579.7 1.6 copy-start.1
  581.3 1.2 copy-start.3
  583.7 33.1 %copy-start.26 = (f32[1,128]{1,0:T(1,128)S(1)}, f32[1,128]{1,0:T(1,128)}, u32[]{:S(2)}) copy-start(f32[1,128]{1,0:T(1,128)} %get-tuple-element.207) | copy-start | bytes 1540
  583.7 33.9 %copy-start.25 = (f32[1,256]{1,0:T(1,128)S(1)}, f32[1,256]{1,0:T(1,128)}, u32[]{:S(2)}) copy-start(f32[1,256]{1,0:T(1,128)} %get-tuple-element.206) | copy-start | bytes 3076
  583.7 34.8 %copy-start.20 = (f32[1,1024]{1,0:T(1,128)S(1)}, f32[1,1024]{1,0:T(1,128)}, u32[]{:S(2)}) copy-start(f32[1,1024]{1,0:T(1,128)} %get-tuple-element.205) | copy-start | bytes 12292
  583.7 34.8 %copy-start.21 = (f32[1,1024]{1,0:T(1,128)S(1)}, f32[1,1024]{1,0:T(1,128)}, u32[]{:S(2)}) copy-start(f32[1,1024]{1,0:T(1,128)} %get-tuple-element.204) | copy-start | bytes 12292
  583.7 34.8 %copy-start.22 = (f32[1,1024]{1,0:T(1,128)S(1)}, f32[1,1024]{1,0:T(1,128)}, u32[]{:S(2)}) copy-start(f32[1,1024]{1,0:T(1,128)} %get-tuple-element.203) | copy-start | bytes 12292
  583.7 36.1 %copy-start.2 = (f32[256,1024]{1,0:T(8,128)S(1)}, f32[256,1024]{1,0:T(8,128)}, u32[]{:S(2)}) copy-start(f32[256,1024]{1,0:T(8,128)} %get-tuple-element.208) | copy-start | bytes 3145732
  684.9 1.5 copy-start.11
  686.4 1.2 copy-start.15
  686.4 1.9 copy-start.13
  686.4 1.9 copy-start.14
  686.4 2.7 copy-start.16
  686.4 2.7 copy-start.17
  686.4 3.5 copy-start.7
  686.4 3.5 copy-start.8
  686.4 3.5 copy-start.9
  686.5 3.5 copy-start.10
  690.0 2.2 copy-start.5
  690.1 2.2 copy-start.6
  692.3 1.2 copy-start.12

commit v5 on v0

v5 whole, which is shorter than its diff:
```python
import functools

import jax
import jax.numpy as jnp
from jax import lax
from jax.experimental import pallas as pl
from jax.experimental.pallas import tpu as pltpu
from jax.sharding import PartitionSpec as P

HEADS = 16
KV_HEADS = 8

EPS = 1e-05
ROPE_BASE = 1000000.0
MASKED = -1e30

MESH = pl.DeviceIdType.MESH
ANY = pl.BlockSpec(memory_space=pl.ANY)
DMA = pltpu.SemaphoreType.DMA
VMEM_BYTES = 63 * 1024 * 1024
BF = jnp.bfloat16
F32 = jnp.float32
ROW_BLOCK = 256


def contract(left_op, right_op, left_dim, right_dim):
    return lax.dot_general(
        left_op, right_op, (((left_dim,), (right_dim,)), ((), ())), preferred_element_type=F32
    )


def norm_rows(values, gain):
    return values * lax.rsqrt(jnp.mean(values * values, axis=-1, keepdims=True) + EPS) * gain


def norm_back(values, gain, grad_in):
    row_scale = lax.rsqrt(jnp.mean(values * values, axis=-1, keepdims=True) + EPS)
    normed = values * row_scale
    gain_grad = jnp.sum(grad_in * normed, axis=0, keepdims=True)
    scaled = grad_in * gain
    value_grad = row_scale * (scaled - normed * jnp.mean(scaled * normed, axis=-1, keepdims=True))
    return (value_grad, gain_grad)


def rotation(length, head_size):
    half_size = head_size // 2
    frequency = ROPE_BASE ** (-(jnp.arange(half_size, dtype=jnp.float32) * 2.0 / head_size))
    angles = jnp.arange(length, dtype=jnp.float32)[:, None] * frequency[None, :]
    cosine_table = jnp.concatenate([jnp.cos(angles), jnp.cos(angles)], axis=1)
    sine_table = jnp.concatenate([jnp.sin(angles), jnp.sin(angles)], axis=1)
    return (cosine_table, sine_table)


def silu_parts(gate):
    sig = 1.0 / (1.0 + jnp.exp(-gate))
    return sig, gate * sig


def dp_size():
    return lax.axis_size("dp")


def spot():
    return tuple(lax.axis_index(a) for a in ("section", "dp", "tensor"))


def block_of(index, size):
    return pl.ds(pl.multiple_of(index * size, size), size)


class Val:
    def __init__(self, shape, dtype):
        self.shape, self.dtype = tuple(shape), dtype
        self.ref = self.array = None


class Kernel:
    def __init__(self, cid):
        self.cid, self.ins, self.arrays, self.outs, self.room = cid, [], [], [], []
        self.early, self.steps, self.late, self.axes = [], [], [], {"tensor"}
        self.once = []

    def input(self, array):
        array = array.array if isinstance(array, Val) else array
        for val, known in zip(self.ins, self.arrays):
            if known is array:
                return val
        val = Val(array.shape, array.dtype)
        self.ins.append(val)
        self.arrays.append(array)
        return val

    def output(self, shape, dtype):
        val = Val(shape, dtype)
        self.outs.append(val)
        return val

    def vmem(self, shape, dtype):
        val = Val(shape, dtype)
        self.room.append((val, pltpu.VMEM(tuple(shape), dtype)))
        return val

    def sem(self, *shape):
        val = Val(shape, None)
        self.room.append((val, DMA(shape)))
        return val

    def do(self, *steps):
        self.steps += steps

    def body(self, *refs):
        vals = self.ins + self.outs + [val for val, _ in self.room]
        for val, ref in zip(vals, refs):
            val.ref = ref
        for item in self.once:
            item.waited = False
        for step in self.early:
            step()
        self.greet()
        for step in self.steps + self.late:
            step()

    def greet(self):
        s, d, t = spot()
        peers = []
        if "section" in self.axes:
            peers.append({"section": 1 - s})
        if "dp" in self.axes:
            peers += [{"dp": (d + k) % dp_size()} for k in range(1, dp_size())]
        peers += [{"tensor": (t + k) % 4} for k in range(1, 4)]
        barrier = pltpu.get_barrier_semaphore()
        for peer in peers:
            pl.semaphore_signal(barrier, inc=1, device_id=peer, device_id_type=MESH)
        pl.semaphore_wait(barrier, len(peers))

    def build(self):
        result = pl.pallas_call(
            self.body,
            out_shape=[jax.ShapeDtypeStruct(v.shape, v.dtype) for v in self.outs],
            in_specs=[ANY] * len(self.ins),
            out_specs=[ANY] * len(self.outs),
            scratch_shapes=[room for _, room in self.room],
            compiler_params=pltpu.CompilerParams(
                collective_id=self.cid, has_side_effects=True, vmem_limit_bytes=VMEM_BYTES
            ),
            name=f"stage{self.cid}",
        )(*self.arrays)
        for val, array in zip(self.outs, result):
            val.array = array


def remote(src, dst, send_sem, recv_sem, peer):
    return pltpu.make_async_remote_copy(
        src_ref=src, dst_ref=dst, send_sem=send_sem, recv_sem=recv_sem,
        device_id=peer, device_id_type=MESH,
    )


class Load:
    def __init__(self, k, sources, shape, dtype, early=False):
        self.k, self.sources, self.waited = k, sources, False
        self.buf, self.sem = k.vmem(shape, dtype), k.sem(1)
        k.once.append(self)
        if early:
            k.early.append(self.start)

    def moves(self):
        for cond, source in self.sources(*spot()):
            yield cond, pltpu.make_async_copy(source, self.buf.ref, self.sem.ref.at[0])

    def start(self):
        for cond, move in self.moves():
            if cond is None:
                move.start()
            else:
                pl.when(cond)(move.start)

    def wait(self):
        if not self.waited:
            self.waited = True
            next(self.moves())[1].wait()


def load_all(k, array, early=True):
    val = k.input(array)
    return Load(k, lambda s, d, t: [(None, val.ref)], val.shape, val.dtype, early)


class Save:
    def __init__(self, k, buf):
        self.buf, self.out, self.sem = buf, k.output(buf.shape, buf.dtype), k.sem(1)
        self.waited = False
        k.once.append(self)
        k.late.append(self.wait)

    def move(self):
        return pltpu.make_async_copy(self.buf.ref, self.out.ref, self.sem.ref.at[0])

    def start(self):
        self.move().start()

    def wait(self):
        if not self.waited:
            self.waited = True
            self.move().wait()


class Task:
    final = None

    def __init__(self, k, out, axis, moves, count, n_local=1, out_dtype=BF):
        self.k, self.axis, self.make = k, axis, moves
        self.out = k.output(out, out_dtype)
        self.send_sem, self.recv_sem, self.local_sem = k.sem(count), k.sem(count), k.sem(n_local)
        self.waited = False
        k.axes.add(axis)
        k.once.append(self)

    def local(self, src, dst, i):
        return pltpu.make_async_copy(src, dst, self.local_sem.ref.at[i])

    def pairs(self, every):
        far, near = self.make(*spot())
        for i, (sources, dst, peer) in enumerate(far):
            for cond, src in sources if every else sources[:1]:
                yield cond, True, remote(
                    src, dst, self.send_sem.ref.at[i], self.recv_sem.ref.at[i], peer
                )
        for i, (sources, dst) in enumerate(near):
            for cond, src in sources if every else sources[:1]:
                yield cond, False, self.local(src, dst, i)

    def send(self):
        for cond, far, move in self.pairs(True):
            if far and self.final is not None:
                cond = lax.axis_index("section") == 1 - self.final
            if cond is None:
                move.start()
            else:
                pl.when(cond)(move.start)

    def wait(self):
        if self.waited:
            return
        self.waited = True
        s = lax.axis_index("section")
        for _, far, move in self.pairs(False):
            if not far:
                move.wait()
            elif self.final is None:
                move.wait_recv()
                move.wait_send()
            else:
                pl.when(s == 1 - self.final)(move.wait_send)
                pl.when(s == self.final)(move.wait_recv)


def as_val(k, value):
    value = value.out if isinstance(value, Task) else value
    known = isinstance(value, Val) and (value.array is None)
    return value if known else k.input(value)


def z_gather(k, value):
    val, count = as_val(k, value), dp_size()

    def moves(s, d, t):
        source = [(None, val.ref)]
        dst = task.out.ref.at[d]
        return [(source, dst, {"dp": (d + i) % count}) for i in range(1, count)], [(source, dst)]

    task = Task(k, (count,) + val.shape, "dp", moves, count - 1, out_dtype=val.dtype)
    return task


def z_gather_half(k, shard, moved, block):
    shard, moved, count = as_val(k, shard), as_val(k, moved), dp_size()
    rows = shard.shape[0] // 2

    def moves(s, d, t):
        sources = [
            (s == block, shard.ref.at[pl.ds(block * rows, rows)]),
            (s == 1 - block, moved.ref),
        ]
        dst = task.out.ref.at[d]
        return [(sources, dst, {"dp": (d + i) % count}) for i in range(1, count)], [(sources, dst)]

    task = Task(k, (count,) + moved.shape, "dp", moves, count - 1)
    return task


def x_move(k, value):
    val = as_val(k, value)

    def moves(s, d, t):
        return [([(None, val.ref)], task.out.ref, {"section": 1 - s})], []

    task = Task(k, val.shape, "section", moves, 1, out_dtype=val.dtype)
    return task


def x_half(k, value):
    val = as_val(k, value)
    rows = val.shape[0] // 2

    def moves(s, d, t):
        src = val.ref.at[block_of(1 - s, rows)]
        return [([(None, src)], task.out.ref, {"section": 1 - s})], []

    task = Task(k, (rows,) + val.shape[1:], "section", moves, 1, out_dtype=val.dtype)
    return task


def x_slots(k, value, kind):
    val, count = as_val(k, value), dp_size()
    rows = val.shape[0] // (2 * count)

    def moves(s, d, t):
        far = []
        for i in range(count):
            slot = 2 * i + 1 - s if kind == "rows" else (1 - s) * count + i
            src = val.ref.at[block_of(slot, rows)]
            far.append(([(None, src)], task.out.ref.at[i], {"section": 1 - s}))
        return far, []

    task = Task(k, (count, rows) + val.shape[1:], "section", moves, count)
    return task


class SumScatter(Task):
    def __init__(self, k, kind, grads, received):
        count = dp_size()
        self.grads, self.got_val = as_val(k, grads), as_val(k, received)
        if kind == "cols":
            rows, cols = self.grads.shape[0] // 2, self.grads.shape[1] // count
            held = (rows, self.grads.shape[1])
        else:
            rows, cols = self.grads.shape[0] // (2 * count), self.grads.shape[1]
            held = (count, rows, cols)
        self.kind, self.rows, self.cols, self.n = kind, rows, cols, count
        self.kept, self.got = k.vmem(held, BF), k.vmem(held, BF)
        self.total = k.vmem((count, rows, cols), BF)

        def moves(s, d, t):
            total = self.total.ref
            far = []
            for i in range(1, count):
                other = (d + i) % count
                far.append(([(None, total.at[other])], self.out.ref.at[d], {"dp": other}))
            return far, [([(None, total.at[d])], self.out.ref.at[d])]

        super().__init__(k, (count, rows, cols), "dp", moves, count - 1, 2 + count)

    def loads(self):
        s, grads, kept = lax.axis_index("section"), self.grads.ref, self.kept.ref
        if self.kind == "cols":
            moves = [self.local(grads.at[block_of(s, self.rows)], kept, 2)]
        else:
            moves = []
            for i in range(self.n):
                slot = 2 * i + s if self.kind == "rows" else s * self.n + i
                moves.append(self.local(grads.at[block_of(slot, self.rows)], kept.at[i], 2 + i))
        return moves + [self.local(self.got_val.ref, self.got.ref, 1)]

    def load(self):
        for move in self.loads():
            move.start()

    def send(self):
        for move in self.loads():
            move.wait()
        kept, got, total = self.kept.ref, self.got.ref, self.total.ref
        for i in range(self.n):
            if self.kind == "cols":
                part = (slice(None), slice(i * self.cols, (i + 1) * self.cols))
            else:
                part = i
            total[i] = (kept[part].astype(F32) + got[part].astype(F32)).astype(BF)
        super().send()

    def add(self):
        self.load()
        self.send()


class Finish(Task):
    def __init__(self, k, pieces, block):
        self.pieces, self.final = as_val(k, pieces), block
        self.n, rows, cols = self.pieces.shape
        self.held, self.total = k.vmem(self.pieces.shape, BF), k.vmem((rows, cols), BF)

        def moves(s, d, t):
            source, dst = [(None, self.total.ref)], self.out.ref.at[s]
            return [(source, dst, {"section": 1 - s})], [(source, dst)]

        super().__init__(k, (2, rows, cols), "section", moves, 1, 2)

    def load(self):
        self.local(self.pieces.ref, self.held.ref, 1).start()

    def send(self):
        self.local(self.pieces.ref, self.held.ref, 1).wait()
        held = self.held.ref
        acc = held[0].astype(F32)
        for i in range(1, self.n):
            acc = acc + held[i].astype(F32)
        self.total.ref[...] = acc.astype(BF)
        super().send()

    def add(self):
        self.load()
        self.send()


class SumShare(Task):
    def __init__(self, k, terms, axis, slotted=False):
        self.terms = [as_val(k, v) for v in terms]
        shape = self.terms[0].shape[1:] if slotted else self.terms[0].shape
        count = dp_size() if axis == "dp" else 4
        self.slotted = slotted
        self.bufs = [k.vmem(v.shape, F32) for v in self.terms]
        self.total = k.vmem(shape, F32)

        def moves(s, d, t):
            source, me = [(None, self.total.ref)], d if axis == "dp" else t
            dst = self.out.ref.at[me]
            far = [(source, dst, {axis: (me + i) % count}) for i in range(1, count)]
            return far, [(source, dst)]

        super().__init__(k, (count,) + shape, axis, moves, count - 1, 3, out_dtype=F32)

    def add(self):
        loads = [self.local(v.ref, b.ref, 1 + i) for i, (v, b) in enumerate(zip(self.terms, self.bufs))]
        for load in loads:
            load.start()
        for load in loads:
            load.wait()
        if self.slotted:
            parts = [self.bufs[0].ref[i] for i in range(self.terms[0].shape[0])]
        else:
            parts = [buf.ref[...] for buf in self.bufs]
        acc = parts[0]
        for part in parts[1:]:
            acc = acc + part
        self.total.ref[...] = acc
        self.send()


class Weight:
    def __init__(self, k, kind, near, far, early=False):
        near, far = as_val(k, near), as_val(k, far)
        self.count, self.rows, self.cols = near.shape
        self.kind, self.near, self.far, self.waited = kind, near, far, False
        if kind == "cols":
            shape = (2 * self.rows, self.count * self.cols)
        else:
            shape = (2 * self.count * self.rows, self.cols)
        self.aside = kind == "cols" and self.cols % 128 != 0
        self.buf, self.sem = k.vmem(shape, BF), k.sem(2 * self.count)
        if self.aside:
            self.held = [k.vmem(near.shape, BF), k.vmem(near.shape, BF)]
        k.once.append(self)
        if early:
            k.early.append(self.start)

    def moves(self):
        s, dst = lax.axis_index("section"), self.buf.ref
        rows, cols = self.rows, self.cols

        def place(sec, own):
            if self.aside:
                return None
            if self.kind == "cols":
                return dst.at[block_of(sec, rows), pl.ds(own * cols, cols)]
            slot = own * 2 + sec if self.kind == "rows" else sec * self.count + own
            return dst.at[block_of(slot, rows)]

        for i in range(self.count):
            for j, (val, sec) in enumerate(((self.near, s), (self.far, 1 - s))):
                to = self.held[j].ref.at[i] if self.aside else place(sec, i)
                yield pltpu.make_async_copy(val.ref.at[i], to, self.sem.ref.at[2 * i + j])

    def start(self):
        for move in self.moves():
            move.start()

    def wait(self):
        if self.waited:
            return
        self.waited = True
        for move in self.moves():
            move.wait()
        if self.aside:
            s = lax.axis_index("section")
            for j, sec in enumerate((s, 1 - s)):
                whole = jnp.concatenate([self.held[j].ref[i] for i in range(self.count)], axis=1)
                self.buf.ref[block_of(sec, self.rows), :] = whole


class Product:
    def __init__(self, k, left, right):
        self.left, self.right = left, right
        rows = left.shape[1]
        self.chunk = 384 if rows % 384 == 0 else 256
        self.count = rows // self.chunk
        self.buf = k.vmem((rows, right.shape[1]), BF)
        self.out, self.sem = k.output(self.buf.shape, BF), k.sem(self.count)

    def copy(self, i):
        part = block_of(i, self.chunk)
        return pltpu.make_async_copy(self.buf.ref.at[part], self.out.ref.at[part], self.sem.ref.at[i])

    def run(self):
        def step(i, carry):
            part = block_of(i, self.chunk)
            value = contract(self.left.ref[:, part], self.right.ref[...], 0, 0)
            self.buf.ref[part, :] = value.astype(BF)
            self.copy(i).start()
            return carry

        lax.fori_loop(0, self.count, step, 0)

    def wait(self):
        for i in range(self.count):
            self.copy(i).wait()


def places():
    me = lax.axis_index("tensor")
    sib = me + 1 - 2 * (me % 2)
    cross = (me + 2) % 4
    diag = (sib + 2) % 4
    return me, sib, cross, diag


class Gather:
    def __init__(self, k, x, gain, weights, extras=(), trans=False, epilogue="plain", save=()):
        rows, width = x.shape
        length = 4 * rows
        self.k, self.x, self.gain, self.weights, self.extras = k, x, gain, weights, extras
        self.trans, self.epilogue, self.rows, self.half = trans, epilogue, rows, rows // 2
        cols = [w.buf.shape[0 if trans else 1] for w in weights]
        kinds = {
            "plain": [(c, F32) for c in cols],
            "ffn": [(cols[0], BF)] * 3,
            "ffn_back": [(cols[0], BF)] * 2,
        }[epilogue]
        self.full = k.vmem((length, width), BF)
        self.values = [k.vmem((length, c), kind) for c, kind in kinds]
        kept = [self.full] + self.values
        self.saved = [(v, k.output(v.shape, v.dtype), k.sem(4, 2)) for v in kept if kept.index(v) in save]
        self.sems = [k.sem(2) for _ in range(6)]
        k.late.append(self.end)

    def span(self, owner, sub):
        return pl.ds(pl.multiple_of(owner * self.rows + sub * self.half, self.half), self.half)

    def move(self, kind, i):
        me, sib, cross, _ = places()
        full = self.full.ref
        owner, peer, at = {"cross": (me, cross, 0), "sib": (me, sib, 2), "relay": (cross, sib, 4)}[kind]
        part = full.at[self.span(owner, i)]
        return remote(
            part, part, self.sems[at].ref.at[i], self.sems[at + 1].ref.at[i], {"tensor": peer}
        )

    def begin(self):
        me = places()[0]
        for i in range(2):
            part = self.x.ref[pl.ds(i * self.half, self.half), :].astype(F32)
            if self.gain is not None:
                val, row = self.gain
                part = norm_rows(part, val.ref[row : row + 1, :])
            self.full.ref[self.span(me, i), :] = part.astype(BF)
            self.move("cross", i).start()
            self.move("sib", i).start()

    def loop(self):
        me, sib, cross, diag = places()
        rows, half = self.rows, self.half
        for w in self.weights:
            w.wait()

        def step(p, carry):
            far, sub = p // 2, p % 2
            near = (1 - sub) * me + sub * sib
            first = (1 - far) * near * rows + far * (cross * rows + sub * half)
            second = (1 - far) * (near * rows + half) + far * (diag * rows + sub * half)
            pair = [pl.ds(pl.multiple_of(v, half), half) for v in (first, second)]

            @pl.when(p == 1)
            def _():
                self.move("sib", 0).wait_recv()
                self.move("sib", 1).wait_recv()

            for i in range(2):

                @pl.when(p == 2 + i)
                def _():
                    self.move("cross", i).wait_recv()
                    self.move("relay", i).start()
                    self.move("relay", i).wait_recv()

            def both(val):
                return jnp.concatenate([val.ref[pair[0], :], val.ref[pair[1], :]], axis=0)

            a = both(self.full)
            prods = [contract(a, w.buf.ref[...], 1, 1 if self.trans else 0) for w in self.weights]
            if self.epilogue == "plain":
                values = prods
            elif self.epilogue == "ffn":
                sig, silu = silu_parts(prods[0])
                values = [prods[0], prods[1], silu * prods[1]]
            else:
                gate, up = (both(v).astype(F32) for v in self.extras)
                sig, silu = silu_parts(gate)
                values = [prods[0] * up * sig * (1.0 + gate * (1.0 - sig)), prods[0] * silu]
            for val, value in zip(self.values, values):
                value = value.astype(val.dtype)
                for j in range(2):
                    val.ref[pair[j], :] = value[j * half : (j + 1) * half]
            for val, out, sem in self.saved:
                for j in range(2):
                    pltpu.make_async_copy(
                        val.ref.at[pair[j]], out.ref.at[pair[j]], sem.ref.at[p, j]
                    ).start()
            return carry

        lax.fori_loop(0, 4, step, 0)

    def end(self):
        for i in range(2):
            for kind in ("cross", "sib", "relay"):
                self.move(kind, i).wait_send()
        part = pl.ds(0, self.half)
        for val, out, sem in self.saved:
            for p in range(4):
                for j in range(2):
                    pltpu.make_async_copy(val.ref.at[part], out.ref.at[part], sem.ref.at[p, j]).wait()


class Scatter:
    def __init__(self, k, operands, weights, resid, back=None, trans=False, low=False):
        rows, width = resid.shape
        half = rows // 2
        self.operands, self.weights, self.resid, self.back = operands, weights, resid, back
        self.trans, self.low, self.rows, self.half = trans, low, rows, half
        self.keep, self.own = k.vmem((2, half, width), F32), k.vmem((rows, width), F32)
        self.to_s, self.from_s, self.to_c, self.from_c = (
            k.vmem((2, half, width), BF) for _ in range(4)
        )
        self.to_o, self.from_o = k.vmem((rows, width), BF), k.vmem((rows, width), BF)
        self.out = k.vmem((rows, width), BF if low else F32)
        self.gain_grad = k.vmem((1, width), F32) if back else None
        self.sems = [k.sem(2) for _ in range(4)] + [k.sem(1) for _ in range(2)]
        k.late.append(self.end)

    def move(self, kind, i=0):
        _, sib, cross, _ = places()
        at, src, dst, peer = {
            "diag": (0, self.to_s, self.from_s, sib),
            "cross": (2, self.to_c, self.from_c, cross),
            "near": (4, self.to_o, self.from_o, sib),
        }[kind]
        src, dst = (src.ref, dst.ref) if kind == "near" else (src.ref.at[i], dst.ref.at[i])
        return remote(
            src, dst, self.sems[at].ref.at[i], self.sems[at + 1].ref.at[i], {"tensor": peer}
        )

    def pass_on(self, i):
        self.move("diag", i).wait_recv()
        total = self.keep.ref[i] + self.from_s.ref[i].astype(F32)
        self.to_c.ref[i] = total.astype(BF)
        self.move("cross", i).start()

    def loop(self):
        me, sib, cross, diag = places()
        rows, half = self.rows, self.half
        for w in self.weights:
            w.wait()

        def step(p, carry):
            near, sub = p // 2, p % 2
            base = near * ((1 - sub) * sib + sub * me) * rows
            first = base + (1 - near) * (cross * rows + sub * half)
            second = base + near * half + (1 - near) * (diag * rows + sub * half)
            pair = [pl.ds(pl.multiple_of(v, half), half) for v in (first, second)]
            total = None
            for y, w in zip(self.operands, self.weights):
                a = jnp.concatenate([y.ref[pair[0], :], y.ref[pair[1], :]], axis=0)
                prod = contract(a, w.buf.ref[...], 1, 1 if self.trans else 0)
                total = prod if total is None else total + prod

            for i in range(2):

                @pl.when(p == i)
                def _():
                    self.keep.ref[i] = total[:half]
                    self.to_s.ref[i] = total[half:].astype(BF)
                    self.move("diag", i).start()

            @pl.when(p == 1)
            def _():
                self.pass_on(0)

            @pl.when(p == 2)
            def _():
                self.to_o.ref[...] = total.astype(BF)
                self.move("near").start()
                self.pass_on(1)

            @pl.when(p == 3)
            def _():
                self.own.ref[...] = total

            return carry

        lax.fori_loop(0, 4, step, 0)

    def finish(self):
        self.move("near").wait_recv()
        gain_sum = None
        for i in range(2):
            part = pl.ds(i * self.half, self.half)
            self.move("cross", i).wait_recv()
            total = self.own.ref[part, :] + self.from_o.ref[part, :].astype(F32)
            total = total + self.from_c.ref[i].astype(F32)
            resid = self.resid.ref[part, :].astype(F32)
            if self.back:
                value, (gain, row) = self.back
                value_grad, gain_grad = norm_back(
                    value.ref[part, :].astype(F32), gain.ref[row : row + 1, :], total
                )
                total = value_grad
                gain_sum = gain_grad if gain_sum is None else gain_sum + gain_grad
            self.out.ref[part, :] = (resid + total).astype(self.out.dtype)
        if self.back:
            self.gain_grad.ref[...] = gain_sum

    def end(self):
        self.move("near").wait_send()
        for i in range(2):
            self.move("diag", i).wait_send()
            self.move("cross", i).wait_send()


def delayed(values, by):
    if by == 0:
        return values
    row = lax.broadcasted_iota(jnp.int32, values.shape, 0)
    return jnp.where(row < by, 0.0, pltpu.roll(values, by, 0))


def advanced(values, by):
    if by == 0:
        return values
    length = values.shape[0]
    row = lax.broadcasted_iota(jnp.int32, values.shape, 0)
    return jnp.where(row >= length - by, 0.0, pltpu.roll(values, length - by, 0))


CONV_COLS = 128


class Conv:
    def __init__(self, k, projected, value, kernel):
        self.projected, self.value, self.kernel = projected, value, kernel
        self.y = k.vmem(value.shape, BF)

    def parts(self, j):
        channels = self.value.shape[1]
        at = slice(j * CONV_COLS, (j + 1) * CONV_COLS)
        b_gate = self.projected.ref[:, at]
        c_gate = self.projected.ref[:, channels + at.start : channels + at.stop]
        x_value, taps = self.value.ref[:, at], self.kernel.ref[:, at]
        product = b_gate * x_value
        count = taps.shape[0]
        causal = jnp.zeros_like(product)
        for i in range(count):
            causal = causal + taps[i : i + 1] * delayed(product, count - 1 - i)
        return at, b_gate, c_gate, x_value, taps, product, causal

    def run(self):
        for j in range(self.value.shape[1] // CONV_COLS):
            at, _, c_gate, _, _, _, causal = self.parts(j)
            self.y.ref[:, at] = (c_gate * causal).astype(BF)


class ConvBack(Conv):
    def __init__(self, k, projected, value, kernel, d_y):
        self.projected, self.value, self.kernel, self.d_y = projected, value, kernel, d_y
        self.d_proj = k.vmem(projected.shape, BF)
        self.d_value = k.vmem(value.shape, BF)
        self.d_kernel = k.vmem(kernel.shape, F32)

    def run(self):
        channels = self.value.shape[1]
        for j in range(channels // CONV_COLS):
            at, b_gate, c_gate, x_value, taps, product, causal = self.parts(j)
            d_y = self.d_y.ref[:, at]
            d_causal = d_y * c_gate
            count = taps.shape[0]
            d_product = jnp.zeros_like(product)
            for i in range(count):
                by = count - 1 - i
                row = jnp.sum(d_causal * delayed(product, by), axis=0, keepdims=True)
                self.d_kernel.ref[i : i + 1, at] = row
                d_product = d_product + taps[i : i + 1] * advanced(d_causal, by)
            self.d_proj.ref[:, at] = (d_product * x_value).astype(BF)
            self.d_proj.ref[:, channels + at.start : channels + at.stop] = (d_y * causal).astype(BF)
            self.d_value.ref[:, at] = (d_product * b_gate).astype(BF)


def head_mean(values, head_size):
    width = values.shape[1]
    row = lax.broadcasted_iota(jnp.int32, (width, width), 0) // head_size
    col = lax.broadcasted_iota(jnp.int32, (width, width), 1) // head_size
    group = jnp.where(row == col, 1.0 / head_size, 0.0).astype(F32)
    return lax.dot_general(
        values, group, (((1,), (0,)), ((), ())),
        precision=lax.Precision.HIGHEST, preferred_element_type=F32,
    )


def turn(values, head_size, back):
    width, half = values.shape[1], head_size // 2
    lane = lax.broadcasted_iota(jnp.int32, values.shape, 1) % head_size
    upper = pltpu.roll(values, width - half, 1)
    lower = pltpu.roll(values, half, 1)
    return jnp.where(lane < half, upper, -lower) if back else jnp.where(lane < half, -upper, lower)


def head_norm(values, gain, head_size):
    return values * lax.rsqrt(head_mean(values * values, head_size) + EPS) * gain


def head_norm_back(values, gain, grad_in, head_size):
    row_scale = lax.rsqrt(head_mean(values * values, head_size) + EPS)
    normed = values * row_scale
    gain_grad = jnp.sum(grad_in * normed, axis=0, keepdims=True)
    scaled = grad_in * gain
    return row_scale * (scaled - normed * head_mean(scaled * normed, head_size)), gain_grad


def block_weights(q_rows, k_rows, first_row):
    rows, length = q_rows.shape[0], k_rows.shape[0]
    scores = contract(q_rows, k_rows, 1, 1) * (q_rows.shape[1] ** -0.5)
    query = first_row + lax.broadcasted_iota(jnp.int32, (rows, length), 0)
    key = lax.broadcasted_iota(jnp.int32, (rows, length), 1)
    scores = jnp.where(key <= query, scores, MASKED)
    exps = jnp.exp(scores - jnp.max(scores, axis=1, keepdims=True))
    return exps * (1.0 / jnp.sum(exps, axis=1, keepdims=True))


class Heads:
    def __init__(self, projected, tables, size):
        self.projected, self.size = projected, size
        self.gain, self.cos, self.sin = (v.buf for v in tables)
        self.loads = tables
        self.length, width = projected.shape
        self.q_cols, self.k_cols = width // 2, width // 4
        self.heads, self.kv_heads = self.q_cols // size, self.k_cols // size
        self.share = self.heads // self.kv_heads

    def per_head(self, k, count, kind):
        return k.vmem((count, self.length, self.size), kind)

    def split(self, val, rows, values):
        for h in range(val.shape[0]):
            val.ref[h, rows, :] = values[:, h * self.size : (h + 1) * self.size]

    def join(self, val, rows):
        return jnp.concatenate([val.ref[h, rows, :] for h in range(val.shape[0])], axis=1)

    def blocks(self, step):
        lax.fori_loop(0, self.length // ROW_BLOCK, lambda p, c: step(block_of(p, ROW_BLOCK)) or c, 0)


class Attend(Heads):
    def __init__(self, k, projected, tables, size):
        super().__init__(projected, tables, size)
        self.q_rot = k.vmem((self.length, self.q_cols), BF)
        self.k_rot = k.vmem((self.length, self.k_cols), BF)
        self.y = k.vmem((self.length, self.q_cols), BF)
        self.q_h, self.y_h = (self.per_head(k, self.heads, BF) for _ in range(2))
        self.k_h, self.v_h = (self.per_head(k, self.kv_heads, BF) for _ in range(2))

    def run(self, *between):
        for load in self.loads:
            load.wait()
        size, q_cols, k_cols, proj = self.size, self.q_cols, self.k_cols, self.projected.ref

        def prepare(rows):
            c, n = self.cos.ref[rows, :], self.sin.ref[rows, :]
            q = head_norm(proj[rows, :q_cols], self.gain.ref[0:1, :], size)
            q = (q * c + turn(q, size, False) * n).astype(BF)
            k = head_norm(proj[rows, q_cols : q_cols + k_cols], self.gain.ref[1:2, :k_cols], size)
            k = (k * c[:, :k_cols] + turn(k, size, False) * n[:, :k_cols]).astype(BF)
            self.q_rot.ref[rows, :] = q
            self.k_rot.ref[rows, :] = k
            self.split(self.q_h, rows, q)
            self.split(self.k_h, rows, k)
            self.split(self.v_h, rows, proj[rows, q_cols + k_cols :].astype(BF))

        self.blocks(prepare)

        def head(h, carry):
            g = h // self.share
            for i in range(self.length // ROW_BLOCK):
                rows, seen = pl.ds(i * ROW_BLOCK, ROW_BLOCK), pl.ds(0, (i + 1) * ROW_BLOCK)
                weights = block_weights(
                    self.q_h.ref[h, rows, :], self.k_h.ref[g, seen, :], i * ROW_BLOCK
                )
                value = contract(weights.astype(BF), self.v_h.ref[g, seen, :], 1, 0)
                self.y_h.ref[h, rows, :] = value.astype(BF)
            return carry

        lax.fori_loop(0, self.heads // 2, head, 0)
        for step in between:
            step()
        lax.fori_loop(self.heads // 2, self.heads, head, 0)
        self.y.ref[...] = self.join(self.y_h, slice(None))


class AttendBack(Heads):
    def __init__(self, k, projected, tables, size, q_rot, k_rot, d_y):
        super().__init__(projected, tables, size)
        self.q_rot, self.k_rot, self.d_y = q_rot, k_rot, d_y
        self.q_h, self.dy_h = (self.per_head(k, self.heads, BF) for _ in range(2))
        self.k_h, self.v_h = (self.per_head(k, self.kv_heads, BF) for _ in range(2))
        self.dq_h = self.per_head(k, self.heads, F32)
        self.dk_h, self.dv_h = (self.per_head(k, self.kv_heads, F32) for _ in range(2))
        self.d_proj = k.vmem(projected.shape, BF)
        self.q_gain, self.k_gain = k.vmem((1, self.q_cols), F32), k.vmem((1, self.k_cols), F32)

    def run(self):
        for load in self.loads:
            load.wait()
        size, q_cols, k_cols, proj = self.size, self.q_cols, self.k_cols, self.projected.ref
        scale = size**-0.5
        dq_h, dk_h, dv_h = self.dq_h.ref, self.dk_h.ref, self.dv_h.ref

        def prepare(rows):
            self.split(self.q_h, rows, self.q_rot.ref[rows, :])
            self.split(self.dy_h, rows, self.d_y.ref[rows, :].astype(BF))
            self.split(self.k_h, rows, self.k_rot.ref[rows, :])
            self.split(self.v_h, rows, proj[rows, q_cols + k_cols :].astype(BF))

        self.blocks(prepare)
        dk_h[...] = jnp.zeros_like(dk_h)
        dv_h[...] = jnp.zeros_like(dv_h)

        def head(h, carry):
            g = h // self.share
            for i in range(self.length // ROW_BLOCK):
                rows, seen = pl.ds(i * ROW_BLOCK, ROW_BLOCK), pl.ds(0, (i + 1) * ROW_BLOCK)
                q, low = self.q_h.ref[h, rows, :], self.dy_h.ref[h, rows, :]
                k = self.k_h.ref[g, seen, :]
                prob = block_weights(q, k, i * ROW_BLOCK)
                d_weights = contract(low, self.v_h.ref[g, seen, :], 1, 1)
                dv_h[g, seen, :] += contract(prob.astype(BF), low, 0, 0)
                inner = jnp.sum(prob * d_weights, axis=1, keepdims=True)
                d_scores = (prob * (d_weights - inner)).astype(BF)
                dq_h[h, rows, :] = contract(d_scores, k, 1, 0) * scale
                dk_h[g, seen, :] += contract(d_scores, q, 0, 0) * scale
            return carry

        lax.fori_loop(0, self.heads, head, 0)
        self.q_gain.ref[...] = jnp.zeros_like(self.q_gain.ref)
        self.k_gain.ref[...] = jnp.zeros_like(self.k_gain.ref)

        def finish(rows):
            c, n = self.cos.ref[rows, :], self.sin.ref[rows, :]
            dq, dk, dv = (self.join(v, rows) for v in (self.dq_h, self.dk_h, self.dv_h))
            dq = dq * c + turn(dq * n, size, True)
            dk = dk * c[:, :k_cols] + turn(dk * n[:, :k_cols], size, True)
            dq, q_sum = head_norm_back(proj[rows, :q_cols], self.gain.ref[0:1, :], dq, size)
            dk, k_sum = head_norm_back(
                proj[rows, q_cols : q_cols + k_cols], self.gain.ref[1:2, :k_cols], dk, size
            )
            self.q_gain.ref[...] += q_sum
            self.k_gain.ref[...] += k_sum
            self.d_proj.ref[rows, :q_cols] = dq.astype(BF)
            self.d_proj.ref[rows, q_cols : q_cols + k_cols] = dk.astype(BF)
            self.d_proj.ref[rows, q_cols + k_cols :] = dv.astype(BF)

        self.blocks(finish)


def body(boundary, norm_gain, mix_in, mix_out, w_gate, w_up, w_down, conv_x, conv_kernel, qk_gain):
    first = lax.axis_index("section") == 0
    tensor_index = lax.axis_index("tensor")
    model_width = boundary.shape[3]
    channels = mix_out.shape[1]
    row_shape = boundary.shape[2:]
    length, size = 4 * row_shape[0], qk_gain.shape[1]

    seqs, own_gain = boundary[0], norm_gain[0]
    sh_in, sh_out, sh_gate, sh_up, sh_down = (v[0] for v in (mix_in, mix_out, w_gate, w_up, w_down))
    cosine_table, sine_table = rotation(length, size)
    heads = channels // size
    table_arrays = [jnp.tile(v, (1, heads)) for v in (qk_gain, cosine_table, sine_table)]

    def gains_of(k, block, other, early=True):
        own, moved = k.input(own_gain), as_val(k, other)
        sources = lambda s, d, t: [(s == block, own.ref), (s == 1 - block, moved.ref)]
        return Load(k, sources, own.shape, F32, early)

    def start_rows(k, slot, other, early=True):
        own, moved = k.input(seqs), as_val(k, other)
        sources = lambda s, d, t: [(s == slot, own.ref.at[slot]), (s == 1 - slot, moved.ref)]
        return Load(k, sources, row_shape, BF, early)

    def wait(*items):
        return [item.wait for item in items]

    k = Kernel(0)
    t_seq = None
    seq_val = k.input(seqs)

    def seq_moves(s, d, t):
        return [([(None, seq_val.ref.at[1 - s])], t_seq.out.ref, {"section": 1 - s})], []

    t_in, t_out, t_gate, t_up, t_down = (
        x_half(k, v) for v in (sh_in, sh_out, sh_gate, sh_up, sh_down)
    )
    t_seq = Task(k, row_shape, "section", seq_moves, 1)
    t_gain, z_cols = x_move(k, own_gain), z_gather(k, conv_x)
    z_in0, z_out0 = z_gather_half(k, sh_in, t_in.out, 0), z_gather_half(k, sh_out, t_out.out, 0)
    z_gate0, z_up0 = z_gather_half(k, sh_gate, t_gate.out, 0), z_gather_half(k, sh_up, t_up.out, 0)
    x_cols, x_in0, x_out0, x_gate0 = (x_move(k, v.out) for v in (z_cols, z_in0, z_out0, z_gate0))
    x_load, gain_load = start_rows(k, 0, t_seq.out, False), gains_of(k, 0, t_gain.out, False)
    taps = load_all(k, conv_kernel)
    w_in0, w_cols = Weight(k, "rows", z_in0.out, x_in0.out), Weight(k, "conv", z_cols.out, x_cols.out)
    w_out0 = Weight(k, "cols", z_out0.out, x_out0.out)
    g0 = Gather(k, x_load.buf, (gain_load.buf, 0), [w_in0, w_cols], save=(0, 1, 2))
    conv = Conv(k, g0.values[0], g0.values[1], taps.buf)
    y0 = Save(k, conv.y)
    s1 = Scatter(k, [conv.y], [w_out0], x_load.buf)
    mid0 = Save(k, s1.out)
    k.do(t_in.send, t_out.send, z_cols.send, t_gate.send, t_gain.send, t_seq.send)
    k.do(t_in.wait, z_in0.send, t_out.wait, z_out0.send, t_up.send)
    k.do(t_gain.wait, gain_load.start, t_seq.wait, x_load.start)
    k.do(gain_load.wait, x_load.wait, g0.begin)
    k.do(t_gate.wait, z_gate0.send)
    k.do(z_cols.wait, x_cols.send, z_in0.wait, x_in0.send, z_out0.wait, x_out0.send, t_down.send)
    k.do(t_up.wait, z_up0.send)
    k.do(x_cols.wait, w_cols.start, x_in0.wait, w_in0.start)
    k.do(z_gate0.wait, x_gate0.send)
    k.do(g0.loop, taps.wait, conv.run, y0.start)
    k.do(x_out0.wait, w_out0.start, s1.loop, s1.finish, mid0.start)
    k.do(*wait(t_down, x_gate0, z_up0))
    k.build()
    a0, proj0, value0 = (out for _, out, _ in g0.saved)
    y0, mid0 = y0.out, mid0.out

    k = Kernel(1)
    x_up0, z_down0 = x_move(k, z_up0.out), z_gather_half(k, sh_down, t_down.out, 0)
    z_in1, z_out1 = z_gather_half(k, sh_in, t_in.out, 1), z_gather_half(k, sh_out, t_out.out, 1)
    z_gate1 = z_gather_half(k, sh_gate, t_gate.out, 1)
    x_down0, x_in1, x_out1 = (x_move(k, v.out) for v in (z_down0, z_in1, z_out1))
    rows, gain_load = load_all(k, mid0), gains_of(k, 0, t_gain.out)
    w_gate0 = Weight(k, "rows", z_gate0.out, x_gate0.out, True)
    w_up0 = Weight(k, "rows", z_up0.out, x_up0.out)
    w_down0 = Weight(k, "cols", z_down0.out, x_down0.out)
    g2 = Gather(
        k, rows.buf, (gain_load.buf, 1), [w_gate0, w_up0], epilogue="ffn", save=(0, 1, 2, 3)
    )
    s3 = Scatter(k, [g2.values[2]], [w_down0], rows.buf, low=True)
    z_rows = Save(k, s3.out)
    k.do(x_up0.send, z_down0.send, z_in1.send, z_out1.send, z_gate1.send)
    k.do(rows.wait, gain_load.wait, g2.begin)
    k.do(z_down0.wait, x_down0.send, x_up0.wait, w_up0.start, g2.loop)
    k.do(z_in1.wait, x_in1.send, z_out1.wait, x_out1.send)
    k.do(x_down0.wait, w_down0.start, s3.loop, s3.finish, z_rows.start)
    k.do(*wait(x_in1, x_out1, z_gate1))
    k.build()
    m0, gate0, up0, hid0 = (out for _, out, _ in g2.saved)
    z_rows = z_rows.out

    k = Kernel(2)
    x_gate1, z_up1 = x_move(k, z_gate1.out), z_gather_half(k, sh_up, t_up.out, 1)
    z_down1, x_up1 = z_gather_half(k, sh_down, t_down.out, 1), x_move(k, z_up1.out)
    rows, gain_load = load_all(k, z_rows), gains_of(k, 1, t_gain.out)
    tables = [load_all(k, v) for v in table_arrays]
    w_in1 = Weight(k, "rows", z_in1.out, x_in1.out, True)
    w_out1 = Weight(k, "cols", z_out1.out, x_out1.out, True)
    g4 = Gather(k, rows.buf, (gain_load.buf, 0), [w_in1], save=(0, 1))
    attend = Attend(k, g4.values[0], tables, size)
    kept = [Save(k, v) for v in (attend.q_rot, attend.k_rot, attend.y)]
    s5 = Scatter(k, [attend.y], [w_out1], rows.buf)
    mid1 = Save(k, s5.out)
    k.do(x_gate1.send, z_up1.send, z_down1.send)
    k.do(rows.wait, gain_load.wait, g4.begin, g4.loop)
    k.do(lambda: attend.run(z_up1.wait, x_up1.send))
    k.do(*(v.start for v in kept))
    k.do(s5.loop, s5.finish, mid1.start)
    k.do(*wait(x_gate1, x_up1, z_down1))
    k.build()
    a1, proj1 = (out for _, out, _ in g4.saved)
    q_rot, k_rot, y1 = (v.out for v in kept)
    mid1 = mid1.out

    k = Kernel(3)
    x_down1 = x_move(k, z_down1.out)
    rows, gain_load = load_all(k, mid1), gains_of(k, 1, t_gain.out)
    cot = start_rows(k, 1, t_seq.out)
    w_gate1 = Weight(k, "rows", z_gate1.out, x_gate1.out, True)
    w_up1 = Weight(k, "rows", z_up1.out, x_up1.out, True)
    w_down1 = Weight(k, "cols", z_down1.out, x_down1.out)
    g6 = Gather(k, rows.buf, (gain_load.buf, 1), [w_gate1, w_up1], epilogue="ffn")
    g8 = Gather(
        k, cot.buf, None, [w_down1], [g6.values[0], g6.values[1]], trans=True, epilogue="ffn_back"
    )
    p_down1 = Product(k, g6.values[2], g8.full)
    p_gate1, p_up1 = Product(k, g6.full, g8.values[0]), Product(k, g6.full, g8.values[1])
    r_down1 = x_half(k, p_down1.out)
    s7 = Scatter(k, [g6.values[2]], [w_down1], rows.buf, low=True)
    s9 = Scatter(k, g8.values, [w_gate1, w_up1], cot.buf, (rows.buf, (gain_load.buf, 1)), True)
    y_rows, d_mid1, gain11 = Save(k, s7.out), Save(k, s9.out), Save(k, s9.gain_grad)
    k.do(x_down1.send, rows.wait, gain_load.wait, g6.begin, cot.wait, g8.begin, g6.loop)
    k.do(x_down1.wait, w_down1.start, g8.loop, p_down1.run, p_down1.wait, r_down1.send)
    k.do(s9.loop, p_gate1.run, p_up1.run, s9.finish, d_mid1.start, gain11.start)
    k.do(s7.loop, s7.finish, y_rows.start, p_gate1.wait, p_up1.wait)
    k.do(*wait(r_down1))
    k.build()
    y_rows, d_mid1, gain11 = y_rows.out, d_mid1.out, gain11.out

    k = Kernel(4)
    q_down1 = SumScatter(k, "cols", p_down1.out, r_down1.out)
    r_gate1, r_up1 = x_slots(k, p_gate1.out, "rows"), x_slots(k, p_up1.out, "rows")
    q_gate1 = SumScatter(k, "rows", p_gate1.out, r_gate1.out)
    rows, gain_load = load_all(k, d_mid1), gains_of(k, 1, t_gain.out)
    value = load_all(k, z_rows)
    tables = [load_all(k, v) for v in table_arrays]
    proj, q_load, k_load, y_load, a_load = (load_all(k, v) for v in (proj1, q_rot, k_rot, y1, a1))
    w_in1 = Weight(k, "rows", z_in1.out, x_in1.out, True)
    w_out1 = Weight(k, "cols", z_out1.out, x_out1.out, True)
    g10 = Gather(k, rows.buf, None, [w_out1], trans=True)
    p_out1 = Product(k, y_load.buf, g10.full)
    back = AttendBack(k, proj.buf, tables, size, q_load.buf, k_load.buf, g10.values[0])
    p_in1 = Product(k, a_load.buf, back.d_proj)
    r_out1 = x_half(k, p_out1.out)
    s11 = Scatter(
        k, [back.d_proj], [w_in1], rows.buf, (value.buf, (gain_load.buf, 0)), True, low=True
    )
    d_z, gain10 = Save(k, s11.out), Save(k, s11.gain_grad)
    head_gains = [Save(k, back.q_gain), Save(k, back.k_gain)]
    k.early.append(q_down1.load)
    k.do(r_gate1.send, r_up1.send, rows.wait, g10.begin, q_down1.send, g10.loop)
    k.do(y_load.wait, p_out1.run, p_out1.wait, r_out1.send)
    k.do(r_gate1.wait, q_gate1.add)
    k.do(proj.wait, q_load.wait, k_load.wait, back.run, *(v.start for v in head_gains))
    k.do(gain_load.wait, value.wait, s11.loop, a_load.wait, p_in1.run)
    k.do(s11.finish, d_z.start, gain10.start, p_in1.wait)
    k.do(*wait(q_down1, q_gate1, r_up1, r_out1))
    k.build()
    d_z, gain10 = d_z.out, gain10.out
    q_gain, k_gain = (v.out.array for v in head_gains)

    k = Kernel(5)
    q_up1 = SumScatter(k, "rows", p_up1.out, r_up1.out)
    q_out1 = SumScatter(k, "cols", p_out1.out, r_out1.out)
    r_in1 = x_slots(k, p_in1.out, "rows")
    q_in1 = SumScatter(k, "rows", p_in1.out, r_in1.out)
    e_down1, e_gate1 = Finish(k, q_down1.out, 1), Finish(k, q_gate1.out, 1)
    rows, value, gain_load = load_all(k, d_z), load_all(k, mid0), gains_of(k, 0, t_gain.out)
    gate_load, up_load, hid_load, m_load = (load_all(k, v) for v in (gate0, up0, hid0, m0))
    w_gate0 = Weight(k, "rows", z_gate0.out, x_gate0.out, True)
    w_up0 = Weight(k, "rows", z_up0.out, x_up0.out, True)
    w_down0 = Weight(k, "cols", z_down0.out, x_down0.out, True)
    g12 = Gather(
        k, rows.buf, None, [w_down0], [gate_load.buf, up_load.buf], trans=True, epilogue="ffn_back"
    )
    p_down0 = Product(k, hid_load.buf, g12.full)
    p_gate0, p_up0 = Product(k, m_load.buf, g12.values[0]), Product(k, m_load.buf, g12.values[1])
    r_down0 = x_half(k, p_down0.out)
    s13 = Scatter(
        k, g12.values, [w_gate0, w_up0], rows.buf, (value.buf, (gain_load.buf, 1)), True
    )
    d_mid0, gain01 = Save(k, s13.out), Save(k, s13.gain_grad)
    k.early += [q_up1.load, q_out1.load, e_down1.load, e_gate1.load]
    k.do(r_in1.send, rows.wait, g12.begin, q_up1.send, q_out1.send, e_down1.send, e_gate1.send)
    k.do(gate_load.wait, up_load.wait, g12.loop)
    k.do(hid_load.wait, p_down0.run, p_down0.wait, r_down0.send)
    k.do(r_in1.wait, q_in1.add)
    k.do(s13.loop, m_load.wait, p_gate0.run, p_up0.run)
    k.do(value.wait, gain_load.wait, s13.finish, d_mid0.start, gain01.start)
    k.do(p_gate0.wait, p_up0.wait)
    k.do(*wait(q_up1, q_out1, q_in1, e_down1, e_gate1, r_down0))
    k.build()
    d_mid0, gain01 = d_mid0.out, gain01.out

    k = Kernel(6)
    r_gate0, r_up0 = x_slots(k, p_gate0.out, "rows"), x_slots(k, p_up0.out, "rows")
    q_down0 = SumScatter(k, "cols", p_down0.out, r_down0.out)
    q_gate0 = SumScatter(k, "rows", p_gate0.out, r_gate0.out)
    q_up0 = SumScatter(k, "rows", p_up0.out, r_up0.out)
    e_up1, e_out1, e_in1 = (Finish(k, v.out, 1) for v in (q_up1, q_out1, q_in1))
    rows, gain_load = load_all(k, d_mid0), gains_of(k, 0, t_gain.out)
    x_load, taps = start_rows(k, 0, t_seq.out), load_all(k, conv_kernel)
    y_load, a_load, proj, value = (load_all(k, v) for v in (y0, a0, proj0, value0))
    w_in0 = Weight(k, "rows", z_in0.out, x_in0.out, True)
    w_cols = Weight(k, "conv", z_cols.out, x_cols.out, True)
    w_out0 = Weight(k, "cols", z_out0.out, x_out0.out, True)
    g14 = Gather(k, rows.buf, None, [w_out0], trans=True)
    p_out0 = Product(k, y_load.buf, g14.full)
    back = ConvBack(k, proj.buf, value.buf, taps.buf, g14.values[0])
    p_in0, p_cols = Product(k, a_load.buf, back.d_proj), Product(k, a_load.buf, back.d_value)
    r_out0, r_in0 = x_half(k, p_out0.out), x_slots(k, p_in0.out, "rows")
    r_cols = x_slots(k, p_cols.out, "conv")
    q_out0, q_in0 = SumScatter(k, "cols", p_out0.out, r_out0.out), SumScatter(k, "rows", p_in0.out, r_in0.out)
    q_cols = SumScatter(k, "conv", p_cols.out, r_cols.out)
    e_down0, e_gate0, e_up0, e_out0, e_in0 = (
        Finish(k, v.out, 0) for v in (q_down0, q_gate0, q_up0, q_out0, q_in0)
    )
    s15 = Scatter(
        k, [back.d_proj, back.d_value], [w_in0, w_cols], rows.buf,
        (x_load.buf, (gain_load.buf, 0)), True, low=True,
    )
    d_x = Save(k, s15.out)
    tap_rows = conv_kernel.shape[0]
    small = k.vmem((8, model_width), F32)
    small_out = Save(k, small)
    ready = [load_all(k, v) for v in (gain01, gain10, gain11)]
    head_row = jnp.pad(
        jnp.stack([jnp.sum(v.reshape(-1, size), axis=0) for v in (q_gain, k_gain)]).reshape(1, -1),
        ((0, 0), (0, model_width - 2 * size)),
    )
    head_load = load_all(k, head_row)

    def fill_small():
        t = lax.axis_index("tensor")
        small.ref[...] = jnp.zeros_like(small.ref)
        small.ref[0:1, :] = s15.gain_grad.ref[...]
        for i, load in enumerate(ready):
            load.wait()
            small.ref[i + 1 : i + 2, :] = load.buf.ref[...]
        small.ref[4 : 4 + tap_rows, block_of(t, channels)] = back.d_kernel.ref[...]
        head_load.wait()
        small.ref[7:8, :] = head_load.buf.ref[...]
        small_out.start()

    t_small = x_move(k, small_out.out)
    z_small = SumShare(k, [small_out.out, t_small.out], "dp")
    t_total = SumShare(k, [z_small.out], "tensor", slotted=True)
    y_val, dx_val = k.input(y_rows), d_x.out

    def result_moves(s, d, t):
        sources = [(s == 0, y_val.ref), (s == 1, dx_val.ref)]
        return [(sources, t_result.out.ref, {"section": 1 - s})], []

    t_result = Task(k, row_shape, "section", result_moves, 1)
    k.early += [q_down0.load, e_up1.load, e_out1.load, e_in1.load]
    k.do(r_gate0.send, r_up0.send, rows.wait, g14.begin, q_down0.send)
    k.do(e_up1.send, e_out1.send, e_in1.send, g14.loop)
    k.do(y_load.wait, p_out0.run, p_out0.wait, r_out0.send)
    k.do(proj.wait, value.wait, taps.wait, back.run, a_load.wait)
    k.do(p_in0.run, p_cols.run, p_in0.wait, r_in0.send, p_cols.wait, r_cols.send)
    k.do(r_gate0.wait, q_gate0.add)
    k.do(x_load.wait, gain_load.wait, s15.loop, s15.finish, d_x.start)
    k.do(fill_small, d_x.wait, t_result.send)
    k.do(small_out.wait, t_small.send)
    k.do(r_up0.wait, q_up0.add)
    k.do(r_out0.wait, q_out0.add, r_in0.wait, q_in0.add, r_cols.wait, q_cols.add)
    k.do(q_down0.wait, e_down0.add, t_small.wait, z_small.add, q_gate0.wait, e_gate0.add)
    k.do(z_small.wait, t_total.add)
    k.do(q_up0.wait, e_up0.add, q_out0.wait, e_out0.add, q_in0.wait, e_in0.add)
    rest = (e_up1, e_out1, e_in1, q_cols, e_down0, e_gate0, e_up0, e_out0, e_in0)
    k.do(*wait(*rest, t_total, t_result))
    k.build()

    def whole(zero, one):
        kept = jnp.where(first, zero.out.array, one.out.array)
        return kept.reshape(1, -1, kept.shape[-1]).astype(F32)

    d_x, y_rows, moved = d_x.out.array, y_rows.array, t_result.out.array
    result = jnp.where(first, jnp.stack([d_x, moved]), jnp.stack([moved, y_rows]))
    small = jnp.sum(t_total.out.array, axis=0)
    gains_total = small[:4].reshape(2, 2, model_width)
    gain_out = lax.dynamic_slice_in_dim(gains_total, lax.axis_index("section"), 1, 0)
    kernel_out = lax.dynamic_slice_in_dim(
        small[4 : 4 + tap_rows], tensor_index * channels, channels, 1
    )
    head_total = small[7, : qk_gain.size].reshape(qk_gain.shape)
    return (
        result[None],
        gain_out,
        whole(e_in0, e_in1),
        whole(e_out0, e_out1),
        whole(e_gate0, e_gate1),
        whole(e_up0, e_up1),
        whole(e_down0, e_down1),
        jnp.sum(q_cols.out.array.astype(F32), axis=0),
        kernel_out,
        head_total,
    )


def solution(mesh):
    in_specs = (
        P("section", "dp", "tensor", None),
        P("section", None, None),
        P("section", "dp", "tensor"),
        P("section", "tensor", "dp"),
        P("section", "dp", "tensor"),
        P("section", "dp", "tensor"),
        P("section", "tensor", "dp"),
        P(("section", "dp"), "tensor"),
        P(None, "tensor"),
        P(),
    )
    out_specs = (
        P("section", "dp", "tensor", None),
        P("section", None, None),
        P("section", "dp", "tensor"),
        P("section", "tensor", "dp"),
        P("section", "dp", "tensor"),
        P("section", "dp", "tensor"),
        P("section", "tensor", "dp"),
        P(("section", "dp"), "tensor"),
        P(None, "tensor"),
        P(),
    )
    return jax.shard_map(body, mesh=mesh, in_specs=in_specs, out_specs=out_specs, check_vma=False)
```

time: 2890 us -> 616 us (0.21)
  waiting for transfers between devices: 2170 us -> 0 us
  Pallas kernels: 0 us -> 586 us
  matrix products: 271 us -> 0 us
  blocking collectives: 191 us -> 0 us
  other arithmetic: 102 us -> 11.3 us
  local copies, waits for them, and re-layouts: 80.8 us -> 7.92 us
    all_gather x36 -> x0, waiting for transfers between devices: 1160 us -> none  [the longest x6 293 us: fetch_weights(): lax.all_gather(w_up[0], 'dp', axis=0, tiled=True)]
    reduce_scatter x18 -> x0, waiting for transfers between devices: 935 us -> none  [the longest x12 576 us: collect(): lax.psum_scatter(partial_value, 'tensor', scatter_dimension=0, tiled=True)]
    pallas_call x0 -> x7, Pallas kernels: none -> 586 us  [build(): pl.pallas_call(self.body, out_shape=[jax.ShapeDtypeStruct(v.shape, v.dtyp...]
    dot_general x63 -> x0, matrix products: 271 us -> none  [the longest x27 134 us: matmul(): return jnp.dot(left_op, right_op, preferred_element_type=jnp.float32)]
    all_gather x7 -> x0, blocking collectives: 150 us -> none  [the longest x6 114 us: fetch_weights(): lax.all_gather(mix_out[0], 'dp', axis=1, tiled=True)]
    ppermute x6 -> x0, waiting for transfers between devices: 61.3 us -> none  [shifted(): return lax.ppermute(shard, axis, pairs)]
    psum x1 -> x0, blocking collectives: 40.6 us -> none  [body(): lax.psum((gains_full, kernel_full, head_sum), ('section', 'dp', 'tensor'))]
    dynamic_update_slice x24 -> x0, other arithmetic: 40.5 us -> none  [store(): lax.dynamic_update_index_in_dim(buffer, jnp.where(is_live, new_item, old_...]
  transfers between devices with their start and end apart: 60 -> 0, of which waited for: 59 -> 0; matrix products, arithmetic and copies ran while one was open for 8% -> 0% of each run, Pallas kernels for 0% -> 0%
where the time goes in v5:
time: 616 us; the launch traced here: 606 us
  Pallas kernels  586 us (95%)
  other arithmetic  11.3 us (2%)
  local copies, waits for them, and re-layouts  7.92 us (1%)
    pallas_call x7, Pallas kernels, build(): pl.pallas_call(self.body, out_shape=[jax.ShapeDtypeStruct(v.shape, v.dtyp...  586 us

profile of v5, /device:TPU:0, one launch (start us, length us, event | category | flops | bytes accessed | tf_op | source)
XLA Modules:
  0.0 606.3 jit_solution(10620001727437498138)
XLA Ops:
  0.6 91.1 %stage0.1 = (bf16[128,512]{1,0:T(8,128)(2,1)}, bf16[128,256]{1,0:T(8,128)(2,1)}, bf16[128,1152]{1,0:T(8,128)(2,1)}, bf16[128,1152]{1,0:T(8,128)(2,1)}, bf16[576,...) custom-call(bf16[2,256,1024]{2,1,0:T(8,128)(2,1)} %bitcast.34, ...), custom_call_target="tpu_custom_call" | custom-call | tf_op jit(solution)/shard_map/stage0/pallas_call | solution.py:137
  91.7 82.3 %stage1.1 = (bf16[4,128,1152]{2,1,0:T(8,128)(2,1)}, bf16[4,576,256]{2,1,0:T(8,128)(2,1)}, bf16[4,128,512]{2,1,0:T(8,128)(2,1)}, bf16[4,128,256]{2,1,0:T(8,128)(2...) custom-call(bf16[4,128,1152]{2,1,0:T(8,128)(2,1)} %get-tuple-element, ...), custom_call_target="tpu_custom_call" | custom-call | tf_op jit(solution)/shard_map/stage1/pallas_call | solution.py:137
  174.1 0.5 fusion
  174.7 0.1 tile.14
  174.8 1.3 copy.20.refs_9_
  176.1 0.1 tile.31
  176.2 0.0 copy-start.14
  176.2 1.3 copy.21.refs_10_
  177.6 0.0 copy-done.14
  177.6 0.7 tile.13.refs_8_
  178.2 75.0 %stage2.1 = (bf16[4,128,1152]{2,1,0:T(8,128)(2,1)}, bf16[4,128,1152]{2,1,0:T(8,128)(2,1)}, bf16[4,576,256]{2,1,0:T(8,128)(2,1)}, bf16[4,128,1152]{2,1,0:T(8,128)...) custom-call(bf16[4,128,1152]{2,1,0:T(8,128)(2,1)} %get-tuple-element, ...), custom_call_target="tpu_custom_call" | custom-call | tf_op jit(solution)/shard_map/stage2/pallas_call | solution.py:137
  253.2 74.9 %stage3.1 = (bf16[4,576,256]{2,1,0:T(8,128)(2,1)}, bf16[1152,1024]{1,0:T(8,128)(2,1)}, bf16[1024,1152]{1,0:T(8,128)(2,1)}, bf16[1024,1152]{1,0:T(8,128)(2,1)}, b...) custom-call(bf16[4,576,256]{2,1,0:T(8,128)(2,1)} %get-tuple-element.110.refs_0_, ...), custom_call_target="tpu_custom_call" | custom-call | tf_op jit(solution)/shard_map/stage3/pallas_call | solution.py:137
  328.2 85.2 %stage4.1 = (bf16[4,576,256]{2,1,0:T(8,128)(2,1)}, bf16[4,128,1152]{2,1,0:T(8,128)(2,1)}, bf16[4,128,1152]{2,1,0:T(8,128)(2,1)}, bf16[4,128,1152]{2,1,0:T(8,128)...) custom-call(bf16[1152,1024]{1,0:T(8,128)(2,1)} %get-tuple-element.11, ...), custom_call_target="tpu_custom_call" | custom-call | tf_op jit(solution)/shard_map/stage4/pallas_call | solution.py:137
  413.3 0.5 broadcast.38
  413.8 1.3 reduce.11
  415.2 0.1 reshape.184
  415.3 1.3 reduce.10
  416.6 0.1 reshape.185
  416.7 0.1 reshape.186
  416.8 0.6 pad.4.refs_26_
  417.4 52.9 %stage5.1 = (bf16[4,128,1152]{2,1,0:T(8,128)(2,1)}, bf16[4,128,256]{2,1,0:T(8,128)(2,1)}, bf16[4,128,512]{2,1,0:T(8,128)(2,1)}, bf16[4,128,512]{2,1,0:T(8,128)(2...) custom-call(bf16[1024,1152]{1,0:T(8,128)(2,1)} %get-tuple-element.11, ...), custom_call_target="tpu_custom_call" | custom-call | tf_op jit(solution)/shard_map/stage5/pallas_call | solution.py:137
  470.3 0.0 copy-start.2
  470.3 124.3 %stage6.1 = (bf16[4,128,1152]{2,1,0:T(8,128)(2,1)}, bf16[4,128,1152]{2,1,0:T(8,128)(2,1)}, bf16[4,576,256]{2,1,0:T(8,128)(2,1)}, bf16[4,128,1152]{2,1,0:T(8,128)...) custom-call(bf16[1024,1152]{1,0:T(8,128)(2,1)} %get-tuple-element.14, ...), custom_call_target="tpu_custom_call" | custom-call | tf_op jit(solution)/shard_map/stage6/pallas_call | solution.py:137
  594.6 0.0 copy-done.2
  594.6 1.1 broadcast_select_fusion
  595.8 1.1 bitcast_convert_fusion
  596.9 0.1 copy-done.4
  597.0 0.5 copy-done.5
  597.5 0.1 broadcast_select_fusion.1
  597.5 1.1 bitcast_convert_fusion.1
  598.6 0.1 copy-done.1
  598.8 0.4 copy-done.3
  599.2 0.1 broadcast_select_fusion.2
  599.3 0.0 copy-start.12
  599.3 0.0 copy-start.13
  599.3 0.0 copy-start.9
  599.3 0.0 copy-start.10
  599.3 1.1 bitcast_convert_fusion.2
  600.4 0.0 copy-done.12
  600.4 0.7 bitcast_convert_fusion.4
  601.2 0.9 bitcast_convert_fusion.3
  602.1 0.0 copy-start.11
  602.1 1.1 maximum_select_fusion
  603.2 0.7 convert_reduce_fusion
  603.9 0.0 copy-done.11
  604.0 0.6 constant_dynamic-slice_fusion.1
  604.6 0.6 constant_dynamic-slice_fusion
  605.2 0.6 reshape_squeeze.3
  (28 shorter events, 0.2 us)
Async XLA Ops:
  176.2 1.3 copy-start.14
  470.3 124.3 %copy-start.2 = (bf16[2,576,256]{2,1,0:T(8,128)(2,1)S(1)}, bf16[2,576,256]{2,1,0:T(8,128)(2,1)}, u32[]{:S(2)}) copy-start(bf16[2,576,256]{2,1,0:T(8,128)(2,1)} %get-tuple-element.176) | copy-start | bytes 1769476
  595.8 1.2 copy-start.4
  595.8 1.7 copy-start.5
  597.5 1.2 copy-start.1
  597.5 1.7 copy-start.3
  599.3 1.1 copy-start.12
  599.3 1.1 copy-start.13
  599.3 1.9 copy-start.9
  599.3 1.9 copy-start.10
  600.4 1.7 copy-start
  600.4 1.7 copy-start.6
  600.4 1.7 copy-start.7
  602.1 1.1 copy-start.8
  602.1 1.8 copy-start.11

commit v6 on v5

--- a/solution.py
+++ b/solution.py
@@ -114,6 +114,7 @@
             val.ref = ref
         for item in self.once:
             item.waited = False
+            item.phase = 0
         for step in self.early:
             step()
         self.greet()
@@ -230,6 +231,9 @@
             for cond, src in sources if every else sources[:1]:
                 yield cond, False, self.local(src, dst, i)
 
+    def step(self):
+        pass
+
     def send(self):
         for cond, far, move in self.pairs(True):
             if far and self.final is not None:
@@ -261,32 +265,100 @@
     return value if known else k.input(value)
 
 
+class Line(Task):
+    def __init__(self, k, out, out_dtype=BF, n_local=1):
+        super().__init__(k, out, "dp", None, 6, n_local, out_dtype)
+        self.send_sem, self.recv_sem = k.sem(2, 3), k.sem(2, 3)
+        self.phase = 0
+
+    def hop(self, j, way, src, dst):
+        d = lax.axis_index("dp")
+        peer = {"dp": (d + 1 if way == 0 else d + 3) % 4}
+        return remote(src, dst, self.send_sem.ref.at[way, j], self.recv_sem.ref.at[way, j], peer)
+
+
+class LineGather(Line):
+    def __init__(self, k, sources, shape, dtype):
+        super().__init__(k, (4,) + shape, dtype)
+        self.sources = sources
+
+    def ends(self, j, way):
+        d = lax.axis_index("dp")
+        if way == 0:
+            return (d >= j) & (d < 3), d >= j + 1
+        return (d <= 3 - j) & (d > 0), d <= 2 - j
+
+    def copy(self, j, way, src=None):
+        d = lax.axis_index("dp")
+        slot = (d + 4 - j if way == 0 else d + j) % 4
+        piece = self.out.ref.at[slot]
+        return self.hop(j, way, piece if src is None else src, piece)
+
+    def send(self):
+        self.phase = 0
+        for cond, src in self.sources(*spot()):
+            own = self.local(src, self.out.ref.at[lax.axis_index("dp")], 0)
+            moves = [(True if cond is None else cond, own)]
+            for way in range(2):
+                sends = self.ends(0, way)[0]
+                moves.append((sends if cond is None else sends & cond, self.copy(0, way, src)))
+            for when, move in moves:
+                if when is True:
+                    move.start()
+                else:
+                    pl.when(when)(move.start)
+
+    def arrive(self, j):
+        for way in range(2):
+            pl.when(self.ends(j, way)[1])(self.copy(j, way).wait_recv)
+
+    def step(self):
+        self.arrive(self.phase)
+        self.phase += 1
+        for way in range(2):
+            pl.when(self.ends(self.phase, way)[0])(self.copy(self.phase, way).start)
+
+    def wait(self):
+        if self.waited:
+            return
+        self.waited = True
+        while self.phase < 2:
+            self.step()
+        self.arrive(2)
+        for j in range(3):
+            for way in range(2):
+                pl.when(self.ends(j, way)[0])(self.copy(j, way).wait_send)
+        d = lax.axis_index("dp")
+        self.local(self.sources(*spot())[0][1], self.out.ref.at[d], 0).wait()
+
+
+def z_gather_from(k, sources, shape, dtype):
+    count = dp_size()
+    if count == 4:
+        return LineGather(k, sources, shape, dtype)
+
+    def moves(s, d, t):
+        dst, found = task.out.ref.at[d], sources(s, d, t)
+        return [(found, dst, {"dp": (d + i) % count}) for i in range(1, count)], [(found, dst)]
+
+    task = Task(k, (count,) + shape, "dp", moves, count - 1, out_dtype=dtype)
+    return task
+
+
 def z_gather(k, value):
-    val, count = as_val(k, value), dp_size()
-
-    def moves(s, d, t):
-        source = [(None, val.ref)]
-        dst = task.out.ref.at[d]
-        return [(source, dst, {"dp": (d + i) % count}) for i in range(1, count)], [(source, dst)]
-
-    task = Task(k, (count,) + val.shape, "dp", moves, count - 1, out_dtype=val.dtype)
-    return task
+    val = as_val(k, value)
+    return z_gather_from(k, lambda s, d, t: [(None, val.ref)], val.shape, val.dtype)
 
 
 def z_gather_half(k, shard, moved, block):
-    shard, moved, count = as_val(k, shard), as_val(k, moved), dp_size()
+    shard, moved = as_val(k, shard), as_val(k, moved)
     rows = shard.shape[0] // 2
 
-    def moves(s, d, t):
-        sources = [
-            (s == block, shard.ref.at[pl.ds(block * rows, rows)]),
-            (s == 1 - block, moved.ref),
-        ]
-        dst = task.out.ref.at[d]
-        return [(sources, dst, {"dp": (d + i) % count}) for i in range(1, count)], [(sources, dst)]
-
-    task = Task(k, (count,) + moved.shape, "dp", moves, count - 1)
-    return task
+    def sources(s, d, t):
+        own = shard.ref.at[pl.ds(block * rows, rows)]
+        return [(s == block, own), (s == 1 - block, moved.ref)]
+
+    return z_gather_from(k, sources, moved.shape, shard.dtype)
 
 
 def x_move(k, value):
@@ -327,29 +399,19 @@
     return task
 
 
-class SumScatter(Task):
-    def __init__(self, k, kind, grads, received):
-        count = dp_size()
-        self.grads, self.got_val = as_val(k, grads), as_val(k, received)
+class Terms:
+    def __init__(self, k, kind, grads, received, local):
+        self.grads, self.received, self.local = as_val(k, grads), as_val(k, received), local
+        self.kind, self.n = kind, dp_size()
         if kind == "cols":
-            rows, cols = self.grads.shape[0] // 2, self.grads.shape[1] // count
-            held = (rows, self.grads.shape[1])
+            self.rows, self.cols = self.grads.shape[0] // 2, self.grads.shape[1] // self.n
+            held = (self.rows, self.grads.shape[1])
         else:
-            rows, cols = self.grads.shape[0] // (2 * count), self.grads.shape[1]
-            held = (count, rows, cols)
-        self.kind, self.rows, self.cols, self.n = kind, rows, cols, count
+            self.rows, self.cols = self.grads.shape[0] // (2 * self.n), self.grads.shape[1]
+            held = (self.n, self.rows, self.cols)
         self.kept, self.got = k.vmem(held, BF), k.vmem(held, BF)
-        self.total = k.vmem((count, rows, cols), BF)
-
-        def moves(s, d, t):
-            total = self.total.ref
-            far = []
-            for i in range(1, count):
-                other = (d + i) % count
-                far.append(([(None, total.at[other])], self.out.ref.at[d], {"dp": other}))
-            return far, [([(None, total.at[d])], self.out.ref.at[d])]
-
-        super().__init__(k, (count, rows, cols), "dp", moves, count - 1, 2 + count)
+        self.shape = (self.n, self.rows, self.cols)
+        self.total = k.vmem(self.shape, BF) if kind == "cols" else self.kept
 
     def loads(self):
         s, grads, kept = lax.axis_index("section"), self.grads.ref, self.kept.ref
@@ -360,13 +422,13 @@
             for i in range(self.n):
                 slot = 2 * i + s if self.kind == "rows" else s * self.n + i
                 moves.append(self.local(grads.at[block_of(slot, self.rows)], kept.at[i], 2 + i))
-        return moves + [self.local(self.got_val.ref, self.got.ref, 1)]
+        return moves + [self.local(self.received.ref, self.got.ref, 1)]
 
     def load(self):
         for move in self.loads():
             move.start()
 
-    def send(self):
+    def add(self):
         for move in self.loads():
             move.wait()
         kept, got, total = self.kept.ref, self.got.ref, self.total.ref
@@ -376,6 +438,26 @@
             else:
                 part = i
             total[i] = (kept[part].astype(F32) + got[part].astype(F32)).astype(BF)
+
+
+class DirectScatter(Task):
+    def __init__(self, k, kind, grads, received):
+        self.terms = Terms(k, kind, grads, received, lambda *a: self.local(*a))
+        count = dp_size()
+
+        def moves(s, d, t):
+            total = self.terms.total.ref
+            far = []
+            for i in range(1, count):
+                other = (d + i) % count
+                far.append(([(None, total.at[other])], self.out.ref.at[d], {"dp": other}))
+            return far, [([(None, total.at[d])], self.out.ref.at[d])]
+
+        super().__init__(k, self.terms.shape, "dp", moves, count - 1, 2 + count)
+        self.load = self.terms.load
+
+    def send(self):
+        self.terms.add()
         super().send()
 
     def add(self):
@@ -383,11 +465,79 @@
         self.send()
 
 
+class LineScatter(Line):
+    def __init__(self, k, kind, grads, received):
+        self.terms = Terms(k, kind, grads, received, lambda *a: self.local(*a))
+        super().__init__(k, self.terms.shape[1:], BF, 6)
+        self.got = k.vmem((2, 3) + self.terms.shape[1:], BF)
+        self.load = self.terms.load
+
+    def ends(self, j, way):
+        d = lax.axis_index("dp")
+        if way == 0:
+            return (d <= j) & (d < 3), (d >= 1) & (d <= j + 1)
+        return (d >= 3 - j) & (d > 0), (d <= 2) & (d >= 2 - j)
+
+    def copy(self, j, way):
+        d = lax.axis_index("dp")
+        to = (d + 3 - j if way == 0 else d + 1 + j) % 4
+        return self.hop(j, way, self.terms.total.ref.at[to], self.got.ref.at[way, j])
+
+    def send(self):
+        self.phase = 0
+        self.terms.add()
+        for way in range(2):
+            pl.when(self.ends(0, way)[0])(self.copy(0, way).start)
+
+    def take(self, j, way):
+        d = lax.axis_index("dp")
+        to = (d + 2 - j if way == 0 else d + 2 + j) % 4
+        self.copy(j, way).wait_recv()
+        total = self.terms.total.ref
+        total[to] = (total[to].astype(F32) + self.got.ref[way, j].astype(F32)).astype(BF)
+
+    def arrive(self, j):
+        for way in range(2):
+            pl.when(self.ends(j, way)[1])(functools.partial(self.take, j, way))
+
+    def step(self):
+        self.arrive(self.phase)
+        self.phase += 1
+        for way in range(2):
+            pl.when(self.ends(self.phase, way)[0])(self.copy(self.phase, way).start)
+
+    def wait(self):
+        if self.waited:
+            return
+        self.waited = True
+        while self.phase < 2:
+            self.step()
+        self.arrive(2)
+        done = self.local(self.terms.total.ref.at[lax.axis_index("dp")], self.out.ref, 0)
+        done.start()
+        for j in range(3):
+            for way in range(2):
+                pl.when(self.ends(j, way)[0])(self.copy(j, way).wait_send)
+        done.wait()
+
+    def add(self):
+        self.load()
+        self.send()
+
+
+def sum_scatter(k, kind, grads, received):
+    return (LineScatter if dp_size() == 4 else DirectScatter)(k, kind, grads, received)
+
+
 class Finish(Task):
     def __init__(self, k, pieces, block):
         self.pieces, self.final = as_val(k, pieces), block
-        self.n, rows, cols = self.pieces.shape
-        self.held, self.total = k.vmem(self.pieces.shape, BF), k.vmem((rows, cols), BF)
+        *slots, rows, cols = self.pieces.shape
+        self.slots = slots[0] if slots else 0
+        if slots:
+            self.held, self.total = k.vmem(self.pieces.shape, BF), k.vmem((rows, cols), BF)
+        else:
+            self.total = self.pieces
 
         def moves(s, d, t):
             source, dst = [(None, self.total.ref)], self.out.ref.at[s]
@@ -396,15 +546,16 @@
         super().__init__(k, (2, rows, cols), "section", moves, 1, 2)
 
     def load(self):
-        self.local(self.pieces.ref, self.held.ref, 1).start()
+        if self.slots:
+            self.local(self.pieces.ref, self.held.ref, 1).start()
 
     def send(self):
-        self.local(self.pieces.ref, self.held.ref, 1).wait()
-        held = self.held.ref
-        acc = held[0].astype(F32)
-        for i in range(1, self.n):
-            acc = acc + held[i].astype(F32)
-        self.total.ref[...] = acc.astype(BF)
+        if self.slots:
+            self.local(self.pieces.ref, self.held.ref, 1).wait()
+            acc = self.held.ref[0].astype(F32)
+            for i in range(1, self.slots):
+                acc = acc + self.held.ref[i].astype(F32)
+            self.total.ref[...] = acc.astype(BF)
         super().send()
 
     def add(self):
@@ -933,7 +1084,7 @@
         self.d_proj = k.vmem(projected.shape, BF)
         self.q_gain, self.k_gain = k.vmem((1, self.q_cols), F32), k.vmem((1, self.k_cols), F32)
 
-    def run(self):
+    def run(self, *between):
         for load in self.loads:
             load.wait()
         size, q_cols, k_cols, proj = self.size, self.q_cols, self.k_cols, self.projected.ref
@@ -965,7 +1116,10 @@
                 dk_h[g, seen, :] += contract(d_scores, q, 0, 0) * scale
             return carry
 
-        lax.fori_loop(0, self.heads, head, 0)
+        lax.fori_loop(0, self.heads // 2, head, 0)
+        for step in between:
+            step()
+        lax.fori_loop(self.heads // 2, self.heads, head, 0)
         self.q_gain.ref[...] = jnp.zeros_like(self.q_gain.ref)
         self.k_gain.ref[...] = jnp.zeros_like(self.k_gain.ref)
 
@@ -1040,13 +1194,13 @@
     mid0 = Save(k, s1.out)
     k.do(t_in.send, t_out.send, z_cols.send, t_gate.send, t_gain.send, t_seq.send)
     k.do(t_in.wait, z_in0.send, t_out.wait, z_out0.send, t_up.send)
+    k.do(z_cols.step, z_in0.step, z_out0.step, t_gate.wait, z_gate0.send)
+    k.do(z_cols.step, z_in0.step, z_out0.step)
     k.do(t_gain.wait, gain_load.start, t_seq.wait, x_load.start)
     k.do(gain_load.wait, x_load.wait, g0.begin)
-    k.do(t_gate.wait, z_gate0.send)
     k.do(z_cols.wait, x_cols.send, z_in0.wait, x_in0.send, z_out0.wait, x_out0.send, t_down.send)
-    k.do(t_up.wait, z_up0.send)
-    k.do(x_cols.wait, w_cols.start, x_in0.wait, w_in0.start)
-    k.do(z_gate0.wait, x_gate0.send)
+    k.do(z_gate0.step, t_up.wait, z_up0.send, z_gate0.step, z_up0.step, z_gate0.wait, x_gate0.send)
+    k.do(x_cols.wait, w_cols.start, x_in0.wait, w_in0.start, z_up0.step)
     k.do(g0.loop, taps.wait, conv.run, y0.start)
     k.do(x_out0.wait, w_out0.start, s1.loop, s1.finish, mid0.start)
     k.do(*wait(t_down, x_gate0, z_up0))
@@ -1068,10 +1222,11 @@
     )
     s3 = Scatter(k, [g2.values[2]], [w_down0], rows.buf, low=True)
     z_rows = Save(k, s3.out)
-    k.do(x_up0.send, z_down0.send, z_in1.send, z_out1.send, z_gate1.send)
+    k.do(x_up0.send, z_down0.send, z_in1.send, z_out1.send)
     k.do(rows.wait, gain_load.wait, g2.begin)
-    k.do(z_down0.wait, x_down0.send, x_up0.wait, w_up0.start, g2.loop)
-    k.do(z_in1.wait, x_in1.send, z_out1.wait, x_out1.send)
+    k.do(z_down0.step, z_in1.step, z_out1.step, z_down0.step, z_gate1.send, z_in1.step, z_out1.step)
+    k.do(z_down0.wait, x_down0.send, x_up0.wait, w_up0.start, z_gate1.step, g2.loop)
+    k.do(z_gate1.step, z_in1.wait, x_in1.send, z_out1.wait, x_out1.send)
     k.do(x_down0.wait, w_down0.start, s3.loop, s3.finish, z_rows.start)
     k.do(*wait(x_in1, x_out1, z_gate1))
     k.build()
@@ -1091,8 +1246,8 @@
     s5 = Scatter(k, [attend.y], [w_out1], rows.buf)
     mid1 = Save(k, s5.out)
     k.do(x_gate1.send, z_up1.send, z_down1.send)
-    k.do(rows.wait, gain_load.wait, g4.begin, g4.loop)
-    k.do(lambda: attend.run(z_up1.wait, x_up1.send))
+    k.do(rows.wait, gain_load.wait, g4.begin, z_up1.step, g4.loop, z_up1.step, z_down1.step)
+    k.do(lambda: attend.run(z_up1.wait, x_up1.send, z_down1.step))
     k.do(*(v.start for v in kept))
     k.do(s5.loop, s5.finish, mid1.start)
     k.do(*wait(x_gate1, x_up1, z_down1))
@@ -1127,9 +1282,9 @@
     y_rows, d_mid1, gain11 = y_rows.out, d_mid1.out, gain11.out
 
     k = Kernel(4)
-    q_down1 = SumScatter(k, "cols", p_down1.out, r_down1.out)
+    q_down1 = sum_scatter(k, "cols", p_down1.out, r_down1.out)
     r_gate1, r_up1 = x_slots(k, p_gate1.out, "rows"), x_slots(k, p_up1.out, "rows")
-    q_gate1 = SumScatter(k, "rows", p_gate1.out, r_gate1.out)
+    q_gate1 = sum_scatter(k, "rows", p_gate1.out, r_gate1.out)
     rows, gain_load = load_all(k, d_mid1), gains_of(k, 1, t_gain.out)
     value = load_all(k, z_rows)
     tables = [load_all(k, v) for v in table_arrays]
@@ -1148,9 +1303,10 @@
     head_gains = [Save(k, back.q_gain), Save(k, back.k_gain)]
     k.early.append(q_down1.load)
     k.do(r_gate1.send, r_up1.send, rows.wait, g10.begin, q_down1.send, g10.loop)
-    k.do(y_load.wait, p_out1.run, p_out1.wait, r_out1.send)
+    k.do(q_down1.step, y_load.wait, p_out1.run, p_out1.wait, r_out1.send, q_down1.step)
     k.do(r_gate1.wait, q_gate1.add)
-    k.do(proj.wait, q_load.wait, k_load.wait, back.run, *(v.start for v in head_gains))
+    k.do(proj.wait, q_load.wait, k_load.wait, lambda: back.run(q_gate1.step))
+    k.do(q_gate1.step, *(v.start for v in head_gains))
     k.do(gain_load.wait, value.wait, s11.loop, a_load.wait, p_in1.run)
     k.do(s11.finish, d_z.start, gain10.start, p_in1.wait)
     k.do(*wait(q_down1, q_gate1, r_up1, r_out1))
@@ -1159,10 +1315,10 @@
     q_gain, k_gain = (v.out.array for v in head_gains)
 
     k = Kernel(5)
-    q_up1 = SumScatter(k, "rows", p_up1.out, r_up1.out)
-    q_out1 = SumScatter(k, "cols", p_out1.out, r_out1.out)
+    q_up1 = sum_scatter(k, "rows", p_up1.out, r_up1.out)
+    q_out1 = sum_scatter(k, "cols", p_out1.out, r_out1.out)
     r_in1 = x_slots(k, p_in1.out, "rows")
-    q_in1 = SumScatter(k, "rows", p_in1.out, r_in1.out)
+    q_in1 = sum_scatter(k, "rows", p_in1.out, r_in1.out)
     e_down1, e_gate1 = Finish(k, q_down1.out, 1), Finish(k, q_gate1.out, 1)
     rows, value, gain_load = load_all(k, d_z), load_all(k, mid0), gains_of(k, 0, t_gain.out)
     gate_load, up_load, hid_load, m_load = (load_all(k, v) for v in (gate0, up0, hid0, m0))
@@ -1182,9 +1338,9 @@
     k.early += [q_up1.load, q_out1.load, e_down1.load, e_gate1.load]
     k.do(r_in1.send, rows.wait, g12.begin, q_up1.send, q_out1.send, e_down1.send, e_gate1.send)
     k.do(gate_load.wait, up_load.wait, g12.loop)
-    k.do(hid_load.wait, p_down0.run, p_down0.wait, r_down0.send)
-    k.do(r_in1.wait, q_in1.add)
-    k.do(s13.loop, m_load.wait, p_gate0.run, p_up0.run)
+    k.do(q_up1.step, q_out1.step, hid_load.wait, p_down0.run, p_down0.wait, r_down0.send)
+    k.do(q_up1.step, q_out1.step, r_in1.wait, q_in1.add)
+    k.do(s13.loop, q_in1.step, m_load.wait, p_gate0.run, q_in1.step, p_up0.run)
     k.do(value.wait, gain_load.wait, s13.finish, d_mid0.start, gain01.start)
     k.do(p_gate0.wait, p_up0.wait)
     k.do(*wait(q_up1, q_out1, q_in1, e_down1, e_gate1, r_down0))
@@ -1193,9 +1349,9 @@
 
     k = Kernel(6)
     r_gate0, r_up0 = x_slots(k, p_gate0.out, "rows"), x_slots(k, p_up0.out, "rows")
-    q_down0 = SumScatter(k, "cols", p_down0.out, r_down0.out)
-    q_gate0 = SumScatter(k, "rows", p_gate0.out, r_gate0.out)
-    q_up0 = SumScatter(k, "rows", p_up0.out, r_up0.out)
+    q_down0 = sum_scatter(k, "cols", p_down0.out, r_down0.out)
+    q_gate0 = sum_scatter(k, "rows", p_gate0.out, r_gate0.out)
+    q_up0 = sum_scatter(k, "rows", p_up0.out, r_up0.out)
     e_up1, e_out1, e_in1 = (Finish(k, v.out, 1) for v in (q_up1, q_out1, q_in1))
     rows, gain_load = load_all(k, d_mid0), gains_of(k, 0, t_gain.out)
     x_load, taps = start_rows(k, 0, t_seq.out), load_all(k, conv_kernel)
@@ -1209,8 +1365,8 @@
     p_in0, p_cols = Product(k, a_load.buf, back.d_proj), Product(k, a_load.buf, back.d_value)
     r_out0, r_in0 = x_half(k, p_out0.out), x_slots(k, p_in0.out, "rows")
     r_cols = x_slots(k, p_cols.out, "conv")
-    q_out0, q_in0 = SumScatter(k, "cols", p_out0.out, r_out0.out), SumScatter(k, "rows", p_in0.out, r_in0.out)
-    q_cols = SumScatter(k, "conv", p_cols.out, r_cols.out)
+    q_out0, q_in0 = sum_scatter(k, "cols", p_out0.out, r_out0.out), sum_scatter(k, "rows", p_in0.out, r_in0.out)
+    q_cols = sum_scatter(k, "conv", p_cols.out, r_cols.out)
     e_down0, e_gate0, e_up0, e_out0, e_in0 = (
         Finish(k, v.out, 0) for v in (q_down0, q_gate0, q_up0, q_out0, q_in0)
     )
@@ -1254,18 +1410,18 @@
     k.early += [q_down0.load, e_up1.load, e_out1.load, e_in1.load]
     k.do(r_gate0.send, r_up0.send, rows.wait, g14.begin, q_down0.send)
     k.do(e_up1.send, e_out1.send, e_in1.send, g14.loop)
-    k.do(y_load.wait, p_out0.run, p_out0.wait, r_out0.send)
+    k.do(q_down0.step, y_load.wait, p_out0.run, p_out0.wait, r_out0.send, q_down0.step)
     k.do(proj.wait, value.wait, taps.wait, back.run, a_load.wait)
     k.do(p_in0.run, p_cols.run, p_in0.wait, r_in0.send, p_cols.wait, r_cols.send)
     k.do(r_gate0.wait, q_gate0.add)
-    k.do(x_load.wait, gain_load.wait, s15.loop, s15.finish, d_x.start)
+    k.do(x_load.wait, gain_load.wait, s15.loop, q_gate0.step, s15.finish, d_x.start, q_gate0.step)
     k.do(fill_small, d_x.wait, t_result.send)
     k.do(small_out.wait, t_small.send)
-    k.do(r_up0.wait, q_up0.add)
-    k.do(r_out0.wait, q_out0.add, r_in0.wait, q_in0.add, r_cols.wait, q_cols.add)
-    k.do(q_down0.wait, e_down0.add, t_small.wait, z_small.add, q_gate0.wait, e_gate0.add)
-    k.do(z_small.wait, t_total.add)
-    k.do(q_up0.wait, e_up0.add, q_out0.wait, e_out0.add, q_in0.wait, e_in0.add)
+    k.do(q_down0.wait, e_down0.add, q_gate0.wait, e_gate0.add)
+    k.do(r_up0.wait, q_up0.add, r_out0.wait, q_out0.add, r_in0.wait, q_in0.add)
+    k.do(q_up0.step, r_cols.wait, q_cols.add, q_out0.step, q_in0.step, t_small.wait, z_small.add)
+    k.do(q_up0.step, q_cols.step, q_out0.step, q_in0.step, z_small.wait, t_total.add)
+    k.do(q_up0.wait, e_up0.add, q_cols.step, q_out0.wait, e_out0.add, q_in0.wait, e_in0.add)
     rest = (e_up1, e_out1, e_in1, q_cols, e_down0, e_gate0, e_up0, e_out0, e_in0)
     k.do(*wait(*rest, t_total, t_result))
     k.build()
@@ -1282,6 +1438,9 @@
     kernel_out = lax.dynamic_slice_in_dim(
         small[4 : 4 + tap_rows], tensor_index * channels, channels, 1
     )
+    cols_grad = q_cols.out.array.astype(F32)
+    if cols_grad.ndim == 3:
+        cols_grad = jnp.sum(cols_grad, axis=0)
     head_total = small[7, : qk_gain.size].reshape(qk_gain.shape)
     return (
         result[None],
@@ -1291,7 +1450,7 @@
         whole(e_gate0, e_gate1),
         whole(e_up0, e_up1),
         whole(e_down0, e_down1),
-        jnp.sum(q_cols.out.array.astype(F32), axis=0),
+        cols_grad,
         kernel_out,
         head_total,
     )

time: 616 us -> 589 us (0.956)
  Pallas kernels: 586 us -> 559 us
    pallas_call x7, Pallas kernels: 586 us -> 559 us  [build(): pl.pallas_call(self.body, out_shape=[jax.ShapeDtypeStruct(v.shape, v.dtyp...]
where the time goes in v6:
time: 589 us; the launch traced here: 580 us
  Pallas kernels  559 us (95%)
  other arithmetic  11.3 us (2%)
  local copies, waits for them, and re-layouts  7.92 us (1%)
    pallas_call x7, Pallas kernels, build(): pl.pallas_call(self.body, out_shape=[jax.ShapeDtypeStruct(v.shape, v.dtyp...  559 us

profile of v6, /device:TPU:0, one launch (start us, length us, event | category | flops | bytes accessed | tf_op | source)
XLA Modules:
  0.0 579.9 jit_solution(5041023572169672562)
XLA Ops:
  0.6 91.9 %stage0.1 = (bf16[128,512]{1,0:T(8,128)(2,1)}, bf16[128,256]{1,0:T(8,128)(2,1)}, bf16[128,1152]{1,0:T(8,128)(2,1)}, bf16[128,1152]{1,0:T(8,128)(2,1)}, bf16[576,...) custom-call(bf16[2,256,1024]{2,1,0:T(8,128)(2,1)} %bitcast.34, ...), custom_call_target="tpu_custom_call" | custom-call | tf_op jit(solution)/shard_map/stage0/pallas_call | solution.py:138
  92.5 79.4 %stage1.1 = (bf16[4,128,1152]{2,1,0:T(8,128)(2,1)}, bf16[4,576,256]{2,1,0:T(8,128)(2,1)}, bf16[4,128,512]{2,1,0:T(8,128)(2,1)}, bf16[4,128,256]{2,1,0:T(8,128)(2...) custom-call(bf16[4,128,1152]{2,1,0:T(8,128)(2,1)} %get-tuple-element, ...), custom_call_target="tpu_custom_call" | custom-call | tf_op jit(solution)/shard_map/stage1/pallas_call | solution.py:138
  171.9 0.5 fusion
  172.5 0.1 tile.14
  172.6 1.3 copy.20.refs_9_
  173.9 0.1 tile.31
  174.1 0.0 copy-start.14
  174.1 1.3 copy.21.refs_10_
  175.4 0.0 copy-done.14
  175.4 0.7 tile.13.refs_8_
  176.0 59.4 %stage2.1 = (bf16[4,128,1152]{2,1,0:T(8,128)(2,1)}, bf16[4,128,1152]{2,1,0:T(8,128)(2,1)}, bf16[4,576,256]{2,1,0:T(8,128)(2,1)}, bf16[4,128,1152]{2,1,0:T(8,128)...) custom-call(bf16[4,128,1152]{2,1,0:T(8,128)(2,1)} %get-tuple-element, ...), custom_call_target="tpu_custom_call" | custom-call | tf_op jit(solution)/shard_map/stage2/pallas_call | solution.py:138
  235.5 75.9 %stage3.1 = (bf16[4,576,256]{2,1,0:T(8,128)(2,1)}, bf16[1152,1024]{1,0:T(8,128)(2,1)}, bf16[1024,1152]{1,0:T(8,128)(2,1)}, bf16[1024,1152]{1,0:T(8,128)(2,1)}, b...) custom-call(bf16[4,576,256]{2,1,0:T(8,128)(2,1)} %get-tuple-element.110.refs_0_, ...), custom_call_target="tpu_custom_call" | custom-call | tf_op jit(solution)/shard_map/stage3/pallas_call | solution.py:138
  311.4 71.4 %stage4.1 = (bf16[576,256]{1,0:T(8,128)(2,1)}, bf16[4,128,1152]{2,1,0:T(8,128)(2,1)}, bf16[4,128,1152]{2,1,0:T(8,128)(2,1)}, bf16[128,1152]{1,0:T(8,128)(2,1)}, ...) custom-call(bf16[1152,1024]{1,0:T(8,128)(2,1)} %get-tuple-element.11, ...), custom_call_target="tpu_custom_call" | custom-call | tf_op jit(solution)/shard_map/stage4/pallas_call | solution.py:138
  382.8 0.5 broadcast.38
  383.3 1.3 reduce.11
  384.7 0.1 reshape.184
  384.8 1.3 reduce.10
  386.1 0.1 reshape.185
  386.2 0.1 reshape.186
  386.3 0.6 pad.4.refs_26_
  386.9 52.9 %stage5.1 = (bf16[128,1152]{1,0:T(8,128)(2,1)}, bf16[128,256]{1,0:T(8,128)(2,1)}, bf16[4,128,512]{2,1,0:T(8,128)(2,1)}, bf16[128,512]{1,0:T(8,128)(2,1)}, bf16[2...) custom-call(bf16[1024,1152]{1,0:T(8,128)(2,1)} %get-tuple-element.11, ...), custom_call_target="tpu_custom_call" | custom-call | tf_op jit(solution)/shard_map/stage5/pallas_call | solution.py:138
  439.9 0.0 copy-start.2
  439.9 128.4 %stage6.1 = (bf16[4,128,1152]{2,1,0:T(8,128)(2,1)}, bf16[4,128,1152]{2,1,0:T(8,128)(2,1)}, bf16[576,256]{1,0:T(8,128)(2,1)}, bf16[128,1152]{1,0:T(8,128)(2,1)}, ...) custom-call(bf16[1024,1152]{1,0:T(8,128)(2,1)} %get-tuple-element.14, ...), custom_call_target="tpu_custom_call" | custom-call | tf_op jit(solution)/shard_map/stage6/pallas_call | solution.py:138
  568.2 0.0 copy-done.2
  568.3 1.1 broadcast_select_fusion
  569.4 0.0 copy-start.4
  569.4 1.1 bitcast_convert_fusion
  570.5 0.1 copy-done.4
  570.6 0.5 copy-done.5
  571.1 0.1 broadcast_select_fusion.1
  571.1 0.0 copy-start.1
  571.1 0.0 copy-start.3
  571.2 1.1 bitcast_convert_fusion.1
  572.2 0.1 copy-done.1
  572.4 0.4 copy-done.3
  572.8 0.1 broadcast_select_fusion.2
  572.9 1.1 bitcast_convert_fusion.2
  574.1 0.7 bitcast_convert_fusion.4
  574.8 0.0 copy-done.8
  574.8 0.9 bitcast_convert_fusion.3
  575.7 0.0 copy-done.6
  575.7 1.1 maximum_select_fusion
  576.8 0.0 copy-done.13
  576.8 0.7 convert_element_type.85
  577.5 0.0 copy-done.10
  577.6 0.6 constant_dynamic-slice_fusion.1
  578.2 0.6 constant_dynamic-slice_fusion
  578.8 0.6 reshape_squeeze.3
  (28 shorter events, 0.2 us)
Async XLA Ops:
  174.1 1.3 copy-start.14
  439.9 128.4 %copy-start.2 = (bf16[2,576,256]{2,1,0:T(8,128)(2,1)S(1)}, bf16[2,576,256]{2,1,0:T(8,128)(2,1)}, u32[]{:S(2)}) copy-start(bf16[2,576,256]{2,1,0:T(8,128)(2,1)} %get-tuple-element.176) | copy-start | bytes 1769476
  569.4 1.2 copy-start.4
  569.4 1.7 copy-start.5
  571.1 1.2 copy-start.1
  571.1 1.7 copy-start.3
  572.9 1.1 copy-start.11
  572.9 1.1 copy-start.12
  572.9 1.9 copy-start.8
  572.9 1.9 copy-start.9
  574.0 1.7 copy-start
  574.0 1.7 copy-start.6
  574.0 1.7 copy-start.7
  575.7 1.1 copy-start.13
  575.7 1.8 copy-start.10

commit v7 on v6

--- a/solution.py
+++ b/solution.py
@@ -42,13 +42,12 @@
     return (value_grad, gain_grad)
 
 
-def rotation(length, head_size):
+def rotation(length, head_size, width):
     half_size = head_size // 2
-    frequency = ROPE_BASE ** (-(jnp.arange(half_size, dtype=jnp.float32) * 2.0 / head_size))
-    angles = jnp.arange(length, dtype=jnp.float32)[:, None] * frequency[None, :]
-    cosine_table = jnp.concatenate([jnp.cos(angles), jnp.cos(angles)], axis=1)
-    sine_table = jnp.concatenate([jnp.sin(angles), jnp.sin(angles)], axis=1)
-    return (cosine_table, sine_table)
+    column = (jnp.arange(width) % half_size).astype(F32)
+    frequency = ROPE_BASE ** (-(column * 2.0 / head_size))
+    angles = jnp.arange(length, dtype=F32)[:, None] * frequency[None, :]
+    return jnp.cos(angles), jnp.sin(angles)
 
 
 def silu_parts(gate):
@@ -361,17 +360,31 @@
     return z_gather_from(k, sources, moved.shape, shard.dtype)
 
 
-def x_move(k, value):
+def one_way(task, sender):
+    task.final = None if sender is None else 1 - sender
+    return task
+
+
+def z_gather_whole(k, shard, moved, block):
+    shard, moved = as_val(k, shard), as_val(k, moved)
+
+    def sources(s, d, t):
+        return [(s == block, shard.ref), (s == 1 - block, moved.ref)]
+
+    return z_gather_from(k, sources, shard.shape, shard.dtype)
+
+
+def x_move(k, value, sender=None):
     val = as_val(k, value)
 
     def moves(s, d, t):
         return [([(None, val.ref)], task.out.ref, {"section": 1 - s})], []
 
     task = Task(k, val.shape, "section", moves, 1, out_dtype=val.dtype)
-    return task
-
-
-def x_half(k, value):
+    return one_way(task, sender)
+
+
+def x_half(k, value, sender=None):
     val = as_val(k, value)
     rows = val.shape[0] // 2
 
@@ -380,7 +393,7 @@
         return [([(None, src)], task.out.ref, {"section": 1 - s})], []
 
     task = Task(k, (rows,) + val.shape[1:], "section", moves, 1, out_dtype=val.dtype)
-    return task
+    return one_way(task, sender)
 
 
 def x_slots(k, value, kind):
@@ -401,8 +414,15 @@
 
 class Terms:
     def __init__(self, k, kind, grads, received, local):
-        self.grads, self.received, self.local = as_val(k, grads), as_val(k, received), local
+        self.grads, self.local = as_val(k, grads), local
         self.kind, self.n = kind, dp_size()
+        self.whole = received is None
+        if self.whole:
+            self.rows, self.cols = self.grads.shape[0] // self.n, self.grads.shape[1]
+            self.shape = (self.n, self.rows, self.cols)
+            self.kept = self.total = k.vmem(self.shape, BF)
+            return
+        self.received = as_val(k, received)
         if kind == "cols":
             self.rows, self.cols = self.grads.shape[0] // 2, self.grads.shape[1] // self.n
             held = (self.rows, self.grads.shape[1])
@@ -415,6 +435,10 @@
 
     def loads(self):
         s, grads, kept = lax.axis_index("section"), self.grads.ref, self.kept.ref
+        if self.whole:
+            return [
+                self.local(grads.at[block_of(i, self.rows)], kept.at[i], 2 + i) for i in range(self.n)
+            ]
         if self.kind == "cols":
             moves = [self.local(grads.at[block_of(s, self.rows)], kept, 2)]
         else:
@@ -431,6 +455,8 @@
     def add(self):
         for move in self.loads():
             move.wait()
+        if self.whole:
+            return
         kept, got, total = self.kept.ref, self.got.ref, self.total.ref
         for i in range(self.n):
             if self.kind == "cols":
@@ -525,7 +551,7 @@
         self.send()
 
 
-def sum_scatter(k, kind, grads, received):
+def sum_scatter(k, kind, grads, received=None):
     return (LineScatter if dp_size() == 4 else DirectScatter)(k, kind, grads, received)
 
 
@@ -598,14 +624,15 @@
 
 
 class Weight:
-    def __init__(self, k, kind, near, far, early=False):
-        near, far = as_val(k, near), as_val(k, far)
+    def __init__(self, k, kind, near, far=None, early=False):
+        near, far = as_val(k, near), None if far is None else as_val(k, far)
         self.count, self.rows, self.cols = near.shape
         self.kind, self.near, self.far, self.waited = kind, near, far, False
+        sides = 1 if far is None else 2
         if kind == "cols":
-            shape = (2 * self.rows, self.count * self.cols)
+            shape = (sides * self.rows, self.count * self.cols)
         else:
-            shape = (2 * self.count * self.rows, self.cols)
+            shape = (sides * self.count * self.rows, self.cols)
         self.aside = kind == "cols" and self.cols % 128 != 0
         self.buf, self.sem = k.vmem(shape, BF), k.sem(2 * self.count)
         if self.aside:
@@ -626,6 +653,15 @@
             slot = own * 2 + sec if self.kind == "rows" else sec * self.count + own
             return dst.at[block_of(slot, rows)]
 
+        if self.far is None:
+            for i in range(self.count):
+                if self.kind == "cols":
+                    to = dst.at[:, pl.ds(i * cols, cols)]
+                else:
+                    to = dst.at[pl.ds(i * rows, rows)]
+                to = self.held[0].ref.at[i] if self.aside else to
+                yield pltpu.make_async_copy(self.near.ref.at[i], to, self.sem.ref.at[2 * i])
+            return
         for i in range(self.count):
             for j, (val, sec) in enumerate(((self.near, s), (self.far, 1 - s))):
                 to = self.held[j].ref.at[i] if self.aside else place(sec, i)
@@ -643,7 +679,7 @@
             move.wait()
         if self.aside:
             s = lax.axis_index("section")
-            for j, sec in enumerate((s, 1 - s)):
+            for j, sec in enumerate((s, 1 - s) if self.far is not None else (0,)):
                 whole = jnp.concatenate([self.held[j].ref[i] for i in range(self.count)], axis=1)
                 self.buf.ref[block_of(sec, self.rows), :] = whole
 
@@ -1023,6 +1059,11 @@
     def join(self, val, rows):
         return jnp.concatenate([val.ref[h, rows, :] for h in range(val.shape[0])], axis=1)
 
+    def angles(self, rows):
+        c, n = self.cos.ref[rows, :], self.sin.ref[rows, :]
+        repeat = self.q_cols // c.shape[1]
+        return jnp.concatenate([c] * repeat, axis=1), jnp.concatenate([n] * repeat, axis=1)
+
     def blocks(self, step):
         lax.fori_loop(0, self.length // ROW_BLOCK, lambda p, c: step(block_of(p, ROW_BLOCK)) or c, 0)
 
@@ -1042,7 +1083,7 @@
         size, q_cols, k_cols, proj = self.size, self.q_cols, self.k_cols, self.projected.ref
 
         def prepare(rows):
-            c, n = self.cos.ref[rows, :], self.sin.ref[rows, :]
+            c, n = self.angles(rows)
             q = head_norm(proj[rows, :q_cols], self.gain.ref[0:1, :], size)
             q = (q * c + turn(q, size, False) * n).astype(BF)
             k = head_norm(proj[rows, q_cols : q_cols + k_cols], self.gain.ref[1:2, :k_cols], size)
@@ -1124,7 +1165,7 @@
         self.k_gain.ref[...] = jnp.zeros_like(self.k_gain.ref)
 
         def finish(rows):
-            c, n = self.cos.ref[rows, :], self.sin.ref[rows, :]
+            c, n = self.angles(rows)
             dq, dk, dv = (self.join(v, rows) for v in (self.dq_h, self.dk_h, self.dv_h))
             dq = dq * c + turn(dq * n, size, True)
             dk = dk * c[:, :k_cols] + turn(dk * n[:, :k_cols], size, True)
@@ -1151,9 +1192,7 @@
 
     seqs, own_gain = boundary[0], norm_gain[0]
     sh_in, sh_out, sh_gate, sh_up, sh_down = (v[0] for v in (mix_in, mix_out, w_gate, w_up, w_down))
-    cosine_table, sine_table = rotation(length, size)
-    heads = channels // size
-    table_arrays = [jnp.tile(v, (1, heads)) for v in (qk_gain, cosine_table, sine_table)]
+    table_arrays = [jnp.tile(qk_gain, (1, channels // size)), *rotation(length, size, 128)]
 
     def gains_of(k, block, other, early=True):
         own, moved = k.input(own_gain), as_val(k, other)
@@ -1175,14 +1214,15 @@
     def seq_moves(s, d, t):
         return [([(None, seq_val.ref.at[1 - s])], t_seq.out.ref, {"section": 1 - s})], []
 
-    t_in, t_out, t_gate, t_up, t_down = (
-        x_half(k, v) for v in (sh_in, sh_out, sh_gate, sh_up, sh_down)
-    )
+    t_in, t_out, t_up = (x_half(k, v) for v in (sh_in, sh_out, sh_up))
+    t_gate0, t_down0 = x_move(k, sh_gate, 0), x_half(k, sh_down, 0)
+    t_gate1, t_down1 = x_half(k, sh_gate, 1), x_move(k, sh_down, 1)
     t_seq = Task(k, row_shape, "section", seq_moves, 1)
     t_gain, z_cols = x_move(k, own_gain), z_gather(k, conv_x)
     z_in0, z_out0 = z_gather_half(k, sh_in, t_in.out, 0), z_gather_half(k, sh_out, t_out.out, 0)
-    z_gate0, z_up0 = z_gather_half(k, sh_gate, t_gate.out, 0), z_gather_half(k, sh_up, t_up.out, 0)
-    x_cols, x_in0, x_out0, x_gate0 = (x_move(k, v.out) for v in (z_cols, z_in0, z_out0, z_gate0))
+    z_gate0 = z_gather_whole(k, sh_gate, t_gate0.out, 0)
+    z_up0 = z_gather_half(k, sh_up, t_up.out, 0)
+    x_cols, x_in0, x_out0 = (x_move(k, v.out) for v in (z_cols, z_in0, z_out0))
     x_load, gain_load = start_rows(k, 0, t_seq.out, False), gains_of(k, 0, t_gain.out, False)
     taps = load_all(k, conv_kernel)
     w_in0, w_cols = Weight(k, "rows", z_in0.out, x_in0.out), Weight(k, "conv", z_cols.out, x_cols.out)
@@ -1192,29 +1232,29 @@
     y0 = Save(k, conv.y)
     s1 = Scatter(k, [conv.y], [w_out0], x_load.buf)
     mid0 = Save(k, s1.out)
-    k.do(t_in.send, t_out.send, z_cols.send, t_gate.send, t_gain.send, t_seq.send)
+    k.do(t_in.send, t_out.send, z_cols.send, t_gate0.send, t_gate1.send, t_gain.send, t_seq.send)
     k.do(t_in.wait, z_in0.send, t_out.wait, z_out0.send, t_up.send)
-    k.do(z_cols.step, z_in0.step, z_out0.step, t_gate.wait, z_gate0.send)
+    k.do(z_cols.step, z_in0.step, z_out0.step, t_gate0.wait, z_gate0.send)
     k.do(z_cols.step, z_in0.step, z_out0.step)
     k.do(t_gain.wait, gain_load.start, t_seq.wait, x_load.start)
     k.do(gain_load.wait, x_load.wait, g0.begin)
-    k.do(z_cols.wait, x_cols.send, z_in0.wait, x_in0.send, z_out0.wait, x_out0.send, t_down.send)
-    k.do(z_gate0.step, t_up.wait, z_up0.send, z_gate0.step, z_up0.step, z_gate0.wait, x_gate0.send)
-    k.do(x_cols.wait, w_cols.start, x_in0.wait, w_in0.start, z_up0.step)
+    k.do(z_cols.wait, x_cols.send, z_in0.wait, x_in0.send, z_out0.wait, x_out0.send)
+    k.do(t_down0.send, t_down1.send, t_up.wait, z_up0.send, z_gate0.step, z_up0.step)
+    k.do(x_cols.wait, w_cols.start, x_in0.wait, w_in0.start, z_gate0.step)
     k.do(g0.loop, taps.wait, conv.run, y0.start)
-    k.do(x_out0.wait, w_out0.start, s1.loop, s1.finish, mid0.start)
-    k.do(*wait(t_down, x_gate0, z_up0))
+    k.do(z_up0.step, x_out0.wait, w_out0.start, s1.loop, s1.finish, mid0.start)
+    k.do(*wait(t_gate1, t_down0, t_down1, z_gate0, z_up0))
     k.build()
     a0, proj0, value0 = (out for _, out, _ in g0.saved)
     y0, mid0 = y0.out, mid0.out
 
     k = Kernel(1)
-    x_up0, z_down0 = x_move(k, z_up0.out), z_gather_half(k, sh_down, t_down.out, 0)
+    x_up0, z_down0 = x_move(k, z_up0.out), z_gather_half(k, sh_down, t_down0.out, 0)
     z_in1, z_out1 = z_gather_half(k, sh_in, t_in.out, 1), z_gather_half(k, sh_out, t_out.out, 1)
-    z_gate1 = z_gather_half(k, sh_gate, t_gate.out, 1)
+    z_gate1 = z_gather_half(k, sh_gate, t_gate1.out, 1)
     x_down0, x_in1, x_out1 = (x_move(k, v.out) for v in (z_down0, z_in1, z_out1))
     rows, gain_load = load_all(k, mid0), gains_of(k, 0, t_gain.out)
-    w_gate0 = Weight(k, "rows", z_gate0.out, x_gate0.out, True)
+    w_gate0 = Weight(k, "rows", z_gate0.out, None, True)
     w_up0 = Weight(k, "rows", z_up0.out, x_up0.out)
     w_down0 = Weight(k, "cols", z_down0.out, x_down0.out)
     g2 = Gather(
@@ -1235,7 +1275,7 @@
 
     k = Kernel(2)
     x_gate1, z_up1 = x_move(k, z_gate1.out), z_gather_half(k, sh_up, t_up.out, 1)
-    z_down1, x_up1 = z_gather_half(k, sh_down, t_down.out, 1), x_move(k, z_up1.out)
+    z_down1, x_up1 = z_gather_whole(k, sh_down, t_down1.out, 1), x_move(k, z_up1.out)
     rows, gain_load = load_all(k, z_rows), gains_of(k, 1, t_gain.out)
     tables = [load_all(k, v) for v in table_arrays]
     w_in1 = Weight(k, "rows", z_in1.out, x_in1.out, True)
@@ -1246,10 +1286,10 @@
     s5 = Scatter(k, [attend.y], [w_out1], rows.buf)
     mid1 = Save(k, s5.out)
     k.do(x_gate1.send, z_up1.send, z_down1.send)
-    k.do(rows.wait, gain_load.wait, g4.begin, z_up1.step, g4.loop, z_up1.step, z_down1.step)
+    k.do(rows.wait, gain_load.wait, g4.begin, z_up1.step, g4.loop, z_up1.step)
     k.do(lambda: attend.run(z_up1.wait, x_up1.send, z_down1.step))
     k.do(*(v.start for v in kept))
-    k.do(s5.loop, s5.finish, mid1.start)
+    k.do(s5.loop, z_down1.step, s5.finish, mid1.start)
     k.do(*wait(x_gate1, x_up1, z_down1))
     k.build()
     a1, proj1 = (out for _, out, _ in g4.saved)
@@ -1257,12 +1297,11 @@
     mid1 = mid1.out
 
     k = Kernel(3)
-    x_down1 = x_move(k, z_down1.out)
     rows, gain_load = load_all(k, mid1), gains_of(k, 1, t_gain.out)
     cot = start_rows(k, 1, t_seq.out)
     w_gate1 = Weight(k, "rows", z_gate1.out, x_gate1.out, True)
     w_up1 = Weight(k, "rows", z_up1.out, x_up1.out, True)
-    w_down1 = Weight(k, "cols", z_down1.out, x_down1.out)
+    w_down1 = Weight(k, "cols", z_down1.out, None, True)
     g6 = Gather(k, rows.buf, (gain_load.buf, 1), [w_gate1, w_up1], epilogue="ffn")
     g8 = Gather(
         k, cot.buf, None, [w_down1], [g6.values[0], g6.values[1]], trans=True, epilogue="ffn_back"
@@ -1273,18 +1312,17 @@
     s7 = Scatter(k, [g6.values[2]], [w_down1], rows.buf, low=True)
     s9 = Scatter(k, g8.values, [w_gate1, w_up1], cot.buf, (rows.buf, (gain_load.buf, 1)), True)
     y_rows, d_mid1, gain11 = Save(k, s7.out), Save(k, s9.out), Save(k, s9.gain_grad)
-    k.do(x_down1.send, rows.wait, gain_load.wait, g6.begin, cot.wait, g8.begin, g6.loop)
-    k.do(x_down1.wait, w_down1.start, g8.loop, p_down1.run, p_down1.wait, r_down1.send)
-    k.do(s9.loop, p_gate1.run, p_up1.run, s9.finish, d_mid1.start, gain11.start)
-    k.do(s7.loop, s7.finish, y_rows.start, p_gate1.wait, p_up1.wait)
+    k.do(rows.wait, gain_load.wait, g6.begin, cot.wait, g8.begin, g6.loop)
+    k.do(g8.loop, p_down1.run, p_down1.wait, r_down1.send)
+    k.do(s9.loop, s7.loop, p_gate1.run, p_up1.run, s9.finish, d_mid1.start, gain11.start)
+    k.do(s7.finish, y_rows.start, p_gate1.wait, p_up1.wait)
     k.do(*wait(r_down1))
     k.build()
     y_rows, d_mid1, gain11 = y_rows.out, d_mid1.out, gain11.out
 
     k = Kernel(4)
     q_down1 = sum_scatter(k, "cols", p_down1.out, r_down1.out)
-    r_gate1, r_up1 = x_slots(k, p_gate1.out, "rows"), x_slots(k, p_up1.out, "rows")
-    q_gate1 = sum_scatter(k, "rows", p_gate1.out, r_gate1.out)
+    r_gate1, q_up1 = x_slots(k, p_gate1.out, "rows"), sum_scatter(k, "rows", p_up1.out)
     rows, gain_load = load_all(k, d_mid1), gains_of(k, 1, t_gain.out)
     value = load_all(k, z_rows)
     tables = [load_all(k, v) for v in table_arrays]
@@ -1301,28 +1339,27 @@
     )
     d_z, gain10 = Save(k, s11.out), Save(k, s11.gain_grad)
     head_gains = [Save(k, back.q_gain), Save(k, back.k_gain)]
-    k.early.append(q_down1.load)
-    k.do(r_gate1.send, r_up1.send, rows.wait, g10.begin, q_down1.send, g10.loop)
-    k.do(q_down1.step, y_load.wait, p_out1.run, p_out1.wait, r_out1.send, q_down1.step)
-    k.do(r_gate1.wait, q_gate1.add)
-    k.do(proj.wait, q_load.wait, k_load.wait, lambda: back.run(q_gate1.step))
-    k.do(q_gate1.step, *(v.start for v in head_gains))
+    k.early += [q_up1.load, q_down1.load]
+    k.do(r_gate1.send, rows.wait, g10.begin, q_up1.send, q_down1.send, g10.loop)
+    k.do(q_up1.step, q_down1.step, y_load.wait, p_out1.run, p_out1.wait, r_out1.send)
+    k.do(proj.wait, q_load.wait, k_load.wait, lambda: back.run(q_up1.step, q_down1.step))
+    k.do(q_up1.wait, *(v.start for v in head_gains))
     k.do(gain_load.wait, value.wait, s11.loop, a_load.wait, p_in1.run)
     k.do(s11.finish, d_z.start, gain10.start, p_in1.wait)
-    k.do(*wait(q_down1, q_gate1, r_up1, r_out1))
+    k.do(*wait(q_down1, q_up1, r_gate1, r_out1))
     k.build()
     d_z, gain10 = d_z.out, gain10.out
-    q_gain, k_gain = (v.out.array for v in head_gains)
+    q_gain, k_gain = (v.out for v in head_gains)
 
     k = Kernel(5)
-    q_up1 = sum_scatter(k, "rows", p_up1.out, r_up1.out)
+    q_gate1, m_up1 = sum_scatter(k, "rows", p_gate1.out, r_gate1.out), x_move(k, q_up1.out, 0)
     q_out1 = sum_scatter(k, "cols", p_out1.out, r_out1.out)
     r_in1 = x_slots(k, p_in1.out, "rows")
     q_in1 = sum_scatter(k, "rows", p_in1.out, r_in1.out)
-    e_down1, e_gate1 = Finish(k, q_down1.out, 1), Finish(k, q_gate1.out, 1)
+    e_down1 = Finish(k, q_down1.out, 1)
     rows, value, gain_load = load_all(k, d_z), load_all(k, mid0), gains_of(k, 0, t_gain.out)
     gate_load, up_load, hid_load, m_load = (load_all(k, v) for v in (gate0, up0, hid0, m0))
-    w_gate0 = Weight(k, "rows", z_gate0.out, x_gate0.out, True)
+    w_gate0 = Weight(k, "rows", z_gate0.out, None, True)
     w_up0 = Weight(k, "rows", z_up0.out, x_up0.out, True)
     w_down0 = Weight(k, "cols", z_down0.out, x_down0.out, True)
     g12 = Gather(
@@ -1335,24 +1372,25 @@
         k, g12.values, [w_gate0, w_up0], rows.buf, (value.buf, (gain_load.buf, 1)), True
     )
     d_mid0, gain01 = Save(k, s13.out), Save(k, s13.gain_grad)
-    k.early += [q_up1.load, q_out1.load, e_down1.load, e_gate1.load]
-    k.do(r_in1.send, rows.wait, g12.begin, q_up1.send, q_out1.send, e_down1.send, e_gate1.send)
+    k.early += [q_gate1.load, q_out1.load, e_down1.load]
+    k.do(r_in1.send, rows.wait, g12.begin, q_gate1.send, q_out1.send, m_up1.send, e_down1.send)
     k.do(gate_load.wait, up_load.wait, g12.loop)
-    k.do(q_up1.step, q_out1.step, hid_load.wait, p_down0.run, p_down0.wait, r_down0.send)
-    k.do(q_up1.step, q_out1.step, r_in1.wait, q_in1.add)
+    k.do(q_gate1.step, q_out1.step, hid_load.wait, p_down0.run, p_down0.wait, r_down0.send)
+    k.do(q_gate1.step, q_out1.step, r_in1.wait, q_in1.add)
     k.do(s13.loop, q_in1.step, m_load.wait, p_gate0.run, q_in1.step, p_up0.run)
     k.do(value.wait, gain_load.wait, s13.finish, d_mid0.start, gain01.start)
     k.do(p_gate0.wait, p_up0.wait)
-    k.do(*wait(q_up1, q_out1, q_in1, e_down1, e_gate1, r_down0))
+    k.do(*wait(q_gate1, q_out1, q_in1, e_down1, m_up1, r_down0))
     k.build()
     d_mid0, gain01 = d_mid0.out, gain01.out
 
     k = Kernel(6)
-    r_gate0, r_up0 = x_slots(k, p_gate0.out, "rows"), x_slots(k, p_up0.out, "rows")
+    r_gate0 = x_slots(k, p_gate0.out, "rows")
     q_down0 = sum_scatter(k, "cols", p_down0.out, r_down0.out)
     q_gate0 = sum_scatter(k, "rows", p_gate0.out, r_gate0.out)
-    q_up0 = sum_scatter(k, "rows", p_up0.out, r_up0.out)
-    e_up1, e_out1, e_in1 = (Finish(k, v.out, 1) for v in (q_up1, q_out1, q_in1))
+    q_up0 = sum_scatter(k, "rows", p_up0.out)
+    m_up0 = x_move(k, q_up0.out, 1)
+    e_gate1, e_out1, e_in1 = (Finish(k, v.out, 1) for v in (q_gate1, q_out1, q_in1))
     rows, gain_load = load_all(k, d_mid0), gains_of(k, 0, t_gain.out)
     x_load, taps = start_rows(k, 0, t_seq.out), load_all(k, conv_kernel)
     y_load, a_load, proj, value = (load_all(k, v) for v in (y0, a0, proj0, value0))
@@ -1367,8 +1405,8 @@
     r_cols = x_slots(k, p_cols.out, "conv")
     q_out0, q_in0 = sum_scatter(k, "cols", p_out0.out, r_out0.out), sum_scatter(k, "rows", p_in0.out, r_in0.out)
     q_cols = sum_scatter(k, "conv", p_cols.out, r_cols.out)
-    e_down0, e_gate0, e_up0, e_out0, e_in0 = (
-        Finish(k, v.out, 0) for v in (q_down0, q_gate0, q_up0, q_out0, q_in0)
+    e_down0, e_gate0, e_out0, e_in0 = (
+        Finish(k, v.out, 0) for v in (q_down0, q_gate0, q_out0, q_in0)
     )
     s15 = Scatter(
         k, [back.d_proj, back.d_value], [w_in0, w_cols], rows.buf,
@@ -1379,11 +1417,7 @@
     small = k.vmem((8, model_width), F32)
     small_out = Save(k, small)
     ready = [load_all(k, v) for v in (gain01, gain10, gain11)]
-    head_row = jnp.pad(
-        jnp.stack([jnp.sum(v.reshape(-1, size), axis=0) for v in (q_gain, k_gain)]).reshape(1, -1),
-        ((0, 0), (0, model_width - 2 * size)),
-    )
-    head_load = load_all(k, head_row)
+    head_loads = [load_all(k, v) for v in (q_gain, k_gain)]
 
     def fill_small():
         t = lax.axis_index("tensor")
@@ -1393,8 +1427,12 @@
             load.wait()
             small.ref[i + 1 : i + 2, :] = load.buf.ref[...]
         small.ref[4 : 4 + tap_rows, block_of(t, channels)] = back.d_kernel.ref[...]
-        head_load.wait()
-        small.ref[7:8, :] = head_load.buf.ref[...]
+        at = 0
+        for load in head_loads:
+            load.wait()
+            width = load.buf.shape[1]
+            small.ref[7:8, at : at + width] = load.buf.ref[...]
+            at += width
         small_out.start()
 
     t_small = x_move(k, small_out.out)
@@ -1407,22 +1445,21 @@
         return [(sources, t_result.out.ref, {"section": 1 - s})], []
 
     t_result = Task(k, row_shape, "section", result_moves, 1)
-    k.early += [q_down0.load, e_up1.load, e_out1.load, e_in1.load]
-    k.do(r_gate0.send, r_up0.send, rows.wait, g14.begin, q_down0.send)
-    k.do(e_up1.send, e_out1.send, e_in1.send, g14.loop)
-    k.do(q_down0.step, y_load.wait, p_out0.run, p_out0.wait, r_out0.send, q_down0.step)
+    k.early += [q_up0.load, q_down0.load, e_gate1.load, e_out1.load, e_in1.load]
+    k.do(r_gate0.send, rows.wait, g14.begin, q_up0.send, q_down0.send)
+    k.do(e_gate1.send, e_out1.send, e_in1.send, g14.loop)
+    k.do(q_up0.step, q_down0.step, y_load.wait, p_out0.run, p_out0.wait, r_out0.send)
     k.do(proj.wait, value.wait, taps.wait, back.run, a_load.wait)
     k.do(p_in0.run, p_cols.run, p_in0.wait, r_in0.send, p_cols.wait, r_cols.send)
-    k.do(r_gate0.wait, q_gate0.add)
-    k.do(x_load.wait, gain_load.wait, s15.loop, q_gate0.step, s15.finish, d_x.start, q_gate0.step)
-    k.do(fill_small, d_x.wait, t_result.send)
-    k.do(small_out.wait, t_small.send)
-    k.do(q_down0.wait, e_down0.add, q_gate0.wait, e_gate0.add)
-    k.do(r_up0.wait, q_up0.add, r_out0.wait, q_out0.add, r_in0.wait, q_in0.add)
-    k.do(q_up0.step, r_cols.wait, q_cols.add, q_out0.step, q_in0.step, t_small.wait, z_small.add)
-    k.do(q_up0.step, q_cols.step, q_out0.step, q_in0.step, z_small.wait, t_total.add)
-    k.do(q_up0.wait, e_up0.add, q_cols.step, q_out0.wait, e_out0.add, q_in0.wait, e_in0.add)
-    rest = (e_up1, e_out1, e_in1, q_cols, e_down0, e_gate0, e_up0, e_out0, e_in0)
+    k.do(r_gate0.wait, q_gate0.add, q_up0.step, q_down0.step)
+    k.do(x_load.wait, gain_load.wait, s15.loop, q_gate0.step, s15.finish, d_x.start)
+    k.do(fill_small, d_x.wait, t_result.send, small_out.wait, t_small.send)
+    k.do(q_up0.wait, m_up0.send, r_out0.wait, q_out0.add, r_in0.wait, q_in0.add)
+    k.do(r_cols.wait, q_cols.add, q_gate0.step, q_down0.wait, e_down0.add)
+    k.do(q_out0.step, q_in0.step, q_cols.step, t_small.wait, z_small.add)
+    k.do(q_gate0.wait, e_gate0.add, q_out0.step, q_in0.step, q_cols.step)
+    k.do(z_small.wait, t_total.add, q_out0.wait, e_out0.add, q_in0.wait, e_in0.add)
+    rest = (e_gate1, e_out1, e_in1, q_cols, e_down0, e_gate0, m_up0, e_out0, e_in0)
     k.do(*wait(*rest, t_total, t_result))
     k.build()
 
@@ -1430,6 +1467,11 @@
         kept = jnp.where(first, zero.out.array, one.out.array)
         return kept.reshape(1, -1, kept.shape[-1]).astype(F32)
 
+    def slot_sum(value):
+        value = value.out.array.astype(F32)
+        return value if value.ndim == 2 else jnp.sum(value, axis=0)
+
+    up_zero, up_one = slot_sum(q_up0) + slot_sum(m_up0), slot_sum(q_up1) + slot_sum(m_up1)
     d_x, y_rows, moved = d_x.out.array, y_rows.array, t_result.out.array
     result = jnp.where(first, jnp.stack([d_x, moved]), jnp.stack([moved, y_rows]))
     small = jnp.sum(t_total.out.array, axis=0)
@@ -1438,17 +1480,21 @@
     kernel_out = lax.dynamic_slice_in_dim(
         small[4 : 4 + tap_rows], tensor_index * channels, channels, 1
     )
-    cols_grad = q_cols.out.array.astype(F32)
-    if cols_grad.ndim == 3:
-        cols_grad = jnp.sum(cols_grad, axis=0)
-    head_total = small[7, : qk_gain.size].reshape(qk_gain.shape)
+    cols_grad = slot_sum(q_cols)
+    split = channels + channels // 2
+    head_total = jnp.stack(
+        [
+            jnp.sum(v.reshape(-1, size), axis=0)
+            for v in (small[7, :channels], small[7, channels:split])
+        ]
+    )
     return (
         result[None],
         gain_out,
         whole(e_in0, e_in1),
         whole(e_out0, e_out1),
         whole(e_gate0, e_gate1),
-        whole(e_up0, e_up1),
+        jnp.where(first, up_zero, up_one)[None],
         whole(e_down0, e_down1),
         cols_grad,
         kernel_out,

time: 589 us -> 566 us (0.961)
  Pallas kernels: 559 us -> 540 us
    pallas_call x7, Pallas kernels: 559 us -> 540 us  [build(): pl.pallas_call(self.body, out_shape=[jax.ShapeDtypeStruct(v.shape, v.dtyp...]
where the time goes in v7:
time: 566 us; the launch traced here: 556 us
  Pallas kernels  540 us (95%)
  other arithmetic  12.5 us (2%)
    pallas_call x7, Pallas kernels, build(): pl.pallas_call(self.body, out_shape=[jax.ShapeDtypeStruct(v.shape, v.dtyp...  540 us

profile of v7, /device:TPU:0, one launch (start us, length us, event | category | flops | bytes accessed | tf_op | source)
XLA Modules:
  0.0 556.4 jit_solution(6415901228555714892)
XLA Ops:
  0.6 87.8 %stage0.1 = (bf16[128,512]{1,0:T(8,128)(2,1)}, bf16[128,256]{1,0:T(8,128)(2,1)}, bf16[128,1152]{1,0:T(8,128)(2,1)}, bf16[256,1152]{1,0:T(8,128)(2,1)}, bf16[576,...) custom-call(bf16[2,256,1024]{2,1,0:T(8,128)(2,1)} %bitcast.30, ...), custom_call_target="tpu_custom_call" | custom-call | tf_op jit(solution)/shard_map/stage0/pallas_call | solution.py:137
  88.4 0.0 copy-start.15
  88.5 81.2 %stage1.1 = (bf16[4,128,1152]{2,1,0:T(8,128)(2,1)}, bf16[4,576,256]{2,1,0:T(8,128)(2,1)}, bf16[4,128,512]{2,1,0:T(8,128)(2,1)}, bf16[4,128,256]{2,1,0:T(8,128)(2...) custom-call(bf16[4,128,1152]{2,1,0:T(8,128)(2,1)} %get-tuple-element, ...), custom_call_target="tpu_custom_call" | custom-call | tf_op jit(solution)/shard_map/stage1/pallas_call | solution.py:137
  169.7 2.8 fusion
  172.5 0.0 copy-done.15
  172.5 0.7 tile.10.refs_8_
  173.2 65.4 %stage2.1 = (bf16[4,128,1152]{2,1,0:T(8,128)(2,1)}, bf16[4,128,1152]{2,1,0:T(8,128)(2,1)}, bf16[4,1152,256]{2,1,0:T(8,128)(2,1)}, bf16[4,128,1152]{2,1,0:T(8,128...) custom-call(bf16[4,128,1152]{2,1,0:T(8,128)(2,1)} %get-tuple-element, ...), custom_call_target="tpu_custom_call" | custom-call | tf_op jit(solution)/shard_map/stage2/pallas_call | solution.py:137
  238.6 61.5 %stage3.1 = (bf16[1152,1024]{1,0:T(8,128)(2,1)}, bf16[1024,1152]{1,0:T(8,128)(2,1)}, bf16[1024,1152]{1,0:T(8,128)(2,1)}, bf16[576,1024]{1,0:T(8,128)(2,1)}, bf16...) custom-call(f32[256,1024]{1,0:T(8,128)} %get-tuple-element.111.refs_0_, f32[2,1024]{1,0:T(2,128)} %bitcast.54, ...), custom_call_target="tpu_custom_call" | custom-call | tf_op jit(solution)/shard_map/stage3/pallas_call | solution.py:137
  300.1 73.8 %stage4.1 = (bf16[576,256]{1,0:T(8,128)(2,1)}, bf16[4,128,1152]{2,1,0:T(8,128)(2,1)}, bf16[256,1152]{1,0:T(8,128)(2,1)}, bf16[256,1024]{1,0:T(8,128)(2,1)}, bf16...) custom-call(bf16[1152,1024]{1,0:T(8,128)(2,1)} %get-tuple-element.11, ...), custom_call_target="tpu_custom_call" | custom-call | tf_op jit(solution)/shard_map/stage4/pallas_call | solution.py:137
  373.9 61.8 %stage5.1 = (bf16[128,1152]{1,0:T(8,128)(2,1)}, bf16[256,1152]{1,0:T(8,128)(2,1)}, bf16[128,256]{1,0:T(8,128)(2,1)}, bf16[4,128,512]{2,1,0:T(8,128)(2,1)}, bf16[...) custom-call(bf16[1024,1152]{1,0:T(8,128)(2,1)} %get-tuple-element.11, ...), custom_call_target="tpu_custom_call" | custom-call | tf_op jit(solution)/shard_map/stage5/pallas_call | solution.py:137
  435.7 0.0 copy-start.2
  435.7 108.1 %stage6.1 = (bf16[4,128,1152]{2,1,0:T(8,128)(2,1)}, bf16[576,256]{1,0:T(8,128)(2,1)}, bf16[128,1152]{1,0:T(8,128)(2,1)}, bf16[256,1152]{1,0:T(8,128)(2,1)}, bf16...) custom-call(bf16[1024,1152]{1,0:T(8,128)(2,1)} %get-tuple-element.14, ...), custom_call_target="tpu_custom_call" | custom-call | tf_op jit(solution)/shard_map/stage6/pallas_call | solution.py:137
  543.8 0.9 reduce_sum.27
  544.8 0.1 reshape_squeeze.6
  544.9 0.1 reshape_squeeze.7
  545.0 0.6 pad_maximum_fusion
  545.6 0.0 copy-done.2
  545.6 1.2 broadcast_select_fusion
  546.8 0.0 copy-start
  546.8 0.0 copy-start.5
  546.8 0.0 copy-start.6
  546.8 1.1 bitcast_convert_fusion
  547.9 0.0 copy-done.7
  547.9 0.1 copy-done
  548.0 0.5 copy-done.5
  548.5 0.2 copy-done.6
  548.6 1.3 select_bitcast_fusion
  549.9 0.0 copy-done.3
  549.9 0.1 copy-done.4
  550.0 0.1 broadcast_select_fusion.1
  550.1 0.0 copy-start.12
  550.1 0.0 copy-start.13
  550.1 0.0 copy-start.10
  550.1 0.0 copy-start.11
  550.2 1.1 bitcast_convert_fusion.1
  551.3 0.0 copy-done.12
  551.3 0.0 copy-done.13
  551.3 0.0 copy-start.9
  551.3 0.7 bitcast_convert_fusion.3
  552.0 0.0 copy-done.10
  552.0 0.0 copy-done.11
  552.1 0.9 bitcast_convert_fusion.2
  552.9 0.0 copy-done.1
  552.9 0.0 copy-done.9
  552.9 1.1 maximum_select_fusion
  554.1 0.7 convert_element_type.97
  554.8 0.6 constant_dynamic-slice_fusion.1
  555.4 0.6 constant_dynamic-slice_fusion
  (19 shorter events, 0.2 us)
Async XLA Ops:
  88.4 84.1 %copy-start.15 = (f32[2,64]{1,0:T(2,128)S(1)}, f32[2,64]{1,0:T(2,128)}, u32[]{:S(2)}) copy-start(f32[2,64]{1,0:T(2,128)} %param.19) | copy-start | bytes 1540
  435.7 109.9 %copy-start.2 = (bf16[2,576,256]{2,1,0:T(8,128)(2,1)S(1)}, bf16[2,576,256]{2,1,0:T(8,128)(2,1)}, u32[]{:S(2)}) copy-start(bf16[2,576,256]{2,1,0:T(8,128)(2,1)} %get-tuple-element.178) | copy-start | bytes 1769476
  545.6 2.3 copy-start.7
  546.8 1.2 copy-start
  546.8 1.7 copy-start.5
  546.8 1.8 copy-start.6
  548.6 1.3 copy-start.3
  548.6 1.4 copy-start.4
  550.1 1.1 copy-start.12
  550.1 1.1 copy-start.13
  550.1 1.9 copy-start.10
  550.1 1.9 copy-start.11
  551.3 1.7 copy-start.1
  551.3 1.7 copy-start.8
  551.3 1.7 copy-start.9
  552.9 1.1 copy-start.14

commit v8 on v7

--- a/solution.py
+++ b/solution.py
@@ -42,12 +42,29 @@
     return (value_grad, gain_grad)
 
 
-def rotation(length, head_size, width):
-    half_size = head_size // 2
-    column = (jnp.arange(width) % half_size).astype(F32)
-    frequency = ROPE_BASE ** (-(column * 2.0 / head_size))
-    angles = jnp.arange(length, dtype=F32)[:, None] * frequency[None, :]
-    return jnp.cos(angles), jnp.sin(angles)
+class Angles:
+    def __init__(self, k, length, head_size, width):
+        self.half = head_size // 2
+        self.tables = [k.vmem((length, width), F32) for _ in range(2)]
+        self.saves = [Save(k, v) for v in self.tables]
+
+    def run(self):
+        cos, sin = self.tables
+        shape = (ROW_BLOCK, cos.shape[1])
+        column = (lax.broadcasted_iota(jnp.int32, shape, 1) % self.half).astype(F32)
+        frequency = ROPE_BASE ** (-(column / self.half))
+        row = lax.broadcasted_iota(jnp.int32, shape, 0)
+
+        def step(i, carry):
+            rows = block_of(i, ROW_BLOCK)
+            angle = (row + i * ROW_BLOCK).astype(F32) * frequency
+            cos.ref[rows, :] = jnp.cos(angle)
+            sin.ref[rows, :] = jnp.sin(angle)
+            return carry
+
+        lax.fori_loop(0, cos.shape[0] // ROW_BLOCK, step, 0)
+        for save in self.saves:
+            save.start()
 
 
 def silu_parts(gate):
@@ -365,13 +382,15 @@
     return task
 
 
-def z_gather_whole(k, shard, moved, block):
+def z_gather_whole(k, shard, moved, block, half=None):
     shard, moved = as_val(k, shard), as_val(k, moved)
+    rows = shard.shape[0] if half is None else shard.shape[0] // 2
+    part = pl.ds(0 if half is None else half * rows, rows)
 
     def sources(s, d, t):
-        return [(s == block, shard.ref), (s == 1 - block, moved.ref)]
-
-    return z_gather_from(k, sources, shard.shape, shard.dtype)
+        return [(s == block, shard.ref.at[part]), (s == 1 - block, moved.ref.at[part])]
+
+    return z_gather_from(k, sources, (rows,) + shard.shape[1:], shard.dtype)
 
 
 def x_move(k, value, sender=None):
@@ -418,9 +437,13 @@
         self.kind, self.n = kind, dp_size()
         self.whole = received is None
         if self.whole:
-            self.rows, self.cols = self.grads.shape[0] // self.n, self.grads.shape[1]
+            rows, cols = self.grads.shape
+            self.rows = rows if kind == "cols" else rows // self.n
+            self.cols = cols // self.n if kind == "cols" else cols
             self.shape = (self.n, self.rows, self.cols)
-            self.kept = self.total = k.vmem(self.shape, BF)
+            self.aside = kind == "cols" and self.cols % 128 != 0
+            self.total = k.vmem(self.shape, BF)
+            self.kept = k.vmem(self.grads.shape, BF) if self.aside else self.total
             return
         self.received = as_val(k, received)
         if kind == "cols":
@@ -435,10 +458,16 @@
 
     def loads(self):
         s, grads, kept = lax.axis_index("section"), self.grads.ref, self.kept.ref
+        if self.whole and self.aside:
+            return [self.local(grads, kept, 2)]
         if self.whole:
-            return [
-                self.local(grads.at[block_of(i, self.rows)], kept.at[i], 2 + i) for i in range(self.n)
+            parts = [
+                grads.at[:, pl.ds(i * self.cols, self.cols)]
+                if self.kind == "cols"
+                else grads.at[block_of(i, self.rows)]
+                for i in range(self.n)
             ]
+            return [self.local(part, kept.at[i], 2 + i) for i, part in enumerate(parts)]
         if self.kind == "cols":
             moves = [self.local(grads.at[block_of(s, self.rows)], kept, 2)]
         else:
@@ -455,6 +484,9 @@
     def add(self):
         for move in self.loads():
             move.wait()
+        if self.whole and self.aside:
+            for i in range(self.n):
+                self.total.ref[i] = self.kept.ref[:, i * self.cols : (i + 1) * self.cols]
         if self.whole:
             return
         kept, got, total = self.kept.ref, self.got.ref, self.total.ref
@@ -624,11 +656,11 @@
 
 
 class Weight:
-    def __init__(self, k, kind, near, far=None, early=False):
+    def __init__(self, k, kind, near, far=None, early=False, fixed=False):
         near, far = as_val(k, near), None if far is None else as_val(k, far)
         self.count, self.rows, self.cols = near.shape
         self.kind, self.near, self.far, self.waited = kind, near, far, False
-        sides = 1 if far is None else 2
+        sides, self.fixed = 1 if far is None else 2, fixed
         if kind == "cols":
             shape = (sides * self.rows, self.count * self.cols)
         else:
@@ -642,7 +674,7 @@
             k.early.append(self.start)
 
     def moves(self):
-        s, dst = lax.axis_index("section"), self.buf.ref
+        s, dst = 0 if self.fixed else lax.axis_index("section"), self.buf.ref
         rows, cols = self.rows, self.cols
 
         def place(sec, own):
@@ -678,7 +710,7 @@
         for move in self.moves():
             move.wait()
         if self.aside:
-            s = lax.axis_index("section")
+            s = 0 if self.fixed else lax.axis_index("section")
             for j, sec in enumerate((s, 1 - s) if self.far is not None else (0,)):
                 whole = jnp.concatenate([self.held[j].ref[i] for i in range(self.count)], axis=1)
                 self.buf.ref[block_of(sec, self.rows), :] = whole
@@ -1029,18 +1061,27 @@
     return row_scale * (scaled - normed * head_mean(scaled * normed, head_size)), gain_grad
 
 
-def block_weights(q_rows, k_rows, first_row):
-    rows, length = q_rows.shape[0], k_rows.shape[0]
-    scores = contract(q_rows, k_rows, 1, 1) * (q_rows.shape[1] ** -0.5)
-    query = first_row + lax.broadcasted_iota(jnp.int32, (rows, length), 0)
-    key = lax.broadcasted_iota(jnp.int32, (rows, length), 1)
-    scores = jnp.where(key <= query, scores, MASKED)
-    exps = jnp.exp(scores - jnp.max(scores, axis=1, keepdims=True))
-    return exps * (1.0 / jnp.sum(exps, axis=1, keepdims=True))
+def block_weights(q_rows, keys):
+    scores = [contract(q_rows, k_rows, 1, 1) for k_rows in keys]
+    query = lax.broadcasted_iota(jnp.int32, scores[-1].shape, 0)
+    key = lax.broadcasted_iota(jnp.int32, scores[-1].shape, 1)
+    scores[-1] = jnp.where(key <= query, scores[-1], MASKED)
+    top = functools.reduce(
+        jnp.maximum, [jnp.max(part, axis=1, keepdims=True) for part in scores]
+    )
+    exps = [jnp.exp(part - top) for part in scores]
+    scale = 1.0 / sum(jnp.sum(part, axis=1, keepdims=True) for part in exps)
+    return [part * scale for part in exps]
+
+
+def key_blocks(i):
+    blocks = [pl.ds(0, i * ROW_BLOCK)] if i else []
+    return blocks + [pl.ds(i * ROW_BLOCK, ROW_BLOCK)]
 
 
 class Heads:
     def __init__(self, projected, tables, size):
+        assert size in (16, 64, 256), size
         self.projected, self.size = projected, size
         self.gain, self.cos, self.sin = (v.buf for v in tables)
         self.loads = tables
@@ -1090,7 +1131,7 @@
             k = (k * c[:, :k_cols] + turn(k, size, False) * n[:, :k_cols]).astype(BF)
             self.q_rot.ref[rows, :] = q
             self.k_rot.ref[rows, :] = k
-            self.split(self.q_h, rows, q)
+            self.split(self.q_h, rows, (q.astype(F32) * size**-0.5).astype(BF))
             self.split(self.k_h, rows, k)
             self.split(self.v_h, rows, proj[rows, q_cols + k_cols :].astype(BF))
 
@@ -1099,11 +1140,14 @@
         def head(h, carry):
             g = h // self.share
             for i in range(self.length // ROW_BLOCK):
-                rows, seen = pl.ds(i * ROW_BLOCK, ROW_BLOCK), pl.ds(0, (i + 1) * ROW_BLOCK)
+                rows, seen = pl.ds(i * ROW_BLOCK, ROW_BLOCK), key_blocks(i)
                 weights = block_weights(
-                    self.q_h.ref[h, rows, :], self.k_h.ref[g, seen, :], i * ROW_BLOCK
+                    self.q_h.ref[h, rows, :], [self.k_h.ref[g, at, :] for at in seen]
                 )
-                value = contract(weights.astype(BF), self.v_h.ref[g, seen, :], 1, 0)
+                value = sum(
+                    contract(part.astype(BF), self.v_h.ref[g, at, :], 1, 0)
+                    for part, at in zip(weights, seen)
+                )
                 self.y_h.ref[h, rows, :] = value.astype(BF)
             return carry
 
@@ -1133,7 +1177,7 @@
         dq_h, dk_h, dv_h = self.dq_h.ref, self.dk_h.ref, self.dv_h.ref
 
         def prepare(rows):
-            self.split(self.q_h, rows, self.q_rot.ref[rows, :])
+            self.split(self.q_h, rows, (self.q_rot.ref[rows, :].astype(F32) * scale).astype(BF))
             self.split(self.dy_h, rows, self.d_y.ref[rows, :].astype(BF))
             self.split(self.k_h, rows, self.k_rot.ref[rows, :])
             self.split(self.v_h, rows, proj[rows, q_cols + k_cols :].astype(BF))
@@ -1145,16 +1189,21 @@
         def head(h, carry):
             g = h // self.share
             for i in range(self.length // ROW_BLOCK):
-                rows, seen = pl.ds(i * ROW_BLOCK, ROW_BLOCK), pl.ds(0, (i + 1) * ROW_BLOCK)
+                rows, seen = pl.ds(i * ROW_BLOCK, ROW_BLOCK), key_blocks(i)
                 q, low = self.q_h.ref[h, rows, :], self.dy_h.ref[h, rows, :]
-                k = self.k_h.ref[g, seen, :]
-                prob = block_weights(q, k, i * ROW_BLOCK)
-                d_weights = contract(low, self.v_h.ref[g, seen, :], 1, 1)
-                dv_h[g, seen, :] += contract(prob.astype(BF), low, 0, 0)
-                inner = jnp.sum(prob * d_weights, axis=1, keepdims=True)
-                d_scores = (prob * (d_weights - inner)).astype(BF)
-                dq_h[h, rows, :] = contract(d_scores, k, 1, 0) * scale
-                dk_h[g, seen, :] += contract(d_scores, q, 0, 0) * scale
+                keys = [self.k_h.ref[g, at, :] for at in seen]
+                probs = block_weights(q, keys)
+                d_weights = [contract(low, self.v_h.ref[g, at, :], 1, 1) for at in seen]
+                inner = sum(
+                    jnp.sum(a * b, axis=1, keepdims=True) for a, b in zip(probs, d_weights)
+                )
+                d_q = 0.0
+                for at, k, prob, d_weight in zip(seen, keys, probs, d_weights):
+                    dv_h[g, at, :] += contract(prob.astype(BF), low, 0, 0)
+                    d_scores = (prob * (d_weight - inner)).astype(BF)
+                    d_q = d_q + contract(d_scores, k, 1, 0)
+                    dk_h[g, at, :] += contract(d_scores, q, 0, 0)
+                dq_h[h, rows, :] = d_q * scale
             return carry
 
         lax.fori_loop(0, self.heads // 2, head, 0)
@@ -1192,7 +1241,7 @@
 
     seqs, own_gain = boundary[0], norm_gain[0]
     sh_in, sh_out, sh_gate, sh_up, sh_down = (v[0] for v in (mix_in, mix_out, w_gate, w_up, w_down))
-    table_arrays = [jnp.tile(qk_gain, (1, channels // size)), *rotation(length, size, 128)]
+    head_gain = jnp.tile(qk_gain, (1, channels // size))
 
     def gains_of(k, block, other, early=True):
         own, moved = k.input(own_gain), as_val(k, other)
@@ -1222,9 +1271,10 @@
     z_in0, z_out0 = z_gather_half(k, sh_in, t_in.out, 0), z_gather_half(k, sh_out, t_out.out, 0)
     z_gate0 = z_gather_whole(k, sh_gate, t_gate0.out, 0)
     z_up0 = z_gather_half(k, sh_up, t_up.out, 0)
-    x_cols, x_in0, x_out0 = (x_move(k, v.out) for v in (z_cols, z_in0, z_out0))
+    x_cols, x_in0, x_out0, x_up0 = (x_move(k, v.out) for v in (z_cols, z_in0, z_out0, z_up0))
     x_load, gain_load = start_rows(k, 0, t_seq.out, False), gains_of(k, 0, t_gain.out, False)
     taps = load_all(k, conv_kernel)
+    angles = Angles(k, length, size, 128)
     w_in0, w_cols = Weight(k, "rows", z_in0.out, x_in0.out), Weight(k, "conv", z_cols.out, x_cols.out)
     w_out0 = Weight(k, "cols", z_out0.out, x_out0.out)
     g0 = Gather(k, x_load.buf, (gain_load.buf, 0), [w_in0, w_cols], save=(0, 1, 2))
@@ -1232,50 +1282,51 @@
     y0 = Save(k, conv.y)
     s1 = Scatter(k, [conv.y], [w_out0], x_load.buf)
     mid0 = Save(k, s1.out)
-    k.do(t_in.send, t_out.send, z_cols.send, t_gate0.send, t_gate1.send, t_gain.send, t_seq.send)
-    k.do(t_in.wait, z_in0.send, t_out.wait, z_out0.send, t_up.send)
-    k.do(z_cols.step, z_in0.step, z_out0.step, t_gate0.wait, z_gate0.send)
-    k.do(z_cols.step, z_in0.step, z_out0.step)
-    k.do(t_gain.wait, gain_load.start, t_seq.wait, x_load.start)
-    k.do(gain_load.wait, x_load.wait, g0.begin)
-    k.do(z_cols.wait, x_cols.send, z_in0.wait, x_in0.send, z_out0.wait, x_out0.send)
-    k.do(t_down0.send, t_down1.send, t_up.wait, z_up0.send, z_gate0.step, z_up0.step)
-    k.do(x_cols.wait, w_cols.start, x_in0.wait, w_in0.start, z_gate0.step)
-    k.do(g0.loop, taps.wait, conv.run, y0.start)
-    k.do(z_up0.step, x_out0.wait, w_out0.start, s1.loop, s1.finish, mid0.start)
-    k.do(*wait(t_gate1, t_down0, t_down1, z_gate0, z_up0))
+    k.do(t_in.send, t_out.send, z_cols.send, t_up.send, t_gain.send, t_seq.send)
+    k.do(t_in.wait, z_in0.send, t_out.wait, z_out0.send)
+    k.do(z_cols.step, z_in0.step, z_out0.step, t_up.wait, z_up0.send)
+    k.do(z_cols.step, z_in0.step, z_out0.step, z_cols.wait, x_cols.send, z_in0.wait, x_in0.send)
+    k.do(z_out0.wait, x_out0.send, t_gate0.send, t_gate1.send)
+    k.do(t_gain.wait, gain_load.start, t_seq.wait, x_load.start, z_up0.step)
+    k.do(gain_load.wait, x_load.wait, g0.begin, z_up0.step, angles.run)
+    k.do(z_up0.wait, x_up0.send, t_down0.send, t_down1.send)
+    k.do(x_cols.wait, w_cols.start, x_in0.wait, w_in0.start, t_gate0.wait, z_gate0.send)
+    k.do(g0.loop, z_gate0.step, taps.wait, conv.run, y0.start)
+    k.do(x_out0.wait, w_out0.start, s1.loop, z_gate0.step, s1.finish, mid0.start)
+    k.do(*wait(t_gate1, t_down0, t_down1, z_gate0, x_up0))
     k.build()
     a0, proj0, value0 = (out for _, out, _ in g0.saved)
+    table_arrays = [head_gain] + [v.out for v in angles.saves]
     y0, mid0 = y0.out, mid0.out
 
     k = Kernel(1)
-    x_up0, z_down0 = x_move(k, z_up0.out), z_gather_half(k, sh_down, t_down0.out, 0)
+    z_down0 = z_gather_half(k, sh_down, t_down0.out, 0)
     z_in1, z_out1 = z_gather_half(k, sh_in, t_in.out, 1), z_gather_half(k, sh_out, t_out.out, 1)
     z_gate1 = z_gather_half(k, sh_gate, t_gate1.out, 1)
+    z_down1a = z_gather_whole(k, sh_down, t_down1.out, 1, 0)
     x_down0, x_in1, x_out1 = (x_move(k, v.out) for v in (z_down0, z_in1, z_out1))
     rows, gain_load = load_all(k, mid0), gains_of(k, 0, t_gain.out)
     w_gate0 = Weight(k, "rows", z_gate0.out, None, True)
-    w_up0 = Weight(k, "rows", z_up0.out, x_up0.out)
+    w_up0 = Weight(k, "rows", z_up0.out, x_up0.out, True)
     w_down0 = Weight(k, "cols", z_down0.out, x_down0.out)
     g2 = Gather(
         k, rows.buf, (gain_load.buf, 1), [w_gate0, w_up0], epilogue="ffn", save=(0, 1, 2, 3)
     )
     s3 = Scatter(k, [g2.values[2]], [w_down0], rows.buf, low=True)
     z_rows = Save(k, s3.out)
-    k.do(x_up0.send, z_down0.send, z_in1.send, z_out1.send)
-    k.do(rows.wait, gain_load.wait, g2.begin)
-    k.do(z_down0.step, z_in1.step, z_out1.step, z_down0.step, z_gate1.send, z_in1.step, z_out1.step)
-    k.do(z_down0.wait, x_down0.send, x_up0.wait, w_up0.start, z_gate1.step, g2.loop)
-    k.do(z_gate1.step, z_in1.wait, x_in1.send, z_out1.wait, x_out1.send)
-    k.do(x_down0.wait, w_down0.start, s3.loop, s3.finish, z_rows.start)
-    k.do(*wait(x_in1, x_out1, z_gate1))
+    k.do(z_down0.send, rows.wait, gain_load.wait, g2.begin, z_down0.step, z_in1.send, z_out1.send)
+    k.do(z_down0.step, z_in1.step, z_out1.step, z_gate1.send, z_down0.wait, x_down0.send)
+    k.do(g2.loop, z_in1.step, z_out1.step, z_gate1.step, z_down1a.send)
+    k.do(z_in1.wait, x_in1.send, z_out1.wait, x_out1.send, z_gate1.step, z_down1a.step)
+    k.do(x_down0.wait, w_down0.start, s3.loop, z_down1a.step, s3.finish, z_rows.start)
+    k.do(*wait(x_in1, x_out1, z_gate1, z_down1a))
     k.build()
     m0, gate0, up0, hid0 = (out for _, out, _ in g2.saved)
     z_rows = z_rows.out
 
     k = Kernel(2)
     x_gate1, z_up1 = x_move(k, z_gate1.out), z_gather_half(k, sh_up, t_up.out, 1)
-    z_down1, x_up1 = z_gather_whole(k, sh_down, t_down1.out, 1), x_move(k, z_up1.out)
+    z_down1, x_up1 = z_gather_whole(k, sh_down, t_down1.out, 1, 1), x_move(k, z_up1.out)
     rows, gain_load = load_all(k, z_rows), gains_of(k, 1, t_gain.out)
     tables = [load_all(k, v) for v in table_arrays]
     w_in1 = Weight(k, "rows", z_in1.out, x_in1.out, True)
@@ -1301,7 +1352,7 @@
     cot = start_rows(k, 1, t_seq.out)
     w_gate1 = Weight(k, "rows", z_gate1.out, x_gate1.out, True)
     w_up1 = Weight(k, "rows", z_up1.out, x_up1.out, True)
-    w_down1 = Weight(k, "cols", z_down1.out, None, True)
+    w_down1 = Weight(k, "cols", z_down1a.out, z_down1.out, True, True)
     g6 = Gather(k, rows.buf, (gain_load.buf, 1), [w_gate1, w_up1], epilogue="ffn")
     g8 = Gather(
         k, cot.buf, None, [w_down1], [g6.values[0], g6.values[1]], trans=True, epilogue="ffn_back"
@@ -1343,7 +1394,7 @@
     k.do(r_gate1.send, rows.wait, g10.begin, q_up1.send, q_down1.send, g10.loop)
     k.do(q_up1.step, q_down1.step, y_load.wait, p_out1.run, p_out1.wait, r_out1.send)
     k.do(proj.wait, q_load.wait, k_load.wait, lambda: back.run(q_up1.step, q_down1.step))
-    k.do(q_up1.wait, *(v.start for v in head_gains))
+    k.do(*(v.start for v in head_gains))
     k.do(gain_load.wait, value.wait, s11.loop, a_load.wait, p_in1.run)
     k.do(s11.finish, d_z.start, gain10.start, p_in1.wait)
     k.do(*wait(q_down1, q_up1, r_gate1, r_out1))
@@ -1367,29 +1418,27 @@
     )
     p_down0 = Product(k, hid_load.buf, g12.full)
     p_gate0, p_up0 = Product(k, m_load.buf, g12.values[0]), Product(k, m_load.buf, g12.values[1])
-    r_down0 = x_half(k, p_down0.out)
+    q_down0, r_gate0 = sum_scatter(k, "cols", p_down0.out), x_slots(k, p_gate0.out, "rows")
     s13 = Scatter(
         k, g12.values, [w_gate0, w_up0], rows.buf, (value.buf, (gain_load.buf, 1)), True
     )
     d_mid0, gain01 = Save(k, s13.out), Save(k, s13.gain_grad)
     k.early += [q_gate1.load, q_out1.load, e_down1.load]
     k.do(r_in1.send, rows.wait, g12.begin, q_gate1.send, q_out1.send, m_up1.send, e_down1.send)
-    k.do(gate_load.wait, up_load.wait, g12.loop)
-    k.do(q_gate1.step, q_out1.step, hid_load.wait, p_down0.run, p_down0.wait, r_down0.send)
-    k.do(q_gate1.step, q_out1.step, r_in1.wait, q_in1.add)
-    k.do(s13.loop, q_in1.step, m_load.wait, p_gate0.run, q_in1.step, p_up0.run)
+    k.do(gate_load.wait, up_load.wait, q_gate1.step, q_out1.step, g12.loop, q_gate1.step)
+    k.do(q_out1.step, hid_load.wait, p_down0.run, p_down0.wait, q_down0.add)
+    k.do(r_in1.wait, q_in1.add, s13.loop, m_load.wait, p_gate0.run, p_gate0.wait, r_gate0.send)
+    k.do(q_in1.step, q_down0.step, p_up0.run, q_in1.step)
     k.do(value.wait, gain_load.wait, s13.finish, d_mid0.start, gain01.start)
-    k.do(p_gate0.wait, p_up0.wait)
-    k.do(*wait(q_gate1, q_out1, q_in1, e_down1, m_up1, r_down0))
+    k.do(q_down0.step, p_up0.wait)
+    k.do(*wait(q_gate1, q_out1, q_in1, e_down1, m_up1, q_down0, r_gate0))
     k.build()
     d_mid0, gain01 = d_mid0.out, gain01.out
 
     k = Kernel(6)
-    r_gate0 = x_slots(k, p_gate0.out, "rows")
-    q_down0 = sum_scatter(k, "cols", p_down0.out, r_down0.out)
     q_gate0 = sum_scatter(k, "rows", p_gate0.out, r_gate0.out)
     q_up0 = sum_scatter(k, "rows", p_up0.out)
-    m_up0 = x_move(k, q_up0.out, 1)
+    m_up0, m_down0 = x_move(k, q_up0.out, 1), x_move(k, q_down0.out, 1)
     e_gate1, e_out1, e_in1 = (Finish(k, v.out, 1) for v in (q_gate1, q_out1, q_in1))
     rows, gain_load = load_all(k, d_mid0), gains_of(k, 0, t_gain.out)
     x_load, taps = start_rows(k, 0, t_seq.out), load_all(k, conv_kernel)
@@ -1405,9 +1454,7 @@
     r_cols = x_slots(k, p_cols.out, "conv")
     q_out0, q_in0 = sum_scatter(k, "cols", p_out0.out, r_out0.out), sum_scatter(k, "rows", p_in0.out, r_in0.out)
     q_cols = sum_scatter(k, "conv", p_cols.out, r_cols.out)
-    e_down0, e_gate0, e_out0, e_in0 = (
-        Finish(k, v.out, 0) for v in (q_down0, q_gate0, q_out0, q_in0)
-    )
+    e_gate0, e_out0, e_in0 = (Finish(k, v.out, 0) for v in (q_gate0, q_out0, q_in0))
     s15 = Scatter(
         k, [back.d_proj, back.d_value], [w_in0, w_cols], rows.buf,
         (x_load.buf, (gain_load.buf, 0)), True, low=True,
@@ -1445,60 +1492,174 @@
         return [(sources, t_result.out.ref, {"section": 1 - s})], []
 
     t_result = Task(k, row_shape, "section", result_moves, 1)
-    k.early += [q_up0.load, q_down0.load, e_gate1.load, e_out1.load, e_in1.load]
-    k.do(r_gate0.send, rows.wait, g14.begin, q_up0.send, q_down0.send)
-    k.do(e_gate1.send, e_out1.send, e_in1.send, g14.loop)
-    k.do(q_up0.step, q_down0.step, y_load.wait, p_out0.run, p_out0.wait, r_out0.send)
+    k.early += [q_gate0.load, q_up0.load, e_gate1.load, e_out1.load, e_in1.load]
+    k.do(m_down0.send, rows.wait, g14.begin, q_gate0.send, q_up0.send)
+    k.do(e_gate1.send, e_out1.send, e_in1.send, q_gate0.step, g14.loop)
+    k.do(q_up0.step, q_gate0.step, y_load.wait, p_out0.run, p_out0.wait, r_out0.send)
     k.do(proj.wait, value.wait, taps.wait, back.run, a_load.wait)
     k.do(p_in0.run, p_cols.run, p_in0.wait, r_in0.send, p_cols.wait, r_cols.send)
-    k.do(r_gate0.wait, q_gate0.add, q_up0.step, q_down0.step)
-    k.do(x_load.wait, gain_load.wait, s15.loop, q_gate0.step, s15.finish, d_x.start)
+    k.do(q_gate0.wait, e_gate0.add, q_up0.step, r_out0.wait, q_out0.add)
+    k.do(x_load.wait, gain_load.wait, s15.loop, q_out0.step, s15.finish, d_x.start)
     k.do(fill_small, d_x.wait, t_result.send, small_out.wait, t_small.send)
-    k.do(q_up0.wait, m_up0.send, r_out0.wait, q_out0.add, r_in0.wait, q_in0.add)
-    k.do(r_cols.wait, q_cols.add, q_gate0.step, q_down0.wait, e_down0.add)
-    k.do(q_out0.step, q_in0.step, q_cols.step, t_small.wait, z_small.add)
-    k.do(q_gate0.wait, e_gate0.add, q_out0.step, q_in0.step, q_cols.step)
-    k.do(z_small.wait, t_total.add, q_out0.wait, e_out0.add, q_in0.wait, e_in0.add)
-    rest = (e_gate1, e_out1, e_in1, q_cols, e_down0, e_gate0, m_up0, e_out0, e_in0)
+    k.do(r_in0.wait, q_in0.add, r_cols.wait, q_cols.add, q_up0.wait, m_up0.send, q_out0.step)
+    k.do(q_in0.step, q_cols.step, t_small.wait, z_small.add, q_in0.step, q_cols.step)
+    k.do(q_out0.wait, e_out0.add, z_small.wait, t_total.add, q_in0.wait, e_in0.add)
+    rest = (e_gate1, e_out1, e_in1, q_cols, m_down0, e_gate0, m_up0, e_out0, e_in0)
     k.do(*wait(*rest, t_total, t_result))
     k.build()
 
-    def whole(zero, one):
-        kept = jnp.where(first, zero.out.array, one.out.array)
-        return kept.reshape(1, -1, kept.shape[-1]).astype(F32)
-
-    def slot_sum(value):
-        value = value.out.array.astype(F32)
-        return value if value.ndim == 2 else jnp.sum(value, axis=0)
-
-    up_zero, up_one = slot_sum(q_up0) + slot_sum(m_up0), slot_sum(q_up1) + slot_sum(m_up1)
-    d_x, y_rows, moved = d_x.out.array, y_rows.array, t_result.out.array
-    result = jnp.where(first, jnp.stack([d_x, moved]), jnp.stack([moved, y_rows]))
-    small = jnp.sum(t_total.out.array, axis=0)
-    gains_total = small[:4].reshape(2, 2, model_width)
-    gain_out = lax.dynamic_slice_in_dim(gains_total, lax.axis_index("section"), 1, 0)
-    kernel_out = lax.dynamic_slice_in_dim(
-        small[4 : 4 + tap_rows], tensor_index * channels, channels, 1
+    owned = [
+        ([e_in0], [e_in1], 1),
+        ([e_out0], [e_out1], 1),
+        ([e_gate0], [e_gate1], 1),
+        ([q_up0, m_up0], [q_up1, m_up1], 1),
+        ([q_down0, m_down0], [e_down1], 1),
+        ([q_cols], [q_cols], 0),
+    ]
+    return pack(
+        [(zero, one, lead) for zero, one, lead in owned], t_total, d_x.out, y_rows, t_result,
+        (norm_gain.shape, conv_kernel.shape, qk_gain.shape),
     )
-    cols_grad = slot_sum(q_cols)
-    split = channels + channels // 2
-    head_total = jnp.stack(
-        [
-            jnp.sum(v.reshape(-1, size), axis=0)
-            for v in (small[7, :channels], small[7, channels:split])
-        ]
-    )
-    return (
-        result[None],
-        gain_out,
-        whole(e_in0, e_in1),
-        whole(e_out0, e_out1),
-        whole(e_gate0, e_gate1),
-        jnp.where(first, up_zero, up_one)[None],
-        whole(e_down0, e_down1),
-        cols_grad,
-        kernel_out,
-        head_total,
+
+
+def slot_free(val, shape):
+    value = val.out.array
+    if value.ndim == 3 and value.shape[0] * value.shape[1] != shape[0]:
+        value = jnp.sum(value.astype(F32), axis=0).astype(BF)
+    return value.reshape(shape)
+
+
+def pack_kernel(plan, *refs):
+    n_in, leads, terms, tap_rows = plan
+    ins, rest = refs[:n_in], refs[n_in:]
+    result, gain_out, *grads, cols, taps, heads = rest[: len(leads) + 4]
+    grads = [*grads, cols]
+    room = iter(rest[len(leads) + 4 :])
+    own_v, moved_v, small_v, *bufs = (next(room) for _ in range(3 + len(terms)))
+    out_v = [next(room) for _ in leads]
+    load_sem, store_sem = room
+    s, t = lax.axis_index("section"), lax.axis_index("tensor")
+    small, d_x, y_rows, moved, *parts = ins
+
+    def either(cond, zero, one, dst, sem):
+        if zero is not None:
+            pl.when(cond)(pltpu.make_async_copy(zero, dst, sem).start)
+        if one is not None:
+            pl.when(jnp.logical_not(cond))(pltpu.make_async_copy(one, dst, sem).start)
+
+    first = s == 0
+    either(first, d_x, y_rows, own_v, load_sem.at[0])
+    pltpu.make_async_copy(moved, moved_v, load_sem.at[1]).start()
+    pltpu.make_async_copy(small, small_v, load_sem.at[2]).start()
+    for j, (zero, one, _) in enumerate(terms):
+        either(
+            first,
+            None if zero is None else parts[zero],
+            None if one is None else parts[one],
+            bufs[j],
+            load_sem.at[3 + j],
+        )
+    for j, (zero, one, i) in enumerate(terms):
+        arrive = pltpu.make_async_copy(parts[one if zero is None else zero], bufs[j], load_sem.at[3 + j])
+        begins = j == 0 or terms[j - 1][2] != i
+
+        def put(j=j, i=i, begins=begins):
+            value = bufs[j][...].astype(F32)
+            value = value if begins else out_v[i][...] + value
+            out_v[i][...] = value
+
+        if zero is None or one is None:
+            cond = first if one is None else jnp.logical_not(first)
+
+            @pl.when(cond)
+            def _(arrive=arrive, put=put):
+                arrive.wait()
+                put()
+        else:
+            arrive.wait()
+            put()
+        if j + 1 == len(terms) or terms[j + 1][2] != i:
+            dst = grads[i].at[0] if leads[i] else grads[i]
+            pltpu.make_async_copy(out_v[i], dst, store_sem.at[i]).start()
+    pltpu.make_async_copy(d_x, own_v, load_sem.at[0]).wait()
+    pltpu.make_async_copy(moved, moved_v, load_sem.at[1]).wait()
+    n = len(leads)
+    stores = [
+        pltpu.make_async_copy(own_v, result.at[0, s], store_sem.at[n]),
+        pltpu.make_async_copy(moved_v, result.at[0, 1 - s], store_sem.at[n + 1]),
+    ]
+    for store in stores:
+        store.start()
+    pltpu.make_async_copy(small, small_v, load_sem.at[2]).wait()
+    total = small_v[0]
+    for i in range(1, small_v.shape[0]):
+        total = total + small_v[i]
+    gain_out[0] = jnp.where(first, total[0:2], total[2:4])
+    channels, size = taps.shape[1], heads.shape[1]
+    chosen = total[4 : 4 + tap_rows, 0:channels]
+    for i in range(1, total.shape[1] // channels):
+        chosen = jnp.where(t == i, total[4 : 4 + tap_rows, i * channels : (i + 1) * channels], chosen)
+    taps[...] = chosen
+    at = 0
+    for row, width in enumerate((channels, channels // 2)):
+        value = total[7:8, at : at + size]
+        for i in range(1, width // size):
+            value = value + total[7:8, at + i * size : at + (i + 1) * size]
+        heads[row : row + 1, :] = value
+        at += width
+    for i, store in enumerate(leads):
+        dst = grads[i].at[0] if store else grads[i]
+        pltpu.make_async_copy(out_v[i], dst, store_sem.at[i]).wait()
+    for store in stores:
+        store.wait()
+
+
+def pack(owned, small, d_x, y_rows, moved, shapes):
+    gain_shape, tap_shape, head_shape = shapes
+    parts, terms, leads, out_shapes = [], [], [], []
+    for i, (zero, one, lead) in enumerate(owned):
+        whole = zero[0].out.shape
+        if lead and len(whole) == 3 and isinstance(zero[0], Finish):
+            shape = (whole[0] * whole[1], whole[2])
+        else:
+            shape = whole[-2:]
+        shape = tuple(shape)
+        leads.append(lead)
+        out_shapes.append(shape)
+        for j in range(max(len(zero), len(one))):
+            pair = []
+            for side in (zero, one):
+                if j < len(side):
+                    parts.append(slot_free(side[j], shape))
+                    pair.append(len(parts) - 1)
+                else:
+                    pair.append(None)
+            terms.append((*pair, i))
+    operands = [small.out.array, d_x.array, y_rows.array, moved.out.array, *parts]
+    rows = d_x.shape
+    smem = pl.BlockSpec(memory_space=pltpu.VMEM)
+    out_shape = [jax.ShapeDtypeStruct((1, 2) + rows, BF), jax.ShapeDtypeStruct(gain_shape, F32)]
+    out_shape += [
+        jax.ShapeDtypeStruct((1,) + v if lead else v, F32) for v, lead in zip(out_shapes, leads)
+    ]
+    out_shape += [jax.ShapeDtypeStruct(v, F32) for v in (tap_shape, head_shape)]
+    n = len(leads)
+    return tuple(
+        pl.pallas_call(
+            functools.partial(
+                pack_kernel, (len(operands), tuple(leads), tuple(terms), tap_shape[0])
+            ),
+            out_shape=out_shape,
+            in_specs=[ANY] * len(operands),
+            out_specs=[ANY, smem] + [ANY] * n + [smem] * 2,
+            scratch_shapes=[pltpu.VMEM(rows, BF)] * 2
+            + [pltpu.VMEM(small.out.shape, F32)]
+            + [pltpu.VMEM(out_shapes[i], BF) for _, _, i in terms]
+            + [pltpu.VMEM(v, F32) for v in out_shapes]
+            + [DMA((3 + len(terms),)), DMA((n + 2,))],
+            compiler_params=pltpu.CompilerParams(vmem_limit_bytes=VMEM_BYTES),
+            name="pack",
+        )(*operands)
     )
 
 

time: 566 us -> 575 us (1.016)
  Pallas kernels: 540 us -> 562 us
  other arithmetic: 12.5 us -> 0 us
    pallas_call x7, Pallas kernels: 540 us -> 558 us  [build(): pl.pallas_call(self.body, out_shape=[jax.ShapeDtypeStruct(v.shape, v.dtyp...]
where the time goes in v8:
time: 575 us; the launch traced here: 565 us
  Pallas kernels  562 us (98%)
    pallas_call x7, Pallas kernels, build(): pl.pallas_call(self.body, out_shape=[jax.ShapeDtypeStruct(v.shape, v.dtyp...  558 us

profile of v8, /device:TPU:0, one launch (start us, length us, event | category | flops | bytes accessed | tf_op | source)
XLA Modules:
  0.0 564.7 jit_solution(4507098207114265828)
XLA Ops:
  0.6 0.7 tile.4
  1.3 0.7 tile.10.refs_8_
  2.0 102.2 %stage0.1 = (bf16[128,512]{1,0:T(8,128)(2,1)}, bf16[128,256]{1,0:T(8,128)(2,1)}, bf16[128,1152]{1,0:T(8,128)(2,1)}, bf16[256,1152]{1,0:T(8,128)(2,1)}, bf16[576,...) custom-call(bf16[2,256,1024]{2,1,0:T(8,128)(2,1)} %bitcast.14, ...), custom_call_target="tpu_custom_call" | custom-call | tf_op jit(solution)/shard_map/stage0/pallas_call | solution.py:154
  104.2 80.5 %stage1.1 = (bf16[4,576,256]{2,1,0:T(8,128)(2,1)}, bf16[4,128,512]{2,1,0:T(8,128)(2,1)}, bf16[4,128,256]{2,1,0:T(8,128)(2,1)}, bf16[4,128,1152]{2,1,0:T(8,128)(2...) custom-call(bf16[1152,256]{1,0:T(8,128)(2,1)} %bitcast.18, ...), custom_call_target="tpu_custom_call" | custom-call | tf_op jit(solution)/shard_map/stage1/pallas_call | solution.py:154
  184.7 57.4 %stage2.1 = (bf16[4,128,1152]{2,1,0:T(8,128)(2,1)}, bf16[4,128,1152]{2,1,0:T(8,128)(2,1)}, bf16[4,576,256]{2,1,0:T(8,128)(2,1)}, bf16[4,128,1152]{2,1,0:T(8,128)...) custom-call(bf16[4,128,1152]{2,1,0:T(8,128)(2,1)} %get-tuple-element, ...), custom_call_target="tpu_custom_call" | custom-call | tf_op jit(solution)/shard_map/stage2/pallas_call | solution.py:154
  242.1 62.1 %stage3.1 = (bf16[1152,1024]{1,0:T(8,128)(2,1)}, bf16[1024,1152]{1,0:T(8,128)(2,1)}, bf16[1024,1152]{1,0:T(8,128)(2,1)}, bf16[576,1024]{1,0:T(8,128)(2,1)}, bf16...) custom-call(f32[256,1024]{1,0:T(8,128)} %get-tuple-element.117.refs_0_, f32[2,1024]{1,0:T(2,128)} %bitcast.34, ...), custom_call_target="tpu_custom_call" | custom-call | tf_op jit(solution)/shard_map/stage3/pallas_call | solution.py:154
  304.2 64.4 %stage4.1 = (bf16[576,256]{1,0:T(8,128)(2,1)}, bf16[4,128,1152]{2,1,0:T(8,128)(2,1)}, bf16[256,1152]{1,0:T(8,128)(2,1)}, bf16[256,1024]{1,0:T(8,128)(2,1)}, bf16...) custom-call(bf16[1152,1024]{1,0:T(8,128)(2,1)} %get-tuple-element.12, ...), custom_call_target="tpu_custom_call" | custom-call | tf_op jit(solution)/shard_map/stage4/pallas_call | solution.py:154
  368.6 89.9 %stage5.1 = (bf16[128,1152]{1,0:T(8,128)(2,1)}, bf16[256,1152]{1,0:T(8,128)(2,1)}, bf16[128,256]{1,0:T(8,128)(2,1)}, bf16[4,128,512]{2,1,0:T(8,128)(2,1)}, bf16[...) custom-call(bf16[1024,1152]{1,0:T(8,128)(2,1)} %get-tuple-element.12, ...), custom_call_target="tpu_custom_call" | custom-call | tf_op jit(solution)/shard_map/stage5/pallas_call | solution.py:154
  458.5 101.2 %stage6.1 = (bf16[128,1152]{1,0:T(8,128)(2,1)}, bf16[256,1152]{1,0:T(8,128)(2,1)}, bf16[256,1152]{1,0:T(8,128)(2,1)}, bf16[1152,256]{1,0:T(8,128)(2,1)}, bf16[2,...) custom-call(bf16[1024,1152]{1,0:T(8,128)(2,1)} %get-tuple-element.14, ...), custom_call_target="tpu_custom_call" | custom-call | tf_op jit(solution)/shard_map/stage6/pallas_call | solution.py:154
  559.6 4.6 pack.1

commit v9 on v8

--- a/solution.py
+++ b/solution.py
@@ -1271,7 +1271,7 @@
     z_in0, z_out0 = z_gather_half(k, sh_in, t_in.out, 0), z_gather_half(k, sh_out, t_out.out, 0)
     z_gate0 = z_gather_whole(k, sh_gate, t_gate0.out, 0)
     z_up0 = z_gather_half(k, sh_up, t_up.out, 0)
-    x_cols, x_in0, x_out0, x_up0 = (x_move(k, v.out) for v in (z_cols, z_in0, z_out0, z_up0))
+    x_cols, x_in0, x_out0 = (x_move(k, v.out) for v in (z_cols, z_in0, z_out0))
     x_load, gain_load = start_rows(k, 0, t_seq.out, False), gains_of(k, 0, t_gain.out, False)
     taps = load_all(k, conv_kernel)
     angles = Angles(k, length, size, 128)
@@ -1282,44 +1282,43 @@
     y0 = Save(k, conv.y)
     s1 = Scatter(k, [conv.y], [w_out0], x_load.buf)
     mid0 = Save(k, s1.out)
-    k.do(t_in.send, t_out.send, z_cols.send, t_up.send, t_gain.send, t_seq.send)
-    k.do(t_in.wait, z_in0.send, t_out.wait, z_out0.send)
-    k.do(z_cols.step, z_in0.step, z_out0.step, t_up.wait, z_up0.send)
-    k.do(z_cols.step, z_in0.step, z_out0.step, z_cols.wait, x_cols.send, z_in0.wait, x_in0.send)
-    k.do(z_out0.wait, x_out0.send, t_gate0.send, t_gate1.send)
-    k.do(t_gain.wait, gain_load.start, t_seq.wait, x_load.start, z_up0.step)
-    k.do(gain_load.wait, x_load.wait, g0.begin, z_up0.step, angles.run)
-    k.do(z_up0.wait, x_up0.send, t_down0.send, t_down1.send)
-    k.do(x_cols.wait, w_cols.start, x_in0.wait, w_in0.start, t_gate0.wait, z_gate0.send)
-    k.do(g0.loop, z_gate0.step, taps.wait, conv.run, y0.start)
-    k.do(x_out0.wait, w_out0.start, s1.loop, z_gate0.step, s1.finish, mid0.start)
-    k.do(*wait(t_gate1, t_down0, t_down1, z_gate0, x_up0))
+    k.do(t_in.send, t_out.send, z_cols.send, t_gate0.send, t_gate1.send, t_gain.send, t_seq.send)
+    k.do(t_in.wait, z_in0.send, t_out.wait, z_out0.send, z_cols.step, z_in0.step, z_out0.step)
+    k.do(z_cols.step, z_in0.step, z_out0.step, t_gate0.wait, z_gate0.send)
+    k.do(z_cols.wait, x_cols.send, z_in0.wait, x_in0.send, z_out0.wait, x_out0.send)
+    k.do(t_up.send, t_down0.send, t_down1.send)
+    k.do(t_gain.wait, gain_load.start, t_seq.wait, x_load.start, gain_load.wait, x_load.wait)
+    k.do(g0.begin, angles.run, z_gate0.step)
+    k.do(x_cols.wait, w_cols.start, x_in0.wait, w_in0.start, z_gate0.step)
+    k.do(g0.loop, t_up.wait, z_up0.send, taps.wait, conv.run, y0.start)
+    k.do(x_out0.wait, w_out0.start, s1.loop, z_up0.step, s1.finish, mid0.start, z_up0.step)
+    k.do(*wait(t_gate1, t_down0, t_down1, z_gate0, z_up0))
     k.build()
     a0, proj0, value0 = (out for _, out, _ in g0.saved)
     table_arrays = [head_gain] + [v.out for v in angles.saves]
     y0, mid0 = y0.out, mid0.out
 
     k = Kernel(1)
-    z_down0 = z_gather_half(k, sh_down, t_down0.out, 0)
+    x_up0, z_down0 = x_move(k, z_up0.out), z_gather_half(k, sh_down, t_down0.out, 0)
     z_in1, z_out1 = z_gather_half(k, sh_in, t_in.out, 1), z_gather_half(k, sh_out, t_out.out, 1)
     z_gate1 = z_gather_half(k, sh_gate, t_gate1.out, 1)
     z_down1a = z_gather_whole(k, sh_down, t_down1.out, 1, 0)
     x_down0, x_in1, x_out1 = (x_move(k, v.out) for v in (z_down0, z_in1, z_out1))
     rows, gain_load = load_all(k, mid0), gains_of(k, 0, t_gain.out)
     w_gate0 = Weight(k, "rows", z_gate0.out, None, True)
-    w_up0 = Weight(k, "rows", z_up0.out, x_up0.out, True)
+    w_up0 = Weight(k, "rows", z_up0.out, x_up0.out)
     w_down0 = Weight(k, "cols", z_down0.out, x_down0.out)
     g2 = Gather(
         k, rows.buf, (gain_load.buf, 1), [w_gate0, w_up0], epilogue="ffn", save=(0, 1, 2, 3)
     )
     s3 = Scatter(k, [g2.values[2]], [w_down0], rows.buf, low=True)
     z_rows = Save(k, s3.out)
-    k.do(z_down0.send, rows.wait, gain_load.wait, g2.begin, z_down0.step, z_in1.send, z_out1.send)
-    k.do(z_down0.step, z_in1.step, z_out1.step, z_gate1.send, z_down0.wait, x_down0.send)
-    k.do(g2.loop, z_in1.step, z_out1.step, z_gate1.step, z_down1a.send)
-    k.do(z_in1.wait, x_in1.send, z_out1.wait, x_out1.send, z_gate1.step, z_down1a.step)
-    k.do(x_down0.wait, w_down0.start, s3.loop, z_down1a.step, s3.finish, z_rows.start)
-    k.do(*wait(x_in1, x_out1, z_gate1, z_down1a))
+    k.do(x_up0.send, z_down0.send, rows.wait, gain_load.wait, g2.begin, z_down0.step)
+    k.do(z_in1.send, z_out1.send, z_down0.step, z_in1.step, z_out1.step, z_gate1.send)
+    k.do(z_down0.wait, x_down0.send, z_down1a.send, x_up0.wait, w_up0.start, z_in1.step, z_out1.step)
+    k.do(g2.loop, z_gate1.step, z_down1a.step, z_in1.wait, x_in1.send, z_out1.wait, x_out1.send)
+    k.do(x_down0.wait, w_down0.start, s3.loop, z_gate1.step, z_down1a.step)
+    k.do(s3.finish, z_rows.start, *wait(x_in1, x_out1, z_gate1, z_down1a))
     k.build()
     m0, gate0, up0, hid0 = (out for _, out, _ in g2.saved)
     z_rows = z_rows.out
@@ -1390,11 +1389,11 @@
     )
     d_z, gain10 = Save(k, s11.out), Save(k, s11.gain_grad)
     head_gains = [Save(k, back.q_gain), Save(k, back.k_gain)]
-    k.early += [q_up1.load, q_down1.load]
-    k.do(r_gate1.send, rows.wait, g10.begin, q_up1.send, q_down1.send, g10.loop)
-    k.do(q_up1.step, q_down1.step, y_load.wait, p_out1.run, p_out1.wait, r_out1.send)
+    k.early += [q_down1.load, q_up1.load]
+    k.do(r_gate1.send, rows.wait, g10.begin, q_down1.send, q_up1.send, g10.loop)
+    k.do(q_down1.step, y_load.wait, p_out1.run, p_out1.wait, r_out1.send)
     k.do(proj.wait, q_load.wait, k_load.wait, lambda: back.run(q_up1.step, q_down1.step))
-    k.do(*(v.start for v in head_gains))
+    k.do(q_up1.step, *(v.start for v in head_gains))
     k.do(gain_load.wait, value.wait, s11.loop, a_load.wait, p_in1.run)
     k.do(s11.finish, d_z.start, gain10.start, p_in1.wait)
     k.do(*wait(q_down1, q_up1, r_gate1, r_out1))
@@ -1418,27 +1417,28 @@
     )
     p_down0 = Product(k, hid_load.buf, g12.full)
     p_gate0, p_up0 = Product(k, m_load.buf, g12.values[0]), Product(k, m_load.buf, g12.values[1])
-    q_down0, r_gate0 = sum_scatter(k, "cols", p_down0.out), x_slots(k, p_gate0.out, "rows")
+    r_down0 = x_half(k, p_down0.out)
     s13 = Scatter(
         k, g12.values, [w_gate0, w_up0], rows.buf, (value.buf, (gain_load.buf, 1)), True
     )
     d_mid0, gain01 = Save(k, s13.out), Save(k, s13.gain_grad)
     k.early += [q_gate1.load, q_out1.load, e_down1.load]
     k.do(r_in1.send, rows.wait, g12.begin, q_gate1.send, q_out1.send, m_up1.send, e_down1.send)
-    k.do(gate_load.wait, up_load.wait, q_gate1.step, q_out1.step, g12.loop, q_gate1.step)
-    k.do(q_out1.step, hid_load.wait, p_down0.run, p_down0.wait, q_down0.add)
-    k.do(r_in1.wait, q_in1.add, s13.loop, m_load.wait, p_gate0.run, p_gate0.wait, r_gate0.send)
-    k.do(q_in1.step, q_down0.step, p_up0.run, q_in1.step)
-    k.do(value.wait, gain_load.wait, s13.finish, d_mid0.start, gain01.start)
-    k.do(q_down0.step, p_up0.wait)
-    k.do(*wait(q_gate1, q_out1, q_in1, e_down1, m_up1, q_down0, r_gate0))
+    k.do(gate_load.wait, up_load.wait, g12.loop, q_gate1.step, q_out1.step)
+    k.do(hid_load.wait, p_down0.run, p_down0.wait, r_down0.send, r_in1.wait, q_in1.add)
+    k.do(s13.loop, q_gate1.step, q_out1.step, q_in1.step)
+    k.do(m_load.wait, p_gate0.run, p_up0.run, q_in1.step, value.wait, gain_load.wait)
+    k.do(s13.finish, d_mid0.start, gain01.start, p_gate0.wait, p_up0.wait)
+    k.do(*wait(q_gate1, q_out1, q_in1, e_down1, m_up1, r_down0))
     k.build()
     d_mid0, gain01 = d_mid0.out, gain01.out
 
     k = Kernel(6)
+    r_gate0 = x_slots(k, p_gate0.out, "rows")
     q_gate0 = sum_scatter(k, "rows", p_gate0.out, r_gate0.out)
+    q_down0 = sum_scatter(k, "cols", p_down0.out, r_down0.out)
     q_up0 = sum_scatter(k, "rows", p_up0.out)
-    m_up0, m_down0 = x_move(k, q_up0.out, 1), x_move(k, q_down0.out, 1)
+    m_up0 = x_move(k, q_up0.out, 1)
     e_gate1, e_out1, e_in1 = (Finish(k, v.out, 1) for v in (q_gate1, q_out1, q_in1))
     rows, gain_load = load_all(k, d_mid0), gains_of(k, 0, t_gain.out)
     x_load, taps = start_rows(k, 0, t_seq.out), load_all(k, conv_kernel)
@@ -1454,7 +1454,9 @@
     r_cols = x_slots(k, p_cols.out, "conv")
     q_out0, q_in0 = sum_scatter(k, "cols", p_out0.out, r_out0.out), sum_scatter(k, "rows", p_in0.out, r_in0.out)
     q_cols = sum_scatter(k, "conv", p_cols.out, r_cols.out)
-    e_gate0, e_out0, e_in0 = (Finish(k, v.out, 0) for v in (q_gate0, q_out0, q_in0))
+    e_down0, e_gate0, e_out0, e_in0 = (
+        Finish(k, v.out, 0) for v in (q_down0, q_gate0, q_out0, q_in0)
+    )
     s15 = Scatter(
         k, [back.d_proj, back.d_value], [w_in0, w_cols], rows.buf,
         (x_load.buf, (gain_load.buf, 0)), True, low=True,
@@ -1492,19 +1494,20 @@
         return [(sources, t_result.out.ref, {"section": 1 - s})], []
 
     t_result = Task(k, row_shape, "section", result_moves, 1)
-    k.early += [q_gate0.load, q_up0.load, e_gate1.load, e_out1.load, e_in1.load]
-    k.do(m_down0.send, rows.wait, g14.begin, q_gate0.send, q_up0.send)
-    k.do(e_gate1.send, e_out1.send, e_in1.send, q_gate0.step, g14.loop)
-    k.do(q_up0.step, q_gate0.step, y_load.wait, p_out0.run, p_out0.wait, r_out0.send)
-    k.do(proj.wait, value.wait, taps.wait, back.run, a_load.wait)
+    k.early += [q_up0.load, q_down0.load, e_gate1.load, e_out1.load, e_in1.load]
+    k.do(r_gate0.send, rows.wait, g14.begin, q_up0.send, q_down0.send)
+    k.do(e_gate1.send, e_out1.send, e_in1.send, g14.loop)
+    k.do(y_load.wait, p_out0.run, p_out0.wait, r_out0.send, q_up0.step)
+    k.do(proj.wait, value.wait, taps.wait, back.run, q_down0.step, a_load.wait)
     k.do(p_in0.run, p_cols.run, p_in0.wait, r_in0.send, p_cols.wait, r_cols.send)
-    k.do(q_gate0.wait, e_gate0.add, q_up0.step, r_out0.wait, q_out0.add)
-    k.do(x_load.wait, gain_load.wait, s15.loop, q_out0.step, s15.finish, d_x.start)
-    k.do(fill_small, d_x.wait, t_result.send, small_out.wait, t_small.send)
-    k.do(r_in0.wait, q_in0.add, r_cols.wait, q_cols.add, q_up0.wait, m_up0.send, q_out0.step)
-    k.do(q_in0.step, q_cols.step, t_small.wait, z_small.add, q_in0.step, q_cols.step)
-    k.do(q_out0.wait, e_out0.add, z_small.wait, t_total.add, q_in0.wait, e_in0.add)
-    rest = (e_gate1, e_out1, e_in1, q_cols, m_down0, e_gate0, m_up0, e_out0, e_in0)
+    k.do(r_gate0.wait, q_gate0.add, x_load.wait, gain_load.wait, s15.loop, q_up0.step)
+    k.do(q_down0.step, s15.finish, d_x.start, fill_small, d_x.wait, t_result.send)
+    k.do(small_out.wait, t_small.send, q_gate0.step, r_out0.wait, q_out0.add, r_in0.wait, q_in0.add)
+    k.do(r_cols.wait, q_cols.add, q_up0.wait, m_up0.send, q_down0.wait, e_down0.add)
+    k.do(q_gate0.step, q_out0.step, q_in0.step, q_cols.step, t_small.wait, z_small.add)
+    k.do(q_gate0.wait, e_gate0.add, q_out0.step, q_in0.step, q_cols.step)
+    k.do(z_small.wait, t_total.add, q_out0.wait, e_out0.add, q_in0.wait, e_in0.add)
+    rest = (e_gate1, e_out1, e_in1, q_cols, e_down0, e_gate0, m_up0, e_out0, e_in0)
     k.do(*wait(*rest, t_total, t_result))
     k.build()
 
@@ -1513,7 +1516,7 @@
         ([e_out0], [e_out1], 1),
         ([e_gate0], [e_gate1], 1),
         ([q_up0, m_up0], [q_up1, m_up1], 1),
-        ([q_down0, m_down0], [e_down1], 1),
+        ([e_down0], [e_down1], 1),
         ([q_cols], [q_cols], 0),
     ]
     return pack(

time: 575 us -> 539 us (0.937)
  Pallas kernels: 562 us -> 527 us
    pallas_call x7, Pallas kernels: 558 us -> 523 us  [build(): pl.pallas_call(self.body, out_shape=[jax.ShapeDtypeStruct(v.shape, v.dtyp...]
where the time goes in v9:
time: 539 us; the launch traced here: 530 us
  Pallas kernels  527 us (98%)
    pallas_call x7, Pallas kernels, build(): pl.pallas_call(self.body, out_shape=[jax.ShapeDtypeStruct(v.shape, v.dtyp...  523 us

profile of v9, /device:TPU:0, one launch (start us, length us, event | category | flops | bytes accessed | tf_op | source)
XLA Modules:
  0.0 529.9 jit_solution(7152640523083476299)
XLA Ops:
  0.6 0.7 tile.4
  1.3 0.7 tile.10.refs_8_
  2.0 90.4 %stage0.1 = (bf16[128,512]{1,0:T(8,128)(2,1)}, bf16[128,256]{1,0:T(8,128)(2,1)}, bf16[128,1152]{1,0:T(8,128)(2,1)}, bf16[256,1152]{1,0:T(8,128)(2,1)}, bf16[576,...) custom-call(bf16[2,256,1024]{2,1,0:T(8,128)(2,1)} %bitcast.15, ...), custom_call_target="tpu_custom_call" | custom-call | tf_op jit(solution)/shard_map/stage0/pallas_call | solution.py:154
  92.4 80.2 %stage1.1 = (bf16[4,128,1152]{2,1,0:T(8,128)(2,1)}, bf16[4,576,256]{2,1,0:T(8,128)(2,1)}, bf16[4,128,512]{2,1,0:T(8,128)(2,1)}, bf16[4,128,256]{2,1,0:T(8,128)(2...) custom-call(bf16[4,128,1152]{2,1,0:T(8,128)(2,1)} %get-tuple-element, ...), custom_call_target="tpu_custom_call" | custom-call | tf_op jit(solution)/shard_map/stage1/pallas_call | solution.py:154
  172.7 57.2 %stage2.1 = (bf16[4,128,1152]{2,1,0:T(8,128)(2,1)}, bf16[4,128,1152]{2,1,0:T(8,128)(2,1)}, bf16[4,576,256]{2,1,0:T(8,128)(2,1)}, bf16[4,128,1152]{2,1,0:T(8,128)...) custom-call(bf16[4,128,1152]{2,1,0:T(8,128)(2,1)} %get-tuple-element, ...), custom_call_target="tpu_custom_call" | custom-call | tf_op jit(solution)/shard_map/stage2/pallas_call | solution.py:154
  229.9 61.6 %stage3.1 = (bf16[1152,1024]{1,0:T(8,128)(2,1)}, bf16[1024,1152]{1,0:T(8,128)(2,1)}, bf16[1024,1152]{1,0:T(8,128)(2,1)}, bf16[576,1024]{1,0:T(8,128)(2,1)}, bf16...) custom-call(f32[256,1024]{1,0:T(8,128)} %get-tuple-element.116.refs_0_, f32[2,1024]{1,0:T(2,128)} %bitcast.36, ...), custom_call_target="tpu_custom_call" | custom-call | tf_op jit(solution)/shard_map/stage3/pallas_call | solution.py:154
  291.5 64.0 %stage4.1 = (bf16[576,256]{1,0:T(8,128)(2,1)}, bf16[4,128,1152]{2,1,0:T(8,128)(2,1)}, bf16[256,1152]{1,0:T(8,128)(2,1)}, bf16[256,1024]{1,0:T(8,128)(2,1)}, bf16...) custom-call(bf16[1152,1024]{1,0:T(8,128)(2,1)} %get-tuple-element.12, ...), custom_call_target="tpu_custom_call" | custom-call | tf_op jit(solution)/shard_map/stage4/pallas_call | solution.py:154
  355.6 61.8 %stage5.1 = (bf16[128,1152]{1,0:T(8,128)(2,1)}, bf16[256,1152]{1,0:T(8,128)(2,1)}, bf16[128,256]{1,0:T(8,128)(2,1)}, bf16[4,128,512]{2,1,0:T(8,128)(2,1)}, bf16[...) custom-call(bf16[1024,1152]{1,0:T(8,128)(2,1)} %get-tuple-element.12, ...), custom_call_target="tpu_custom_call" | custom-call | tf_op jit(solution)/shard_map/stage5/pallas_call | solution.py:154
  417.4 107.4 %stage6.1 = (bf16[4,128,1152]{2,1,0:T(8,128)(2,1)}, bf16[128,1152]{1,0:T(8,128)(2,1)}, bf16[576,256]{1,0:T(8,128)(2,1)}, bf16[256,1152]{1,0:T(8,128)(2,1)}, bf16...) custom-call(bf16[1024,1152]{1,0:T(8,128)(2,1)} %get-tuple-element.14, ...), custom_call_target="tpu_custom_call" | custom-call | tf_op jit(solution)/shard_map/stage6/pallas_call | solution.py:154
  524.8 4.6 pack.1

commit v10 on v9

--- a/solution.py
+++ b/solution.py
@@ -93,7 +93,7 @@
 class Kernel:
     def __init__(self, cid):
         self.cid, self.ins, self.arrays, self.outs, self.room = cid, [], [], [], []
-        self.early, self.steps, self.late, self.axes = [], [], [], {"tensor"}
+        self.early, self.steps, self.late, self.axes = [], [], [], set()
         self.once = []
 
     def input(self, array):
@@ -139,16 +139,27 @@
 
     def greet(self):
         s, d, t = spot()
-        peers = []
+        _, sib, cross, diag = places()
+        barrier = pltpu.get_barrier_semaphore()
+        peers = [{"tensor": sib}, {"tensor": cross}]
+        if "tensor" in self.axes:
+            peers.append({"tensor": diag})
         if "section" in self.axes:
             peers.append({"section": 1 - s})
         if "dp" in self.axes:
-            peers += [{"dp": (d + k) % dp_size()} for k in range(1, dp_size())]
-        peers += [{"tensor": (t + k) % 4} for k in range(1, 4)]
-        barrier = pltpu.get_barrier_semaphore()
+            peers += [{"dp": (d + i) % dp_size()} for i in range(1, dp_size())]
+
+        def signal(peer):
+            pl.semaphore_signal(barrier, inc=1, device_id=peer, device_id_type=MESH)
+
         for peer in peers:
-            pl.semaphore_signal(barrier, inc=1, device_id=peer, device_id_type=MESH)
-        pl.semaphore_wait(barrier, len(peers))
+            signal(peer)
+        expected = len(peers)
+        if "line" in self.axes and "dp" not in self.axes:
+            pl.when(d < 3)(lambda: signal({"dp": (d + 1) % 4}))
+            pl.when(d > 0)(lambda: signal({"dp": (d + 3) % 4}))
+            expected = expected + (d + 2) // 3 + (5 - d) // 3
+        pl.semaphore_wait(barrier, expected)
 
     def build(self):
         result = pl.pallas_call(
@@ -283,7 +294,7 @@
 
 class Line(Task):
     def __init__(self, k, out, out_dtype=BF, n_local=1):
-        super().__init__(k, out, "dp", None, 6, n_local, out_dtype)
+        super().__init__(k, out, "line", None, 6, n_local, out_dtype)
         self.send_sem, self.recv_sem = k.sem(2, 3), k.sem(2, 3)
         self.phase = 0
 
@@ -1358,20 +1369,17 @@
     )
     p_down1 = Product(k, g6.values[2], g8.full)
     p_gate1, p_up1 = Product(k, g6.full, g8.values[0]), Product(k, g6.full, g8.values[1])
-    r_down1 = x_half(k, p_down1.out)
     s7 = Scatter(k, [g6.values[2]], [w_down1], rows.buf, low=True)
     s9 = Scatter(k, g8.values, [w_gate1, w_up1], cot.buf, (rows.buf, (gain_load.buf, 1)), True)
     y_rows, d_mid1, gain11 = Save(k, s7.out), Save(k, s9.out), Save(k, s9.gain_grad)
-    k.do(rows.wait, gain_load.wait, g6.begin, cot.wait, g8.begin, g6.loop)
-    k.do(g8.loop, p_down1.run, p_down1.wait, r_down1.send)
-    k.do(s9.loop, s7.loop, p_gate1.run, p_up1.run, s9.finish, d_mid1.start, gain11.start)
-    k.do(s7.finish, y_rows.start, p_gate1.wait, p_up1.wait)
-    k.do(*wait(r_down1))
+    k.do(rows.wait, gain_load.wait, g6.begin, cot.wait, g8.begin, g6.loop, s7.loop, g8.loop)
+    k.do(s9.loop, p_down1.run, s7.finish, y_rows.start, p_gate1.run, p_up1.run)
+    k.do(s9.finish, d_mid1.start, gain11.start, p_down1.wait, p_gate1.wait, p_up1.wait)
     k.build()
     y_rows, d_mid1, gain11 = y_rows.out, d_mid1.out, gain11.out
 
     k = Kernel(4)
-    q_down1 = sum_scatter(k, "cols", p_down1.out, r_down1.out)
+    r_down1 = x_half(k, p_down1.out)
     r_gate1, q_up1 = x_slots(k, p_gate1.out, "rows"), sum_scatter(k, "rows", p_up1.out)
     rows, gain_load = load_all(k, d_mid1), gains_of(k, 1, t_gain.out)
     value = load_all(k, z_rows)
@@ -1389,14 +1397,14 @@
     )
     d_z, gain10 = Save(k, s11.out), Save(k, s11.gain_grad)
     head_gains = [Save(k, back.q_gain), Save(k, back.k_gain)]
-    k.early += [q_down1.load, q_up1.load]
-    k.do(r_gate1.send, rows.wait, g10.begin, q_down1.send, q_up1.send, g10.loop)
-    k.do(q_down1.step, y_load.wait, p_out1.run, p_out1.wait, r_out1.send)
-    k.do(proj.wait, q_load.wait, k_load.wait, lambda: back.run(q_up1.step, q_down1.step))
-    k.do(q_up1.step, *(v.start for v in head_gains))
+    k.early.append(q_up1.load)
+    k.do(r_down1.send, r_gate1.send, rows.wait, g10.begin, q_up1.send, g10.loop)
+    k.do(y_load.wait, p_out1.run, q_up1.step, p_out1.wait, r_out1.send)
+    k.do(proj.wait, q_load.wait, k_load.wait, lambda: back.run(q_up1.step))
+    k.do(*(v.start for v in head_gains))
     k.do(gain_load.wait, value.wait, s11.loop, a_load.wait, p_in1.run)
     k.do(s11.finish, d_z.start, gain10.start, p_in1.wait)
-    k.do(*wait(q_down1, q_up1, r_gate1, r_out1))
+    k.do(*wait(r_down1, q_up1, r_gate1, r_out1))
     k.build()
     d_z, gain10 = d_z.out, gain10.out
     q_gain, k_gain = (v.out for v in head_gains)
@@ -1406,7 +1414,7 @@
     q_out1 = sum_scatter(k, "cols", p_out1.out, r_out1.out)
     r_in1 = x_slots(k, p_in1.out, "rows")
     q_in1 = sum_scatter(k, "rows", p_in1.out, r_in1.out)
-    e_down1 = Finish(k, q_down1.out, 1)
+    q_down1 = sum_scatter(k, "cols", p_down1.out, r_down1.out)
     rows, value, gain_load = load_all(k, d_z), load_all(k, mid0), gains_of(k, 0, t_gain.out)
     gate_load, up_load, hid_load, m_load = (load_all(k, v) for v in (gate0, up0, hid0, m0))
     w_gate0 = Weight(k, "rows", z_gate0.out, None, True)
@@ -1422,14 +1430,14 @@
         k, g12.values, [w_gate0, w_up0], rows.buf, (value.buf, (gain_load.buf, 1)), True
     )
     d_mid0, gain01 = Save(k, s13.out), Save(k, s13.gain_grad)
-    k.early += [q_gate1.load, q_out1.load, e_down1.load]
-    k.do(r_in1.send, rows.wait, g12.begin, q_gate1.send, q_out1.send, m_up1.send, e_down1.send)
-    k.do(gate_load.wait, up_load.wait, g12.loop, q_gate1.step, q_out1.step)
+    k.early += [q_gate1.load, q_down1.load, q_out1.load]
+    k.do(r_in1.send, m_up1.send, rows.wait, g12.begin, q_gate1.send, q_down1.send, q_out1.send)
+    k.do(gate_load.wait, up_load.wait, g12.loop, q_gate1.step, q_down1.step, q_out1.step)
     k.do(hid_load.wait, p_down0.run, p_down0.wait, r_down0.send, r_in1.wait, q_in1.add)
-    k.do(s13.loop, q_gate1.step, q_out1.step, q_in1.step)
-    k.do(m_load.wait, p_gate0.run, p_up0.run, q_in1.step, value.wait, gain_load.wait)
-    k.do(s13.finish, d_mid0.start, gain01.start, p_gate0.wait, p_up0.wait)
-    k.do(*wait(q_gate1, q_out1, q_in1, e_down1, m_up1, r_down0))
+    k.do(s13.loop, q_gate1.step, q_down1.step, q_out1.step)
+    k.do(m_load.wait, p_gate0.run, q_in1.step, p_up0.run, value.wait, gain_load.wait)
+    k.do(s13.finish, d_mid0.start, gain01.start, q_in1.step, p_gate0.wait, p_up0.wait)
+    k.do(*wait(q_gate1, q_out1, q_in1, q_down1, m_up1, r_down0))
     k.build()
     d_mid0, gain01 = d_mid0.out, gain01.out
 
@@ -1439,6 +1447,7 @@
     q_down0 = sum_scatter(k, "cols", p_down0.out, r_down0.out)
     q_up0 = sum_scatter(k, "rows", p_up0.out)
     m_up0 = x_move(k, q_up0.out, 1)
+    e_down1 = Finish(k, q_down1.out, 1)
     e_gate1, e_out1, e_in1 = (Finish(k, v.out, 1) for v in (q_gate1, q_out1, q_in1))
     rows, gain_load = load_all(k, d_mid0), gains_of(k, 0, t_gain.out)
     x_load, taps = start_rows(k, 0, t_seq.out), load_all(k, conv_kernel)
@@ -1494,9 +1503,10 @@
         return [(sources, t_result.out.ref, {"section": 1 - s})], []
 
     t_result = Task(k, row_shape, "section", result_moves, 1)
-    k.early += [q_up0.load, q_down0.load, e_gate1.load, e_out1.load, e_in1.load]
+    k.early += [q_up0.load, q_down0.load]
+    k.early += [v.load for v in (e_down1, e_gate1, e_out1, e_in1)]
     k.do(r_gate0.send, rows.wait, g14.begin, q_up0.send, q_down0.send)
-    k.do(e_gate1.send, e_out1.send, e_in1.send, g14.loop)
+    k.do(e_down1.send, e_gate1.send, e_out1.send, e_in1.send, g14.loop)
     k.do(y_load.wait, p_out0.run, p_out0.wait, r_out0.send, q_up0.step)
     k.do(proj.wait, value.wait, taps.wait, back.run, q_down0.step, a_load.wait)
     k.do(p_in0.run, p_cols.run, p_in0.wait, r_in0.send, p_cols.wait, r_cols.send)
@@ -1507,7 +1517,7 @@
     k.do(q_gate0.step, q_out0.step, q_in0.step, q_cols.step, t_small.wait, z_small.add)
     k.do(q_gate0.wait, e_gate0.add, q_out0.step, q_in0.step, q_cols.step)
     k.do(z_small.wait, t_total.add, q_out0.wait, e_out0.add, q_in0.wait, e_in0.add)
-    rest = (e_gate1, e_out1, e_in1, q_cols, e_down0, e_gate0, m_up0, e_out0, e_in0)
+    rest = (e_down1, e_gate1, e_out1, e_in1, q_cols, e_down0, e_gate0, m_up0, e_out0, e_in0)
     k.do(*wait(*rest, t_total, t_result))
     k.build()
 

time: 539 us -> 524 us (0.972)
  Pallas kernels: 527 us -> 515 us
    pallas_call x7, Pallas kernels: 523 us -> 511 us  [build(): pl.pallas_call(self.body, out_shape=[jax.ShapeDtypeStruct(v.shape, v.dtyp...]
where the time goes in v10:
time: 524 us; the launch traced here: 518 us
  Pallas kernels  515 us (98%)
    pallas_call x7, Pallas kernels, build(): pl.pallas_call(self.body, out_shape=[jax.ShapeDtypeStruct(v.shape, v.dtyp...  511 us

profile of v10, /device:TPU:0, one launch (start us, length us, event | category | flops | bytes accessed | tf_op | source)
XLA Modules:
  0.0 517.6 jit_solution(16894258613332431213)
XLA Ops:
  0.6 0.7 tile.4
  1.3 0.7 tile.10.refs_8_.refs_7_
  2.0 89.4 %stage0.1 = (bf16[128,512]{1,0:T(8,128)(2,1)}, bf16[128,256]{1,0:T(8,128)(2,1)}, bf16[128,1152]{1,0:T(8,128)(2,1)}, bf16[256,1152]{1,0:T(8,128)(2,1)}, bf16[576,...) custom-call(bf16[2,256,1024]{2,1,0:T(8,128)(2,1)} %bitcast.15, ...), custom_call_target="tpu_custom_call" | custom-call | tf_op jit(solution)/shard_map/stage0/pallas_call | solution.py:165
  91.4 80.3 %stage1.1 = (bf16[4,128,1152]{2,1,0:T(8,128)(2,1)}, bf16[4,576,256]{2,1,0:T(8,128)(2,1)}, bf16[4,128,512]{2,1,0:T(8,128)(2,1)}, bf16[4,128,256]{2,1,0:T(8,128)(2...) custom-call(bf16[4,128,1152]{2,1,0:T(8,128)(2,1)} %get-tuple-element, ...), custom_call_target="tpu_custom_call" | custom-call | tf_op jit(solution)/shard_map/stage1/pallas_call | solution.py:165
  171.8 57.2 %stage2.1 = (bf16[4,128,1152]{2,1,0:T(8,128)(2,1)}, bf16[4,128,1152]{2,1,0:T(8,128)(2,1)}, bf16[4,576,256]{2,1,0:T(8,128)(2,1)}, bf16[4,128,1152]{2,1,0:T(8,128)...) custom-call(bf16[4,128,1152]{2,1,0:T(8,128)(2,1)} %get-tuple-element, ...), custom_call_target="tpu_custom_call" | custom-call | tf_op jit(solution)/shard_map/stage2/pallas_call | solution.py:165
  229.0 50.7 %stage3.1 = (bf16[1152,1024]{1,0:T(8,128)(2,1)}, bf16[1024,1152]{1,0:T(8,128)(2,1)}, bf16[1024,1152]{1,0:T(8,128)(2,1)}, bf16[256,1024]{1,0:T(8,128)(2,1)}, f32[256,1024]{1,0:T(8,128)}, /*index=5*/f32[1,1024]{1,0:T(1,128)}) custom-call(f32[256,1024]{1,0:T(8,128)} %get-tuple-element.116.refs_0_, f32[2,1024]{1,0:T(2,128)} %bitcast.36, ...), custom_call_target="tpu_custom_call" | custom-call | tf_op jit(solution)/shard_map/stage3/pallas_call | solution.py:165
  279.6 60.9 %stage4.1 = (bf16[576,1024]{1,0:T(8,128)(2,1)}, bf16[4,128,1152]{2,1,0:T(8,128)(2,1)}, bf16[256,1152]{1,0:T(8,128)(2,1)}, bf16[256,1024]{1,0:T(8,128)(2,1)}, bf1...) custom-call(bf16[1152,1024]{1,0:T(8,128)(2,1)} %get-tuple-element.12, ...), custom_call_target="tpu_custom_call" | custom-call | tf_op jit(solution)/shard_map/stage4/pallas_call | solution.py:165
  340.5 64.0 %stage5.1 = (bf16[128,1152]{1,0:T(8,128)(2,1)}, bf16[256,1152]{1,0:T(8,128)(2,1)}, bf16[128,256]{1,0:T(8,128)(2,1)}, bf16[4,128,512]{2,1,0:T(8,128)(2,1)}, bf16[...) custom-call(bf16[1024,1152]{1,0:T(8,128)(2,1)} %get-tuple-element.12, ...), custom_call_target="tpu_custom_call" | custom-call | tf_op jit(solution)/shard_map/stage5/pallas_call | solution.py:165
  404.5 108.1 %stage6.1 = (bf16[4,128,1152]{2,1,0:T(8,128)(2,1)}, bf16[128,1152]{1,0:T(8,128)(2,1)}, bf16[576,256]{1,0:T(8,128)(2,1)}, bf16[256,1152]{1,0:T(8,128)(2,1)}, bf16...) custom-call(bf16[1024,1152]{1,0:T(8,128)(2,1)} %get-tuple-element.14, ...), custom_call_target="tpu_custom_call" | custom-call | tf_op jit(solution)/shard_map/stage6/pallas_call | solution.py:165
  512.6 4.6 pack.1

commit v11 on v10

--- a/solution.py
+++ b/solution.py
@@ -286,7 +286,20 @@
                 pl.when(s == self.final)(move.wait_recv)
 
 
+class Part:
+    def __init__(self, base, start, rows):
+        self.base, self.start, self.rows = base, start, rows
+        self.shape, self.dtype = (rows,) + tuple(base.shape[1:]), base.dtype
+        self.array = None
+
+    @property
+    def ref(self):
+        return self.base.ref.at[pl.ds(self.start, self.rows)]
+
+
 def as_val(k, value):
+    if isinstance(value, Part):
+        return Part(as_val(k, value.base), value.start, value.rows)
     value = value.out if isinstance(value, Task) else value
     known = isinstance(value, Val) and (value.array is None)
     return value if known else k.input(value)
@@ -667,48 +680,53 @@
 
 
 class Weight:
-    def __init__(self, k, kind, near, far=None, early=False, fixed=False):
-        near, far = as_val(k, near), None if far is None else as_val(k, far)
-        self.count, self.rows, self.cols = near.shape
-        self.kind, self.near, self.far, self.waited = kind, near, far, False
-        sides, self.fixed = 1 if far is None else 2, fixed
+    def __init__(self, k, kind, *segments, early=False):
+        self.kind, self.waited = kind, False
+        self.segments, start = [], 0
+        for near, far in segments:
+            near, far = as_val(k, near), None if far is None else as_val(k, far)
+            self.segments.append((near, far, start))
+            start += near.shape[1] * (1 if far is None else 2)
+        self.count, _, self.cols = self.segments[0][0].shape
+        self.rows = start
         if kind == "cols":
-            shape = (sides * self.rows, self.count * self.cols)
+            shape = (self.rows, self.count * self.cols)
         else:
-            shape = (sides * self.count * self.rows, self.cols)
+            shape = (self.count * self.rows, self.cols)
         self.aside = kind == "cols" and self.cols % 128 != 0
-        self.buf, self.sem = k.vmem(shape, BF), k.sem(2 * self.count)
+        self.buf = k.vmem(shape, BF)
+        sides = [v for near, far, _ in self.segments for v in (near, far) if v is not None]
+        self.sem = k.sem(len(sides), self.count)
         if self.aside:
-            self.held = [k.vmem(near.shape, BF), k.vmem(near.shape, BF)]
+            self.held = [k.vmem(v.shape, BF) for v in sides]
         k.once.append(self)
         if early:
             k.early.append(self.start)
 
+    def sides(self):
+        s = lax.axis_index("section")
+        for near, far, start in self.segments:
+            rows = near.shape[1]
+            if far is None:
+                yield near, start, None
+            else:
+                yield near, start + s * rows, s
+                yield far, start + (1 - s) * rows, 1 - s
+
     def moves(self):
-        s, dst = 0 if self.fixed else lax.axis_index("section"), self.buf.ref
-        rows, cols = self.rows, self.cols
-
-        def place(sec, own):
-            if self.aside:
-                return None
-            if self.kind == "cols":
-                return dst.at[block_of(sec, rows), pl.ds(own * cols, cols)]
-            slot = own * 2 + sec if self.kind == "rows" else sec * self.count + own
-            return dst.at[block_of(slot, rows)]
-
-        if self.far is None:
+        dst = self.buf.ref
+        for j, (val, start, sec) in enumerate(self.sides()):
+            rows = val.shape[1]
             for i in range(self.count):
-                if self.kind == "cols":
-                    to = dst.at[:, pl.ds(i * cols, cols)]
+                if self.aside:
+                    to = self.held[j].ref.at[i]
+                elif self.kind == "cols":
+                    at = pl.ds(pl.multiple_of(start, 16), rows)
+                    to = dst.at[at, pl.ds(i * self.cols, self.cols)]
                 else:
-                    to = dst.at[pl.ds(i * rows, rows)]
-                to = self.held[0].ref.at[i] if self.aside else to
-                yield pltpu.make_async_copy(self.near.ref.at[i], to, self.sem.ref.at[2 * i])
-            return
-        for i in range(self.count):
-            for j, (val, sec) in enumerate(((self.near, s), (self.far, 1 - s))):
-                to = self.held[j].ref.at[i] if self.aside else place(sec, i)
-                yield pltpu.make_async_copy(val.ref.at[i], to, self.sem.ref.at[2 * i + j])
+                    top = (sec * self.count + i) * rows if self.kind == "conv" else i * self.rows + start
+                    to = dst.at[pl.ds(pl.multiple_of(top, 16), rows)]
+                yield pltpu.make_async_copy(val.ref.at[i], to, self.sem.ref.at[j, i])
 
     def start(self):
         for move in self.moves():
@@ -721,10 +739,9 @@
         for move in self.moves():
             move.wait()
         if self.aside:
-            s = 0 if self.fixed else lax.axis_index("section")
-            for j, sec in enumerate((s, 1 - s) if self.far is not None else (0,)):
+            for j, (val, start, _) in enumerate(self.sides()):
                 whole = jnp.concatenate([self.held[j].ref[i] for i in range(self.count)], axis=1)
-                self.buf.ref[block_of(sec, self.rows), :] = whole
+                self.buf.ref[pl.ds(pl.multiple_of(start, 16), val.shape[1]), :] = whole
 
 
 class Product:
@@ -1275,83 +1292,91 @@
         return [([(None, seq_val.ref.at[1 - s])], t_seq.out.ref, {"section": 1 - s})], []
 
     t_in, t_out, t_up = (x_half(k, v) for v in (sh_in, sh_out, sh_up))
-    t_gate0, t_down0 = x_move(k, sh_gate, 0), x_half(k, sh_down, 0)
+    gate_lo, gate_hi = (Part(sh_gate, i * (sh_gate.shape[0] // 2), sh_gate.shape[0] // 2) for i in range(2))
+    down_lo, down_hi = (Part(sh_down, i * (sh_down.shape[0] // 2), sh_down.shape[0] // 2) for i in range(2))
+    t_gate0a, t_gate0b = x_half(k, gate_lo, 0), x_move(k, gate_hi, 0)
+    t_down0a, t_down0b = x_half(k, down_lo, 0), x_move(k, down_hi, 0)
     t_gate1, t_down1 = x_half(k, sh_gate, 1), x_move(k, sh_down, 1)
     t_seq = Task(k, row_shape, "section", seq_moves, 1)
     t_gain, z_cols = x_move(k, own_gain), z_gather(k, conv_x)
     z_in0, z_out0 = z_gather_half(k, sh_in, t_in.out, 0), z_gather_half(k, sh_out, t_out.out, 0)
-    z_gate0 = z_gather_whole(k, sh_gate, t_gate0.out, 0)
+    z_gate0a = z_gather_half(k, gate_lo, t_gate0a.out, 0)
+    z_gate0b, x_gate0a = z_gather_whole(k, gate_hi, t_gate0b.out, 0), x_move(k, z_gate0a.out)
     z_up0 = z_gather_half(k, sh_up, t_up.out, 0)
     x_cols, x_in0, x_out0 = (x_move(k, v.out) for v in (z_cols, z_in0, z_out0))
     x_load, gain_load = start_rows(k, 0, t_seq.out, False), gains_of(k, 0, t_gain.out, False)
     taps = load_all(k, conv_kernel)
     angles = Angles(k, length, size, 128)
-    w_in0, w_cols = Weight(k, "rows", z_in0.out, x_in0.out), Weight(k, "conv", z_cols.out, x_cols.out)
-    w_out0 = Weight(k, "cols", z_out0.out, x_out0.out)
+    w_in0, w_cols = Weight(k, "rows", (z_in0.out, x_in0.out)), Weight(k, "conv", (z_cols.out, x_cols.out))
+    w_out0 = Weight(k, "cols", (z_out0.out, x_out0.out))
     g0 = Gather(k, x_load.buf, (gain_load.buf, 0), [w_in0, w_cols], save=(0, 1, 2))
     conv = Conv(k, g0.values[0], g0.values[1], taps.buf)
     y0 = Save(k, conv.y)
     s1 = Scatter(k, [conv.y], [w_out0], x_load.buf)
     mid0 = Save(k, s1.out)
-    k.do(t_in.send, t_out.send, z_cols.send, t_gate0.send, t_gate1.send, t_gain.send, t_seq.send)
+    k.do(t_in.send, t_out.send, z_cols.send, t_gate0b.send, t_gate0a.send, t_gate1.send)
+    k.do(t_gain.send, t_seq.send)
     k.do(t_in.wait, z_in0.send, t_out.wait, z_out0.send, z_cols.step, z_in0.step, z_out0.step)
-    k.do(z_cols.step, z_in0.step, z_out0.step, t_gate0.wait, z_gate0.send)
-    k.do(z_cols.wait, x_cols.send, z_in0.wait, x_in0.send, z_out0.wait, x_out0.send)
-    k.do(t_up.send, t_down0.send, t_down1.send)
+    k.do(z_cols.step, z_in0.step, z_out0.step, t_gate0b.wait, z_gate0b.send)
+    k.do(t_gate0a.wait, z_gate0a.send)
+    k.do(z_cols.wait, x_cols.send, z_in0.wait, x_in0.send, z_out0.wait, x_out0.send, t_up.send)
     k.do(t_gain.wait, gain_load.start, t_seq.wait, x_load.start, gain_load.wait, x_load.wait)
-    k.do(g0.begin, angles.run, z_gate0.step)
-    k.do(x_cols.wait, w_cols.start, x_in0.wait, w_in0.start, z_gate0.step)
-    k.do(g0.loop, t_up.wait, z_up0.send, taps.wait, conv.run, y0.start)
-    k.do(x_out0.wait, w_out0.start, s1.loop, z_up0.step, s1.finish, mid0.start, z_up0.step)
-    k.do(*wait(t_gate1, t_down0, t_down1, z_gate0, z_up0))
+    k.do(g0.begin, z_gate0b.step, z_gate0a.step, angles.run, z_gate0b.step, z_gate0a.step)
+    k.do(x_cols.wait, w_cols.start, x_in0.wait, w_in0.start, z_gate0a.wait, x_gate0a.send)
+    k.do(t_down0b.send, t_down0a.send, t_down1.send, t_up.wait, z_up0.send)
+    k.do(g0.loop, z_up0.step, taps.wait, conv.run, y0.start)
+    k.do(x_out0.wait, w_out0.start, s1.loop, z_up0.step, s1.finish, mid0.start)
+    k.do(*wait(t_gate1, t_down0a, t_down0b, t_down1, z_gate0b, x_gate0a, z_up0))
     k.build()
     a0, proj0, value0 = (out for _, out, _ in g0.saved)
     table_arrays = [head_gain] + [v.out for v in angles.saves]
     y0, mid0 = y0.out, mid0.out
 
     k = Kernel(1)
-    x_up0, z_down0 = x_move(k, z_up0.out), z_gather_half(k, sh_down, t_down0.out, 0)
+    x_up0, z_gate1 = x_move(k, z_up0.out), z_gather_half(k, sh_gate, t_gate1.out, 1)
+    z_down0a = z_gather_half(k, down_lo, t_down0a.out, 0)
+    z_down0b = z_gather_whole(k, down_hi, t_down0b.out, 0)
     z_in1, z_out1 = z_gather_half(k, sh_in, t_in.out, 1), z_gather_half(k, sh_out, t_out.out, 1)
-    z_gate1 = z_gather_half(k, sh_gate, t_gate1.out, 1)
-    z_down1a = z_gather_whole(k, sh_down, t_down1.out, 1, 0)
-    x_down0, x_in1, x_out1 = (x_move(k, v.out) for v in (z_down0, z_in1, z_out1))
+    x_down0a, x_in1, x_out1 = (x_move(k, v.out) for v in (z_down0a, z_in1, z_out1))
     rows, gain_load = load_all(k, mid0), gains_of(k, 0, t_gain.out)
-    w_gate0 = Weight(k, "rows", z_gate0.out, None, True)
-    w_up0 = Weight(k, "rows", z_up0.out, x_up0.out)
-    w_down0 = Weight(k, "cols", z_down0.out, x_down0.out)
+    w_gate0 = Weight(k, "rows", (z_gate0a.out, x_gate0a.out), (z_gate0b.out, None), early=True)
+    w_up0 = Weight(k, "rows", (z_up0.out, x_up0.out))
+    w_down0 = Weight(k, "cols", (z_down0a.out, x_down0a.out), (z_down0b.out, None))
     g2 = Gather(
         k, rows.buf, (gain_load.buf, 1), [w_gate0, w_up0], epilogue="ffn", save=(0, 1, 2, 3)
     )
     s3 = Scatter(k, [g2.values[2]], [w_down0], rows.buf, low=True)
     z_rows = Save(k, s3.out)
-    k.do(x_up0.send, z_down0.send, rows.wait, gain_load.wait, g2.begin, z_down0.step)
-    k.do(z_in1.send, z_out1.send, z_down0.step, z_in1.step, z_out1.step, z_gate1.send)
-    k.do(z_down0.wait, x_down0.send, z_down1a.send, x_up0.wait, w_up0.start, z_in1.step, z_out1.step)
-    k.do(g2.loop, z_gate1.step, z_down1a.step, z_in1.wait, x_in1.send, z_out1.wait, x_out1.send)
-    k.do(x_down0.wait, w_down0.start, s3.loop, z_gate1.step, z_down1a.step)
-    k.do(s3.finish, z_rows.start, *wait(x_in1, x_out1, z_gate1, z_down1a))
+    k.do(x_up0.send, z_down0a.send, z_down0b.send, rows.wait, gain_load.wait, g2.begin)
+    k.do(z_in1.send, z_out1.send, z_down0a.step, z_in1.step, z_out1.step, z_down0b.step)
+    k.do(z_down0a.step, z_in1.step, z_out1.step, z_gate1.send, z_down0a.wait, x_down0a.send)
+    k.do(x_up0.wait, w_up0.start, z_down0b.step, g2.loop, z_gate1.step)
+    k.do(z_in1.wait, x_in1.send, z_out1.wait, x_out1.send, z_down0b.wait, x_down0a.wait)
+    k.do(w_down0.start, s3.loop, z_gate1.step, s3.finish, z_rows.start)
+    k.do(*wait(x_in1, x_out1, z_gate1))
     k.build()
     m0, gate0, up0, hid0 = (out for _, out, _ in g2.saved)
     z_rows = z_rows.out
 
     k = Kernel(2)
     x_gate1, z_up1 = x_move(k, z_gate1.out), z_gather_half(k, sh_up, t_up.out, 1)
-    z_down1, x_up1 = z_gather_whole(k, sh_down, t_down1.out, 1, 1), x_move(k, z_up1.out)
+    z_down1a, z_down1b = (z_gather_whole(k, sh_down, t_down1.out, 1, i) for i in range(2))
+    x_up1 = x_move(k, z_up1.out)
     rows, gain_load = load_all(k, z_rows), gains_of(k, 1, t_gain.out)
     tables = [load_all(k, v) for v in table_arrays]
-    w_in1 = Weight(k, "rows", z_in1.out, x_in1.out, True)
-    w_out1 = Weight(k, "cols", z_out1.out, x_out1.out, True)
+    w_in1 = Weight(k, "rows", (z_in1.out, x_in1.out), early=True)
+    w_out1 = Weight(k, "cols", (z_out1.out, x_out1.out), early=True)
     g4 = Gather(k, rows.buf, (gain_load.buf, 0), [w_in1], save=(0, 1))
     attend = Attend(k, g4.values[0], tables, size)
     kept = [Save(k, v) for v in (attend.q_rot, attend.k_rot, attend.y)]
     s5 = Scatter(k, [attend.y], [w_out1], rows.buf)
     mid1 = Save(k, s5.out)
-    k.do(x_gate1.send, z_up1.send, z_down1.send)
-    k.do(rows.wait, gain_load.wait, g4.begin, z_up1.step, g4.loop, z_up1.step)
-    k.do(lambda: attend.run(z_up1.wait, x_up1.send, z_down1.step))
+    k.do(x_gate1.send, z_up1.send, rows.wait, gain_load.wait, g4.begin, z_up1.step)
+    k.do(z_down1a.send, g4.loop, z_up1.step, z_down1b.send)
+    k.do(lambda: attend.run(z_up1.wait, x_up1.send, z_down1a.step))
     k.do(*(v.start for v in kept))
-    k.do(s5.loop, z_down1.step, s5.finish, mid1.start)
-    k.do(*wait(x_gate1, x_up1, z_down1))
+    k.do(z_down1b.step, s5.loop, z_down1a.step, z_down1b.step, s5.finish, mid1.start)
+    k.do(*wait(x_gate1, x_up1, z_down1a, z_down1b))
     k.build()
     a1, proj1 = (out for _, out, _ in g4.saved)
     q_rot, k_rot, y1 = (v.out for v in kept)
@@ -1360,9 +1385,9 @@
     k = Kernel(3)
     rows, gain_load = load_all(k, mid1), gains_of(k, 1, t_gain.out)
     cot = start_rows(k, 1, t_seq.out)
-    w_gate1 = Weight(k, "rows", z_gate1.out, x_gate1.out, True)
-    w_up1 = Weight(k, "rows", z_up1.out, x_up1.out, True)
-    w_down1 = Weight(k, "cols", z_down1a.out, z_down1.out, True, True)
+    w_gate1 = Weight(k, "rows", (z_gate1.out, x_gate1.out), early=True)
+    w_up1 = Weight(k, "rows", (z_up1.out, x_up1.out), early=True)
+    w_down1 = Weight(k, "cols", (z_down1a.out, None), (z_down1b.out, None), early=True)
     g6 = Gather(k, rows.buf, (gain_load.buf, 1), [w_gate1, w_up1], epilogue="ffn")
     g8 = Gather(
         k, cot.buf, None, [w_down1], [g6.values[0], g6.values[1]], trans=True, epilogue="ffn_back"
@@ -1385,8 +1410,8 @@
     value = load_all(k, z_rows)
     tables = [load_all(k, v) for v in table_arrays]
     proj, q_load, k_load, y_load, a_load = (load_all(k, v) for v in (proj1, q_rot, k_rot, y1, a1))
-    w_in1 = Weight(k, "rows", z_in1.out, x_in1.out, True)
-    w_out1 = Weight(k, "cols", z_out1.out, x_out1.out, True)
+    w_in1 = Weight(k, "rows", (z_in1.out, x_in1.out), early=True)
+    w_out1 = Weight(k, "cols", (z_out1.out, x_out1.out), early=True)
     g10 = Gather(k, rows.buf, None, [w_out1], trans=True)
     p_out1 = Product(k, y_load.buf, g10.full)
     back = AttendBack(k, proj.buf, tables, size, q_load.buf, k_load.buf, g10.values[0])
@@ -1417,9 +1442,9 @@
     q_down1 = sum_scatter(k, "cols", p_down1.out, r_down1.out)
     rows, value, gain_load = load_all(k, d_z), load_all(k, mid0), gains_of(k, 0, t_gain.out)
     gate_load, up_load, hid_load, m_load = (load_all(k, v) for v in (gate0, up0, hid0, m0))
-    w_gate0 = Weight(k, "rows", z_gate0.out, None, True)
-    w_up0 = Weight(k, "rows", z_up0.out, x_up0.out, True)
-    w_down0 = Weight(k, "cols", z_down0.out, x_down0.out, True)
+    w_gate0 = Weight(k, "rows", (z_gate0a.out, x_gate0a.out), (z_gate0b.out, None), early=True)
+    w_up0 = Weight(k, "rows", (z_up0.out, x_up0.out), early=True)
+    w_down0 = Weight(k, "cols", (z_down0a.out, x_down0a.out), (z_down0b.out, None), early=True)
     g12 = Gather(
         k, rows.buf, None, [w_down0], [gate_load.buf, up_load.buf], trans=True, epilogue="ffn_back"
     )
@@ -1452,9 +1477,9 @@
     rows, gain_load = load_all(k, d_mid0), gains_of(k, 0, t_gain.out)
     x_load, taps = start_rows(k, 0, t_seq.out), load_all(k, conv_kernel)
     y_load, a_load, proj, value = (load_all(k, v) for v in (y0, a0, proj0, value0))
-    w_in0 = Weight(k, "rows", z_in0.out, x_in0.out, True)
-    w_cols = Weight(k, "conv", z_cols.out, x_cols.out, True)
-    w_out0 = Weight(k, "cols", z_out0.out, x_out0.out, True)
+    w_in0 = Weight(k, "rows", (z_in0.out, x_in0.out), early=True)
+    w_cols = Weight(k, "conv", (z_cols.out, x_cols.out), early=True)
+    w_out0 = Weight(k, "cols", (z_out0.out, x_out0.out), early=True)
     g14 = Gather(k, rows.buf, None, [w_out0], trans=True)
     p_out0 = Product(k, y_load.buf, g14.full)
     back = ConvBack(k, proj.buf, value.buf, taps.buf, g14.values[0])

time: 524 us -> 518 us (0.989)
    pallas_call x7, Pallas kernels: 511 us -> 505 us  [build(): pl.pallas_call(self.body, out_shape=[jax.ShapeDtypeStruct(v.shape, v.dtyp...]
where the time goes in v11:
time: 518 us; the launch traced here: 512 us
  Pallas kernels  510 us (98%)
    pallas_call x7, Pallas kernels, build(): pl.pallas_call(self.body, out_shape=[jax.ShapeDtypeStruct(v.shape, v.dtyp...  505 us

profile of v11, /device:TPU:0, one launch (start us, length us, event | category | flops | bytes accessed | tf_op | source)
XLA Modules:
  0.0 512.1 jit_solution(10921028634718704877)
XLA Ops:
  0.6 0.7 tile.4
  1.3 0.7 tile.10.refs_8_.refs_7_
  2.0 85.1 %stage0.1 = (bf16[128,512]{1,0:T(8,128)(2,1)}, bf16[128,256]{1,0:T(8,128)(2,1)}, bf16[128,1152]{1,0:T(8,128)(2,1)}, bf16[64,1152]{1,0:T(8,128)(2,1)}, bf16[128,1...) custom-call(bf16[2,256,1024]{2,1,0:T(8,128)(2,1)} %bitcast.15, ...), custom_call_target="tpu_custom_call" | custom-call | tf_op jit(solution)/shard_map/stage0/pallas_call | solution.py:165
  87.0 73.3 %stage1.1 = (bf16[4,128,1152]{2,1,0:T(8,128)(2,1)}, bf16[4,128,1152]{2,1,0:T(8,128)(2,1)}, bf16[4,288,256]{2,1,0:T(8,128)(2,1)}, bf16[4,576,256]{2,1,0:T(8,128)(...) custom-call(bf16[4,128,1152]{2,1,0:T(8,128)(2,1)} %get-tuple-element, ...), custom_call_target="tpu_custom_call" | custom-call | tf_op jit(solution)/shard_map/stage1/pallas_call | solution.py:165
  160.3 63.1 %stage2.1 = (bf16[4,128,1152]{2,1,0:T(8,128)(2,1)}, bf16[4,128,1152]{2,1,0:T(8,128)(2,1)}, bf16[4,576,256]{2,1,0:T(8,128)(2,1)}, bf16[4,576,256]{2,1,0:T(8,128)(...) custom-call(bf16[4,128,1152]{2,1,0:T(8,128)(2,1)} %get-tuple-element, ...), custom_call_target="tpu_custom_call" | custom-call | tf_op jit(solution)/shard_map/stage2/pallas_call | solution.py:165
  223.4 51.4 %stage3.1 = (bf16[1152,1024]{1,0:T(8,128)(2,1)}, bf16[1024,1152]{1,0:T(8,128)(2,1)}, bf16[1024,1152]{1,0:T(8,128)(2,1)}, bf16[256,1024]{1,0:T(8,128)(2,1)}, f32[256,1024]{1,0:T(8,128)}, /*index=5*/f32[1,1024]{1,0:T(1,128)}) custom-call(f32[256,1024]{1,0:T(8,128)} %get-tuple-element.123.refs_0_, f32[2,1024]{1,0:T(2,128)} %bitcast.36, ...), custom_call_target="tpu_custom_call" | custom-call | tf_op jit(solution)/shard_map/stage3/pallas_call | solution.py:165
  274.9 60.2 %stage4.1 = (bf16[576,1024]{1,0:T(8,128)(2,1)}, bf16[4,128,1152]{2,1,0:T(8,128)(2,1)}, bf16[256,1152]{1,0:T(8,128)(2,1)}, bf16[256,1024]{1,0:T(8,128)(2,1)}, bf1...) custom-call(bf16[1152,1024]{1,0:T(8,128)(2,1)} %get-tuple-element.13, ...), custom_call_target="tpu_custom_call" | custom-call | tf_op jit(solution)/shard_map/stage4/pallas_call | solution.py:165
  335.1 64.5 %stage5.1 = (bf16[128,1152]{1,0:T(8,128)(2,1)}, bf16[256,1152]{1,0:T(8,128)(2,1)}, bf16[128,256]{1,0:T(8,128)(2,1)}, bf16[4,128,512]{2,1,0:T(8,128)(2,1)}, bf16[...) custom-call(bf16[1024,1152]{1,0:T(8,128)(2,1)} %get-tuple-element.13, ...), custom_call_target="tpu_custom_call" | custom-call | tf_op jit(solution)/shard_map/stage5/pallas_call | solution.py:165
  399.6 107.5 %stage6.1 = (bf16[4,128,1152]{2,1,0:T(8,128)(2,1)}, bf16[128,1152]{1,0:T(8,128)(2,1)}, bf16[576,256]{1,0:T(8,128)(2,1)}, bf16[256,1152]{1,0:T(8,128)(2,1)}, bf16...) custom-call(bf16[1024,1152]{1,0:T(8,128)(2,1)} %get-tuple-element.15, ...), custom_call_target="tpu_custom_call" | custom-call | tf_op jit(solution)/shard_map/stage6/pallas_call | solution.py:165
  507.1 4.6 pack.1

commit v12 on v11

--- a/solution.py
+++ b/solution.py
@@ -1314,47 +1314,41 @@
     y0 = Save(k, conv.y)
     s1 = Scatter(k, [conv.y], [w_out0], x_load.buf)
     mid0 = Save(k, s1.out)
-    k.do(t_in.send, t_out.send, z_cols.send, t_gate0b.send, t_gate0a.send, t_gate1.send)
-    k.do(t_gain.send, t_seq.send)
-    k.do(t_in.wait, z_in0.send, t_out.wait, z_out0.send, z_cols.step, z_in0.step, z_out0.step)
-    k.do(z_cols.step, z_in0.step, z_out0.step, t_gate0b.wait, z_gate0b.send)
-    k.do(t_gate0a.wait, z_gate0a.send)
-    k.do(z_cols.wait, x_cols.send, z_in0.wait, x_in0.send, z_out0.wait, x_out0.send, t_up.send)
-    k.do(t_gain.wait, gain_load.start, t_seq.wait, x_load.start, gain_load.wait, x_load.wait)
-    k.do(g0.begin, z_gate0b.step, z_gate0a.step, angles.run, z_gate0b.step, z_gate0a.step)
-    k.do(x_cols.wait, w_cols.start, x_in0.wait, w_in0.start, z_gate0a.wait, x_gate0a.send)
-    k.do(t_down0b.send, t_down0a.send, t_down1.send, t_up.wait, z_up0.send)
-    k.do(g0.loop, z_up0.step, taps.wait, conv.run, y0.start)
-    k.do(x_out0.wait, w_out0.start, s1.loop, z_up0.step, s1.finish, mid0.start)
-    k.do(*wait(t_gate1, t_down0a, t_down0b, t_down1, z_gate0b, x_gate0a, z_up0))
-    k.build()
-    a0, proj0, value0 = (out for _, out, _ in g0.saved)
-    table_arrays = [head_gain] + [v.out for v in angles.saves]
-    y0, mid0 = y0.out, mid0.out
-
-    k = Kernel(1)
     x_up0, z_gate1 = x_move(k, z_up0.out), z_gather_half(k, sh_gate, t_gate1.out, 1)
     z_down0a = z_gather_half(k, down_lo, t_down0a.out, 0)
     z_down0b = z_gather_whole(k, down_hi, t_down0b.out, 0)
     z_in1, z_out1 = z_gather_half(k, sh_in, t_in.out, 1), z_gather_half(k, sh_out, t_out.out, 1)
     x_down0a, x_in1, x_out1 = (x_move(k, v.out) for v in (z_down0a, z_in1, z_out1))
-    rows, gain_load = load_all(k, mid0), gains_of(k, 0, t_gain.out)
-    w_gate0 = Weight(k, "rows", (z_gate0a.out, x_gate0a.out), (z_gate0b.out, None), early=True)
+    w_gate0 = Weight(k, "rows", (z_gate0a.out, x_gate0a.out), (z_gate0b.out, None))
     w_up0 = Weight(k, "rows", (z_up0.out, x_up0.out))
     w_down0 = Weight(k, "cols", (z_down0a.out, x_down0a.out), (z_down0b.out, None))
-    g2 = Gather(
-        k, rows.buf, (gain_load.buf, 1), [w_gate0, w_up0], epilogue="ffn", save=(0, 1, 2, 3)
-    )
-    s3 = Scatter(k, [g2.values[2]], [w_down0], rows.buf, low=True)
+    g2 = Gather(k, s1.out, (gain_load.buf, 1), [w_gate0, w_up0], epilogue="ffn", save=(0, 1, 2, 3))
+    s3 = Scatter(k, [g2.values[2]], [w_down0], s1.out, low=True)
     z_rows = Save(k, s3.out)
-    k.do(x_up0.send, z_down0a.send, z_down0b.send, rows.wait, gain_load.wait, g2.begin)
-    k.do(z_in1.send, z_out1.send, z_down0a.step, z_in1.step, z_out1.step, z_down0b.step)
-    k.do(z_down0a.step, z_in1.step, z_out1.step, z_gate1.send, z_down0a.wait, x_down0a.send)
-    k.do(x_up0.wait, w_up0.start, z_down0b.step, g2.loop, z_gate1.step)
-    k.do(z_in1.wait, x_in1.send, z_out1.wait, x_out1.send, z_down0b.wait, x_down0a.wait)
-    k.do(w_down0.start, s3.loop, z_gate1.step, s3.finish, z_rows.start)
-    k.do(*wait(x_in1, x_out1, z_gate1))
+    k.do(t_in.send, t_out.send, z_cols.send, t_up.send, t_gain.send, t_seq.send)
+    k.do(t_gate0a.send, t_gate1.send)
+    k.do(t_in.wait, z_in0.send, t_out.wait, z_out0.send, z_cols.step, z_in0.step, z_out0.step)
+    k.do(z_cols.step, z_in0.step, z_out0.step, t_up.wait, z_up0.send)
+    k.do(z_cols.wait, x_cols.send, z_in0.wait, x_in0.send, z_out0.wait, x_out0.send)
+    k.do(t_gate0b.send, t_down0a.send, t_down0b.send, t_down1.send)
+    k.do(t_gain.wait, gain_load.start, t_seq.wait, x_load.start, gain_load.wait, x_load.wait)
+    k.do(g0.begin, z_up0.step, t_gate0a.wait, z_gate0a.send, angles.run, z_up0.step, z_gate0a.step)
+    k.do(z_in1.send, z_out1.send, x_cols.wait, w_cols.start, x_in0.wait, w_in0.start)
+    k.do(g0.loop, z_gate0a.step, t_gate0b.wait, z_gate0b.send, z_in1.step, z_out1.step)
+    k.do(z_gate0a.wait, x_gate0a.send, z_up0.wait, x_up0.send, taps.wait, conv.run, y0.start)
+    k.do(x_out0.wait, w_out0.start, s1.loop, z_gate0b.step, t_down0a.wait, z_down0a.send)
+    k.do(t_down0b.wait, z_down0b.send, z_in1.step, z_out1.step, s1.finish, mid0.start)
+    k.do(g2.begin, z_gate0b.step, z_down0a.step, z_down0b.step, t_gate1.wait, z_gate1.send)
+    k.do(z_down0a.step)
+    k.do(z_down0b.step, z_down0a.wait, x_down0a.send, z_in1.wait, x_in1.send, z_out1.wait, x_out1.send)
+    k.do(z_gate0b.wait, x_gate0a.wait, w_gate0.start, z_gate1.step, x_up0.wait, w_up0.start)
+    k.do(z_gate1.step, g2.loop, z_down0b.wait, x_down0a.wait, w_down0.start)
+    k.do(s3.loop, s3.finish, z_rows.start)
+    k.do(*wait(t_down1, x_in1, x_out1, z_gate1))
     k.build()
+    a0, proj0, value0 = (out for _, out, _ in g0.saved)
+    table_arrays = [head_gain] + [v.out for v in angles.saves]
+    y0, mid0 = y0.out, mid0.out
     m0, gate0, up0, hid0 = (out for _, out, _ in g2.saved)
     z_rows = z_rows.out
 
@@ -1371,37 +1365,32 @@
     kept = [Save(k, v) for v in (attend.q_rot, attend.k_rot, attend.y)]
     s5 = Scatter(k, [attend.y], [w_out1], rows.buf)
     mid1 = Save(k, s5.out)
-    k.do(x_gate1.send, z_up1.send, rows.wait, gain_load.wait, g4.begin, z_up1.step)
-    k.do(z_down1a.send, g4.loop, z_up1.step, z_down1b.send)
-    k.do(lambda: attend.run(z_up1.wait, x_up1.send, z_down1a.step))
-    k.do(*(v.start for v in kept))
-    k.do(z_down1b.step, s5.loop, z_down1a.step, z_down1b.step, s5.finish, mid1.start)
-    k.do(*wait(x_gate1, x_up1, z_down1a, z_down1b))
-    k.build()
-    a1, proj1 = (out for _, out, _ in g4.saved)
-    q_rot, k_rot, y1 = (v.out for v in kept)
-    mid1 = mid1.out
-
-    k = Kernel(3)
-    rows, gain_load = load_all(k, mid1), gains_of(k, 1, t_gain.out)
     cot = start_rows(k, 1, t_seq.out)
-    w_gate1 = Weight(k, "rows", (z_gate1.out, x_gate1.out), early=True)
-    w_up1 = Weight(k, "rows", (z_up1.out, x_up1.out), early=True)
-    w_down1 = Weight(k, "cols", (z_down1a.out, None), (z_down1b.out, None), early=True)
-    g6 = Gather(k, rows.buf, (gain_load.buf, 1), [w_gate1, w_up1], epilogue="ffn")
+    w_gate1 = Weight(k, "rows", (z_gate1.out, x_gate1.out))
+    w_up1 = Weight(k, "rows", (z_up1.out, x_up1.out))
+    w_down1 = Weight(k, "cols", (z_down1a.out, None), (z_down1b.out, None))
+    g6 = Gather(k, s5.out, (gain_load.buf, 1), [w_gate1, w_up1], epilogue="ffn", save=(3,))
     g8 = Gather(
         k, cot.buf, None, [w_down1], [g6.values[0], g6.values[1]], trans=True, epilogue="ffn_back"
     )
     p_down1 = Product(k, g6.values[2], g8.full)
     p_gate1, p_up1 = Product(k, g6.full, g8.values[0]), Product(k, g6.full, g8.values[1])
-    s7 = Scatter(k, [g6.values[2]], [w_down1], rows.buf, low=True)
-    s9 = Scatter(k, g8.values, [w_gate1, w_up1], cot.buf, (rows.buf, (gain_load.buf, 1)), True)
-    y_rows, d_mid1, gain11 = Save(k, s7.out), Save(k, s9.out), Save(k, s9.gain_grad)
-    k.do(rows.wait, gain_load.wait, g6.begin, cot.wait, g8.begin, g6.loop, s7.loop, g8.loop)
-    k.do(s9.loop, p_down1.run, s7.finish, y_rows.start, p_gate1.run, p_up1.run)
+    s9 = Scatter(k, g8.values, [w_gate1, w_up1], cot.buf, (s5.out, (gain_load.buf, 1)), True)
+    d_mid1, gain11 = Save(k, s9.out), Save(k, s9.gain_grad)
+    k.do(x_gate1.send, z_up1.send, rows.wait, gain_load.wait, g4.begin, z_up1.step)
+    k.do(cot.wait, g8.begin, z_down1a.send, g4.loop, z_up1.step, z_down1b.send)
+    k.do(lambda: attend.run(z_up1.wait, x_up1.send, z_down1a.step))
+    k.do(*(v.start for v in kept))
+    k.do(x_gate1.wait, w_gate1.start, z_down1b.step, s5.loop, z_down1a.step, s5.finish, mid1.start)
+    k.do(g6.begin, z_down1b.step, x_up1.wait, w_up1.start, g6.loop)
+    k.do(*wait(z_down1a, z_down1b), w_down1.start, g8.loop)
+    k.do(s9.loop, p_down1.run, p_gate1.run, p_up1.run)
     k.do(s9.finish, d_mid1.start, gain11.start, p_down1.wait, p_gate1.wait, p_up1.wait)
     k.build()
-    y_rows, d_mid1, gain11 = y_rows.out, d_mid1.out, gain11.out
+    a1, proj1 = (out for _, out, _ in g4.saved)
+    (hid1,) = (out for _, out, _ in g6.saved)
+    q_rot, k_rot, y1 = (v.out for v in kept)
+    mid1, d_mid1, gain11 = mid1.out, d_mid1.out, gain11.out
 
     k = Kernel(4)
     r_down1 = x_half(k, p_down1.out)
@@ -1521,13 +1510,11 @@
     t_small = x_move(k, small_out.out)
     z_small = SumShare(k, [small_out.out, t_small.out], "dp")
     t_total = SumShare(k, [z_small.out], "tensor", slotted=True)
-    y_val, dx_val = k.input(y_rows), d_x.out
-
-    def result_moves(s, d, t):
-        sources = [(s == 0, y_val.ref), (s == 1, dx_val.ref)]
-        return [(sources, t_result.out.ref, {"section": 1 - s})], []
-
-    t_result = Task(k, row_shape, "section", result_moves, 1)
+    hid_load, mid_load = load_all(k, hid1), load_all(k, mid1)
+    w_down1 = Weight(k, "cols", (z_down1a.out, None), (z_down1b.out, None), early=True)
+    s7 = Scatter(k, [hid_load.buf], [w_down1], mid_load.buf, low=True)
+    y_rows = Save(k, s7.out)
+    t_x, t_y = x_move(k, d_x.out, 1), x_move(k, y_rows.out, 0)
     k.early += [q_up0.load, q_down0.load]
     k.early += [v.load for v in (e_down1, e_gate1, e_out1, e_in1)]
     k.do(r_gate0.send, rows.wait, g14.begin, q_up0.send, q_down0.send)
@@ -1536,14 +1523,16 @@
     k.do(proj.wait, value.wait, taps.wait, back.run, q_down0.step, a_load.wait)
     k.do(p_in0.run, p_cols.run, p_in0.wait, r_in0.send, p_cols.wait, r_cols.send)
     k.do(r_gate0.wait, q_gate0.add, x_load.wait, gain_load.wait, s15.loop, q_up0.step)
-    k.do(q_down0.step, s15.finish, d_x.start, fill_small, d_x.wait, t_result.send)
-    k.do(small_out.wait, t_small.send, q_gate0.step, r_out0.wait, q_out0.add, r_in0.wait, q_in0.add)
+    k.do(q_down0.step, s15.finish, d_x.start, fill_small, d_x.wait, t_x.send)
+    k.do(small_out.wait, t_small.send, q_gate0.step, hid_load.wait, mid_load.wait, s7.loop)
+    k.do(r_out0.wait, q_out0.add, r_in0.wait, q_in0.add)
     k.do(r_cols.wait, q_cols.add, q_up0.wait, m_up0.send, q_down0.wait, e_down0.add)
+    k.do(s7.finish, y_rows.start, y_rows.wait, t_y.send)
     k.do(q_gate0.step, q_out0.step, q_in0.step, q_cols.step, t_small.wait, z_small.add)
     k.do(q_gate0.wait, e_gate0.add, q_out0.step, q_in0.step, q_cols.step)
     k.do(z_small.wait, t_total.add, q_out0.wait, e_out0.add, q_in0.wait, e_in0.add)
     rest = (e_down1, e_gate1, e_out1, e_in1, q_cols, e_down0, e_gate0, m_up0, e_out0, e_in0)
-    k.do(*wait(*rest, t_total, t_result))
+    k.do(*wait(*rest, t_total, t_x, t_y))
     k.build()
 
     owned = [
@@ -1555,7 +1544,7 @@
         ([q_cols], [q_cols], 0),
     ]
     return pack(
-        [(zero, one, lead) for zero, one, lead in owned], t_total, d_x.out, y_rows, t_result,
+        [(zero, one, lead) for zero, one, lead in owned], t_total, d_x.out, y_rows.out, t_x, t_y,
         (norm_gain.shape, conv_kernel.shape, qk_gain.shape),
     )
 
@@ -1577,7 +1566,7 @@
     out_v = [next(room) for _ in leads]
     load_sem, store_sem = room
     s, t = lax.axis_index("section"), lax.axis_index("tensor")
-    small, d_x, y_rows, moved, *parts = ins
+    small, d_x, y_rows, moved, moved_y, *parts = ins
 
     def either(cond, zero, one, dst, sem):
         if zero is not None:
@@ -1587,7 +1576,7 @@
 
     first = s == 0
     either(first, d_x, y_rows, own_v, load_sem.at[0])
-    pltpu.make_async_copy(moved, moved_v, load_sem.at[1]).start()
+    either(first, moved, moved_y, moved_v, load_sem.at[1])
     pltpu.make_async_copy(small, small_v, load_sem.at[2]).start()
     for j, (zero, one, _) in enumerate(terms):
         either(
@@ -1652,7 +1641,7 @@
         store.wait()
 
 
-def pack(owned, small, d_x, y_rows, moved, shapes):
+def pack(owned, small, d_x, y_rows, moved_x, moved_y, shapes):
     gain_shape, tap_shape, head_shape = shapes
     parts, terms, leads, out_shapes = [], [], [], []
     for i, (zero, one, lead) in enumerate(owned):
@@ -1673,7 +1662,7 @@
                 else:
                     pair.append(None)
             terms.append((*pair, i))
-    operands = [small.out.array, d_x.array, y_rows.array, moved.out.array, *parts]
+    operands = [v.array for v in (small.out, d_x, y_rows, moved_x.out, moved_y.out)] + parts
     rows = d_x.shape
     smem = pl.BlockSpec(memory_space=pltpu.VMEM)
     out_shape = [jax.ShapeDtypeStruct((1, 2) + rows, BF), jax.ShapeDtypeStruct(gain_shape, F32)]

time: 518 us -> 525 us (1.014)
  Pallas kernels: 510 us -> 516 us
    pallas_call x7 -> x5, Pallas kernels: 505 us -> 512 us  [build(): pl.pallas_call(self.body, out_shape=[jax.ShapeDtypeStruct(v.shape, v.dtyp...]
where the time goes in v12:
time: 525 us; the launch traced here: 519 us
  Pallas kernels  516 us (98%)
    pallas_call x5, Pallas kernels, build(): pl.pallas_call(self.body, out_shape=[jax.ShapeDtypeStruct(v.shape, v.dtyp...  512 us

profile of v12, /device:TPU:0, one launch (start us, length us, event | category | flops | bytes accessed | tf_op | source)
XLA Modules:
  0.0 518.8 jit_solution(13946478952230099716)
XLA Ops:
  0.6 0.7 tile.4
  1.3 0.7 tile.10.refs_8_.refs_7_
  2.0 165.6 %stage0.1 = (bf16[128,512]{1,0:T(8,128)(2,1)}, bf16[128,256]{1,0:T(8,128)(2,1)}, bf16[128,1152]{1,0:T(8,128)(2,1)}, bf16[64,1152]{1,0:T(8,128)(2,1)}, bf16[128,1...) custom-call(bf16[2,256,1024]{2,1,0:T(8,128)(2,1)} %bitcast.15, ...), custom_call_target="tpu_custom_call" | custom-call | tf_op jit(solution)/shard_map/stage0/pallas_call | solution.py:165
  167.6 111.6 %stage2.1 = (bf16[4,128,1152]{2,1,0:T(8,128)(2,1)}, bf16[4,128,1152]{2,1,0:T(8,128)(2,1)}, bf16[4,576,256]{2,1,0:T(8,128)(2,1)}, bf16[4,576,256]{2,1,0:T(8,128)(...) custom-call(bf16[4,128,1152]{2,1,0:T(8,128)(2,1)} %get-tuple-element, ...), custom_call_target="tpu_custom_call" | custom-call | tf_op jit(solution)/shard_map/stage2/pallas_call | solution.py:165
  279.2 60.6 %stage4.1 = (bf16[576,1024]{1,0:T(8,128)(2,1)}, bf16[4,128,1152]{2,1,0:T(8,128)(2,1)}, bf16[256,1152]{1,0:T(8,128)(2,1)}, bf16[256,1024]{1,0:T(8,128)(2,1)}, bf1...) custom-call(bf16[1152,1024]{1,0:T(8,128)(2,1)} %get-tuple-element.10, ...), custom_call_target="tpu_custom_call" | custom-call | tf_op jit(solution)/shard_map/stage4/pallas_call | solution.py:165
  339.8 65.3 %stage5.1 = (bf16[128,1152]{1,0:T(8,128)(2,1)}, bf16[256,1152]{1,0:T(8,128)(2,1)}, bf16[128,256]{1,0:T(8,128)(2,1)}, bf16[4,128,512]{2,1,0:T(8,128)(2,1)}, bf16[...) custom-call(bf16[1024,1152]{1,0:T(8,128)(2,1)} %get-tuple-element.10, ...), custom_call_target="tpu_custom_call" | custom-call | tf_op jit(solution)/shard_map/stage5/pallas_call | solution.py:165
  405.1 108.7 %stage6.1 = (bf16[4,128,1152]{2,1,0:T(8,128)(2,1)}, bf16[128,1152]{1,0:T(8,128)(2,1)}, bf16[576,256]{1,0:T(8,128)(2,1)}, bf16[256,1152]{1,0:T(8,128)(2,1)}, bf16...) custom-call(bf16[1024,1152]{1,0:T(8,128)(2,1)} %get-tuple-element.13, ...), custom_call_target="tpu_custom_call" | custom-call | tf_op jit(solution)/shard_map/stage6/pallas_call | solution.py:165
  513.8 4.6 pack.1

commit v13 on v11

--- a/solution.py
+++ b/solution.py
@@ -70,6 +70,14 @@
 def silu_parts(gate):
     sig = 1.0 / (1.0 + jnp.exp(-gate))
     return sig, gate * sig
+
+
+def chunked(rows, step):
+    size = next((n for n in (32, 16) if rows % n == 0), rows)
+    if size == rows:
+        step(pl.ds(0, rows))
+    else:
+        lax.fori_loop(0, rows // size, lambda i, c: step(block_of(i, size)) or c, 0)
 
 
 def dp_size():
@@ -514,12 +522,24 @@
         if self.whole:
             return
         kept, got, total = self.kept.ref, self.got.ref, self.total.ref
-        for i in range(self.n):
-            if self.kind == "cols":
-                part = (slice(None), slice(i * self.cols, (i + 1) * self.cols))
-            else:
-                part = i
-            total[i] = (kept[part].astype(F32) + got[part].astype(F32)).astype(BF)
+        if self.kind != "cols":
+
+            def piece(i, carry):
+                chunked(self.rows, lambda at: total.__setitem__(
+                    (i, at), (kept[i, at, :].astype(F32) + got[i, at, :].astype(F32)).astype(BF)
+                ))
+                return carry
+
+            lax.fori_loop(0, self.n, piece, 0)
+            return
+
+        def add_rows(at):
+            for i in range(self.n):
+                part = slice(i * self.cols, (i + 1) * self.cols)
+                value = kept[at, part].astype(F32) + got[at, part].astype(F32)
+                total[i, at, :] = value.astype(BF)
+
+        chunked(self.rows, add_rows)
 
 
 class DirectScatter(Task):
@@ -575,8 +595,13 @@
         d = lax.axis_index("dp")
         to = (d + 2 - j if way == 0 else d + 2 + j) % 4
         self.copy(j, way).wait_recv()
-        total = self.terms.total.ref
-        total[to] = (total[to].astype(F32) + self.got.ref[way, j].astype(F32)).astype(BF)
+        total, got = self.terms.total.ref, self.got.ref
+
+        def add_rows(at):
+            value = total[to, at, :].astype(F32) + got[way, j, at, :].astype(F32)
+            total[to, at, :] = value.astype(BF)
+
+        chunked(self.terms.rows, add_rows)
 
     def arrive(self, j):
         for way in range(2):
@@ -814,11 +839,17 @@
     def begin(self):
         me = places()[0]
         for i in range(2):
-            part = self.x.ref[pl.ds(i * self.half, self.half), :].astype(F32)
-            if self.gain is not None:
-                val, row = self.gain
-                part = norm_rows(part, val.ref[row : row + 1, :])
-            self.full.ref[self.span(me, i), :] = part.astype(BF)
+
+            def put(j, carry):
+                at = i * self.half + j * 32
+                part = self.x.ref[pl.ds(pl.multiple_of(at, 32), 32), :].astype(F32)
+                if self.gain is not None:
+                    val, row = self.gain
+                    part = norm_rows(part, val.ref[row : row + 1, :])
+                self.full.ref[pl.ds(pl.multiple_of(me * self.rows + at, 32), 32), :] = part.astype(BF)
+                return carry
+
+            lax.fori_loop(0, self.half // 32, put, 0)
             self.move("cross", i).start()
             self.move("sib", i).start()
 
@@ -916,8 +947,12 @@
 
     def pass_on(self, i):
         self.move("diag", i).wait_recv()
-        total = self.keep.ref[i] + self.from_s.ref[i].astype(F32)
-        self.to_c.ref[i] = total.astype(BF)
+
+        def add_rows(at):
+            total = self.keep.ref[i, at, :] + self.from_s.ref[i, at, :].astype(F32)
+            self.to_c.ref[i, at, :] = total.astype(BF)
+
+        chunked(self.half, add_rows)
         self.move("cross", i).start()
 
     def loop(self):
@@ -938,27 +973,29 @@
                 prod = contract(a, w.buf.ref[...], 1, 1 if self.trans else 0)
                 total = prod if total is None else total + prod
 
-            for i in range(2):
-
-                @pl.when(p == i)
-                def _():
-                    self.keep.ref[i] = total[:half]
-                    self.to_s.ref[i] = total[half:].astype(BF)
-                    self.move("diag", i).start()
-
-            @pl.when(p == 1)
+            self.own.ref[...] = total
+
+            @pl.when(p < 2)
             def _():
-                self.pass_on(0)
+                def put(at):
+                    self.keep.ref[p, at, :] = self.own.ref[at, :]
+                    lower = pl.ds(pl.multiple_of(at.start + half, 16), at.size)
+                    self.to_s.ref[p, at, :] = self.own.ref[lower, :].astype(BF)
+
+                chunked(half, put)
+                self.move("diag", p).start()
 
             @pl.when(p == 2)
             def _():
-                self.to_o.ref[...] = total.astype(BF)
+                def put(at):
+                    self.to_o.ref[at, :] = self.own.ref[at, :].astype(BF)
+
+                chunked(rows, put)
                 self.move("near").start()
-                self.pass_on(1)
-
-            @pl.when(p == 3)
+
+            @pl.when((p == 1) | (p == 2))
             def _():
-                self.own.ref[...] = total
+                self.pass_on(p - 1)
 
             return carry
 
@@ -966,23 +1003,27 @@
 
     def finish(self):
         self.move("near").wait_recv()
-        gain_sum = None
+        if self.back:
+            self.gain_grad.ref[...] = jnp.zeros_like(self.gain_grad.ref)
         for i in range(2):
-            part = pl.ds(i * self.half, self.half)
             self.move("cross", i).wait_recv()
-            total = self.own.ref[part, :] + self.from_o.ref[part, :].astype(F32)
-            total = total + self.from_c.ref[i].astype(F32)
-            resid = self.resid.ref[part, :].astype(F32)
-            if self.back:
-                value, (gain, row) = self.back
-                value_grad, gain_grad = norm_back(
-                    value.ref[part, :].astype(F32), gain.ref[row : row + 1, :], total
-                )
-                total = value_grad
-                gain_sum = gain_grad if gain_sum is None else gain_sum + gain_grad
-            self.out.ref[part, :] = (resid + total).astype(self.out.dtype)
-        if self.back:
-            self.gain_grad.ref[...] = gain_sum
+
+            def add_rows(j, carry):
+                inner = pl.ds(pl.multiple_of(j * 32, 32), 32)
+                part = pl.ds(pl.multiple_of(i * self.half + j * 32, 32), 32)
+                total = self.own.ref[part, :] + self.from_o.ref[part, :].astype(F32)
+                total = total + self.from_c.ref[i, inner, :].astype(F32)
+                resid = self.resid.ref[part, :].astype(F32)
+                if self.back:
+                    value, (gain, row) = self.back
+                    total, gain_grad = norm_back(
+                        value.ref[part, :].astype(F32), gain.ref[row : row + 1, :], total
+                    )
+                    self.gain_grad.ref[...] += gain_grad
+                self.out.ref[part, :] = (resid + total).astype(self.out.dtype)
+                return carry
+
+            lax.fori_loop(0, self.half // 32, add_rows, 0)
 
     def end(self):
         self.move("near").wait_send()
@@ -1016,9 +1057,9 @@
 
     def parts(self, j):
         channels = self.value.shape[1]
-        at = slice(j * CONV_COLS, (j + 1) * CONV_COLS)
+        at = block_of(j, CONV_COLS)
         b_gate = self.projected.ref[:, at]
-        c_gate = self.projected.ref[:, channels + at.start : channels + at.stop]
+        c_gate = self.projected.ref[:, block_of(j + channels // CONV_COLS, CONV_COLS)]
         x_value, taps = self.value.ref[:, at], self.kernel.ref[:, at]
         product = b_gate * x_value
         count = taps.shape[0]
@@ -1028,9 +1069,12 @@
         return at, b_gate, c_gate, x_value, taps, product, causal
 
     def run(self):
-        for j in range(self.value.shape[1] // CONV_COLS):
+        def step(j, carry):
             at, _, c_gate, _, _, _, causal = self.parts(j)
             self.y.ref[:, at] = (c_gate * causal).astype(BF)
+            return carry
+
+        lax.fori_loop(0, self.value.shape[1] // CONV_COLS, step, 0)
 
 
 class ConvBack(Conv):
@@ -1042,7 +1086,8 @@
 
     def run(self):
         channels = self.value.shape[1]
-        for j in range(channels // CONV_COLS):
+
+        def step(j, carry):
             at, b_gate, c_gate, x_value, taps, product, causal = self.parts(j)
             d_y = self.d_y.ref[:, at]
             d_causal = d_y * c_gate
@@ -1054,8 +1099,12 @@
                 self.d_kernel.ref[i : i + 1, at] = row
                 d_product = d_product + taps[i : i + 1] * advanced(d_causal, by)
             self.d_proj.ref[:, at] = (d_product * x_value).astype(BF)
-            self.d_proj.ref[:, channels + at.start : channels + at.stop] = (d_y * causal).astype(BF)
+            upper = block_of(j + channels // CONV_COLS, CONV_COLS)
+            self.d_proj.ref[:, upper] = (d_y * causal).astype(BF)
             self.d_value.ref[:, at] = (d_product * b_gate).astype(BF)
+            return carry
+
+        lax.fori_loop(0, channels // CONV_COLS, step, 0)
 
 
 def head_mean(values, head_size):
@@ -1167,6 +1216,12 @@
 
         def head(h, carry):
             g = h // self.share
+
+            @pl.when(h == self.heads // 2)
+            def _():
+                for step in between:
+                    step()
+
             for i in range(self.length // ROW_BLOCK):
                 rows, seen = pl.ds(i * ROW_BLOCK, ROW_BLOCK), key_blocks(i)
                 weights = block_weights(
@@ -1179,11 +1234,12 @@
                 self.y_h.ref[h, rows, :] = value.astype(BF)
             return carry
 
-        lax.fori_loop(0, self.heads // 2, head, 0)
-        for step in between:
-            step()
-        lax.fori_loop(self.heads // 2, self.heads, head, 0)
-        self.y.ref[...] = self.join(self.y_h, slice(None))
+        lax.fori_loop(0, self.heads, head, 0)
+
+        def place(rows):
+            self.y.ref[rows, :] = self.join(self.y_h, rows)
+
+        self.blocks(place)
 
 
 class AttendBack(Heads):
@@ -1211,11 +1267,21 @@
             self.split(self.v_h, rows, proj[rows, q_cols + k_cols :].astype(BF))
 
         self.blocks(prepare)
-        dk_h[...] = jnp.zeros_like(dk_h)
-        dv_h[...] = jnp.zeros_like(dv_h)
+
+        def clear(rows):
+            for val in (dk_h, dv_h):
+                val[:, rows, :] = jnp.zeros((self.kv_heads, ROW_BLOCK, size), F32)
+
+        self.blocks(clear)
 
         def head(h, carry):
             g = h // self.share
+
+            @pl.when(h == self.heads // 2)
+            def _():
+                for step in between:
+                    step()
+
             for i in range(self.length // ROW_BLOCK):
                 rows, seen = pl.ds(i * ROW_BLOCK, ROW_BLOCK), key_blocks(i)
                 q, low = self.q_h.ref[h, rows, :], self.dy_h.ref[h, rows, :]
@@ -1234,10 +1300,7 @@
                 dq_h[h, rows, :] = d_q * scale
             return carry
 
-        lax.fori_loop(0, self.heads // 2, head, 0)
-        for step in between:
-            step()
-        lax.fori_loop(self.heads // 2, self.heads, head, 0)
+        lax.fori_loop(0, self.heads, head, 0)
         self.q_gain.ref[...] = jnp.zeros_like(self.q_gain.ref)
         self.k_gain.ref[...] = jnp.zeros_like(self.k_gain.ref)
 
@@ -1394,14 +1457,14 @@
     )
     p_down1 = Product(k, g6.values[2], g8.full)
     p_gate1, p_up1 = Product(k, g6.full, g8.values[0]), Product(k, g6.full, g8.values[1])
-    s7 = Scatter(k, [g6.values[2]], [w_down1], rows.buf, low=True)
     s9 = Scatter(k, g8.values, [w_gate1, w_up1], cot.buf, (rows.buf, (gain_load.buf, 1)), True)
-    y_rows, d_mid1, gain11 = Save(k, s7.out), Save(k, s9.out), Save(k, s9.gain_grad)
-    k.do(rows.wait, gain_load.wait, g6.begin, cot.wait, g8.begin, g6.loop, s7.loop, g8.loop)
-    k.do(s9.loop, p_down1.run, s7.finish, y_rows.start, p_gate1.run, p_up1.run)
+    hid1 = Save(k, g6.values[2])
+    d_mid1, gain11 = Save(k, s9.out), Save(k, s9.gain_grad)
+    k.do(rows.wait, gain_load.wait, g6.begin, cot.wait, g8.begin, g6.loop, hid1.start, g8.loop)
+    k.do(s9.loop, p_down1.run, p_gate1.run, p_up1.run)
     k.do(s9.finish, d_mid1.start, gain11.start, p_down1.wait, p_gate1.wait, p_up1.wait)
     k.build()
-    y_rows, d_mid1, gain11 = y_rows.out, d_mid1.out, gain11.out
+    hid1, d_mid1, gain11 = hid1.out, d_mid1.out, gain11.out
 
     k = Kernel(4)
     r_down1 = x_half(k, p_down1.out)
@@ -1521,13 +1584,11 @@
     t_small = x_move(k, small_out.out)
     z_small = SumShare(k, [small_out.out, t_small.out], "dp")
     t_total = SumShare(k, [z_small.out], "tensor", slotted=True)
-    y_val, dx_val = k.input(y_rows), d_x.out
-
-    def result_moves(s, d, t):
-        sources = [(s == 0, y_val.ref), (s == 1, dx_val.ref)]
-        return [(sources, t_result.out.ref, {"section": 1 - s})], []
-
-    t_result = Task(k, row_shape, "section", result_moves, 1)
+    hid_load, mid_load = load_all(k, hid1), load_all(k, mid1)
+    w_down1 = Weight(k, "cols", (z_down1a.out, None), (z_down1b.out, None), early=True)
+    s7 = Scatter(k, [hid_load.buf], [w_down1], mid_load.buf, low=True)
+    y_rows = Save(k, s7.out)
+    t_x, t_y = x_move(k, d_x.out, 1), x_move(k, y_rows.out, 0)
     k.early += [q_up0.load, q_down0.load]
     k.early += [v.load for v in (e_down1, e_gate1, e_out1, e_in1)]
     k.do(r_gate0.send, rows.wait, g14.begin, q_up0.send, q_down0.send)
@@ -1536,14 +1597,16 @@
     k.do(proj.wait, value.wait, taps.wait, back.run, q_down0.step, a_load.wait)
     k.do(p_in0.run, p_cols.run, p_in0.wait, r_in0.send, p_cols.wait, r_cols.send)
     k.do(r_gate0.wait, q_gate0.add, x_load.wait, gain_load.wait, s15.loop, q_up0.step)
-    k.do(q_down0.step, s15.finish, d_x.start, fill_small, d_x.wait, t_result.send)
-    k.do(small_out.wait, t_small.send, q_gate0.step, r_out0.wait, q_out0.add, r_in0.wait, q_in0.add)
+    k.do(q_down0.step, s15.finish, d_x.start, fill_small, d_x.wait, t_x.send)
+    k.do(small_out.wait, t_small.send, q_gate0.step, hid_load.wait, mid_load.wait, s7.loop)
+    k.do(r_out0.wait, q_out0.add, r_in0.wait, q_in0.add)
     k.do(r_cols.wait, q_cols.add, q_up0.wait, m_up0.send, q_down0.wait, e_down0.add)
+    k.do(s7.finish, y_rows.start, y_rows.wait, t_y.send)
     k.do(q_gate0.step, q_out0.step, q_in0.step, q_cols.step, t_small.wait, z_small.add)
     k.do(q_gate0.wait, e_gate0.add, q_out0.step, q_in0.step, q_cols.step)
     k.do(z_small.wait, t_total.add, q_out0.wait, e_out0.add, q_in0.wait, e_in0.add)
     rest = (e_down1, e_gate1, e_out1, e_in1, q_cols, e_down0, e_gate0, m_up0, e_out0, e_in0)
-    k.do(*wait(*rest, t_total, t_result))
+    k.do(*wait(*rest, t_total, t_x, t_y))
     k.build()
 
     owned = [
@@ -1555,7 +1618,7 @@
         ([q_cols], [q_cols], 0),
     ]
     return pack(
-        [(zero, one, lead) for zero, one, lead in owned], t_total, d_x.out, y_rows, t_result,
+        [(zero, one, lead) for zero, one, lead in owned], t_total, d_x.out, y_rows.out, t_x, t_y,
         (norm_gain.shape, conv_kernel.shape, qk_gain.shape),
     )
 
@@ -1577,7 +1640,7 @@
     out_v = [next(room) for _ in leads]
     load_sem, store_sem = room
     s, t = lax.axis_index("section"), lax.axis_index("tensor")
-    small, d_x, y_rows, moved, *parts = ins
+    small, d_x, y_rows, moved, moved_y, *parts = ins
 
     def either(cond, zero, one, dst, sem):
         if zero is not None:
@@ -1587,7 +1650,7 @@
 
     first = s == 0
     either(first, d_x, y_rows, own_v, load_sem.at[0])
-    pltpu.make_async_copy(moved, moved_v, load_sem.at[1]).start()
+    either(first, moved, moved_y, moved_v, load_sem.at[1])
     pltpu.make_async_copy(small, small_v, load_sem.at[2]).start()
     for j, (zero, one, _) in enumerate(terms):
         either(
@@ -1602,9 +1665,11 @@
         begins = j == 0 or terms[j - 1][2] != i
 
         def put(j=j, i=i, begins=begins):
-            value = bufs[j][...].astype(F32)
-            value = value if begins else out_v[i][...] + value
-            out_v[i][...] = value
+            def add_rows(at):
+                value = bufs[j][at, :].astype(F32)
+                out_v[i][at, :] = value if begins else out_v[i][at, :] + value
+
+            chunked(bufs[j].shape[0], add_rows)
 
         if zero is None or one is None:
             cond = first if one is None else jnp.logical_not(first)
@@ -1652,7 +1717,7 @@
         store.wait()
 
 
-def pack(owned, small, d_x, y_rows, moved, shapes):
+def pack(owned, small, d_x, y_rows, moved_x, moved_y, shapes):
     gain_shape, tap_shape, head_shape = shapes
     parts, terms, leads, out_shapes = [], [], [], []
     for i, (zero, one, lead) in enumerate(owned):
@@ -1673,7 +1738,7 @@
                 else:
                     pair.append(None)
             terms.append((*pair, i))
-    operands = [small.out.array, d_x.array, y_rows.array, moved.out.array, *parts]
+    operands = [v.array for v in (small.out, d_x, y_rows, moved_x.out, moved_y.out)] + parts
     rows = d_x.shape
     smem = pl.BlockSpec(memory_space=pltpu.VMEM)
     out_shape = [jax.ShapeDtypeStruct((1, 2) + rows, BF), jax.ShapeDtypeStruct(gain_shape, F32)]

time: 518 us -> 515 us (level)
  no operation moved by 1% of the time
where the time goes in v13:
time: 515 us; the launch traced here: 514 us
  Pallas kernels  512 us (99%)
    pallas_call x7, Pallas kernels, build(): pl.pallas_call(self.body, out_shape=[jax.ShapeDtypeStruct(v.shape, v.dtyp...  507 us

profile of v13, /device:TPU:0, one launch (start us, length us, event | category | flops | bytes accessed | tf_op | source)
XLA Modules:
  0.0 514.2 jit_solution(6872422887110260382)
XLA Ops:
  0.6 0.7 tile.4
  1.3 0.7 tile.10.refs_8_.refs_7_
  2.0 85.3 %stage0.1 = (bf16[128,512]{1,0:T(8,128)(2,1)}, bf16[128,256]{1,0:T(8,128)(2,1)}, bf16[128,1152]{1,0:T(8,128)(2,1)}, bf16[64,1152]{1,0:T(8,128)(2,1)}, bf16[128,1...) custom-call(bf16[2,256,1024]{2,1,0:T(8,128)(2,1)} %bitcast.15, ...), custom_call_target="tpu_custom_call" | custom-call | tf_op jit(solution)/shard_map/stage0/pallas_call | solution.py:173
  87.3 73.3 %stage1.1 = (bf16[4,128,1152]{2,1,0:T(8,128)(2,1)}, bf16[4,128,1152]{2,1,0:T(8,128)(2,1)}, bf16[4,288,256]{2,1,0:T(8,128)(2,1)}, bf16[4,576,256]{2,1,0:T(8,128)(...) custom-call(bf16[4,128,1152]{2,1,0:T(8,128)(2,1)} %get-tuple-element, ...), custom_call_target="tpu_custom_call" | custom-call | tf_op jit(solution)/shard_map/stage1/pallas_call | solution.py:173
  160.6 63.1 %stage2.1 = (bf16[4,128,1152]{2,1,0:T(8,128)(2,1)}, bf16[4,128,1152]{2,1,0:T(8,128)(2,1)}, bf16[4,576,256]{2,1,0:T(8,128)(2,1)}, bf16[4,576,256]{2,1,0:T(8,128)(...) custom-call(bf16[4,128,1152]{2,1,0:T(8,128)(2,1)} %get-tuple-element, ...), custom_call_target="tpu_custom_call" | custom-call | tf_op jit(solution)/shard_map/stage2/pallas_call | solution.py:173
  223.7 49.0 %stage3.1 = (bf16[1152,1024]{1,0:T(8,128)(2,1)}, bf16[1024,1152]{1,0:T(8,128)(2,1)}, bf16[1024,1152]{1,0:T(8,128)(2,1)}, bf16[1024,1152]{1,0:T(8,128)(2,1)}, f32[256,1024]{1,0:T(8,128)}, /*index=5*/f32[1,1024]{1,0:T(1,128)}) custom-call(f32[256,1024]{1,0:T(8,128)} %get-tuple-element.125.refs_0_.refs_30_, f32[2,1024]{1,0:T(2,128)} %bitcast.36, ...), custom_call_target="tpu_custom_call" | custom-call | tf_op jit(solution)/shard_map/stage3/pallas_call | solution.py:173
  272.7 60.9 %stage4.1 = (bf16[576,1024]{1,0:T(8,128)(2,1)}, bf16[4,128,1152]{2,1,0:T(8,128)(2,1)}, bf16[256,1152]{1,0:T(8,128)(2,1)}, bf16[256,1024]{1,0:T(8,128)(2,1)}, bf1...) custom-call(bf16[1152,1024]{1,0:T(8,128)(2,1)} %get-tuple-element.13, ...), custom_call_target="tpu_custom_call" | custom-call | tf_op jit(solution)/shard_map/stage4/pallas_call | solution.py:173
  333.6 66.0 %stage5.1 = (bf16[128,1152]{1,0:T(8,128)(2,1)}, bf16[256,1152]{1,0:T(8,128)(2,1)}, bf16[128,256]{1,0:T(8,128)(2,1)}, bf16[4,128,512]{2,1,0:T(8,128)(2,1)}, bf16[...) custom-call(bf16[1024,1152]{1,0:T(8,128)(2,1)} %get-tuple-element.13, ...), custom_call_target="tpu_custom_call" | custom-call | tf_op jit(solution)/shard_map/stage5/pallas_call | solution.py:173
  399.7 109.8 %stage6.1 = (bf16[4,128,1152]{2,1,0:T(8,128)(2,1)}, bf16[128,1152]{1,0:T(8,128)(2,1)}, bf16[576,256]{1,0:T(8,128)(2,1)}, bf16[256,1152]{1,0:T(8,128)(2,1)}, bf16...) custom-call(bf16[1024,1152]{1,0:T(8,128)(2,1)} %get-tuple-element.15, ...), custom_call_target="tpu_custom_call" | custom-call | tf_op jit(solution)/shard_map/stage6/pallas_call | solution.py:173
  509.5 4.6 pack.1

commit v14 on v13

--- a/solution.py
+++ b/solution.py
@@ -21,6 +21,7 @@
 BF = jnp.bfloat16
 F32 = jnp.float32
 ROW_BLOCK = 256
+STRIP = 32
 
 
 def contract(left_op, right_op, left_dim, right_dim):
@@ -841,15 +842,16 @@
         for i in range(2):
 
             def put(j, carry):
-                at = i * self.half + j * 32
-                part = self.x.ref[pl.ds(pl.multiple_of(at, 32), 32), :].astype(F32)
+                at = i * self.half + j * STRIP
+                part = self.x.ref[pl.ds(pl.multiple_of(at, STRIP), STRIP), :].astype(F32)
                 if self.gain is not None:
                     val, row = self.gain
                     part = norm_rows(part, val.ref[row : row + 1, :])
-                self.full.ref[pl.ds(pl.multiple_of(me * self.rows + at, 32), 32), :] = part.astype(BF)
+                to = pl.ds(pl.multiple_of(me * self.rows + at, STRIP), STRIP)
+                self.full.ref[to, :] = part.astype(BF)
                 return carry
 
-            lax.fori_loop(0, self.half // 32, put, 0)
+            lax.fori_loop(0, self.half // STRIP, put, 0)
             self.move("cross", i).start()
             self.move("sib", i).start()
 
@@ -1009,8 +1011,8 @@
             self.move("cross", i).wait_recv()
 
             def add_rows(j, carry):
-                inner = pl.ds(pl.multiple_of(j * 32, 32), 32)
-                part = pl.ds(pl.multiple_of(i * self.half + j * 32, 32), 32)
+                inner = block_of(j, STRIP)
+                part = pl.ds(pl.multiple_of(i * self.half + j * STRIP, STRIP), STRIP)
                 total = self.own.ref[part, :] + self.from_o.ref[part, :].astype(F32)
                 total = total + self.from_c.ref[i, inner, :].astype(F32)
                 resid = self.resid.ref[part, :].astype(F32)
@@ -1023,7 +1025,7 @@
                 self.out.ref[part, :] = (resid + total).astype(self.out.dtype)
                 return carry
 
-            lax.fori_loop(0, self.half // 32, add_rows, 0)
+            lax.fori_loop(0, self.half // STRIP, add_rows, 0)
 
     def end(self):
         self.move("near").wait_send()
@@ -1177,6 +1179,13 @@
     def join(self, val, rows):
         return jnp.concatenate([val.ref[h, rows, :] for h in range(val.shape[0])], axis=1)
 
+    def gains(self):
+        gain = self.gain.ref[...]
+        return (
+            jnp.concatenate([gain[0:1]] * self.heads, axis=1),
+            jnp.concatenate([gain[1:2]] * self.kv_heads, axis=1),
+        )
+
     def angles(self, rows):
         c, n = self.cos.ref[rows, :], self.sin.ref[rows, :]
         repeat = self.q_cols // c.shape[1]
@@ -1202,9 +1211,10 @@
 
         def prepare(rows):
             c, n = self.angles(rows)
-            q = head_norm(proj[rows, :q_cols], self.gain.ref[0:1, :], size)
+            q_gain, k_gain = self.gains()
+            q = head_norm(proj[rows, :q_cols], q_gain, size)
             q = (q * c + turn(q, size, False) * n).astype(BF)
-            k = head_norm(proj[rows, q_cols : q_cols + k_cols], self.gain.ref[1:2, :k_cols], size)
+            k = head_norm(proj[rows, q_cols : q_cols + k_cols], k_gain, size)
             k = (k * c[:, :k_cols] + turn(k, size, False) * n[:, :k_cols]).astype(BF)
             self.q_rot.ref[rows, :] = q
             self.k_rot.ref[rows, :] = k
@@ -1309,10 +1319,9 @@
             dq, dk, dv = (self.join(v, rows) for v in (self.dq_h, self.dk_h, self.dv_h))
             dq = dq * c + turn(dq * n, size, True)
             dk = dk * c[:, :k_cols] + turn(dk * n[:, :k_cols], size, True)
-            dq, q_sum = head_norm_back(proj[rows, :q_cols], self.gain.ref[0:1, :], dq, size)
-            dk, k_sum = head_norm_back(
-                proj[rows, q_cols : q_cols + k_cols], self.gain.ref[1:2, :k_cols], dk, size
-            )
+            q_gain, k_gain = self.gains()
+            dq, q_sum = head_norm_back(proj[rows, :q_cols], q_gain, dq, size)
+            dk, k_sum = head_norm_back(proj[rows, q_cols : q_cols + k_cols], k_gain, dk, size)
             self.q_gain.ref[...] += q_sum
             self.k_gain.ref[...] += k_sum
             self.d_proj.ref[rows, :q_cols] = dq.astype(BF)
@@ -1332,7 +1341,6 @@
 
     seqs, own_gain = boundary[0], norm_gain[0]
     sh_in, sh_out, sh_gate, sh_up, sh_down = (v[0] for v in (mix_in, mix_out, w_gate, w_up, w_down))
-    head_gain = jnp.tile(qk_gain, (1, channels // size))
 
     def gains_of(k, block, other, early=True):
         own, moved = k.input(own_gain), as_val(k, other)
@@ -1392,7 +1400,7 @@
     k.do(*wait(t_gate1, t_down0a, t_down0b, t_down1, z_gate0b, x_gate0a, z_up0))
     k.build()
     a0, proj0, value0 = (out for _, out, _ in g0.saved)
-    table_arrays = [head_gain] + [v.out for v in angles.saves]
+    table_arrays = [qk_gain] + [v.out for v in angles.saves]
     y0, mid0 = y0.out, mid0.out
 
     k = Kernel(1)
@@ -1469,6 +1477,7 @@
     k = Kernel(4)
     r_down1 = x_half(k, p_down1.out)
     r_gate1, q_up1 = x_slots(k, p_gate1.out, "rows"), sum_scatter(k, "rows", p_up1.out)
+    q_gate1 = sum_scatter(k, "rows", p_gate1.out, r_gate1.out)
     rows, gain_load = load_all(k, d_mid1), gains_of(k, 1, t_gain.out)
     value = load_all(k, z_rows)
     tables = [load_all(k, v) for v in table_arrays]
@@ -1479,26 +1488,26 @@
     p_out1 = Product(k, y_load.buf, g10.full)
     back = AttendBack(k, proj.buf, tables, size, q_load.buf, k_load.buf, g10.values[0])
     p_in1 = Product(k, a_load.buf, back.d_proj)
-    r_out1 = x_half(k, p_out1.out)
     s11 = Scatter(
         k, [back.d_proj], [w_in1], rows.buf, (value.buf, (gain_load.buf, 0)), True, low=True
     )
     d_z, gain10 = Save(k, s11.out), Save(k, s11.gain_grad)
     head_gains = [Save(k, back.q_gain), Save(k, back.k_gain)]
     k.early.append(q_up1.load)
-    k.do(r_down1.send, r_gate1.send, rows.wait, g10.begin, q_up1.send, g10.loop)
-    k.do(y_load.wait, p_out1.run, q_up1.step, p_out1.wait, r_out1.send)
-    k.do(proj.wait, q_load.wait, k_load.wait, lambda: back.run(q_up1.step))
-    k.do(*(v.start for v in head_gains))
+    k.do(r_gate1.send, r_down1.send, rows.wait, g10.begin, q_up1.send, g10.loop)
+    k.do(y_load.wait, p_out1.run, q_up1.step)
+    k.do(proj.wait, q_load.wait, k_load.wait)
+    k.do(lambda: back.run(r_gate1.wait, q_gate1.add, q_up1.step))
+    k.do(q_gate1.step, *(v.start for v in head_gains))
     k.do(gain_load.wait, value.wait, s11.loop, a_load.wait, p_in1.run)
-    k.do(s11.finish, d_z.start, gain10.start, p_in1.wait)
-    k.do(*wait(r_down1, q_up1, r_gate1, r_out1))
+    k.do(s11.finish, d_z.start, gain10.start, q_gate1.step, p_out1.wait, p_in1.wait)
+    k.do(*wait(r_down1, q_up1, q_gate1))
     k.build()
     d_z, gain10 = d_z.out, gain10.out
     q_gain, k_gain = (v.out for v in head_gains)
 
     k = Kernel(5)
-    q_gate1, m_up1 = sum_scatter(k, "rows", p_gate1.out, r_gate1.out), x_move(k, q_up1.out, 0)
+    m_up1, r_out1 = x_move(k, q_up1.out, 0), x_half(k, p_out1.out)
     q_out1 = sum_scatter(k, "cols", p_out1.out, r_out1.out)
     r_in1 = x_slots(k, p_in1.out, "rows")
     q_in1 = sum_scatter(k, "rows", p_in1.out, r_in1.out)
@@ -1518,14 +1527,15 @@
         k, g12.values, [w_gate0, w_up0], rows.buf, (value.buf, (gain_load.buf, 1)), True
     )
     d_mid0, gain01 = Save(k, s13.out), Save(k, s13.gain_grad)
-    k.early += [q_gate1.load, q_down1.load, q_out1.load]
-    k.do(r_in1.send, m_up1.send, rows.wait, g12.begin, q_gate1.send, q_down1.send, q_out1.send)
-    k.do(gate_load.wait, up_load.wait, g12.loop, q_gate1.step, q_down1.step, q_out1.step)
-    k.do(hid_load.wait, p_down0.run, p_down0.wait, r_down0.send, r_in1.wait, q_in1.add)
-    k.do(s13.loop, q_gate1.step, q_down1.step, q_out1.step)
-    k.do(m_load.wait, p_gate0.run, q_in1.step, p_up0.run, value.wait, gain_load.wait)
-    k.do(s13.finish, d_mid0.start, gain01.start, q_in1.step, p_gate0.wait, p_up0.wait)
-    k.do(*wait(q_gate1, q_out1, q_in1, q_down1, m_up1, r_down0))
+    k.early.append(q_down1.load)
+    k.do(r_in1.send, r_out1.send, m_up1.send, rows.wait, g12.begin, q_down1.send)
+    k.do(gate_load.wait, up_load.wait, g12.loop, q_down1.step)
+    k.do(hid_load.wait, p_down0.run, p_down0.wait, r_down0.send)
+    k.do(r_in1.wait, q_in1.add, r_out1.wait, q_out1.add, q_down1.step)
+    k.do(s13.loop, q_in1.step, q_out1.step, m_load.wait, p_gate0.run, q_in1.step, q_out1.step)
+    k.do(p_up0.run, value.wait, gain_load.wait)
+    k.do(s13.finish, d_mid0.start, gain01.start, p_gate0.wait, p_up0.wait)
+    k.do(*wait(q_out1, q_in1, q_down1, m_up1, r_down0))
     k.build()
     d_mid0, gain01 = d_mid0.out, gain01.out
 

time: 515 us -> 519 us (level)
  Pallas kernels: 512 us -> 518 us
    pallas_call x7, Pallas kernels: 507 us -> 513 us  [build(): pl.pallas_call(self.body, out_shape=[jax.ShapeDtypeStruct(v.shape, v.dtyp...]
where the time goes in v14:
time: 519 us; the launch traced here: 518 us
  Pallas kernels  518 us (100%)
    pallas_call x7, Pallas kernels, build(): pl.pallas_call(self.body, out_shape=[jax.ShapeDtypeStruct(v.shape, v.dtyp...  513 us

profile of v14, /device:TPU:0, one launch (start us, length us, event | category | flops | bytes accessed | tf_op | source)
XLA Modules:
  0.0 518.4 jit_solution(15317902436300423247)
XLA Ops:
  0.6 85.5 %stage0.1 = (bf16[128,512]{1,0:T(8,128)(2,1)}, bf16[128,256]{1,0:T(8,128)(2,1)}, bf16[128,1152]{1,0:T(8,128)(2,1)}, bf16[64,1152]{1,0:T(8,128)(2,1)}, bf16[128,1...) custom-call(bf16[2,256,1024]{2,1,0:T(8,128)(2,1)} %bitcast.15, ...), custom_call_target="tpu_custom_call" | custom-call | tf_op jit(solution)/shard_map/stage0/pallas_call | solution.py:174
  86.1 73.3 %stage1.1 = (bf16[4,128,1152]{2,1,0:T(8,128)(2,1)}, bf16[4,128,1152]{2,1,0:T(8,128)(2,1)}, bf16[4,288,256]{2,1,0:T(8,128)(2,1)}, bf16[4,576,256]{2,1,0:T(8,128)(...) custom-call(bf16[4,128,1152]{2,1,0:T(8,128)(2,1)} %get-tuple-element, ...), custom_call_target="tpu_custom_call" | custom-call | tf_op jit(solution)/shard_map/stage1/pallas_call | solution.py:174
  159.5 63.0 %stage2.1 = (bf16[4,128,1152]{2,1,0:T(8,128)(2,1)}, bf16[4,128,1152]{2,1,0:T(8,128)(2,1)}, bf16[4,576,256]{2,1,0:T(8,128)(2,1)}, bf16[4,576,256]{2,1,0:T(8,128)(...) custom-call(bf16[4,128,1152]{2,1,0:T(8,128)(2,1)} %get-tuple-element, ...), custom_call_target="tpu_custom_call" | custom-call | tf_op jit(solution)/shard_map/stage2/pallas_call | solution.py:174
  222.5 49.0 %stage3.1 = (bf16[1152,1024]{1,0:T(8,128)(2,1)}, bf16[1024,1152]{1,0:T(8,128)(2,1)}, bf16[1024,1152]{1,0:T(8,128)(2,1)}, bf16[1024,1152]{1,0:T(8,128)(2,1)}, f32[256,1024]{1,0:T(8,128)}, /*index=5*/f32[1,1024]{1,0:T(1,128)}) custom-call(f32[256,1024]{1,0:T(8,128)} %get-tuple-element.123.refs_0_.refs_30_, f32[2,1024]{1,0:T(2,128)} %bitcast.36, ...), custom_call_target="tpu_custom_call" | custom-call | tf_op jit(solution)/shard_map/stage3/pallas_call | solution.py:174
  271.5 74.3 %stage4.1 = (bf16[576,1024]{1,0:T(8,128)(2,1)}, bf16[4,128,1152]{2,1,0:T(8,128)(2,1)}, bf16[256,1152]{1,0:T(8,128)(2,1)}, bf16[128,1152]{1,0:T(8,128)(2,1)}, bf1...) custom-call(bf16[1152,1024]{1,0:T(8,128)(2,1)} %get-tuple-element.13, ...), custom_call_target="tpu_custom_call" | custom-call | tf_op jit(solution)/shard_map/stage4/pallas_call | solution.py:174
  345.8 57.8 %stage5.1 = (bf16[256,1152]{1,0:T(8,128)(2,1)}, bf16[128,1024]{1,0:T(8,128)(2,1)}, bf16[128,256]{1,0:T(8,128)(2,1)}, bf16[4,128,512]{2,1,0:T(8,128)(2,1)}, bf16[...) custom-call(bf16[256,1152]{1,0:T(8,128)(2,1)} %get-tuple-element.139, ...), custom_call_target="tpu_custom_call" | custom-call | tf_op jit(solution)/shard_map/stage5/pallas_call | solution.py:174
  403.6 110.1 %stage6.1 = (bf16[4,128,1152]{2,1,0:T(8,128)(2,1)}, bf16[128,1152]{1,0:T(8,128)(2,1)}, bf16[576,256]{1,0:T(8,128)(2,1)}, bf16[256,1152]{1,0:T(8,128)(2,1)}, bf16...) custom-call(bf16[1024,1152]{1,0:T(8,128)(2,1)} %get-tuple-element.15, ...), custom_call_target="tpu_custom_call" | custom-call | tf_op jit(solution)/shard_map/stage6/pallas_call | solution.py:174
  513.7 4.6 pack.1

commit v15 on v14

--- a/solution.py
+++ b/solution.py
@@ -1477,7 +1477,6 @@
     k = Kernel(4)
     r_down1 = x_half(k, p_down1.out)
     r_gate1, q_up1 = x_slots(k, p_gate1.out, "rows"), sum_scatter(k, "rows", p_up1.out)
-    q_gate1 = sum_scatter(k, "rows", p_gate1.out, r_gate1.out)
     rows, gain_load = load_all(k, d_mid1), gains_of(k, 1, t_gain.out)
     value = load_all(k, z_rows)
     tables = [load_all(k, v) for v in table_arrays]
@@ -1494,19 +1493,19 @@
     d_z, gain10 = Save(k, s11.out), Save(k, s11.gain_grad)
     head_gains = [Save(k, back.q_gain), Save(k, back.k_gain)]
     k.early.append(q_up1.load)
-    k.do(r_gate1.send, r_down1.send, rows.wait, g10.begin, q_up1.send, g10.loop)
+    k.do(r_down1.send, r_gate1.send, rows.wait, g10.begin, q_up1.send, g10.loop)
     k.do(y_load.wait, p_out1.run, q_up1.step)
-    k.do(proj.wait, q_load.wait, k_load.wait)
-    k.do(lambda: back.run(r_gate1.wait, q_gate1.add, q_up1.step))
-    k.do(q_gate1.step, *(v.start for v in head_gains))
+    k.do(proj.wait, q_load.wait, k_load.wait, lambda: back.run(q_up1.step))
+    k.do(*(v.start for v in head_gains))
     k.do(gain_load.wait, value.wait, s11.loop, a_load.wait, p_in1.run)
-    k.do(s11.finish, d_z.start, gain10.start, q_gate1.step, p_out1.wait, p_in1.wait)
-    k.do(*wait(r_down1, q_up1, q_gate1))
+    k.do(s11.finish, d_z.start, gain10.start, p_out1.wait, p_in1.wait)
+    k.do(*wait(r_down1, r_gate1, q_up1))
     k.build()
     d_z, gain10 = d_z.out, gain10.out
     q_gain, k_gain = (v.out for v in head_gains)
 
     k = Kernel(5)
+    q_gate1 = sum_scatter(k, "rows", p_gate1.out, r_gate1.out)
     m_up1, r_out1 = x_move(k, q_up1.out, 0), x_half(k, p_out1.out)
     q_out1 = sum_scatter(k, "cols", p_out1.out, r_out1.out)
     r_in1 = x_slots(k, p_in1.out, "rows")
@@ -1527,15 +1526,15 @@
         k, g12.values, [w_gate0, w_up0], rows.buf, (value.buf, (gain_load.buf, 1)), True
     )
     d_mid0, gain01 = Save(k, s13.out), Save(k, s13.gain_grad)
-    k.early.append(q_down1.load)
-    k.do(r_in1.send, r_out1.send, m_up1.send, rows.wait, g12.begin, q_down1.send)
-    k.do(gate_load.wait, up_load.wait, g12.loop, q_down1.step)
+    k.early += [q_gate1.load, q_down1.load]
+    k.do(r_in1.send, r_out1.send, m_up1.send, q_gate1.send, rows.wait, g12.begin, q_down1.send)
+    k.do(gate_load.wait, up_load.wait, g12.loop, q_gate1.step, q_down1.step)
     k.do(hid_load.wait, p_down0.run, p_down0.wait, r_down0.send)
-    k.do(r_in1.wait, q_in1.add, r_out1.wait, q_out1.add, q_down1.step)
-    k.do(s13.loop, q_in1.step, q_out1.step, m_load.wait, p_gate0.run, q_in1.step, q_out1.step)
-    k.do(p_up0.run, value.wait, gain_load.wait)
-    k.do(s13.finish, d_mid0.start, gain01.start, p_gate0.wait, p_up0.wait)
-    k.do(*wait(q_out1, q_in1, q_down1, m_up1, r_down0))
+    k.do(r_in1.wait, q_in1.add, r_out1.wait, q_out1.add)
+    k.do(s13.loop, q_gate1.step, q_down1.step, q_in1.step, q_out1.step)
+    k.do(m_load.wait, p_gate0.run, p_up0.run, value.wait, gain_load.wait)
+    k.do(s13.finish, d_mid0.start, gain01.start, q_in1.step, q_out1.step)
+    k.do(p_gate0.wait, p_up0.wait, *wait(q_gate1, q_out1, q_in1, q_down1, m_up1, r_down0))
     k.build()
     d_mid0, gain01 = d_mid0.out, gain01.out
 
@@ -1601,7 +1600,7 @@
     t_x, t_y = x_move(k, d_x.out, 1), x_move(k, y_rows.out, 0)
     k.early += [q_up0.load, q_down0.load]
     k.early += [v.load for v in (e_down1, e_gate1, e_out1, e_in1)]
-    k.do(r_gate0.send, rows.wait, g14.begin, q_up0.send, q_down0.send)
+    k.do(r_gate0.send, q_up0.send, rows.wait, g14.begin, q_down0.send)
     k.do(e_down1.send, e_gate1.send, e_out1.send, e_in1.send, g14.loop)
     k.do(y_load.wait, p_out0.run, p_out0.wait, r_out0.send, q_up0.step)
     k.do(proj.wait, value.wait, taps.wait, back.run, q_down0.step, a_load.wait)

time: 519 us -> 518 us (level)
  no operation moved by 1% of the time
where the time goes in v15:
time: 518 us; the launch traced here: 517 us
  Pallas kernels  516 us (100%)
    pallas_call x7, Pallas kernels, build(): pl.pallas_call(self.body, out_shape=[jax.ShapeDtypeStruct(v.shape, v.dtyp...  512 us

profile of v15, /device:TPU:0, one launch (start us, length us, event | category | flops | bytes accessed | tf_op | source)
XLA Modules:
  0.0 517.1 jit_solution(10229482407210381552)
XLA Ops:
  0.6 85.4 %stage0.1 = (bf16[128,512]{1,0:T(8,128)(2,1)}, bf16[128,256]{1,0:T(8,128)(2,1)}, bf16[128,1152]{1,0:T(8,128)(2,1)}, bf16[64,1152]{1,0:T(8,128)(2,1)}, bf16[128,1...) custom-call(bf16[2,256,1024]{2,1,0:T(8,128)(2,1)} %bitcast.15, ...), custom_call_target="tpu_custom_call" | custom-call | tf_op jit(solution)/shard_map/stage0/pallas_call | solution.py:174
  86.1 73.4 %stage1.1 = (bf16[4,128,1152]{2,1,0:T(8,128)(2,1)}, bf16[4,128,1152]{2,1,0:T(8,128)(2,1)}, bf16[4,288,256]{2,1,0:T(8,128)(2,1)}, bf16[4,576,256]{2,1,0:T(8,128)(...) custom-call(bf16[4,128,1152]{2,1,0:T(8,128)(2,1)} %get-tuple-element, ...), custom_call_target="tpu_custom_call" | custom-call | tf_op jit(solution)/shard_map/stage1/pallas_call | solution.py:174
  159.5 63.0 %stage2.1 = (bf16[4,128,1152]{2,1,0:T(8,128)(2,1)}, bf16[4,128,1152]{2,1,0:T(8,128)(2,1)}, bf16[4,576,256]{2,1,0:T(8,128)(2,1)}, bf16[4,576,256]{2,1,0:T(8,128)(...) custom-call(bf16[4,128,1152]{2,1,0:T(8,128)(2,1)} %get-tuple-element, ...), custom_call_target="tpu_custom_call" | custom-call | tf_op jit(solution)/shard_map/stage2/pallas_call | solution.py:174
  222.5 49.0 %stage3.1 = (bf16[1152,1024]{1,0:T(8,128)(2,1)}, bf16[1024,1152]{1,0:T(8,128)(2,1)}, bf16[1024,1152]{1,0:T(8,128)(2,1)}, bf16[1024,1152]{1,0:T(8,128)(2,1)}, f32[256,1024]{1,0:T(8,128)}, /*index=5*/f32[1,1024]{1,0:T(1,128)}) custom-call(f32[256,1024]{1,0:T(8,128)} %get-tuple-element.124.refs_0_.refs_30_, f32[2,1024]{1,0:T(2,128)} %bitcast.36, ...), custom_call_target="tpu_custom_call" | custom-call | tf_op jit(solution)/shard_map/stage3/pallas_call | solution.py:174
  271.5 57.9 %stage4.1 = (bf16[576,1024]{1,0:T(8,128)(2,1)}, bf16[4,128,1152]{2,1,0:T(8,128)(2,1)}, bf16[256,1152]{1,0:T(8,128)(2,1)}, bf16[256,1024]{1,0:T(8,128)(2,1)}, bf1...) custom-call(bf16[1152,1024]{1,0:T(8,128)(2,1)} %get-tuple-element.13, ...), custom_call_target="tpu_custom_call" | custom-call | tf_op jit(solution)/shard_map/stage4/pallas_call | solution.py:174
  329.4 73.5 %stage5.1 = (bf16[128,1152]{1,0:T(8,128)(2,1)}, bf16[256,1152]{1,0:T(8,128)(2,1)}, bf16[128,1024]{1,0:T(8,128)(2,1)}, bf16[128,256]{1,0:T(8,128)(2,1)}, bf16[4,1...) custom-call(bf16[1024,1152]{1,0:T(8,128)(2,1)} %get-tuple-element.13, ...), custom_call_target="tpu_custom_call" | custom-call | tf_op jit(solution)/shard_map/stage5/pallas_call | solution.py:174
  402.9 109.4 %stage6.1 = (bf16[4,128,1152]{2,1,0:T(8,128)(2,1)}, bf16[128,1152]{1,0:T(8,128)(2,1)}, bf16[576,256]{1,0:T(8,128)(2,1)}, bf16[256,1152]{1,0:T(8,128)(2,1)}, bf16...) custom-call(bf16[1024,1152]{1,0:T(8,128)(2,1)} %get-tuple-element.15, ...), custom_call_target="tpu_custom_call" | custom-call | tf_op jit(solution)/shard_map/stage6/pallas_call | solution.py:174
  512.3 4.6 pack.1

commit v16 on v15

--- a/solution.py
+++ b/solution.py
@@ -1487,6 +1487,7 @@
     p_out1 = Product(k, y_load.buf, g10.full)
     back = AttendBack(k, proj.buf, tables, size, q_load.buf, k_load.buf, g10.values[0])
     p_in1 = Product(k, a_load.buf, back.d_proj)
+    r_out1 = x_half(k, p_out1.out)
     s11 = Scatter(
         k, [back.d_proj], [w_in1], rows.buf, (value.buf, (gain_load.buf, 0)), True, low=True
     )
@@ -1494,19 +1495,18 @@
     head_gains = [Save(k, back.q_gain), Save(k, back.k_gain)]
     k.early.append(q_up1.load)
     k.do(r_down1.send, r_gate1.send, rows.wait, g10.begin, q_up1.send, g10.loop)
-    k.do(y_load.wait, p_out1.run, q_up1.step)
+    k.do(y_load.wait, p_out1.run, q_up1.step, p_out1.wait, r_out1.send)
     k.do(proj.wait, q_load.wait, k_load.wait, lambda: back.run(q_up1.step))
     k.do(*(v.start for v in head_gains))
     k.do(gain_load.wait, value.wait, s11.loop, a_load.wait, p_in1.run)
-    k.do(s11.finish, d_z.start, gain10.start, p_out1.wait, p_in1.wait)
-    k.do(*wait(r_down1, r_gate1, q_up1))
+    k.do(s11.finish, d_z.start, gain10.start, p_in1.wait)
+    k.do(*wait(r_down1, q_up1, r_gate1, r_out1))
     k.build()
     d_z, gain10 = d_z.out, gain10.out
     q_gain, k_gain = (v.out for v in head_gains)
 
     k = Kernel(5)
-    q_gate1 = sum_scatter(k, "rows", p_gate1.out, r_gate1.out)
-    m_up1, r_out1 = x_move(k, q_up1.out, 0), x_half(k, p_out1.out)
+    q_gate1, m_up1 = sum_scatter(k, "rows", p_gate1.out, r_gate1.out), x_move(k, q_up1.out, 0)
     q_out1 = sum_scatter(k, "cols", p_out1.out, r_out1.out)
     r_in1 = x_slots(k, p_in1.out, "rows")
     q_in1 = sum_scatter(k, "rows", p_in1.out, r_in1.out)
@@ -1526,15 +1526,14 @@
         k, g12.values, [w_gate0, w_up0], rows.buf, (value.buf, (gain_load.buf, 1)), True
     )
     d_mid0, gain01 = Save(k, s13.out), Save(k, s13.gain_grad)
-    k.early += [q_gate1.load, q_down1.load]
-    k.do(r_in1.send, r_out1.send, m_up1.send, q_gate1.send, rows.wait, g12.begin, q_down1.send)
-    k.do(gate_load.wait, up_load.wait, g12.loop, q_gate1.step, q_down1.step)
-    k.do(hid_load.wait, p_down0.run, p_down0.wait, r_down0.send)
-    k.do(r_in1.wait, q_in1.add, r_out1.wait, q_out1.add)
-    k.do(s13.loop, q_gate1.step, q_down1.step, q_in1.step, q_out1.step)
-    k.do(m_load.wait, p_gate0.run, p_up0.run, value.wait, gain_load.wait)
-    k.do(s13.finish, d_mid0.start, gain01.start, q_in1.step, q_out1.step)
-    k.do(p_gate0.wait, p_up0.wait, *wait(q_gate1, q_out1, q_in1, q_down1, m_up1, r_down0))
+    k.early += [q_gate1.load, q_down1.load, q_out1.load]
+    k.do(r_in1.send, m_up1.send, rows.wait, g12.begin, q_gate1.send, q_down1.send, q_out1.send)
+    k.do(gate_load.wait, up_load.wait, g12.loop, q_gate1.step, q_down1.step, q_out1.step)
+    k.do(hid_load.wait, p_down0.run, p_down0.wait, r_down0.send, r_in1.wait, q_in1.add)
+    k.do(s13.loop, q_gate1.step, q_down1.step, q_out1.step)
+    k.do(m_load.wait, p_gate0.run, q_in1.step, p_up0.run, value.wait, gain_load.wait)
+    k.do(s13.finish, d_mid0.start, gain01.start, q_in1.step, p_gate0.wait, p_up0.wait)
+    k.do(*wait(q_gate1, q_out1, q_in1, q_down1, m_up1, r_down0))
     k.build()
     d_mid0, gain01 = d_mid0.out, gain01.out
 

time: 518 us -> 513 us (level)
  no operation moved by 1% of the time
where the time goes in v16:
time: 513 us
  Pallas kernels  512 us (100%)
    pallas_call x7, Pallas kernels, build(): pl.pallas_call(self.body, out_shape=[jax.ShapeDtypeStruct(v.shape, v.dtyp...  507 us

profile of v16, /device:TPU:0, one launch (start us, length us, event | category | flops | bytes accessed | tf_op | source)
XLA Modules:
  0.0 512.7 jit_solution(15577385799237284795)
XLA Ops:
  0.6 85.4 %stage0.1 = (bf16[128,512]{1,0:T(8,128)(2,1)}, bf16[128,256]{1,0:T(8,128)(2,1)}, bf16[128,1152]{1,0:T(8,128)(2,1)}, bf16[64,1152]{1,0:T(8,128)(2,1)}, bf16[128,1...) custom-call(bf16[2,256,1024]{2,1,0:T(8,128)(2,1)} %bitcast.15, ...), custom_call_target="tpu_custom_call" | custom-call | tf_op jit(solution)/shard_map/stage0/pallas_call | solution.py:174
  86.1 73.4 %stage1.1 = (bf16[4,128,1152]{2,1,0:T(8,128)(2,1)}, bf16[4,128,1152]{2,1,0:T(8,128)(2,1)}, bf16[4,288,256]{2,1,0:T(8,128)(2,1)}, bf16[4,576,256]{2,1,0:T(8,128)(...) custom-call(bf16[4,128,1152]{2,1,0:T(8,128)(2,1)} %get-tuple-element, ...), custom_call_target="tpu_custom_call" | custom-call | tf_op jit(solution)/shard_map/stage1/pallas_call | solution.py:174
  159.5 63.0 %stage2.1 = (bf16[4,128,1152]{2,1,0:T(8,128)(2,1)}, bf16[4,128,1152]{2,1,0:T(8,128)(2,1)}, bf16[4,576,256]{2,1,0:T(8,128)(2,1)}, bf16[4,576,256]{2,1,0:T(8,128)(...) custom-call(bf16[4,128,1152]{2,1,0:T(8,128)(2,1)} %get-tuple-element, ...), custom_call_target="tpu_custom_call" | custom-call | tf_op jit(solution)/shard_map/stage2/pallas_call | solution.py:174
  222.5 49.0 %stage3.1 = (bf16[1152,1024]{1,0:T(8,128)(2,1)}, bf16[1024,1152]{1,0:T(8,128)(2,1)}, bf16[1024,1152]{1,0:T(8,128)(2,1)}, bf16[1024,1152]{1,0:T(8,128)(2,1)}, f32[256,1024]{1,0:T(8,128)}, /*index=5*/f32[1,1024]{1,0:T(1,128)}) custom-call(f32[256,1024]{1,0:T(8,128)} %get-tuple-element.125.refs_0_.refs_30_, f32[2,1024]{1,0:T(2,128)} %bitcast.36, ...), custom_call_target="tpu_custom_call" | custom-call | tf_op jit(solution)/shard_map/stage3/pallas_call | solution.py:174
  271.5 60.9 %stage4.1 = (bf16[576,1024]{1,0:T(8,128)(2,1)}, bf16[4,128,1152]{2,1,0:T(8,128)(2,1)}, bf16[256,1152]{1,0:T(8,128)(2,1)}, bf16[256,1024]{1,0:T(8,128)(2,1)}, bf1...) custom-call(bf16[1152,1024]{1,0:T(8,128)(2,1)} %get-tuple-element.13, ...), custom_call_target="tpu_custom_call" | custom-call | tf_op jit(solution)/shard_map/stage4/pallas_call | solution.py:174
  332.4 66.0 %stage5.1 = (bf16[128,1152]{1,0:T(8,128)(2,1)}, bf16[256,1152]{1,0:T(8,128)(2,1)}, bf16[128,256]{1,0:T(8,128)(2,1)}, bf16[4,128,512]{2,1,0:T(8,128)(2,1)}, bf16[...) custom-call(bf16[1024,1152]{1,0:T(8,128)(2,1)} %get-tuple-element.13, ...), custom_call_target="tpu_custom_call" | custom-call | tf_op jit(solution)/shard_map/stage5/pallas_call | solution.py:174
  398.4 109.5 %stage6.1 = (bf16[4,128,1152]{2,1,0:T(8,128)(2,1)}, bf16[128,1152]{1,0:T(8,128)(2,1)}, bf16[576,256]{1,0:T(8,128)(2,1)}, bf16[256,1152]{1,0:T(8,128)(2,1)}, bf16...) custom-call(bf16[1024,1152]{1,0:T(8,128)(2,1)} %get-tuple-element.15, ...), custom_call_target="tpu_custom_call" | custom-call | tf_op jit(solution)/shard_map/stage6/pallas_call | solution.py:174
  507.9 4.6 pack.1

commit v17 on v16

--- a/solution.py
+++ b/solution.py
@@ -1494,7 +1494,7 @@
     d_z, gain10 = Save(k, s11.out), Save(k, s11.gain_grad)
     head_gains = [Save(k, back.q_gain), Save(k, back.k_gain)]
     k.early.append(q_up1.load)
-    k.do(r_down1.send, r_gate1.send, rows.wait, g10.begin, q_up1.send, g10.loop)
+    k.do(r_down1.send, r_gate1.send, q_up1.send, rows.wait, g10.begin, g10.loop)
     k.do(y_load.wait, p_out1.run, q_up1.step, p_out1.wait, r_out1.send)
     k.do(proj.wait, q_load.wait, k_load.wait, lambda: back.run(q_up1.step))
     k.do(*(v.start for v in head_gains))
@@ -1527,7 +1527,7 @@
     )
     d_mid0, gain01 = Save(k, s13.out), Save(k, s13.gain_grad)
     k.early += [q_gate1.load, q_down1.load, q_out1.load]
-    k.do(r_in1.send, m_up1.send, rows.wait, g12.begin, q_gate1.send, q_down1.send, q_out1.send)
+    k.do(r_in1.send, m_up1.send, q_gate1.send, rows.wait, g12.begin, q_down1.send, q_out1.send)
     k.do(gate_load.wait, up_load.wait, g12.loop, q_gate1.step, q_down1.step, q_out1.step)
     k.do(hid_load.wait, p_down0.run, p_down0.wait, r_down0.send, r_in1.wait, q_in1.add)
     k.do(s13.loop, q_gate1.step, q_down1.step, q_out1.step)

time: 513 us -> 518 us (level)
  no operation moved by 1% of the time
where the time goes in v17:
time: 518 us; the launch traced here: 517 us
  Pallas kernels  516 us (100%)
    pallas_call x7, Pallas kernels, build(): pl.pallas_call(self.body, out_shape=[jax.ShapeDtypeStruct(v.shape, v.dtyp...  512 us

profile of v17, /device:TPU:0, one launch (start us, length us, event | category | flops | bytes accessed | tf_op | source)
XLA Modules:
  0.0 517.3 jit_solution(4951482801291499873)
XLA Ops:
  0.6 85.4 %stage0.1 = (bf16[128,512]{1,0:T(8,128)(2,1)}, bf16[128,256]{1,0:T(8,128)(2,1)}, bf16[128,1152]{1,0:T(8,128)(2,1)}, bf16[64,1152]{1,0:T(8,128)(2,1)}, bf16[128,1...) custom-call(bf16[2,256,1024]{2,1,0:T(8,128)(2,1)} %bitcast.15, ...), custom_call_target="tpu_custom_call" | custom-call | tf_op jit(solution)/shard_map/stage0/pallas_call | solution.py:174
  86.1 73.4 %stage1.1 = (bf16[4,128,1152]{2,1,0:T(8,128)(2,1)}, bf16[4,128,1152]{2,1,0:T(8,128)(2,1)}, bf16[4,288,256]{2,1,0:T(8,128)(2,1)}, bf16[4,576,256]{2,1,0:T(8,128)(...) custom-call(bf16[4,128,1152]{2,1,0:T(8,128)(2,1)} %get-tuple-element, ...), custom_call_target="tpu_custom_call" | custom-call | tf_op jit(solution)/shard_map/stage1/pallas_call | solution.py:174
  159.5 63.0 %stage2.1 = (bf16[4,128,1152]{2,1,0:T(8,128)(2,1)}, bf16[4,128,1152]{2,1,0:T(8,128)(2,1)}, bf16[4,576,256]{2,1,0:T(8,128)(2,1)}, bf16[4,576,256]{2,1,0:T(8,128)(...) custom-call(bf16[4,128,1152]{2,1,0:T(8,128)(2,1)} %get-tuple-element, ...), custom_call_target="tpu_custom_call" | custom-call | tf_op jit(solution)/shard_map/stage2/pallas_call | solution.py:174
  222.5 49.0 %stage3.1 = (bf16[1152,1024]{1,0:T(8,128)(2,1)}, bf16[1024,1152]{1,0:T(8,128)(2,1)}, bf16[1024,1152]{1,0:T(8,128)(2,1)}, bf16[1024,1152]{1,0:T(8,128)(2,1)}, f32[256,1024]{1,0:T(8,128)}, /*index=5*/f32[1,1024]{1,0:T(1,128)}) custom-call(f32[256,1024]{1,0:T(8,128)} %get-tuple-element.125.refs_0_.refs_30_, f32[2,1024]{1,0:T(2,128)} %bitcast.36, ...), custom_call_target="tpu_custom_call" | custom-call | tf_op jit(solution)/shard_map/stage3/pallas_call | solution.py:174
  271.5 60.9 %stage4.1 = (bf16[576,1024]{1,0:T(8,128)(2,1)}, bf16[4,128,1152]{2,1,0:T(8,128)(2,1)}, bf16[256,1152]{1,0:T(8,128)(2,1)}, bf16[256,1024]{1,0:T(8,128)(2,1)}, bf1...) custom-call(bf16[1152,1024]{1,0:T(8,128)(2,1)} %get-tuple-element.13, ...), custom_call_target="tpu_custom_call" | custom-call | tf_op jit(solution)/shard_map/stage4/pallas_call | solution.py:174
  332.4 70.4 %stage5.1 = (bf16[128,1152]{1,0:T(8,128)(2,1)}, bf16[256,1152]{1,0:T(8,128)(2,1)}, bf16[128,256]{1,0:T(8,128)(2,1)}, bf16[4,128,512]{2,1,0:T(8,128)(2,1)}, bf16[...) custom-call(bf16[1024,1152]{1,0:T(8,128)(2,1)} %get-tuple-element.13, ...), custom_call_target="tpu_custom_call" | custom-call | tf_op jit(solution)/shard_map/stage5/pallas_call | solution.py:174
  402.8 109.7 %stage6.1 = (bf16[4,128,1152]{2,1,0:T(8,128)(2,1)}, bf16[128,1152]{1,0:T(8,128)(2,1)}, bf16[576,256]{1,0:T(8,128)(2,1)}, bf16[256,1152]{1,0:T(8,128)(2,1)}, bf16...) custom-call(bf16[1024,1152]{1,0:T(8,128)(2,1)} %get-tuple-element.15, ...), custom_call_target="tpu_custom_call" | custom-call | tf_op jit(solution)/shard_map/stage6/pallas_call | solution.py:174
  512.5 4.6 pack.1

commit v18 on v16

--- a/solution.py
+++ b/solution.py
@@ -1528,8 +1528,8 @@
     d_mid0, gain01 = Save(k, s13.out), Save(k, s13.gain_grad)
     k.early += [q_gate1.load, q_down1.load, q_out1.load]
     k.do(r_in1.send, m_up1.send, rows.wait, g12.begin, q_gate1.send, q_down1.send, q_out1.send)
-    k.do(gate_load.wait, up_load.wait, g12.loop, q_gate1.step, q_down1.step, q_out1.step)
-    k.do(hid_load.wait, p_down0.run, p_down0.wait, r_down0.send, r_in1.wait, q_in1.add)
+    k.do(gate_load.wait, up_load.wait, g12.loop, hid_load.wait, p_down0.run)
+    k.do(q_gate1.step, p_down0.wait, r_down0.send, q_down1.step, q_out1.step, r_in1.wait, q_in1.add)
     k.do(s13.loop, q_gate1.step, q_down1.step, q_out1.step)
     k.do(m_load.wait, p_gate0.run, q_in1.step, p_up0.run, value.wait, gain_load.wait)
     k.do(s13.finish, d_mid0.start, gain01.start, q_in1.step, p_gate0.wait, p_up0.wait)

time: 513 us -> 516 us (level)
  no operation moved by 1% of the time
where the time goes in v18:
time: 516 us
  Pallas kernels  515 us (100%)
    pallas_call x7, Pallas kernels, build(): pl.pallas_call(self.body, out_shape=[jax.ShapeDtypeStruct(v.shape, v.dtyp...  510 us

profile of v18, /device:TPU:0, one launch (start us, length us, event | category | flops | bytes accessed | tf_op | source)
XLA Modules:
  0.0 515.8 jit_solution(6876132066332818406)
XLA Ops:
  0.6 85.4 %stage0.1 = (bf16[128,512]{1,0:T(8,128)(2,1)}, bf16[128,256]{1,0:T(8,128)(2,1)}, bf16[128,1152]{1,0:T(8,128)(2,1)}, bf16[64,1152]{1,0:T(8,128)(2,1)}, bf16[128,1...) custom-call(bf16[2,256,1024]{2,1,0:T(8,128)(2,1)} %bitcast.15, ...), custom_call_target="tpu_custom_call" | custom-call | tf_op jit(solution)/shard_map/stage0/pallas_call | solution.py:174
  86.1 73.4 %stage1.1 = (bf16[4,128,1152]{2,1,0:T(8,128)(2,1)}, bf16[4,128,1152]{2,1,0:T(8,128)(2,1)}, bf16[4,288,256]{2,1,0:T(8,128)(2,1)}, bf16[4,576,256]{2,1,0:T(8,128)(...) custom-call(bf16[4,128,1152]{2,1,0:T(8,128)(2,1)} %get-tuple-element, ...), custom_call_target="tpu_custom_call" | custom-call | tf_op jit(solution)/shard_map/stage1/pallas_call | solution.py:174
  159.5 63.0 %stage2.1 = (bf16[4,128,1152]{2,1,0:T(8,128)(2,1)}, bf16[4,128,1152]{2,1,0:T(8,128)(2,1)}, bf16[4,576,256]{2,1,0:T(8,128)(2,1)}, bf16[4,576,256]{2,1,0:T(8,128)(...) custom-call(bf16[4,128,1152]{2,1,0:T(8,128)(2,1)} %get-tuple-element, ...), custom_call_target="tpu_custom_call" | custom-call | tf_op jit(solution)/shard_map/stage2/pallas_call | solution.py:174
  222.5 49.0 %stage3.1 = (bf16[1152,1024]{1,0:T(8,128)(2,1)}, bf16[1024,1152]{1,0:T(8,128)(2,1)}, bf16[1024,1152]{1,0:T(8,128)(2,1)}, bf16[1024,1152]{1,0:T(8,128)(2,1)}, f32[256,1024]{1,0:T(8,128)}, /*index=5*/f32[1,1024]{1,0:T(1,128)}) custom-call(f32[256,1024]{1,0:T(8,128)} %get-tuple-element.125.refs_0_.refs_30_, f32[2,1024]{1,0:T(2,128)} %bitcast.36, ...), custom_call_target="tpu_custom_call" | custom-call | tf_op jit(solution)/shard_map/stage3/pallas_call | solution.py:174
  271.5 60.9 %stage4.1 = (bf16[576,1024]{1,0:T(8,128)(2,1)}, bf16[4,128,1152]{2,1,0:T(8,128)(2,1)}, bf16[256,1152]{1,0:T(8,128)(2,1)}, bf16[256,1024]{1,0:T(8,128)(2,1)}, bf1...) custom-call(bf16[1152,1024]{1,0:T(8,128)(2,1)} %get-tuple-element.13, ...), custom_call_target="tpu_custom_call" | custom-call | tf_op jit(solution)/shard_map/stage4/pallas_call | solution.py:174
  332.4 69.1 %stage5.1 = (bf16[128,1152]{1,0:T(8,128)(2,1)}, bf16[256,1152]{1,0:T(8,128)(2,1)}, bf16[128,256]{1,0:T(8,128)(2,1)}, bf16[4,128,512]{2,1,0:T(8,128)(2,1)}, bf16[...) custom-call(bf16[1024,1152]{1,0:T(8,128)(2,1)} %get-tuple-element.13, ...), custom_call_target="tpu_custom_call" | custom-call | tf_op jit(solution)/shard_map/stage5/pallas_call | solution.py:174
  401.5 109.5 %stage6.1 = (bf16[4,128,1152]{2,1,0:T(8,128)(2,1)}, bf16[128,1152]{1,0:T(8,128)(2,1)}, bf16[576,256]{1,0:T(8,128)(2,1)}, bf16[256,1152]{1,0:T(8,128)(2,1)}, bf16...) custom-call(bf16[1024,1152]{1,0:T(8,128)(2,1)} %get-tuple-element.15, ...), custom_call_target="tpu_custom_call" | custom-call | tf_op jit(solution)/shard_map/stage6/pallas_call | solution.py:174
  511.0 4.6 pack.1

commit v19 on v16

--- a/solution.py
+++ b/solution.py
@@ -1606,10 +1606,9 @@
     k.do(p_in0.run, p_cols.run, p_in0.wait, r_in0.send, p_cols.wait, r_cols.send)
     k.do(r_gate0.wait, q_gate0.add, x_load.wait, gain_load.wait, s15.loop, q_up0.step)
     k.do(q_down0.step, s15.finish, d_x.start, fill_small, d_x.wait, t_x.send)
-    k.do(small_out.wait, t_small.send, q_gate0.step, hid_load.wait, mid_load.wait, s7.loop)
-    k.do(r_out0.wait, q_out0.add, r_in0.wait, q_in0.add)
-    k.do(r_cols.wait, q_cols.add, q_up0.wait, m_up0.send, q_down0.wait, e_down0.add)
-    k.do(s7.finish, y_rows.start, y_rows.wait, t_y.send)
+    k.do(small_out.wait, t_small.send, q_gate0.step, r_out0.wait, q_out0.add, r_in0.wait, q_in0.add)
+    k.do(r_cols.wait, q_cols.add, q_up0.wait, m_up0.send, hid_load.wait, mid_load.wait, s7.loop)
+    k.do(q_down0.wait, e_down0.add, s7.finish, y_rows.start, y_rows.wait, t_y.send)
     k.do(q_gate0.step, q_out0.step, q_in0.step, q_cols.step, t_small.wait, z_small.add)
     k.do(q_gate0.wait, e_gate0.add, q_out0.step, q_in0.step, q_cols.step)
     k.do(z_small.wait, t_total.add, q_out0.wait, e_out0.add, q_in0.wait, e_in0.add)

time: 513 us -> 520 us (1.014)
  Pallas kernels: 512 us -> 518 us
    pallas_call x7, Pallas kernels: 507 us -> 513 us  [build(): pl.pallas_call(self.body, out_shape=[jax.ShapeDtypeStruct(v.shape, v.dtyp...]
where the time goes in v19:
time: 520 us; the launch traced here: 519 us
  Pallas kernels  518 us (100%)
    pallas_call x7, Pallas kernels, build(): pl.pallas_call(self.body, out_shape=[jax.ShapeDtypeStruct(v.shape, v.dtyp...  513 us

profile of v19, /device:TPU:0, one launch (start us, length us, event | category | flops | bytes accessed | tf_op | source)
XLA Modules:
  0.0 518.8 jit_solution(10028328750454184598)
XLA Ops:
  0.6 85.4 %stage0.1 = (bf16[128,512]{1,0:T(8,128)(2,1)}, bf16[128,256]{1,0:T(8,128)(2,1)}, bf16[128,1152]{1,0:T(8,128)(2,1)}, bf16[64,1152]{1,0:T(8,128)(2,1)}, bf16[128,1...) custom-call(bf16[2,256,1024]{2,1,0:T(8,128)(2,1)} %bitcast.15, ...), custom_call_target="tpu_custom_call" | custom-call | tf_op jit(solution)/shard_map/stage0/pallas_call | solution.py:174
  86.1 73.4 %stage1.1 = (bf16[4,128,1152]{2,1,0:T(8,128)(2,1)}, bf16[4,128,1152]{2,1,0:T(8,128)(2,1)}, bf16[4,288,256]{2,1,0:T(8,128)(2,1)}, bf16[4,576,256]{2,1,0:T(8,128)(...) custom-call(bf16[4,128,1152]{2,1,0:T(8,128)(2,1)} %get-tuple-element, ...), custom_call_target="tpu_custom_call" | custom-call | tf_op jit(solution)/shard_map/stage1/pallas_call | solution.py:174
  159.5 63.0 %stage2.1 = (bf16[4,128,1152]{2,1,0:T(8,128)(2,1)}, bf16[4,128,1152]{2,1,0:T(8,128)(2,1)}, bf16[4,576,256]{2,1,0:T(8,128)(2,1)}, bf16[4,576,256]{2,1,0:T(8,128)(...) custom-call(bf16[4,128,1152]{2,1,0:T(8,128)(2,1)} %get-tuple-element, ...), custom_call_target="tpu_custom_call" | custom-call | tf_op jit(solution)/shard_map/stage2/pallas_call | solution.py:174
  222.5 49.0 %stage3.1 = (bf16[1152,1024]{1,0:T(8,128)(2,1)}, bf16[1024,1152]{1,0:T(8,128)(2,1)}, bf16[1024,1152]{1,0:T(8,128)(2,1)}, bf16[1024,1152]{1,0:T(8,128)(2,1)}, f32[256,1024]{1,0:T(8,128)}, /*index=5*/f32[1,1024]{1,0:T(1,128)}) custom-call(f32[256,1024]{1,0:T(8,128)} %get-tuple-element.125.refs_0_.refs_30_, f32[2,1024]{1,0:T(2,128)} %bitcast.36, ...), custom_call_target="tpu_custom_call" | custom-call | tf_op jit(solution)/shard_map/stage3/pallas_call | solution.py:174
  271.5 60.9 %stage4.1 = (bf16[576,1024]{1,0:T(8,128)(2,1)}, bf16[4,128,1152]{2,1,0:T(8,128)(2,1)}, bf16[256,1152]{1,0:T(8,128)(2,1)}, bf16[256,1024]{1,0:T(8,128)(2,1)}, bf1...) custom-call(bf16[1152,1024]{1,0:T(8,128)(2,1)} %get-tuple-element.13, ...), custom_call_target="tpu_custom_call" | custom-call | tf_op jit(solution)/shard_map/stage4/pallas_call | solution.py:174
  332.4 66.0 %stage5.1 = (bf16[128,1152]{1,0:T(8,128)(2,1)}, bf16[256,1152]{1,0:T(8,128)(2,1)}, bf16[128,256]{1,0:T(8,128)(2,1)}, bf16[4,128,512]{2,1,0:T(8,128)(2,1)}, bf16[...) custom-call(bf16[1024,1152]{1,0:T(8,128)(2,1)} %get-tuple-element.13, ...), custom_call_target="tpu_custom_call" | custom-call | tf_op jit(solution)/shard_map/stage5/pallas_call | solution.py:174
  398.4 115.6 %stage6.1 = (bf16[4,128,1152]{2,1,0:T(8,128)(2,1)}, bf16[128,1152]{1,0:T(8,128)(2,1)}, bf16[576,256]{1,0:T(8,128)(2,1)}, bf16[256,1152]{1,0:T(8,128)(2,1)}, bf16...) custom-call(bf16[1024,1152]{1,0:T(8,128)(2,1)} %get-tuple-element.15, ...), custom_call_target="tpu_custom_call" | custom-call | tf_op jit(solution)/shard_map/stage6/pallas_call | solution.py:174
  514.0 4.6 pack.1
